TPU v7x, 32 devices: a whole 2x2x4 slice. The times are simulated.
32 devices in a mesh: expert: 16 (over z, y, x), wshard: 2 (over core).
Axes of the slice: x: 2, y: 2, z: 4, core: 2. Of those that a mesh axis runs over, the one named last changes fastest.
Arguments:
- layer_input: bfloat16 [4096, 2048], P(('expert', 'wshard')), may hold values from -40 to 40
- attn_gain: bfloat16 [2048], P(('expert', 'wshard')), may hold values from 0.5 to 4
- w_query: bfloat16 [2048, 3072], P(('expert', 'wshard')), may hold values from -1 to 1
- w_latent: bfloat16 [2048, 576], P(('expert', 'wshard')), may hold values from -1 to 1
- kv_gain: bfloat16 [512], P(('expert', 'wshard')), may hold values from 0.5 to 1.5
- w_expand: bfloat16 [512, 4096], P(('expert', 'wshard')), may hold values from -2 to 2
- w_output: bfloat16 [2048, 2048], P(('expert', 'wshard')), may hold values from -2 to 2
- ffn_gain: bfloat16 [2048], P(('expert', 'wshard')), may hold values from 0.5 to 4
- w_router: bfloat16 [2048, 16], P(('expert', 'wshard')), may hold values from -3 to 3
- shared_gate: bfloat16 [2048, 2816], P(('expert', 'wshard')), may hold values from -0.125 to 0.125
- shared_up: bfloat16 [2048, 2816], P(('expert', 'wshard')), may hold values from -0.125 to 0.125
- shared_down: bfloat16 [2816, 2048], P(('expert', 'wshard')), may hold values from -0.109375 to 0.109375
- expert_gate: bfloat16 [16, 2048, 1408], P('expert', None, 'wshard'), may hold values from -0.125 to 0.125
- expert_up: bfloat16 [16, 2048, 1408], P('expert', None, 'wshard'), may hold values from -0.125 to 0.125
- expert_down: bfloat16 [16, 1408, 2048], P('expert', 'wshard'), may hold values from -0.875 to 0.875
- routes: int32 [4096, 6], P(('expert', 'wshard')), may hold values from 0 to 15, all different within a row; in each aligned block of 128 rows (0 to 127, 128 to 255, ...) at most 96 rows name the same one
- segments: int32 [4096], P(('expert', 'wshard')), may hold values from 0 to 7, never falling along the last dimension, each value on 1 to 1024 neighbouring positions
- cotangent: bfloat16 [4096, 2048], P(('expert', 'wshard')), may hold values from -6 to 6
Outputs:
- layer_output: float32 [4096, 2048], P(('expert', 'wshard'))
- grad_x: float32 [4096, 2048], P(('expert', 'wshard'))
- grad_attn_gain: float32 [2048], P(('expert', 'wshard'))
- grad_w_query: float32 [2048, 3072], P(('expert', 'wshard'))
- grad_w_latent: float32 [2048, 576], P(('expert', 'wshard'))
- grad_kv_gain: float32 [512], P(('expert', 'wshard'))
- grad_w_expand: float32 [512, 4096], P(('expert', 'wshard'))
- grad_w_output: float32 [2048, 2048], P(('expert', 'wshard'))
- grad_ffn_gain: float32 [2048], P(('expert', 'wshard'))
- grad_w_router: float32 [2048, 16], P(('expert', 'wshard'))
- grad_shared_gate: float32 [2048, 2816], P(('expert', 'wshard'))
- grad_shared_up: float32 [2048, 2816], P(('expert', 'wshard'))
- grad_shared_down: float32 [2816, 2048], P(('expert', 'wshard'))
- grad_expert_gate: float32 [16, 2048, 1408], P('expert', None, 'wshard')
- grad_expert_up: float32 [16, 2048, 1408], P('expert', None, 'wshard')
- grad_expert_down: float32 [16, 1408, 2048], P('expert', 'wshard')
Inputs may be any that keep to these rules, and one draw needn't show every extreme that they name: `routes`: each row names 6 different experts. Among the 128 rows of one device (aligned blocks) no expert is named by more than 96 rows, a bound that some block reaches. `segments`: document numbers never fall along the tokens; each document holds 1 to 1024 consecutive tokens and one holds exactly 1024.
All inputs are finite; a program needn't handle non-finite values.
Results may differ from a plain program's by a relative error of at most 0.025.
The roundings to bfloat16 on the way count: a program that leaves them out, or rounds other values in their place, can miss the bound.
Values may be sent and summed in bfloat16 or wider, within the bound.
A program may use at most 448 MiB of HBM per device.

v0:
```python
import functools

import jax
import jax.numpy as jnp
from jax import lax
from jax.experimental import pallas as pl
from jax.experimental.pallas import tpu as pltpu
from jax.sharding import Mesh, PartitionSpec as P

HEADS = 16
NOPE = 128
ROPE = 64
VDIM = 128
RANK = 512
TOP = 6
DOC_MAX = 1024
QUERY_BLOCK = 256

BF = jnp.bfloat16
F32 = jnp.float32
ALL = ("g", "p", "c")
PLANE = ("p", "c")

epsilon = 1e-06


def rms_norm(vector, scaling):
    return vector * lax.rsqrt(jnp.mean(vector * vector, axis=-1, keepdims=True) + epsilon) * scaling


def rotate(vector, cosine, sine_part):
    half_width = vector.shape[-1] // 2
    front_half = vector[..., :half_width]
    back_half = vector[..., half_width:]
    return jnp.concatenate(
        [front_half * cosine - back_half * sine_part, back_half * cosine + front_half * sine_part],
        axis=-1,
    )


def unrotate(vector, cosine, sine_part):
    return rotate(vector, cosine, -sine_part)


def matmul(left, right):
    return jnp.dot(left, right, preferred_element_type=F32)


def dot_nt(left, right):
    return lax.dot_general(left, right, (((1,), (1,)), ((), ())), preferred_element_type=F32)


def dot_tn(left, right):
    return lax.dot_general(left, right, (((0,), (0,)), ((), ())), preferred_element_type=F32)


def swiglu(gate_pre, up_pre):
    return jax.nn.silu(gate_pre) * up_pre


def softmax_rows(scores):
    row_top = jnp.max(scores, axis=-1, keepdims=True)
    exp_scores = jnp.exp(scores - row_top)
    return exp_scores / jnp.sum(exp_scores, axis=-1, keepdims=True)


def masked_scores(base, low_bound, q_nope, q_rope, k_nope, k_rope, scale):
    rows, span = q_nope.shape[0], k_nope.shape[0]
    key_at = lax.broadcasted_iota(jnp.int32, (rows, span), 1) + base
    query_at = lax.broadcasted_iota(jnp.int32, (rows, span), 0) + (base + DOC_MAX)
    allowed = (key_at >= low_bound) & (key_at <= query_at)
    scores = (dot_nt(q_nope, k_nope) + dot_nt(q_rope, k_rope)) * scale
    return jnp.where(allowed, scores, -1e30)


def attend_kernel(heads, scale, low_ref, qn_ref, qr_ref, ex_ref, kr_ref, out_ref, lse_ref):
    rows = qn_ref.shape[0]
    base = pl.multiple_of(pl.program_id(0) * rows, rows)
    window = pl.ds(base, rows + DOC_MAX)
    k_rope = kr_ref[window, :]
    low_bound = low_ref[...]
    for h in range(heads):
        at = h * (NOPE + VDIM)
        k_nope = ex_ref[window, at : at + NOPE]
        value = ex_ref[window, at + NOPE : at + NOPE + VDIM]
        scores = masked_scores(
            base,
            low_bound,
            qn_ref[:, h * NOPE : (h + 1) * NOPE],
            qr_ref[:, h * ROPE : (h + 1) * ROPE],
            k_nope,
            k_rope,
            scale,
        )
        top = jnp.max(scores, axis=-1, keepdims=True)
        exps = jnp.exp(scores - top)
        total = jnp.sum(exps, axis=-1, keepdims=True)
        probs = (exps / total).astype(BF)
        out_ref[:, h * VDIM : (h + 1) * VDIM] = jnp.dot(
            probs, value, preferred_element_type=F32
        ).astype(BF)
        lse_ref[:, h : h + 1] = top + jnp.log(total)


def attend(low_bound, q_nope, q_rope, expanded, key_rope, scale):
    queries = q_nope.shape[0]
    heads = q_nope.shape[1] // NOPE
    rows = QUERY_BLOCK

    def whole(array):
        return pl.BlockSpec(array.shape, lambda i: (0, 0))

    def blocked(width):
        return pl.BlockSpec((rows, width), lambda i: (i, 0))

    flops = 2 * heads * queries * (rows + DOC_MAX) * (NOPE + ROPE + VDIM)
    return pl.pallas_call(
        functools.partial(attend_kernel, heads, scale),
        grid=(queries // rows,),
        in_specs=[
            blocked(1),
            blocked(heads * NOPE),
            blocked(heads * ROPE),
            whole(expanded),
            whole(key_rope),
        ],
        out_specs=[blocked(heads * VDIM), blocked(heads)],
        out_shape=[
            jax.ShapeDtypeStruct((queries, heads * VDIM), BF),
            jax.ShapeDtypeStruct((queries, heads), F32),
        ],
        cost_estimate=pl.CostEstimate(
            flops=flops, bytes_accessed=4 * expanded.size, transcendentals=flops // 640
        ),
        compiler_params=pltpu.CompilerParams(vmem_limit_bytes=50 * 1024 * 1024),
        name="attend",
    )(low_bound, q_nope, q_rope, expanded, key_rope)


def attend_back_kernel(
    heads, scale, low_ref, qn_ref, qr_ref, ex_ref, kr_ref, lse_ref, gm_ref,
    dqn_ref, dqr_ref, dex_ref, dkr_ref,
):
    rows = qn_ref.shape[0]
    step = pl.program_id(0)
    base = pl.multiple_of(step * rows, rows)
    window = pl.ds(base, rows + DOC_MAX)

    @pl.when(step == 0)
    def _():
        dex_ref[...] = jnp.zeros_like(dex_ref)
        dkr_ref[...] = jnp.zeros_like(dkr_ref)

    k_rope = kr_ref[window, :]
    low_bound = low_ref[...]
    for h in range(heads):
        at = h * (NOPE + VDIM)
        k_nope = ex_ref[window, at : at + NOPE]
        value = ex_ref[window, at + NOPE : at + NOPE + VDIM]
        q_nope = qn_ref[:, h * NOPE : (h + 1) * NOPE]
        q_rope = qr_ref[:, h * ROPE : (h + 1) * ROPE]
        grad_out = gm_ref[:, h * VDIM : (h + 1) * VDIM]
        scores = masked_scores(base, low_bound, q_nope, q_rope, k_nope, k_rope, scale)
        probs = jnp.exp(scores - lse_ref[:, h : h + 1])
        grad_probs = dot_nt(grad_out, value)
        mean_grad = jnp.sum(probs * grad_probs, axis=-1, keepdims=True)
        grad_scores = (probs * (grad_probs - mean_grad) * scale).astype(BF)
        probs_low = probs.astype(BF)
        dqn_ref[:, h * NOPE : (h + 1) * NOPE] = jnp.dot(
            grad_scores, k_nope, preferred_element_type=F32
        )
        dqr_ref[:, h * ROPE : (h + 1) * ROPE] = jnp.dot(
            grad_scores, k_rope, preferred_element_type=F32
        )
        dex_ref[window, at : at + NOPE] += dot_tn(grad_scores, q_nope)
        dex_ref[window, at + NOPE : at + NOPE + VDIM] += dot_tn(probs_low, grad_out)
        dkr_ref[window, :] += dot_tn(grad_scores, q_rope)


def attend_back(low_bound, q_nope, q_rope, expanded, key_rope, lse, grad_mixed, scale):
    queries = q_nope.shape[0]
    heads = q_nope.shape[1] // NOPE
    rows = QUERY_BLOCK

    def whole(shape):
        return pl.BlockSpec(shape, lambda i: (0, 0))

    def blocked(width):
        return pl.BlockSpec((rows, width), lambda i: (i, 0))

    flops = 2 * heads * queries * (rows + DOC_MAX) * (3 * NOPE + 3 * ROPE + 2 * VDIM)
    return pl.pallas_call(
        functools.partial(attend_back_kernel, heads, scale),
        grid=(queries // rows,),
        in_specs=[
            blocked(1),
            blocked(heads * NOPE),
            blocked(heads * ROPE),
            whole(expanded.shape),
            whole(key_rope.shape),
            blocked(heads),
            blocked(heads * VDIM),
        ],
        out_specs=[
            blocked(heads * NOPE),
            blocked(heads * ROPE),
            whole(expanded.shape),
            whole(key_rope.shape),
        ],
        out_shape=[
            jax.ShapeDtypeStruct(q_nope.shape, F32),
            jax.ShapeDtypeStruct(q_rope.shape, F32),
            jax.ShapeDtypeStruct(expanded.shape, F32),
            jax.ShapeDtypeStruct(key_rope.shape, F32),
        ],
        cost_estimate=pl.CostEstimate(
            flops=flops, bytes_accessed=8 * expanded.size, transcendentals=flops // 1664
        ),
        compiler_params=pltpu.CompilerParams(vmem_limit_bytes=56 * 1024 * 1024),
        name="attend_back",
    )(low_bound, q_nope, q_rope, expanded, key_rope, lse, grad_mixed)


def gather_all(x):
    return lax.all_gather(x, ALL, axis=0, tiled=True)


def experts_chunk(h2, cot, weight, slots, expert_w, shared_w):
    w_gate, w_up, w_down = expert_w
    s_both, s_down = shared_w
    blocks, rows, width = h2.shape
    per_block = slots.shape[1]
    hidden_s = s_down.shape[0]
    flat_h2 = h2.reshape(blocks * rows, width)
    flat_cot = cot.reshape(blocks * rows, width)

    def pick(table):
        return (
            jnp.einsum("bst,btd->bsd", slots, table, preferred_element_type=F32)
            .astype(BF)
            .reshape(blocks * per_block, width)
        )

    def place(table):
        return jnp.einsum(
            "bst,bsd->btd",
            slots,
            table.astype(BF).reshape(blocks, per_block, width),
            preferred_element_type=F32,
        ).reshape(blocks * rows, width)

    cot_rows = pick(cot)
    back_act = dot_nt(cot_rows, w_down)
    shared_back = dot_nt(flat_cot, s_down)
    row_weight = jnp.sum(slots.astype(F32) * weight[:, None, :], axis=2).reshape(-1, 1)
    rows_in = pick(h2)
    gate_pre = matmul(rows_in, w_gate)
    up_pre = matmul(rows_in, w_up)
    act, act_vjp = jax.vjp(swiglu, gate_pre, up_pre)
    act_low = act.astype(BF)
    grad_gate, grad_up = act_vjp(back_act * row_weight)
    grad_gate = grad_gate.astype(BF)
    grad_up = grad_up.astype(BF)
    picked_grad = jnp.sum(act_low.astype(F32) * back_act, axis=1).reshape(blocks, per_block, 1)
    token_grad = jnp.sum(slots.astype(F32) * picked_grad, axis=1)
    grad_rows = dot_nt(grad_gate, w_gate) + dot_nt(grad_up, w_up)

    shared_pre = matmul(flat_h2, s_both)
    s_act, s_vjp = jax.vjp(swiglu, shared_pre[:, :hidden_s], shared_pre[:, hidden_s:])
    s_act = s_act.astype(BF)
    s_grad = jnp.concatenate(s_vjp(shared_back), axis=1).astype(BF)
    grad_h2 = (place(grad_rows) + dot_nt(s_grad, s_both)).astype(BF)

    out_rows = matmul(act_low, w_down) * row_weight
    out = (place(out_rows) + matmul(s_act, s_down)).astype(BF)

    grad_in = (cot_rows.astype(F32) * row_weight).astype(BF)
    grads = (
        dot_tn(rows_in, grad_gate),
        dot_tn(rows_in, grad_up),
        dot_tn(act_low, grad_in),
        dot_tn(flat_h2, s_grad),
        dot_tn(s_act, flat_cot),
    )
    return out, grad_h2, token_grad, grads


def body(
    n_groups, n_plane, layer_input, attn_gain, w_query, w_latent, kv_gain, w_expand, w_output,
    ffn_gain, w_router, shared_gate, shared_up, shared_down, expert_gate, expert_up,
    expert_down, routes, segments, cotangent,
):
    tok, width = layer_input.shape
    devices = n_groups * n_plane
    experts = w_router.shape[1]
    local_heads = HEADS // n_plane
    scale = (NOPE + ROPE) ** (-0.5)
    group = lax.axis_index("g")
    place_in = lax.axis_index(PLANE)
    me = lax.axis_index(ALL)
    expert_id = lax.axis_index(("g", "p"))
    plane_tok = n_plane * tok
    plane_start = group * plane_tok

    rows_w = w_router.shape[0]
    kv_n = kv_gain.shape[0]
    small = jnp.concatenate([attn_gain, ffn_gain, kv_gain, w_router.reshape(-1)])
    small = gather_all(small[None, :])
    gain_one = small[:, :rows_w].reshape(-1).astype(F32)
    gain_two = small[:, rows_w : 2 * rows_w].reshape(-1).astype(F32)
    gain_kv = small[:, 2 * rows_w : 2 * rows_w + kv_n].reshape(-1).astype(F32)
    router_weight = small[:, 2 * rows_w + kv_n :].reshape(width, experts)
    ints = gather_all(jnp.concatenate([routes.reshape(-1), segments])[None, :])
    routes_all = ints[:, : tok * TOP].reshape(devices, tok, TOP)
    segments_all = ints[:, tok * TOP :].reshape(-1)

    x_plane = lax.all_gather(layer_input, PLANE, axis=0, tiled=True).astype(F32)

    def to_heads(weight):
        rows, cols = weight.shape
        split = weight.reshape(rows, n_plane, cols // n_plane)
        mine = lax.all_to_all(split, PLANE, split_axis=1, concat_axis=0)
        mine = mine.reshape(n_plane * rows, cols // n_plane)
        return lax.all_gather(mine, "g", axis=0, tiled=True)

    query_weight = to_heads(w_query).reshape(width, local_heads, NOPE + ROPE)
    wq_nope = query_weight[:, :, :NOPE].reshape(width, local_heads * NOPE)
    wq_rope = query_weight[:, :, NOPE:].reshape(width, local_heads * ROPE)
    expand_weight = to_heads(w_expand)
    latent_weight = gather_all(w_latent)
    output_weight = gather_all(w_output)

    shared_n = shared_down.shape[0]
    s_both = jnp.concatenate(
        [
            shared_gate.reshape(rows_w, devices, shared_n),
            shared_up.reshape(rows_w, devices, shared_n),
        ],
        axis=2,
    )
    s_both = lax.all_to_all(s_both, ALL, split_axis=1, concat_axis=0).reshape(width, 2 * shared_n)

    hidden = rms_norm(x_plane, gain_one).astype(BF)
    rope_half = ROPE // 2
    positions = plane_start + jnp.arange(plane_tok, dtype=jnp.int32)
    frequency = 10000.0 ** (-jnp.arange(rope_half, dtype=F32) / rope_half)
    angles = positions.astype(F32)[:, None] * frequency[None, :]
    cosine = jnp.cos(angles)
    sine_part = jnp.sin(angles)
    cos_h, sin_h = cosine[:, None, :], sine_part[:, None, :]
    latent = matmul(hidden, latent_weight)
    compressed_own = rms_norm(latent[:, :RANK], gain_kv).astype(BF)
    key_rope_own = rotate(latent[:, RANK:], cosine, sine_part).astype(BF)

    def own_rows(table):
        return lax.dynamic_slice_in_dim(table, place_in * tok, tok, 0)

    up_pairs = [(i, i + 1) for i in range(n_groups - 1)]
    down_pairs = [(i + 1, i) for i in range(n_groups - 1)]
    piece = own_rows(jnp.concatenate([compressed_own, key_rope_own], axis=1))
    before = lax.ppermute(piece, "g", up_pairs)
    before = lax.all_gather(before, PLANE, axis=0, tiled=True)
    compressed = jnp.concatenate([before[:, :RANK], compressed_own], axis=0)
    key_rope = jnp.concatenate([before[:, RANK:], key_rope_own], axis=0)
    q_nope = matmul(hidden, wq_nope).astype(BF)
    q_rope = rotate(
        matmul(hidden, wq_rope).reshape(plane_tok, local_heads, ROPE), cos_h, sin_h
    ).reshape(plane_tok, local_heads * ROPE).astype(BF)
    expanded = matmul(compressed, expand_weight).astype(BF)
    plane_segments = lax.dynamic_slice_in_dim(segments_all, plane_start, plane_tok, 0)
    doc_start = jnp.sum(
        (segments_all[None, :] < plane_segments[:, None]).astype(jnp.int32), axis=1, keepdims=True
    )
    low_bound = doc_start - plane_start + DOC_MAX
    mixed_heads, lse = attend(low_bound, q_nope, q_rope, expanded, key_rope, scale)
    mixed = lax.all_to_all(mixed_heads, PLANE, split_axis=0, concat_axis=1, tiled=True)

    input_float = layer_input.astype(F32)
    residual_one = input_float + matmul(mixed, output_weight)
    h_two_f, norm_two_back = jax.vjp(rms_norm, residual_one, gain_two)
    h_two = h_two_f.astype(BF)
    router_probs = softmax_rows(matmul(h_two, router_weight))

    expert_w = (expert_gate[0], expert_up[0], expert_down[0])
    shared_w = (s_both, shared_down)
    slot_limit = 2 * tok * TOP // experts

    def scatter_all(x):
        return lax.psum_scatter(x, ALL, scatter_dimension=0, tiled=True)

    def on_rows(h2, probs, cot_gathered, routes_here):
        rows = h2.shape[0]
        h2_all = gather_all(h2).reshape(devices, rows, width)
        probs_all = gather_all(probs.T[None])
        weight_all = lax.dynamic_index_in_dim(probs_all, expert_id, 1, keepdims=False)
        slot_count = min(slot_limit, rows)
        member = jnp.any(routes_here == expert_id, axis=2)
        member_int = member.astype(jnp.int32)
        rank = jnp.cumsum(member_int, axis=1) - member_int
        slots = (
            (rank[:, None, :] == jnp.arange(slot_count, dtype=jnp.int32)[None, :, None])
            & member[:, None, :]
        ).astype(BF)
        out, grad_h2, token_grad, grads = experts_chunk(
            h2_all, cot_gathered, weight_all, slots, expert_w, shared_w
        )
        table = (jnp.arange(experts, dtype=jnp.int32) == expert_id).astype(F32)
        picked = scatter_all((token_grad[:, None, :] * table[None, :, None]).reshape(devices, -1))
        picked = picked.reshape(experts, rows).T
        return scatter_all(out), scatter_all(grad_h2), picked, grads

    parts = max(1, devices * tok // 4096)
    if parts == 1:
        cot_all = gather_all(cotangent).reshape(devices, tok, width)
        out_own, grad_h2_own, grad_router_probs, grads = on_rows(
            h_two, router_probs, cot_all, routes_all
        )
    else:
        rows = tok // parts

        def step(total, inputs):
            h2, probs, cot, routes_here = inputs
            cot_part = gather_all(cot).reshape(devices, rows, width)
            out, grad_h2, picked, grads = on_rows(h2, probs, cot_part, routes_here)
            total = tuple(a + b for a, b in zip(total, grads))
            return total, (out, grad_h2, picked)

        shapes = expert_w + shared_w
        grads, (out_own, grad_h2_own, grad_router_probs) = lax.scan(
            step,
            tuple(jnp.zeros(s.shape, F32) for s in shapes),
            (
                h_two.reshape(parts, rows, width),
                router_probs.reshape(parts, rows, experts),
                cotangent.reshape(parts, rows, width),
                routes_all.reshape(devices, parts, rows, TOP).transpose(1, 0, 2, 3),
            ),
        )
        out_own = out_own.reshape(tok, width)
        grad_h2_own = grad_h2_own.reshape(tok, width)
        grad_router_probs = grad_router_probs.reshape(tok, experts)
    g_gate, g_up, g_down, g_both, g_sdown = grads
    grad_logits = router_probs * (
        grad_router_probs - jnp.sum(router_probs * grad_router_probs, axis=1, keepdims=True)
    )
    grad_logits = grad_logits.astype(BF)
    grad_router = dot_tn(h_two, grad_logits)
    grad_h_two = grad_h2_own.astype(F32) + dot_nt(grad_logits, router_weight)
    output = residual_one + out_own.astype(F32)

    grad_x_one, grad_gain_two = norm_two_back(grad_h_two)
    grad_x_one = grad_x_one + cotangent.astype(F32)
    grad_attn_out = grad_x_one.astype(BF)
    grad_mixed = dot_nt(grad_attn_out, output_weight).astype(BF)
    grad_mixed = lax.all_to_all(grad_mixed, PLANE, split_axis=1, concat_axis=0, tiled=True)
    dqn, dqr, dex, dkr = attend_back(
        low_bound, q_nope, q_rope, expanded, key_rope, lse, grad_mixed, scale
    )

    def own_columns(table):
        rows = table.shape[0]
        split = table.reshape(rows, n_groups, n_plane, rows_w)
        mine = lax.dynamic_index_in_dim(split, place_in, 2, keepdims=False)
        return mine.reshape(rows, n_groups * rows_w)

    def scatter_groups(partial):
        return lax.psum_scatter(partial.astype(BF), "g", scatter_dimension=0, tiled=True)

    mixed_split = mixed.reshape(tok, n_groups, n_plane, rows_w).transpose(0, 2, 1, 3)
    mixed_cols = lax.all_to_all(mixed_split, PLANE, split_axis=1, concat_axis=0)
    mixed_cols = mixed_cols.reshape(plane_tok, n_groups * rows_w)
    plane_grad = lax.all_gather(grad_attn_out, PLANE, axis=0, tiled=True)
    grad_output_weight = scatter_groups(dot_tn(mixed_cols, plane_grad)).astype(F32)

    grad_expanded = dex.astype(BF)
    grad_expand = dot_tn(compressed, grad_expanded)
    grad_comp = dot_nt(grad_expanded, expand_weight)
    key_grads = jnp.concatenate([grad_comp, dkr], axis=1).astype(BF)
    key_grads = key_grads.reshape(2, n_plane, tok, RANK + ROPE).transpose(1, 0, 2, 3)
    key_grads = lax.psum_scatter(key_grads, PLANE, scatter_dimension=0, tiled=False)
    later = lax.ppermute(key_grads[0], "g", down_pairs).astype(F32)
    key_grad = key_grads[1].astype(F32) + later
    latent_own = own_rows(latent)
    kv_norm_back = jax.vjp(rms_norm, latent_own[:, :RANK], gain_kv)[1]
    grad_comp_in, grad_gain_kv = kv_norm_back(key_grad[:, :RANK])
    grad_rope_in = unrotate(key_grad[:, RANK:], own_rows(cosine), own_rows(sine_part))
    grad_latent = jnp.concatenate([grad_comp_in, grad_rope_in], axis=1).astype(BF)

    gq_nope = dqn.astype(BF)
    gq_rope = (
        unrotate(dqr.reshape(plane_tok, local_heads, ROPE), cos_h, sin_h)
        .reshape(plane_tok, local_heads * ROPE)
        .astype(BF)
    )
    grad_hidden_q = (dot_nt(gq_nope, wq_nope) + dot_nt(gq_rope, wq_rope)).astype(BF)
    grad_hidden = lax.psum_scatter(grad_hidden_q, PLANE, scatter_dimension=0, tiled=True)
    g_query = jnp.concatenate(
        [
            dot_tn(hidden, gq_nope).reshape(width, local_heads, NOPE),
            dot_tn(hidden, gq_rope).reshape(width, local_heads, ROPE),
        ],
        axis=2,
    ).reshape(width, local_heads * (NOPE + ROPE))

    def from_heads(partial):
        mine = scatter_groups(partial)
        rows, cols = mine.shape
        split = mine.reshape(n_plane, rows // n_plane, cols)
        full = lax.all_to_all(split, PLANE, split_axis=0, concat_axis=1)
        return full.reshape(rows // n_plane, n_plane * cols).astype(F32)

    grad_query_weight = from_heads(g_query)
    grad_expand_weight = from_heads(grad_expand)

    latent_grads = lax.all_gather(grad_latent, PLANE, axis=0, tiled=True)
    grad_latent_weight = scatter_groups(dot_tn(own_columns(hidden), latent_grads)).astype(F32)

    grad_hidden = grad_hidden.astype(F32) + dot_nt(grad_latent, latent_weight)
    norm_one_back = jax.vjp(rms_norm, input_float, gain_one)[1]
    grad_x_norm, grad_gain_one = norm_one_back(grad_hidden)
    grad_input = grad_x_one + grad_x_norm

    small_grads = jnp.concatenate(
        [
            grad_gain_one.reshape(devices, rows_w),
            grad_gain_two.reshape(devices, rows_w),
            grad_gain_kv.reshape(devices, kv_n),
            grad_router.reshape(devices, rows_w * experts),
        ],
        axis=1,
    )
    small_grads = scatter_all(small_grads)[0]
    g_shared = lax.all_to_all(
        g_both.reshape(devices, rows_w, 2 * shared_n), ALL, split_axis=0, concat_axis=1
    )
    grad_shared_gate = g_shared[:, :, :shared_n].reshape(rows_w, devices * shared_n)
    grad_shared_up = g_shared[:, :, shared_n:].reshape(rows_w, devices * shared_n)
    return (
        output,
        grad_input,
        small_grads[:rows_w],
        grad_query_weight,
        grad_latent_weight,
        small_grads[2 * rows_w : 2 * rows_w + kv_n],
        grad_expand_weight,
        grad_output_weight,
        small_grads[rows_w : 2 * rows_w],
        small_grads[2 * rows_w + kv_n :].reshape(rows_w, experts),
        grad_shared_gate,
        grad_shared_up,
        g_sdown,
        g_gate[None],
        g_up[None],
        g_down[None],
    )


def solution(mesh):
    n_expert, n_shard = mesh.shape["expert"], mesh.shape["wshard"]
    devices = n_expert * n_shard

    def program(*args):
        tok = args[0].shape[0] // devices
        n_plane = DOC_MAX // tok
        n_groups = devices // n_plane
        inner = Mesh(mesh.devices.reshape(n_groups, n_plane // n_shard, n_shard), ALL)
        rows, vector = P(ALL, None), P(ALL)
        wide, tall = P(("g", "p"), None, "c"), P(("g", "p"), "c", None)
        step = jax.shard_map(
            functools.partial(body, n_groups, n_plane),
            mesh=inner,
            in_specs=(
                rows, vector, rows, rows, vector, rows, rows, vector, rows, rows, rows, rows,
                wide, wide, tall, rows, vector, rows,
            ),
            out_specs=(
                rows, rows, vector, rows, rows, vector, rows, rows, vector, rows, rows, rows,
                rows, wide, wide, tall,
            ),
            check_vma=False,
        )
        return step(*args)

    return program
```

profile of v0, /device:TPU:1, one launch (start us, length us, event | category | flops | bytes accessed | tf_op | source)
XLA Modules:
  0.0 1480.2 jit_solution(4241566347353738990)
XLA Ops:
  16.7 5.2 all-to-all-start
  21.9 121.6 %all-reduce.7.cloned.1.call-done = bf16[37376]{0:T(1024)(128)(2,1)} async-done(((bf16[37376]{0:T(1024)(128)(2,1)}), bf16[37376]{0:T(1024)(128)(2,1)}) %all-reduce.7.cloned.1.call-update) | async-done | bytes 74768
  151.7 6.1 fusion.99
  164.1 6.0 collective-permute-done
  173.0 8.6 all-to-all-start.1
  182.0 46.5 %all-gather.3 = s32[32,1,896]{2,1,0:T(1,128)S(1)} all-gather(s32[1,1,896]{2,1,0:T(1,128)S(1)} %reshape.445), channel_id=2, replica_groups=mesh['g'=4,'p'=4,'c'=2] {'g','p','c'}, dimensions={0}, use_global_device_ids=true | all-gather | bytes 118272 | tf_op jit(solution)/shard_map/all_gather | solution.py:225
  231.8 15.0 %all_gather.45 = bf16[512,512]{1,0:T(8,128)(2,1)} all-gather(bf16[128,512]{1,0:T(8,128)(2,1)S(1)} %bitcast.285), channel_id=1, replica_groups=mesh['g'=4,'p'=4,'c'=2] {'g'}, dimensions={0}, use_global_device_ids=true | all-gather | bytes 655360 | tf_op jit(solution)/shard_map/all_gather | solution.py:324
  273.4 11.2 attend.1
  288.3 6.2 all-to-all-start.2
  294.5 6.7 all-to-all-done.2
  317.8 6.1 all-to-all-start.3
  330.8 63.5 %all-gather.2 = f32[512,128]{1,0:T(8,128)S(1)} all-gather(f32[16,128]{1,0:T(8,128)S(1)} %fusion.93), channel_id=4, replica_groups=mesh['g'=4,'p'=4,'c'=2] {'g','p','c'}, dimensions={0}, use_global_device_ids=true | all-gather | bytes 270336 | tf_op jit(solution)/shard_map/all_gather | solution.py:225
  394.2 38.0 %all-gather.26.cloned.1.call-done = bf16[4096,2048]{1,0:T(8,128)(2,1)} async-done(((bf16[128,2048]{1,0:T(8,128)(2,1)}), bf16[4096,2048]{1,0:T(8,128)(2,1)}) %all-gather.26.cloned.1.call-update) | async-done | bytes 16777232 | tf_op jit(solution)/shard_map/all_gather | solution.py:225
  432.2 13.7 convolution_convert_fusion
  446.0 101.6 %all-gather.24.cloned.1.call-done = bf16[4096,2048]{1,0:T(8,128)(2,1)} async-done(((bf16[128,2048]{1,0:T(8,128)(2,1)}), bf16[4096,2048]{1,0:T(8,128)(2,1)}) %all-gather.24.cloned.1.call-update) | async-done | bytes 16777232 | tf_op jit(solution)/shard_map/all_gather | solution.py:225
  547.6 13.8 convolution_convert_fusion.1
  561.4 15.8 %fusion.21 = f32[3072,704]{0,1:T(8,128)} fusion(bf16[3072,2048]{1,0:T(8,128)(2,1)} %bitcast.255, bf16[1,2048,704]{1,2,0:T(8,128)(2,1)} %param.31), kind=kOutput, calls=%fused_computation.41 | convolution fusion | flops 8858370048 | bytes 24117248 | tf_op jit(solution)/shard_map/dot_general | solution.py:46
  577.2 11.5 fusion.25
  588.7 20.5 %multiply_reduce_fusion = (f32[3072]{0:T(1024)S(1)}, bf16[3072,704]{0,1:T(8,128)(2,1)}, f32[3072,704]{0,1:T(8,128)}) fusion(f32[3072,704]{0,1:T(8,128)} %fusion.21, f32[3072,704]{0,1:T(8,128)} %fusion.25, bf16[3072,2048]{1,0:T(8,128)(2,1)} %bitcast.253, bf16[1,704,2048]{2,1,0:T(8,128)(2,1)S(1)} %copy-done), kind=kOutput, calls=%fused_computation.16 | convolution fusion | flops 8877831168 | bytes 45756416 | tf_op jit(solution)/shard_map/dot_general | solution.py:50
  611.6 12.5 multiply_convert_fusion.3
  624.1 13.6 fusion.23
  637.7 19.3 %add_convert_fusion = bf16[3072,2048]{1,0:T(8,128)(2,1)} fusion(f32[3072,2048]{1,0:T(8,128)} %fusion.23, bf16[3072,704]{0,1:T(8,128)(2,1)} %get-tuple-element.134, bf16[1,2048,704]{1,2,0:T(8,128)(2,1)} %param.31), kind=kOutput, calls=%fused_computation.5 | convolution fusion | flops 8870952960 | bytes 44957696 | tf_op jit(solution)/shard_map/dot_general | solution.py:50
  657.0 20.3 %fusion.33 = f32[32,128,2048]{2,1,0:T(8,128)} fusion(bf16[32,96,2048]{2,1,0:T(8,128)(2,1)} %bitcast.262, s32[32,128]{1,0:T(8,128)S(1)} %convert_subtract_fusion, pred[32,128]{1,0:T(8,128)(4,1)S(1)} %copy.258), kind=kOutput, calls=%fused_computation.73 | convolution fusion | flops 1611399168 | bytes 46157824 | tf_op jit(solution)/shard_map/bst,bsd->btd/dot_general | solution.py:245
  677.3 13.5 fusion.100
  690.7 13.1 fusion.42
  705.0 19.4 %fusion = bf16[4096,2048]{1,0:T(8,128)(2,1)} fusion(f32[32,128,2048]{2,1,0:T(8,128)} %fusion.33, bf16[2048,176]{1,0:T(8,128)(2,1)} %bitcast.31, bf16[4096,88]{0,1:T(8,128)(2,1)S(1)} %get-tuple-element.137, bf16[4096,88]{0,1:T(8,128)(2,1)S(1)} %get-tuple-element.136), kind=kOutput, calls=%fused_computation.1 | convolution fusion | flops 2972450816 | bytes 52494336 | tf_op jit(solution)/shard_map/dot_general | solution.py:50
  724.5 10.7 all-reduce.9.cloned.1.call-done
  736.2 184.6 %reduce-scatter.11.cloned.1.call-done = bf16[128,2048]{1,0:T(8,128)(2,1)} async-done(((bf16[4096,2048]{1,0:T(8,128)(2,1)}), bf16[128,2048]{1,0:T(8,128)(2,1)}) %reduce-scatter.11.cloned.1.call-update) | async-done | bytes 524304 | tf_op jit(solution)/shard_map/reduce_scatter | solution.py:389
  926.8 6.4 convolution_convert_fusion.6
  933.3 11.9 all_to_all.131
  945.2 20.6 %attend_back.1 = (f32[1024,256]{1,0:T(8,128)}, f32[1024,128]{1,0:T(8,128)}, f32[2048,512]{1,0:T(8,128)}, f32[2048,64]{1,0:T(8,128)}) custom-call(s32[1024,1]{1,0:T(8,128)} %copy-done.1, bf16[1024,256]{1,0:T(8,128)(2,1)} %convolution_convert_fusion.7.qn_ref, bf16[1024,128]{1,0:T(8,128)(2,1)} %copy.255.qr_ref, ...), custom_call_target="tpu_custom_call" | custom-call | flops 4362076160 | bytes 8388608 | tf_op jit(solution)/shard_map/attend_back/pallas_call | solution.py:192
  974.0 42.5 %reduce-scatter.15.cloned.1.call-done = bf16[1,2,128,576]{3,2,1,0:T(8,128)(2,1)} async-done(((bf16[8,2,128,576]{3,2,1,0:T(8,128)(2,1)}), bf16[1,2,128,576]{3,2,1,0:T(8,128)(2,1)}) %reduce-scatter.15.cloned.1.call-update) | async-done | bytes 294928 | tf_op jit(solution)/shard_map/reduce_scatter | solution.py:480
  1046.4 15.1 %multiply_convert_fusion.1 = bf16[3072,2048]{1,0:T(8,128)(2,1)} fusion(bf16[3072,704]{0,1:T(8,128)(2,1)} %get-tuple-element.133, f32[3072]{0:T(1024)S(1)} %copy-done.54, bf16[1,704,2048]{2,1,0:T(8,128)(2,1)S(1)} %copy-done), kind=kOutput, calls=%fused_computation.6 | convolution fusion | flops 8870952960 | bytes 19804160 | tf_op jit(solution)/shard_map/dot_general | solution.py:46
  1066.0 22.3 %fusion.36 = f32[32,128,2048]{2,1,0:T(8,128)} fusion(bf16[32,96,2048]{2,1,0:T(8,128)(2,1)} %bitcast.261, s32[32,128]{1,0:T(8,128)S(1)} %convert_subtract_fusion, pred[32,128]{1,0:T(8,128)(4,1)S(1)} %copy-done.37), kind=kOutput, calls=%fused_computation.74 | convolution fusion | flops 1611399168 | bytes 46157824 | tf_op jit(solution)/shard_map/bst,bsd->btd/dot_general | solution.py:245
  1088.3 19.1 %fusion.1 = bf16[4096,2048]{1,0:T(8,128)(2,1)} fusion(f32[32,128,2048]{2,1,0:T(8,128)} %fusion.36, bf16[4096,88]{0,1:T(8,128)(2,1)S(1)} %copy-done.16, bf16[88,2048]{1,0:T(8,128)(2,1)S(1)} %copy-done.42), kind=kOutput, calls=%fused_computation.3 | convolution fusion | flops 1493172224 | bytes 51412992 | tf_op jit(solution)/shard_map/dot_general | solution.py:46
  1109.4 5.8 all-to-all-start.7
  1117.8 5.5 all-to-all-done.7
  1125.5 12.4 fusion.54
  1137.9 8.3 all-to-all-start.8
  1146.3 15.1 %convolution_bitcast_fusion = f32[1,2048,704]{1,2,0:T(8,128)} fusion(bf16[3072,704]{0,1:T(8,128)(2,1)} %get-tuple-element.134, bf16[3072,2048]{1,0:T(8,128)(2,1)} %bitcast.256), kind=kOutput, calls=%fused_computation.32 | convolution fusion | flops 8858370048 | bytes 22675456 | tf_op jit(solution)/shard_map/dot_general | solution.py:54
  1161.4 15.3 %fusion.16 = f32[1,704,2048]{2,1,0:T(8,128)} fusion(bf16[3072,704]{0,1:T(8,128)(2,1)} %get-tuple-element.133, bf16[3072,2048]{1,0:T(8,128)(2,1)} %bitcast.254, f32[3072]{0:T(1024)S(1)} %copy-done.54), kind=kOutput, calls=%fused_computation.34 | convolution fusion | flops 8877244416 | bytes 22687744 | tf_op jit(solution)/shard_map/dot_general | solution.py:54
  1176.6 12.5 convolution_bitcast_fusion.1
  1209.9 15.3 %all-to-all-done.8 = f32[32,64,1,176]{3,1,2,0:T(8,128)} async-done(((f32[32,64,1,176]{3,1,2,0:T(8,128)}), f32[32,64,1,176]{3,1,2,0:T(8,128)}, u32[]{:S(2)}, u32[]{:S(2)}) %all-to-all-start.8) | async-done | bytes 1441824 | tf_op jit(solution)/shard_map/all_to_all | solution.py:533
  1225.2 5.4 all-to-all-start.6
  1230.6 9.7 fusion.102
  1262.9 156.0 %reduce-scatter.9.cloned.1.call-done = bf16[128,2048]{1,0:T(8,128)(2,1)} async-done(((bf16[4096,2048]{1,0:T(8,128)(2,1)}), bf16[128,2048]{1,0:T(8,128)(2,1)}) %reduce-scatter.9.cloned.1.call-update) | async-done | bytes 524304 | tf_op jit(solution)/shard_map/reduce_scatter | solution.py:389
  1422.9 18.5 %reduce-scatter.19.cloned.1.call-done = bf16[64,576]{1,0:T(8,128)(2,1)} async-done(((bf16[256,576]{1,0:T(8,128)(2,1)}), bf16[64,576]{1,0:T(8,128)(2,1)}) %reduce-scatter.19.cloned.1.call-update) | async-done | bytes 73744 | tf_op jit(solution)/shard_map/reduce_scatter | solution.py:467
  1447.2 23.4 %reduce-scatter.23.cloned.1.call-done = bf16[64,2048]{1,0:T(8,128)(2,1)} async-done(((bf16[256,2048]{1,0:T(8,128)(2,1)}), bf16[64,2048]{1,0:T(8,128)(2,1)}) %reduce-scatter.23.cloned.1.call-update) | async-done | bytes 262160 | tf_op jit(solution)/shard_map/reduce_scatter | solution.py:467
  (352 shorter events, 197.2 us)
Async XLA Ops:
  8.0 580.7 %copy-start = (bf16[1,704,2048]{2,1,0:T(8,128)(2,1)S(1)}, bf16[1,704,2048]{2,1,0:T(8,128)(2,1)}, u32[]{:S(2)}) copy-start(bf16[1,704,2048]{2,1,0:T(8,128)(2,1)} %param.32) | copy-start | bytes 8650756
  8.0 135.5 %all-reduce.7.cloned.1.call-start = ((), (), s32[]{:S(2)}) async-start(), calls=%async_computation.34 | async-start | bytes 151552
  12.2 133.6 %all-gather.14.cloned.1.call-start = ((), (), s32[]{:S(2)}) async-start(), calls=%async_computation.17 | async-start | bytes 4718592 | tf_op jit(solution)/shard_map/all_gather | solution.py:317
  14.3 137.4 %all-gather.18.cloned.1.call-start = ((), (), s32[]{:S(2)}) async-start(), calls=%async_computation.19 | async-start | bytes 2703360 | tf_op jit(solution)/shard_map/all_gather | solution.py:225
  16.7 128.1 %all-to-all-start = ((bf16[1,64,8,384]{3,1,0,2:T(8,128)(2,1)}), bf16[1,64,8,384]{3,1,0,2:T(8,128)(2,1)S(1)}, u32[]{:S(2)}, u32[]{:S(2)}) async-start(bf16[1,64,8,384]{3,1,0,2:T(8,128)(2,1)} %copy.244), calls=%async_computation | async-start | bytes 786432 | tf_op jit(solution)/shard_map/all_to_all | solution.py:322
  21.9 225.0 %all-gather.16.cloned.1.call-start = ((), (), s32[]{:S(2)}) async-start(), calls=%async_computation.18 | async-start | bytes 1966080 | tf_op jit(solution)/shard_map/all_gather | solution.py:324
  145.6 119.6 %all-gather.20.cloned.1.call-start = ((), (), s32[]{:S(2)}) async-start(), calls=%async_computation.20 | async-start | bytes 1474560 | tf_op jit(solution)/shard_map/all_gather | solution.py:362
  158.1 23.6 %copy-start.65 = (s32[128,6]{0,1:T(8,128)S(1)}, s32[128,6]{0,1:T(8,128)}, u32[]{:S(2)}) copy-start(s32[128,6]{0,1:T(8,128)} %param.33) | copy-start | bytes 9220
  158.1 23.8 %copy-start.70 = (s32[128]{0:T(128)S(1)}, s32[128]{0:T(128)}, u32[]{:S(2)}) copy-start(s32[128]{0:T(128)} %param.34) | copy-start | bytes 1540
  162.8 7.3 collective-permute-start
  170.8 130.5 %all-gather.22.cloned.1.call-start = ((), (), s32[]{:S(2)}) async-start(), calls=%async_computation.21 | async-start | bytes 8650752 | tf_op jit(solution)/shard_map/all_gather | solution.py:225
  171.5 260.7 %all-gather.26.cloned.1.call-start = ((), (), s32[]{:S(2)}) async-start(), calls=%async_computation.24 | async-start | bytes 17301504 | tf_op jit(solution)/shard_map/all_gather | solution.py:225
  173.0 58.8 %all-to-all-start.1 = ((bf16[1,16,8,512]{3,1,0,2:T(8,128)(2,1)}), bf16[1,16,8,512]{3,1,0,2:T(8,128)(2,1)S(1)}, u32[]{:S(2)}, u32[]{:S(2)}) async-start(bf16[1,16,8,512]{3,1,0,2:T(8,128)(2,1)} %copy.253), calls=%async_computation.1 | async-start | bytes 262144 | tf_op jit(solution)/shard_map/all_to_all | solution.py:322
  231.8 41.5 %copy-start.1 = (s32[1024,1]{1,0:T(8,128)}, s32[1024,1]{1,0:T(8,128)S(1)}, u32[]{:S(2)}) copy-start(s32[1024,1]{1,0:T(8,128)S(1)} %copy.254.low_ref) | copy-start | bytes 12292
  288.3 13.0 all-to-all-start.2
  294.5 253.1 %all-gather.24.cloned.1.call-start = ((), (), s32[]{:S(2)}) async-start(), calls=%async_computation.22 | async-start | bytes 17301504 | tf_op jit(solution)/shard_map/all_gather | solution.py:225
  317.8 359.5 %all-to-all-start.3 = ((bf16[1,64,32,176]{3,1,0,2:T(8,128)(2,1)}), bf16[1,64,32,176]{3,1,0,2:T(8,128)(2,1)}, u32[]{:S(2)}, u32[]{:S(2)}) async-start(bf16[1,64,32,176]{3,1,0,2:T(8,128)(2,1)} %copy.260), calls=%async_computation.3 | async-start | bytes 2097152 | tf_op jit(solution)/shard_map/all_to_all | solution.py:341
  323.9 411.4 %all-reduce.9.cloned.1.call-start = ((), (), s32[]{:S(2)}) async-start(), calls=%async_computation.35 | async-start | bytes 524288
  326.2 330.7 %copy-start.36 = (pred[32,128]{1,0:T(8,128)(4,1)}, pred[32,128]{1,0:T(8,128)(4,1)S(1)}, u32[]{:S(2)}) copy-start(pred[32,128]{1,0:T(8,128)(4,1)S(1)} %copy.258) | copy-start | bytes 12292
  330.2 115.8 %copy-start.59 = (f32[128]{0:T(128)}, f32[128]{0:T(128)S(1)}, u32[]{:S(2)}) copy-start(f32[128]{0:T(128)S(1)} %get-tuple-element.163) | copy-start | bytes 1540
  330.8 115.2 %copy-start.63 = (f32[128]{0:T(128)}, f32[128]{0:T(128)S(1)}, u32[]{:S(2)}) copy-start(f32[128]{0:T(128)S(1)} %fusion.83) | copy-start | bytes 1540
  611.5 309.2 %reduce-scatter.11.cloned.1.call-start = ((), (), s32[]{:S(2)}) async-start(), calls=%async_computation.25 | async-start | bytes 17301504 | tf_op jit(solution)/shard_map/reduce_scatter | solution.py:389
  724.4 196.4 %copy-start.45 = (f32[2048]{0:T(1024)S(1)}, f32[2048]{0:T(1024)}, u32[]{:S(2)}) copy-start(f32[2048]{0:T(1024)} %copy-done.44) | copy-start | bytes 24580
  724.4 196.4 %copy-start.62 = (f32[128]{0:T(128)S(1)}, f32[128]{0:T(128)}, u32[]{:S(2)}) copy-start(f32[128]{0:T(128)} %copy-done.61) | copy-start | bytes 1540
  724.4 199.0 %copy-start.68 = (f32[128]{0:T(128)S(1)}, f32[128]{0:T(128)}, u32[]{:S(2)}) copy-start(f32[128]{0:T(128)} %copy-done.67) | copy-start | bytes 1540
  724.4 200.0 %copy-start.17 = (bf16[128,2048]{1,0:T(8,128)(2,1)S(1)}, bf16[128,2048]{1,0:T(8,128)(2,1)}, u32[]{:S(2)}) copy-start(bf16[128,2048]{1,0:T(8,128)(2,1)} %param.35) | copy-start | bytes 1572868
  724.5 292.0 %reduce-scatter.15.cloned.1.call-start = ((), (), s32[]{:S(2)}) async-start(), calls=%async_computation.27 | async-start | bytes 2949120 | tf_op jit(solution)/shard_map/reduce_scatter | solution.py:480
  736.2 197.1 %copy-start.55 = (bf16[128,16]{0,1:T(8,128)(2,1)}, bf16[128,16]{0,1:T(8,128)(2,1)S(1)}, u32[]{:S(2)}) copy-start(bf16[128,16]{0,1:T(8,128)(2,1)S(1)} %multiply_convert_fusion.11) | copy-start | bytes 12292
  972.3 58.1 %copy-start.22 = (f32[1024,32]{1,0:T(8,128)S(1)}, f32[1024,32]{1,0:T(8,128)}, u32[]{:S(2)}) copy-start(f32[1024,32]{1,0:T(8,128)} %get-tuple-element.155) | copy-start | bytes 393220
  972.3 60.2 %copy-start.27 = (f32[1024,32]{0,1:T(8,128)S(1)}, f32[1024,32]{0,1:T(8,128)}, u32[]{:S(2)}) copy-start(f32[1024,32]{0,1:T(8,128)} %copy-done.26) | copy-start | bytes 393220
  972.3 216.8 %all-gather.28.cloned.1.call-start = ((), (), s32[]{:S(2)}) async-start(), calls=%async_computation.29 | async-start | bytes 1474560 | tf_op jit(solution)/shard_map/all_gather | solution.py:515
  1017.4 6.8 collective-permute-start.1
  1030.3 168.2 %reduce-scatter.13.cloned.1.call-start = ((), (), s32[]{:S(2)}) async-start(), calls=%async_computation.26 | async-start | bytes 4718592 | tf_op jit(solution)/shard_map/reduce_scatter | solution.py:496
  1040.7 164.6 %all-gather.30.cloned.1.call-start = ((), (), s32[]{:S(2)}) async-start(), calls=%async_computation.32 | async-start | bytes 4718592 | tf_op jit(solution)/shard_map/all_gather | solution.py:472
  1041.3 183.9 %reduce-scatter.21.cloned.1.call-start = ((), (), s32[]{:S(2)}) async-start(), calls=%async_computation.31 | async-start | bytes 655360 | tf_op jit(solution)/shard_map/reduce_scatter | solution.py:467
  1046.3 194.1 %reduce-scatter.17.cloned.1.call-start = ((), (), s32[]{:S(2)}) async-start(), calls=%async_computation.28 | async-start | bytes 1966080 | tf_op jit(solution)/shard_map/reduce_scatter | solution.py:467
  1065.8 353.2 %reduce-scatter.9.cloned.1.call-start = ((), (), s32[]{:S(2)}) async-start(), calls=%async_computation.23 | async-start | bytes 17301504 | tf_op jit(solution)/shard_map/reduce_scatter | solution.py:389
  1109.4 13.9 all-to-all-start.7
  1115.4 22.5 %copy-start.69 = (f32[128]{0:T(128)}, f32[128]{0:T(128)S(1)}, u32[]{:S(2)}) copy-start(f32[128]{0:T(128)S(1)} %fusion.48) | copy-start | bytes 1540
  1137.9 87.4 %all-to-all-start.8 = ((f32[32,64,1,176]{3,1,2,0:T(8,128)}), f32[32,64,1,176]{3,1,2,0:T(8,128)}, u32[]{:S(2)}, u32[]{:S(2)}) async-start(f32[32,64,1,176]{3,1,2,0:T(8,128)} %bitcast.275), calls=%async_computation.16 | async-start | bytes 4194304 | tf_op jit(solution)/shard_map/all_to_all | solution.py:533
  1146.2 295.2 %reduce-scatter.19.cloned.1.call-start = ((), (), s32[]{:S(2)}) async-start(), calls=%async_computation.30 | async-start | bytes 409600 | tf_op jit(solution)/shard_map/reduce_scatter | solution.py:467
  1146.2 30.4 %slice-start = ((s8[12582912]{0:T(1024)(128)(4,1)}), s8[4194304]{0:T(1024)(128)(4,1)S(1)}, s32[]{:S(2)}) async-start(s8[12582912]{0:T(1024)(128)(4,1)} %bitcast.258), calls=%async_computation.37 | async-start | bytes 8388608
  1146.2 30.4 %slice-start.1 = ((s8[12582912]{0:T(1024)(128)(4,1)}), s8[4194304]{0:T(1024)(128)(4,1)S(1)}, s32[]{:S(2)}) async-start(s8[12582912]{0:T(1024)(128)(4,1)} %bitcast.258), calls=%async_computation.38 | async-start | bytes 8388608
  1191.9 251.0 %all-reduce.11.cloned.1.call-start = ((), (), s32[]{:S(2)}) async-start(), calls=%async_computation.36 | async-start | bytes 327680
  1205.2 265.4 %reduce-scatter.23.cloned.1.call-start = ((), (), s32[]{:S(2)}) async-start(), calls=%async_computation.33 | async-start | bytes 1310720 | tf_op jit(solution)/shard_map/reduce_scatter | solution.py:467
  1225.2 17.0 %all-to-all-start.6 = ((bf16[8,16,1,512]{3,1,2,0:T(8,128)(2,1)}), bf16[8,16,1,512]{3,1,2,0:T(8,128)(2,1)S(1)}, u32[]{:S(2)}, u32[]{:S(2)}) async-start(bf16[8,16,1,512]{3,1,2,0:T(8,128)(2,1)} %bitcast.296), calls=%async_computation.13 | async-start | bytes 262144 | tf_op jit(solution)/shard_map/all_to_all | solution.py:509
  1242.3 18.0 %all-to-all-start.5 = ((bf16[8,64,1,384]{3,1,2,0:T(8,128)(2,1)}), bf16[8,64,1,384]{3,1,2,0:T(8,128)(2,1)}, u32[]{:S(2)}, u32[]{:S(2)}) async-start(bf16[8,64,1,384]{3,1,2,0:T(8,128)(2,1)} %bitcast.279), calls=%async_computation.10 | async-start | bytes 786432 | tf_op jit(solution)/shard_map/all_to_all | solution.py:509
  1254.0 165.0 %copy-start.46 = (f32[2048]{0:T(1024)S(1)}, f32[2048]{0:T(1024)}, u32[]{:S(2)}) copy-start(f32[2048]{0:T(1024)} %copy-done.44) | copy-start | bytes 24580
  (58 other events, 463.4 us)
Sparse Core Ops, SparseCore 0:
  15.0 128.5 all-reduce.6
  611.6 123.5 all-reduce.8
  737.6 183.1 reduce-scatter.10
  1205.3 155.3 all-reduce.10
Sparse Core Ops, SparseCore 1:
  15.1 41.2 all-gather.13
  59.0 57.8 all-gather.17
  145.7 38.0 all-gather.15
  186.3 27.1 all-gather.19
  216.3 78.9 all-gather.21
  298.1 134.1 all-gather.25
  435.0 112.5 all-gather.23
  972.4 44.0 reduce-scatter.14
  1030.4 24.9 all-gather.27
  1058.7 50.4 reduce-scatter.12
  1110.9 38.1 all-gather.29
  1152.0 28.1 reduce-scatter.20
  1182.3 44.2 reduce-scatter.16
  1228.9 190.0 reduce-scatter.8
  1421.3 20.1 reduce-scatter.18
  1443.7 26.8 reduce-scatter.22
where the time goes:
time: 1490 us; the launch traced here: 1480 us
  waiting for transfers between devices  738 us (50%)
  matrix products  362 us (24%)
  blocking collectives  137 us (9%)
  local copies, waits for them, and re-layouts  82.1 us (6%)
  other arithmetic  58.3 us (4%)
  starting transfers between devices  54.2 us (4%)
  Pallas kernels  31.8 us (2%)
  between operations  17.2 us (1%)
    reduce_scatter x2, waiting for transfers between devices, scatter_all(): return lax.psum_scatter(x, ALL, scatter_dimension=0, tiled=True)  341 us
    all_gather x4, waiting for transfers between devices, gather_all(): return lax.all_gather(x, ALL, axis=0, tiled=True)  140 us
    unnamed x23, waiting for transfers between devices  135 us
    dot_general x11, matrix products, dot_nt(): lax.dot_general(left, right, (((1,), (1,)), ((), ())), preferred_element_...  110 us
    all_gather x2, blocking collectives, gather_all(): return lax.all_gather(x, ALL, axis=0, tiled=True)  110 us
    dot_general x11, matrix products, matmul(): return jnp.dot(left, right, preferred_element_type=F32)  99.4 us
    dot_general x11, matrix products, dot_tn(): lax.dot_general(left, right, (((0,), (0,)), ((), ())), preferred_element_...  82.4 us
    dot_general x2, matrix products, place(): jnp.einsum('bst,bsd->btd', slots, table.astype(BF).reshape(blocks, per_bl...  42.6 us
  transfers between devices with their start and end apart: 30, of which 14 were waited for; matrix products, arithmetic and copies ran while one was open for 31% of the time, Pallas kernels for 1%

commit v1 on v0

--- a/solution.py
+++ b/solution.py
@@ -221,11 +221,328 @@
     )(low_bound, q_nope, q_rope, expanded, key_rope, lse, grad_mixed)
 
 
+MESH = pl.DeviceIdType.MESH
+
+
+class Wires:
+    def __init__(self, n_groups, n_plane, send, recv):
+        self.n_groups, self.n_plane, self.send, self.recv = n_groups, n_plane, send, recv
+        self.cores = 2
+        self.g, self.p, self.c = lax.axis_index("g"), lax.axis_index("p"), lax.axis_index("c")
+        self.j = self.p * self.cores + self.c
+        self.used = 0
+
+    def at_plane(self, j):
+        return {"g": self.g, "p": j // self.cores, "c": j % self.cores}
+
+    def at_chip(self, p):
+        return {"g": self.g, "p": p, "c": self.c}
+
+    def at_group(self, g):
+        return {"g": g, "p": self.p, "c": self.c}
+
+    def partner(self):
+        return {"g": self.g, "p": self.p, "c": 1 - self.c}
+
+    def plane_peer(self, d):
+        return lax.rem(self.j + d, self.n_plane)
+
+    def group_peer(self, d):
+        return lax.rem(self.g + d, self.n_groups)
+
+    def start(self, src, dst, device):
+        copy = pltpu.make_async_remote_copy(
+            src_ref=src,
+            dst_ref=dst,
+            send_sem=self.send.at[self.used],
+            recv_sem=self.recv.at[self.used],
+            device_id=device,
+            device_id_type=MESH,
+        )
+        self.used += 1
+        copy.start()
+        return copy
+
+    def meet(self):
+        barrier = pltpu.get_barrier_semaphore()
+        for d in range(1, self.n_plane):
+            pl.semaphore_signal(
+                barrier, inc=1, device_id=self.at_plane(self.plane_peer(d)), device_id_type=MESH
+            )
+        for d in range(1, self.n_groups):
+            pl.semaphore_signal(
+                barrier, inc=1, device_id=self.at_group(self.group_peer(d)), device_id_type=MESH
+            )
+        pl.semaphore_wait(barrier, self.n_plane - 1 + self.n_groups - 1)
+
+
+def sum_rows(dst, sources):
+    rows = dst.shape[0]
+    tile = 32 if rows % 32 == 0 else rows
+
+    def step(i, carry):
+        at = pl.ds(pl.multiple_of(i * tile, tile), tile)
+        total = sources[0][at, :].astype(F32)
+        for source in sources[1:]:
+            total = total + source[at, :].astype(F32)
+        dst[at, :] = total.astype(dst.dtype)
+        return carry
+
+    lax.fori_loop(0, rows // tile, step, 0)
+
+
+def wait_all(copies):
+    for copy in copies:
+        copy.wait()
+
+
+def wait_received(copies):
+    for copy in copies:
+        copy.wait_recv()
+
+
+def wait_sent(copies):
+    for copy in copies:
+        copy.wait_send()
+
+
+def plane_gather(w, src, out):
+    chips = w.n_plane // w.cores
+    first = [
+        w.start(src, out.at[w.j], w.at_chip(lax.rem(w.p + d, chips))) for d in range(1, chips)
+    ]
+    second = [w.start(src, out.at[w.j], w.partner())]
+    out[w.j] = src[...]
+    yield
+    for d in range(1, chips):
+        first[d - 1].wait_recv()
+        at = lax.rem(w.p + chips - d, chips) * w.cores + w.c
+        second.append(w.start(out.at[at], out.at[at], w.partner()))
+    yield
+    wait_sent(first)
+    wait_all(second)
+
+
+def shift_gather(w, src, mid, out):
+    copy = w.start(src, mid, w.at_group(lax.rem(w.g + 1, w.n_groups)))
+    yield
+    copy.wait()
+    yield from plane_gather(w, mid, out)
+
+
+def whole_gather(w, src, out):
+    first = [
+        w.start(src, out.at[w.g, w.j], w.at_group(w.group_peer(d))) for d in range(1, w.n_groups)
+    ]
+    out[w.g, w.j] = src[...]
+    yield
+    wait_received(first)
+    second = [
+        w.start(out.at[:, w.j], out.at[:, w.j], w.at_plane(w.plane_peer(d)))
+        for d in range(1, w.n_plane)
+    ]
+    yield
+    wait_sent(first)
+    wait_all(second)
+
+
+def plane_swap_gather(w, src, out):
+    first = []
+    for d in range(1, w.n_plane):
+        to = w.plane_peer(d)
+        first.append(w.start(src.at[to], out.at[w.g, w.j], w.at_plane(to)))
+    out[w.g, w.j] = src[w.j]
+    yield
+    wait_received(first)
+    second = [
+        w.start(out.at[w.g], out.at[w.g], w.at_group(w.group_peer(d)))
+        for d in range(1, w.n_groups)
+    ]
+    yield
+    wait_sent(first)
+    wait_all(second)
+
+
+def plane_swap(w, src, out):
+    copies = []
+    for d in range(1, w.n_plane):
+        to = w.plane_peer(d)
+        copies.append(w.start(src.at[to], out.at[w.j], w.at_plane(to)))
+    out[w.j] = src[w.j]
+    yield
+    wait_all(copies)
+
+
+def plane_sum(w, src, out, from_core, pairs, from_chips):
+    chips = w.n_plane // w.cores
+    first = []
+    for d in range(chips):
+        p = lax.rem(w.p + d, chips)
+        first.append(w.start(src.at[p * w.cores + 1 - w.c], from_core.at[d], w.partner()))
+    yield
+    second = []
+    for d in list(range(1, chips)) + [0]:
+        p = lax.rem(w.p + d, chips)
+        first[d].wait_recv()
+        sum_rows(pairs.at[d], [src.at[p * w.cores + w.c], from_core.at[d]])
+        if d:
+            second.append(w.start(pairs.at[d], from_chips.at[d - 1], w.at_chip(p)))
+    yield
+    wait_received(second)
+    sum_rows(out, [pairs.at[0]] + [from_chips.at[d] for d in range(chips - 1)])
+    wait_sent(first)
+    wait_sent(second)
+
+
+def whole_sum(w, src, out, from_plane, total, parts):
+    first = []
+    for d in range(1, w.n_plane):
+        to = w.plane_peer(d)
+        first.append(w.start(src.at[:, to], from_plane.at[d - 1], w.at_plane(to)))
+    yield
+    wait_received(first)
+
+    def step(i, carry):
+        sum_rows(
+            total.at[i], [src.at[i, w.j]] + [from_plane.at[d, i] for d in range(w.n_plane - 1)]
+        )
+        return carry
+
+    lax.fori_loop(0, w.n_groups, step, 0)
+    wait_sent(first)
+    yield from group_sum(w, total, out, parts)
+
+
+def group_sum(w, src, out, parts):
+    copies = []
+    for d in range(1, w.n_groups):
+        to = w.group_peer(d)
+        copies.append(w.start(src.at[to], parts.at[d - 1], w.at_group(to)))
+    yield
+    wait_received(copies)
+    sum_rows(out, [src.at[w.g]] + [parts.at[d] for d in range(w.n_groups - 1)])
+    wait_sent(copies)
+
+
+def group_sum_swap(w, src, out, total, parts):
+    copies = []
+    for d in range(1, w.n_groups):
+        to = w.group_peer(d)
+        copies.append(w.start(src.at[to], parts.at[d - 1], w.at_group(to)))
+    yield
+    wait_received(copies)
+
+    def step(i, carry):
+        sum_rows(total.at[i], [src.at[w.g, i]] + [parts.at[d, i] for d in range(w.n_groups - 1)])
+        return carry
+
+    lax.fori_loop(0, w.n_plane, step, 0)
+    second = []
+    for d in range(1, w.n_plane):
+        to = w.plane_peer(d)
+        second.append(w.start(total.at[to], out.at[w.j], w.at_plane(to)))
+    out[w.j] = total[w.j]
+    yield
+    wait_sent(copies)
+    wait_all(second)
+
+
+ROUTINES = {
+    "plane_gather": plane_gather,
+    "shift_gather": shift_gather,
+    "whole_gather": whole_gather,
+    "plane_swap_gather": plane_swap_gather,
+    "plane_swap": plane_swap,
+    "plane_sum": plane_sum,
+    "group_sum": group_sum,
+    "whole_sum": whole_sum,
+    "group_sum_swap": group_sum_swap,
+}
+
+
+def exchange_kernel(n_groups, n_plane, kinds, extra, *refs):
+    count = len(kinds)
+    sources, outs = refs[:count], refs[count : 2 * count]
+    scratch = list(refs[2 * count : -2])
+    w = Wires(n_groups, n_plane, refs[-2], refs[-1])
+    w.meet()
+    running = []
+    for kind, source, out, number in zip(kinds, sources, outs, extra):
+        mine, scratch = scratch[:number], scratch[number:]
+        if kind == "shift_gather":
+            running.append(shift_gather(w, source, mine[0], out))
+        else:
+            running.append(ROUTINES[kind](w, source, out, *mine))
+    while running:
+        still = []
+        for routine in running:
+            try:
+                next(routine)
+                still.append(routine)
+            except StopIteration:
+                pass
+        running = still
+
+
+def exchange(n_groups, n_plane, number, *items):
+    kinds = [kind for kind, _ in items]
+    arrays = [array for _, array in items]
+    shapes, scratch, extra = [], [], []
+    chips = n_plane // 2
+    for kind, array in items:
+        shape, dtype = array.shape, array.dtype
+        own = []
+        if kind in ("plane_gather", "shift_gather"):
+            out = (n_plane,) + shape
+            if kind == "shift_gather":
+                own = [shape]
+        elif kind == "whole_gather":
+            out = (n_groups, n_plane) + shape
+        elif kind == "plane_swap_gather":
+            out = (n_groups,) + shape
+        elif kind == "plane_swap":
+            out = shape
+        elif kind == "plane_sum":
+            out = shape[1:]
+            own = [(chips,) + out, (chips,) + out, (chips - 1,) + out]
+        elif kind == "group_sum":
+            out = shape[1:]
+            own = [(n_groups - 1,) + out]
+        elif kind == "whole_sum":
+            out = shape[2:]
+            own = [(n_plane - 1, n_groups) + out, (n_groups,) + out, (n_groups - 1,) + out]
+        elif kind == "group_sum_swap":
+            out = shape[1:]
+            own = [out, (n_groups - 1,) + out]
+        if kind in ("plane_sum", "group_sum", "whole_sum"):
+            shapes.append(jax.ShapeDtypeStruct(out, F32))
+        else:
+            shapes.append(jax.ShapeDtypeStruct(out, dtype))
+        scratch += [pltpu.VMEM(s, dtype) for s in own]
+        extra.append(len(own))
+    copies = 64 + 32 * len(items)
+    vmem = pl.BlockSpec(memory_space=pltpu.VMEM)
+    return pl.pallas_call(
+        functools.partial(exchange_kernel, n_groups, n_plane, kinds, extra),
+        out_shape=shapes,
+        in_specs=[vmem] * len(items),
+        out_specs=[vmem] * len(items),
+        scratch_shapes=scratch
+        + [pltpu.SemaphoreType.DMA((copies,)), pltpu.SemaphoreType.DMA((copies,))],
+        compiler_params=pltpu.CompilerParams(
+            collective_id=number,
+            has_side_effects=True,
+            vmem_limit_bytes=60 * 1024 * 1024,
+        ),
+        name="exchange_%d" % number,
+    )(*arrays)
+
+
 def gather_all(x):
     return lax.all_gather(x, ALL, axis=0, tiled=True)
 
 
-def experts_chunk(h2, cot, weight, slots, expert_w, shared_w):
+def experts_chunk(h2, cot, expert_id, slots, expert_w, shared_w, router_weight):
     w_gate, w_up, w_down = expert_w
     s_both, s_down = shared_w
     blocks, rows, width = h2.shape
@@ -252,7 +569,11 @@
     cot_rows = pick(cot)
     back_act = dot_nt(cot_rows, w_down)
     shared_back = dot_nt(flat_cot, s_down)
-    row_weight = jnp.sum(slots.astype(F32) * weight[:, None, :], axis=2).reshape(-1, 1)
+    shared_pre = matmul(flat_h2, jnp.concatenate([s_both, router_weight], axis=1))
+    probs = softmax_rows(shared_pre[:, 2 * hidden_s :])
+    chosen = jnp.arange(probs.shape[1], dtype=jnp.int32) == expert_id
+    weight = jnp.sum(jnp.where(chosen, probs, 0.0), axis=1).reshape(blocks, 1, rows)
+    row_weight = jnp.sum(slots.astype(F32) * weight, axis=2).reshape(-1, 1)
     rows_in = pick(h2)
     gate_pre = matmul(rows_in, w_gate)
     up_pre = matmul(rows_in, w_up)
@@ -261,16 +582,17 @@
     grad_gate, grad_up = act_vjp(back_act * row_weight)
     grad_gate = grad_gate.astype(BF)
     grad_up = grad_up.astype(BF)
-    picked_grad = jnp.sum(act_low.astype(F32) * back_act, axis=1).reshape(blocks, per_block, 1)
-    token_grad = jnp.sum(slots.astype(F32) * picked_grad, axis=1)
     grad_rows = dot_nt(grad_gate, w_gate) + dot_nt(grad_up, w_up)
-
-    shared_pre = matmul(flat_h2, s_both)
-    s_act, s_vjp = jax.vjp(swiglu, shared_pre[:, :hidden_s], shared_pre[:, hidden_s:])
+    s_act, s_vjp = jax.vjp(swiglu, shared_pre[:, :hidden_s], shared_pre[:, hidden_s : 2 * hidden_s])
     s_act = s_act.astype(BF)
     s_grad = jnp.concatenate(s_vjp(shared_back), axis=1).astype(BF)
     grad_h2 = (place(grad_rows) + dot_nt(s_grad, s_both)).astype(BF)
 
+    grad_h2, act_low, back_act, grad_gate, grad_up, s_act, s_grad = lax.optimization_barrier(
+        (grad_h2, act_low, back_act, grad_gate, grad_up, s_act, s_grad)
+    )
+    picked_grad = jnp.sum(act_low.astype(F32) * back_act, axis=1).reshape(blocks, per_block, 1)
+    token_grad = jnp.sum(slots.astype(F32) * picked_grad, axis=1)
     out_rows = matmul(act_low, w_down) * row_weight
     out = (place(out_rows) + matmul(s_act, s_down)).astype(BF)
 
@@ -304,30 +626,54 @@
 
     rows_w = w_router.shape[0]
     kv_n = kv_gain.shape[0]
-    small = jnp.concatenate([attn_gain, ffn_gain, kv_gain, w_router.reshape(-1)])
-    small = gather_all(small[None, :])
-    gain_one = small[:, :rows_w].reshape(-1).astype(F32)
-    gain_two = small[:, rows_w : 2 * rows_w].reshape(-1).astype(F32)
-    gain_kv = small[:, 2 * rows_w : 2 * rows_w + kv_n].reshape(-1).astype(F32)
-    router_weight = small[:, 2 * rows_w + kv_n :].reshape(width, experts)
-    ints = gather_all(jnp.concatenate([routes.reshape(-1), segments])[None, :])
-    routes_all = ints[:, : tok * TOP].reshape(devices, tok, TOP)
-    segments_all = ints[:, tok * TOP :].reshape(-1)
-
-    x_plane = lax.all_gather(layer_input, PLANE, axis=0, tiled=True).astype(F32)
-
-    def to_heads(weight):
-        rows, cols = weight.shape
-        split = weight.reshape(rows, n_plane, cols // n_plane)
-        mine = lax.all_to_all(split, PLANE, split_axis=1, concat_axis=0)
-        mine = mine.reshape(n_plane * rows, cols // n_plane)
-        return lax.all_gather(mine, "g", axis=0, tiled=True)
-
-    query_weight = to_heads(w_query).reshape(width, local_heads, NOPE + ROPE)
+    small = jnp.concatenate(
+        [
+            attn_gain,
+            ffn_gain,
+            kv_gain,
+            w_router.reshape(-1),
+            routes.reshape(-1).astype(BF),
+            segments.astype(BF),
+        ]
+    )
+    small = jnp.pad(small, (0, -small.shape[0] % 4096)).reshape(-1, 128)
+    head_cols = local_heads * (NOPE + ROPE)
+    kv_cols = local_heads * (NOPE + VDIM)
+    fold = kv_n * kv_cols // rows_w
+    pair = jnp.concatenate(
+        [
+            w_query.reshape(rows_w, n_plane, head_cols).transpose(1, 0, 2),
+            w_expand.reshape(kv_n, n_plane, kv_cols // fold, fold)
+            .transpose(1, 0, 2, 3)
+            .reshape(n_plane, rows_w, fold),
+        ],
+        axis=2,
+    )
+    swap = functools.partial(exchange, n_groups, n_plane)
+    x_plane, small, latent_weight, pair = swap(
+        0,
+        ("plane_gather", layer_input),
+        ("whole_gather", small),
+        ("whole_gather", w_latent),
+        ("plane_swap_gather", pair),
+    )
+    x_plane = x_plane.reshape(plane_tok, width).astype(F32)
+    latent_weight = latent_weight.reshape(width, RANK + ROPE)
+    pair = pair.reshape(width, head_cols + fold)
+    small = small.reshape(devices, -1)
+    cuts = [rows_w, 2 * rows_w, 2 * rows_w + kv_n, 2 * rows_w + kv_n + rows_w * experts]
+    cuts = cuts + [cuts[-1] + tok * TOP, cuts[-1] + tok * TOP + tok]
+    gain_one = small[:, : cuts[0]].reshape(-1).astype(F32)
+    gain_two = small[:, cuts[0] : cuts[1]].reshape(-1).astype(F32)
+    gain_kv = small[:, cuts[1] : cuts[2]].reshape(-1).astype(F32)
+    router_weight = small[:, cuts[2] : cuts[3]].reshape(width, experts)
+    routes_all = small[:, cuts[3] : cuts[4]].astype(jnp.int32).reshape(devices, tok, TOP)
+    segments_all = small[:, cuts[4] : cuts[5]].astype(jnp.int32).reshape(-1)
+
+    query_weight = pair[:, :head_cols].reshape(width, local_heads, NOPE + ROPE)
     wq_nope = query_weight[:, :, :NOPE].reshape(width, local_heads * NOPE)
     wq_rope = query_weight[:, :, NOPE:].reshape(width, local_heads * ROPE)
-    expand_weight = to_heads(w_expand)
-    latent_weight = gather_all(w_latent)
+    expand_weight = pair[:, head_cols:].reshape(RANK, kv_cols)
     output_weight = gather_all(w_output)
 
     shared_n = shared_down.shape[0]
@@ -355,11 +701,9 @@
     def own_rows(table):
         return lax.dynamic_slice_in_dim(table, place_in * tok, tok, 0)
 
-    up_pairs = [(i, i + 1) for i in range(n_groups - 1)]
     down_pairs = [(i + 1, i) for i in range(n_groups - 1)]
     piece = own_rows(jnp.concatenate([compressed_own, key_rope_own], axis=1))
-    before = lax.ppermute(piece, "g", up_pairs)
-    before = lax.all_gather(before, PLANE, axis=0, tiled=True)
+    before = swap(1, ("shift_gather", piece))[0].reshape(plane_tok, RANK + ROPE)
     compressed = jnp.concatenate([before[:, :RANK], compressed_own], axis=0)
     key_rope = jnp.concatenate([before[:, RANK:], key_rope_own], axis=0)
     q_nope = matmul(hidden, wq_nope).astype(BF)
@@ -373,7 +717,8 @@
     )
     low_bound = doc_start - plane_start + DOC_MAX
     mixed_heads, lse = attend(low_bound, q_nope, q_rope, expanded, key_rope, scale)
-    mixed = lax.all_to_all(mixed_heads, PLANE, split_axis=0, concat_axis=1, tiled=True)
+    mixed = swap(2, ("plane_swap", mixed_heads.reshape(n_plane, tok, local_heads * VDIM)))[0]
+    mixed = mixed.transpose(1, 0, 2).reshape(tok, width)
 
     input_float = layer_input.astype(F32)
     residual_one = input_float + matmul(mixed, output_weight)
@@ -388,11 +733,9 @@
     def scatter_all(x):
         return lax.psum_scatter(x, ALL, scatter_dimension=0, tiled=True)
 
-    def on_rows(h2, probs, cot_gathered, routes_here):
+    def on_rows(h2, cot_gathered, routes_here):
         rows = h2.shape[0]
         h2_all = gather_all(h2).reshape(devices, rows, width)
-        probs_all = gather_all(probs.T[None])
-        weight_all = lax.dynamic_index_in_dim(probs_all, expert_id, 1, keepdims=False)
         slot_count = min(slot_limit, rows)
         member = jnp.any(routes_here == expert_id, axis=2)
         member_int = member.astype(jnp.int32)
@@ -402,26 +745,28 @@
             & member[:, None, :]
         ).astype(BF)
         out, grad_h2, token_grad, grads = experts_chunk(
-            h2_all, cot_gathered, weight_all, slots, expert_w, shared_w
-        )
-        table = (jnp.arange(experts, dtype=jnp.int32) == expert_id).astype(F32)
-        picked = scatter_all((token_grad[:, None, :] * table[None, :, None]).reshape(devices, -1))
-        picked = picked.reshape(experts, rows).T
-        return scatter_all(out), scatter_all(grad_h2), picked, grads
+            h2_all, cot_gathered, expert_id, slots, expert_w, shared_w, router_weight
+        )
+        picked = lax.all_to_all(token_grad, ALL, split_axis=0, concat_axis=0, tiled=True)
+        picked = jnp.sum(picked.reshape(experts, devices // experts, rows), axis=1).T
+        grad_h2, out, grads, picked = lax.optimization_barrier(
+            (scatter_all(grad_h2), out, grads, picked)
+        )
+        return scatter_all(out), grad_h2, picked, grads
 
     parts = max(1, devices * tok // 4096)
     if parts == 1:
         cot_all = gather_all(cotangent).reshape(devices, tok, width)
         out_own, grad_h2_own, grad_router_probs, grads = on_rows(
-            h_two, router_probs, cot_all, routes_all
+            h_two, cot_all, routes_all
         )
     else:
         rows = tok // parts
 
         def step(total, inputs):
-            h2, probs, cot, routes_here = inputs
+            h2, cot, routes_here = inputs
             cot_part = gather_all(cot).reshape(devices, rows, width)
-            out, grad_h2, picked, grads = on_rows(h2, probs, cot_part, routes_here)
+            out, grad_h2, picked, grads = on_rows(h2, cot_part, routes_here)
             total = tuple(a + b for a, b in zip(total, grads))
             return total, (out, grad_h2, picked)
 
@@ -431,7 +776,6 @@
             tuple(jnp.zeros(s.shape, F32) for s in shapes),
             (
                 h_two.reshape(parts, rows, width),
-                router_probs.reshape(parts, rows, experts),
                 cotangent.reshape(parts, rows, width),
                 routes_all.reshape(devices, parts, rows, TOP).transpose(1, 0, 2, 3),
             ),
@@ -451,8 +795,10 @@
     grad_x_one, grad_gain_two = norm_two_back(grad_h_two)
     grad_x_one = grad_x_one + cotangent.astype(F32)
     grad_attn_out = grad_x_one.astype(BF)
-    grad_mixed = dot_nt(grad_attn_out, output_weight).astype(BF)
-    grad_mixed = lax.all_to_all(grad_mixed, PLANE, split_axis=1, concat_axis=0, tiled=True)
+    plane_grad = swap(3, ("plane_gather", grad_attn_out))[0].reshape(plane_tok, width)
+    head_rows = local_heads * VDIM
+    own_output = lax.dynamic_slice_in_dim(output_weight, place_in * head_rows, head_rows, 0)
+    grad_mixed = dot_nt(plane_grad, own_output).astype(BF)
     dqn, dqr, dex, dkr = attend_back(
         low_bound, q_nope, q_rope, expanded, key_rope, lse, grad_mixed, scale
     )
@@ -463,37 +809,42 @@
         mine = lax.dynamic_index_in_dim(split, place_in, 2, keepdims=False)
         return mine.reshape(rows, n_groups * rows_w)
 
-    def scatter_groups(partial):
-        return lax.psum_scatter(partial.astype(BF), "g", scatter_dimension=0, tiled=True)
-
     mixed_split = mixed.reshape(tok, n_groups, n_plane, rows_w).transpose(0, 2, 1, 3)
     mixed_cols = lax.all_to_all(mixed_split, PLANE, split_axis=1, concat_axis=0)
     mixed_cols = mixed_cols.reshape(plane_tok, n_groups * rows_w)
-    plane_grad = lax.all_gather(grad_attn_out, PLANE, axis=0, tiled=True)
-    grad_output_weight = scatter_groups(dot_tn(mixed_cols, plane_grad)).astype(F32)
+    g_output = dot_tn(mixed_cols, plane_grad).astype(BF).reshape(n_groups, rows_w, width)
 
     grad_expanded = dex.astype(BF)
     grad_expand = dot_tn(compressed, grad_expanded)
     grad_comp = dot_nt(grad_expanded, expand_weight)
     key_grads = jnp.concatenate([grad_comp, dkr], axis=1).astype(BF)
-    key_grads = key_grads.reshape(2, n_plane, tok, RANK + ROPE).transpose(1, 0, 2, 3)
-    key_grads = lax.psum_scatter(key_grads, PLANE, scatter_dimension=0, tiled=False)
-    later = lax.ppermute(key_grads[0], "g", down_pairs).astype(F32)
-    key_grad = key_grads[1].astype(F32) + later
+    key_grads = (
+        key_grads.reshape(2, n_plane, tok, RANK + ROPE)
+        .transpose(1, 0, 2, 3)
+        .reshape(n_plane, 2 * tok, RANK + ROPE)
+    )
+
+    gq_nope = dqn.astype(BF)
+    gq_rope = (
+        unrotate(dqr.reshape(plane_tok, local_heads, ROPE), cos_h, sin_h)
+        .reshape(plane_tok, local_heads * ROPE)
+        .astype(BF)
+    )
+    grad_hidden = (dot_nt(gq_nope, wq_nope) + dot_nt(gq_rope, wq_rope)).astype(BF)
+    key_grads, grad_hidden, grad_output_weight = swap(
+        4,
+        ("plane_sum", key_grads),
+        ("plane_sum", grad_hidden.reshape(n_plane, tok, width)),
+        ("group_sum", g_output),
+    )
+    later = lax.ppermute(key_grads[:tok].astype(BF), "g", down_pairs).astype(F32)
+    key_grad = key_grads[tok:] + later
     latent_own = own_rows(latent)
     kv_norm_back = jax.vjp(rms_norm, latent_own[:, :RANK], gain_kv)[1]
     grad_comp_in, grad_gain_kv = kv_norm_back(key_grad[:, :RANK])
     grad_rope_in = unrotate(key_grad[:, RANK:], own_rows(cosine), own_rows(sine_part))
     grad_latent = jnp.concatenate([grad_comp_in, grad_rope_in], axis=1).astype(BF)
 
-    gq_nope = dqn.astype(BF)
-    gq_rope = (
-        unrotate(dqr.reshape(plane_tok, local_heads, ROPE), cos_h, sin_h)
-        .reshape(plane_tok, local_heads * ROPE)
-        .astype(BF)
-    )
-    grad_hidden_q = (dot_nt(gq_nope, wq_nope) + dot_nt(gq_rope, wq_rope)).astype(BF)
-    grad_hidden = lax.psum_scatter(grad_hidden_q, PLANE, scatter_dimension=0, tiled=True)
     g_query = jnp.concatenate(
         [
             dot_tn(hidden, gq_nope).reshape(width, local_heads, NOPE),
@@ -502,34 +853,38 @@
         axis=2,
     ).reshape(width, local_heads * (NOPE + ROPE))
 
-    def from_heads(partial):
-        mine = scatter_groups(partial)
-        rows, cols = mine.shape
-        split = mine.reshape(n_plane, rows // n_plane, cols)
-        full = lax.all_to_all(split, PLANE, split_axis=0, concat_axis=1)
-        return full.reshape(rows // n_plane, n_plane * cols).astype(F32)
-
-    grad_query_weight = from_heads(g_query)
-    grad_expand_weight = from_heads(grad_expand)
-
-    latent_grads = lax.all_gather(grad_latent, PLANE, axis=0, tiled=True)
-    grad_latent_weight = scatter_groups(dot_tn(own_columns(hidden), latent_grads)).astype(F32)
-
-    grad_hidden = grad_hidden.astype(F32) + dot_nt(grad_latent, latent_weight)
+    g_query = g_query.astype(BF).reshape(n_groups, n_plane, rows_w, head_cols)
+    g_expand = grad_expand.astype(BF).reshape(n_groups, n_plane, kv_n, kv_cols)
+    g_query, g_expand, latent_grads = swap(
+        5,
+        ("group_sum_swap", g_query),
+        ("group_sum_swap", g_expand),
+        ("plane_gather", grad_latent),
+    )
+    grad_query_weight = g_query.transpose(1, 0, 2).reshape(rows_w, -1).astype(F32)
+    grad_expand_weight = g_expand.transpose(1, 0, 2).reshape(kv_n, -1).astype(F32)
+
+    latent_grads = latent_grads.reshape(plane_tok, RANK + ROPE)
+    g_latent = dot_tn(own_columns(hidden), latent_grads).astype(BF)
+    grad_hidden = grad_hidden + dot_nt(grad_latent, latent_weight)
     norm_one_back = jax.vjp(rms_norm, input_float, gain_one)[1]
     grad_x_norm, grad_gain_one = norm_one_back(grad_hidden)
     grad_input = grad_x_one + grad_x_norm
 
     small_grads = jnp.concatenate(
         [
-            grad_gain_one.reshape(devices, rows_w),
-            grad_gain_two.reshape(devices, rows_w),
-            grad_gain_kv.reshape(devices, kv_n),
-            grad_router.reshape(devices, rows_w * experts),
+            p.reshape(devices, -1)
+            for p in (grad_gain_one, grad_gain_two, grad_gain_kv, grad_router)
         ],
         axis=1,
     )
-    small_grads = scatter_all(small_grads)[0]
+    small_grads = jnp.pad(small_grads, ((0, 0), (0, -small_grads.shape[1] % 1024)))
+    grad_latent_weight, small_grads = swap(
+        6,
+        ("group_sum", g_latent.reshape(n_groups, rows_w, RANK + ROPE)),
+        ("whole_sum", small_grads.reshape(n_groups, n_plane, -1, 128)),
+    )
+    small_grads = small_grads.reshape(-1)
     g_shared = lax.all_to_all(
         g_both.reshape(devices, rows_w, 2 * shared_n), ALL, split_axis=0, concat_axis=1
     )
@@ -538,14 +893,14 @@
     return (
         output,
         grad_input,
-        small_grads[:rows_w],
+        small_grads[: cuts[0]],
         grad_query_weight,
         grad_latent_weight,
-        small_grads[2 * rows_w : 2 * rows_w + kv_n],
+        small_grads[cuts[1] : cuts[2]],
         grad_expand_weight,
         grad_output_weight,
-        small_grads[rows_w : 2 * rows_w],
-        small_grads[2 * rows_w + kv_n :].reshape(rows_w, experts),
+        small_grads[cuts[0] : cuts[1]],
+        small_grads[cuts[2] : cuts[3]].reshape(rows_w, experts),
         grad_shared_gate,
         grad_shared_up,
         g_sdown,

time: 1490 us -> 1150 us (0.77)
  waiting for transfers between devices: 738 us -> 164 us
  Pallas kernels: 31.8 us -> 441 us
  blocking collectives: 137 us -> 0 us
  starting transfers between devices: 54.2 us -> 18.4 us
  local copies, waits for them, and re-layouts: 82.1 us -> 101 us
    pallas_call x0 -> x7, Pallas kernels: none -> 409 us  [exchange(): pl.pallas_call(functools.partial(exchange_kernel, n_groups, n_plane, kind...]
    reduce_scatter x2, waiting for transfers between devices: 341 us -> 54.9 us  [scatter_all(): return lax.psum_scatter(x, ALL, scatter_dimension=0, tiled=True)]
    unnamed x23 -> x5, waiting for transfers between devices: 135 us -> 1.43 us
    all_gather x3 -> x0, blocking collectives: 125 us -> none  [the longest x2 110 us: gather_all(): return lax.all_gather(x, ALL, axis=0, tiled=True)]
    reduce_scatter x6 -> x0, waiting for transfers between devices: 84.4 us -> none  [the longest x1 42.5 us: body(): lax.psum_scatter(key_grads, PLANE, scatter_dimension=0, tiled=False)]
    all_gather x4 -> x3, waiting for transfers between devices: 140 us -> 88.9 us  [gather_all(): return lax.all_gather(x, ALL, axis=0, tiled=True)]
    all_to_all x5 -> x1, starting transfers between devices: 29.7 us -> 2.72 us  [on_rows(): lax.all_to_all(token_grad, ALL, split_axis=0, concat_axis=0, tiled=True)]
    convert_element_type x3 -> x11, local copies, waits for them, and re-layouts: 0.22 us -> 21.8 us  [the longest x2 16.8 us: body(): x_plane = x_plane.reshape(plane_tok, width).astype(F32)]
  transfers between devices with their start and end apart: 30 -> 10, of which waited for: 14 -> 3; matrix products, arithmetic and copies ran while one was open for 31% -> 28% of each run, Pallas kernels for 1% -> 39%
where the time goes in v1:
time: 1150 us; the launch traced here: 1140 us
  Pallas kernels  441 us (38%)
  matrix products  349 us (30%)
  waiting for transfers between devices  164 us (14%)
  local copies, waits for them, and re-layouts  101 us (9%)
  other arithmetic  53.3 us (5%)
  starting transfers between devices  18.4 us (2%)
  between operations  15.6 us (1%)
    pallas_call x7, Pallas kernels, exchange(): pl.pallas_call(functools.partial(exchange_kernel, n_groups, n_plane, kind...  409 us
    dot_general x11, matrix products, dot_nt(): lax.dot_general(left, right, (((1,), (1,)), ((), ())), preferred_element_...  111 us
    dot_general x11, matrix products, matmul(): return jnp.dot(left, right, preferred_element_type=F32)  93.3 us
    all_gather x3, waiting for transfers between devices, gather_all(): return lax.all_gather(x, ALL, axis=0, tiled=True)  88.9 us
    dot_general x11, matrix products, dot_tn(): lax.dot_general(left, right, (((0,), (0,)), ((), ())), preferred_element_...  75.7 us
    reduce_scatter x2, waiting for transfers between devices, scatter_all(): return lax.psum_scatter(x, ALL, scatter_dimension=0, tiled=True)  54.9 us
    dot_general x2, matrix products, place(): jnp.einsum('bst,bsd->btd', slots, table.astype(BF).reshape(blocks, per_bl...  41.1 us
    dot_general x2, matrix products, pick(): jnp.einsum('bst,btd->bsd', slots, table, preferred_element_type=F32)  27.9 us
  transfers between devices with their start and end apart: 10, of which 3 were waited for; matrix products, arithmetic and copies ran while one was open for 28% of the time, Pallas kernels for 39%

profile of v1, /device:TPU:1, one launch (start us, length us, event | category | flops | bytes accessed | tf_op | source)
XLA Modules:
  0.0 1141.8 jit_solution(5156394594277880569)
XLA Ops:
  16.9 89.5 %exchange_0.1 = (bf16[8,128,2048]{2,1,0:T(8,128)(2,1)}, bf16[4,8,32,128]{3,2,1,0:T(8,128)(2,1)}, bf16[4,8,64,576]{3,2,1,0:T(8,128)(2,1)}, bf16[4,8,64,512]{3,2,1,0:T(8,128)(2,1)}) custom-call(bf16[128,2048]{1,0:T(8,128)(2,1)} %refs_0_.1, bf16[32,128]{1,0:T(8,128)(2,1)} %pad_bitcast_fusion.1.refs_1_, bf16[64,576]{1,0:T(8,128)(2,1)} %refs_2_.1, ...), custom_call_target="tpu_custom_call" | custom-call | tf_op jit(solution)/shard_map/exchange_0/pallas_call | solution.py:525
  117.6 3.4 fusion.95
  123.1 3.5 fusion.56
  128.6 47.2 %exchange_1.1 = bf16[8,128,576]{2,1,0:T(8,128)(2,1)} custom-call(bf16[128,576]{1,0:T(8,128)(2,1)} %fusion.76.refs_0_), custom_call_target="tpu_custom_call" | custom-call | tf_op jit(solution)/shard_map/exchange_1/pallas_call | solution.py:525
  190.5 3.9 fusion.65
  198.3 4.6 convolution_convert_fusion.2.ex_ref
  204.2 11.4 attend.1
  217.2 21.1 %exchange_2.1 = bf16[8,128,256]{2,1,0:T(8,128)(2,1)} custom-call(bf16[8,128,256]{2,1,0:T(8,128)(2,1)} %bitcast.214), custom_call_target="tpu_custom_call" | custom-call | tf_op jit(solution)/shard_map/exchange_2/pallas_call | solution.py:525
  239.6 5.3 multiply_reduce_fusion.5
  255.4 3.3 all-to-all-start
  262.5 13.9 %convolution_convert_fusion.1 = bf16[32,96,2048]{2,1,0:T(8,128)(2,1)} fusion(bf16[32,128,2048]{2,1,0:T(8,128)(2,1)} %bitcast.215, s32[32,128]{1,0:T(8,128)S(1)} %convert_subtract_fusion, pred[32,128]{1,0:T(8,128)(4,1)S(1)} %copy.249), kind=kOutput, calls=%fused_computation.24 | convolution fusion | flops 1617690624 | bytes 29380608 | tf_op jit(solution)/shard_map/bst,btd->bsd/dot_general | solution.py:556
  276.4 18.9 %all-to-all-done = bf16[1,64,32,176]{3,1,0,2:T(8,128)(2,1)} async-done(((bf16[1,64,32,176]{3,1,0,2:T(8,128)(2,1)}), bf16[1,64,32,176]{3,1,0,2:T(8,128)(2,1)}, u32[]{:S(2)}, u32[]{:S(2)}) %all-to-all-start) | async-done | bytes 720928 | tf_op jit(solution)/shard_map/all_to_all | solution.py:687
  295.3 88.9 %all-gather.8.cloned.1.call-done = bf16[4096,2048]{1,0:T(8,128)(2,1)} async-done(((bf16[128,2048]{1,0:T(8,128)(2,1)}), bf16[4096,2048]{1,0:T(8,128)(2,1)}) %all-gather.8.cloned.1.call-update) | async-done | bytes 16777232 | tf_op jit(solution)/shard_map/all_gather | solution.py:542
  384.2 13.3 %fusion.43 = f32[4096,192]{0,1:T(8,128)} fusion(bf16[4096,2048]{1,0:T(8,128)(2,1)} %all-gather.8.cloned.1.call-done, bf16[2048,16]{1,0:T(8,128)(2,1)S(1)} %reshape.531, bf16[2048,176]{1,0:T(8,128)(2,1)} %bitcast.27), kind=kOutput, calls=%fused_computation.90 | convolution fusion | flops 3222798336 | bytes 20709376 | tf_op jit(solution)/shard_map/dot_general | solution.py:46
  401.3 13.9 %convolution_convert_fusion = bf16[32,96,2048]{2,1,0:T(8,128)(2,1)} fusion(bf16[32,128,2048]{2,1,0:T(8,128)(2,1)} %bitcast.216, s32[32,128]{1,0:T(8,128)S(1)} %convert_subtract_fusion, pred[32,128]{1,0:T(8,128)(4,1)S(1)} %copy.249), kind=kOutput, calls=%fused_computation.23 | convolution fusion | flops 1617690624 | bytes 29380608 | tf_op jit(solution)/shard_map/bst,btd->bsd/dot_general | solution.py:556
  415.2 15.7 %fusion.11 = f32[3072,704]{0,1:T(8,128)} fusion(bf16[3072,2048]{1,0:T(8,128)(2,1)} %bitcast.221, bf16[1,2048,704]{1,2,0:T(8,128)(2,1)} %param.30), kind=kOutput, calls=%fused_computation.28 | convolution fusion | flops 8858370048 | bytes 24117248 | tf_op jit(solution)/shard_map/dot_general | solution.py:46
  431.0 11.5 %fusion.14 = f32[3072,704]{0,1:T(8,128)} fusion(bf16[3072,2048]{1,0:T(8,128)(2,1)S(1)} %bitcast.223, bf16[1,2048,704]{1,2,0:T(8,128)(2,1)S(1)} %copy-done.78), kind=kOutput, calls=%fused_computation.31 | convolution fusion | flops 8858370048 | bytes 24117248 | tf_op jit(solution)/shard_map/dot_general | solution.py:46
  442.4 24.1 %multiply_convert_fusion.4 = (bf16[3072,704]{0,1:T(8,128)(2,1)}, bf16[3072,704]{0,1:T(8,128)(2,1)}, bf16[3072,704]{0,1:T(8,128)(2,1)}, f32[3072,704]{0,1:T(8,128)}) fusion(f32[3072]{0:T(1024)S(1)} %mul.471, f32[3072,704]{0,1:T(8,128)} %fusion.11, f32[3072,704]{0,1:T(8,128)} %fusion.14, bf16[3072,2048]{1,0:T(8,128)(2,1)} %bitcast.217, ...), kind=kOutput, calls=%fused_computation.16 | convolution fusion | flops 8895135744 | bytes 54407168 | tf_op jit(solution)/shard_map/dot_general | solution.py:50
  466.5 17.3 %fusion.9 = f32[3072,2048]{1,0:T(8,128)} fusion(bf16[3072,704]{0,1:T(8,128)(2,1)} %get-tuple-element.57, bf16[1,2048,704]{1,2,0:T(8,128)(2,1)} %param.30), kind=kOutput, calls=%fused_computation.26 | convolution fusion | flops 8858370048 | bytes 32374784 | tf_op jit(solution)/shard_map/dot_general | solution.py:50
  483.8 19.5 %add_convert_fusion = bf16[3072,2048]{1,0:T(8,128)(2,1)} fusion(f32[3072,2048]{1,0:T(8,128)} %fusion.9, bf16[3072,704]{0,1:T(8,128)(2,1)} %get-tuple-element.58, bf16[1,2048,704]{1,2,0:T(8,128)(2,1)} %param.31), kind=kOutput, calls=%fused_computation.6 | convolution fusion | flops 8870952960 | bytes 44957696 | tf_op jit(solution)/shard_map/dot_general | solution.py:50
  503.4 20.2 %fusion.24 = f32[32,128,2048]{2,1,0:T(8,128)} fusion(bf16[32,96,2048]{2,1,0:T(8,128)(2,1)} %bitcast.228, s32[32,128]{1,0:T(8,128)S(1)} %convert_subtract_fusion, pred[32,128]{1,0:T(8,128)(4,1)S(1)} %copy.249), kind=kOutput, calls=%fused_computation.62 | convolution fusion | flops 1611399168 | bytes 46157824 | tf_op jit(solution)/shard_map/bst,bsd->btd/dot_general | solution.py:562
  523.6 12.9 %fusion.31 = (bf16[4096,88]{0,1:T(8,128)(2,1)S(1)}, bf16[4096,88]{0,1:T(8,128)(2,1)S(1)}, bf16[4096,88]{0,1:T(8,128)(2,1)}) fusion(f32[4096,192]{0,1:T(8,128)} %fusion.43, bf16[4096,2048]{1,0:T(8,128)(2,1)} %all-gather.6.cloned.1.call-done, bf16[88,2048]{1,0:T(8,128)(2,1)S(1)} %copy-done.50), kind=kOutput, calls=%fused_computation.66 | convolution fusion | flops 1482162176 | bytes 22183936 | tf_op jit(solution)/shard_map/dot_general | solution.py:50
  537.7 19.6 %fusion.1 = bf16[4096,2048]{1,0:T(8,128)(2,1)} fusion(f32[32,128,2048]{2,1,0:T(8,128)} %fusion.24, bf16[2048,176]{1,0:T(8,128)(2,1)} %bitcast.27, bf16[4096,88]{0,1:T(8,128)(2,1)S(1)} %get-tuple-element.188, bf16[4096,88]{0,1:T(8,128)(2,1)S(1)} %get-tuple-element.187), kind=kOutput, calls=%fused_computation.3 | convolution fusion | flops 2972450816 | bytes 52494336 | tf_op jit(solution)/shard_map/dot_general | solution.py:50
  557.3 6.0 multiply_reduce_fusion
  567.4 10.8 fusion.100
  578.2 14.9 %multiply_convert_fusion.1 = bf16[3072,2048]{1,0:T(8,128)(2,1)} fusion(bf16[3072,704]{0,1:T(8,128)(2,1)} %get-tuple-element.55, f32[3072]{0:T(1024)S(1)} %mul.471, bf16[1,704,2048]{2,1,0:T(8,128)(2,1)S(1)} %copy-done), kind=kOutput, calls=%fused_computation.5 | convolution fusion | flops 8870952960 | bytes 19804160 | tf_op jit(solution)/shard_map/dot_general | solution.py:46
  593.2 12.6 %fusion.98 = f32[2048,704]{0,1:T(8,128)} fusion(bf16[3072,704]{0,1:T(8,128)(2,1)} %get-tuple-element.57, bf16[3072,2048]{1,0:T(8,128)(2,1)S(1)} %bitcast.226), kind=kOutput, calls=%fused_computation.204 | convolution fusion | flops 8858370048 | bytes 22675456 | tf_op jit(solution)/shard_map/dot_general | solution.py:54
  605.9 15.2 %fusion.99 = f32[2048,704]{0,1:T(8,128)} fusion(bf16[3072,704]{0,1:T(8,128)(2,1)} %get-tuple-element.58, bf16[3072,2048]{1,0:T(8,128)(2,1)} %bitcast.222), kind=kOutput, calls=%fused_computation.205 | convolution fusion | flops 8858370048 | bytes 22675456 | tf_op jit(solution)/shard_map/dot_general | solution.py:54
  621.0 13.2 %fusion.2 = f32[704,2048]{1,0:T(8,128)} fusion(bf16[3072,704]{0,1:T(8,128)(2,1)} %get-tuple-element.55, bf16[3072,2048]{1,0:T(8,128)(2,1)S(1)} %bitcast.220, f32[3072]{0:T(1024)S(1)} %mul.471), kind=kOutput, calls=%fused_computation.9 | convolution fusion | flops 8877244416 | bytes 22687744 | tf_op jit(solution)/shard_map/dot_general | solution.py:54
  634.2 20.8 %fusion.22 = f32[32,128,2048]{2,1,0:T(8,128)} fusion(bf16[32,96,2048]{2,1,0:T(8,128)(2,1)} %bitcast.227, s32[32,128]{1,0:T(8,128)S(1)} %convert_subtract_fusion, pred[32,128]{1,0:T(8,128)(4,1)S(1)} %copy.249), kind=kOutput, calls=%fused_computation.61 | convolution fusion | flops 1611399168 | bytes 46157824 | tf_op jit(solution)/shard_map/bst,bsd->btd/dot_general | solution.py:562
  655.1 19.1 %fusion = bf16[4096,2048]{1,0:T(8,128)(2,1)} fusion(f32[32,128,2048]{2,1,0:T(8,128)} %fusion.22, bf16[4096,88]{0,1:T(8,128)(2,1)S(1)} %copy-done.19, bf16[88,2048]{1,0:T(8,128)(2,1)S(1)} %copy-done.50), kind=kOutput, calls=%fused_computation.1 | convolution fusion | flops 1493172224 | bytes 51412992 | tf_op jit(solution)/shard_map/dot_general | solution.py:46
  674.2 9.6 fusion.96
  683.8 54.9 %reduce-scatter.3.cloned.1.call-done = bf16[128,2048]{1,0:T(8,128)(2,1)} async-done(((bf16[4096,2048]{1,0:T(8,128)(2,1)}), bf16[128,2048]{1,0:T(8,128)(2,1)}) %reduce-scatter.3.cloned.1.call-update) | async-done | bytes 524304 | tf_op jit(solution)/shard_map/reduce_scatter | solution.py:734
  740.6 3.7 all-to-all-start.2
  745.4 7.3 copy.261
  753.6 9.5 reshape.560
  778.6 6.8 all-to-all-start.3
  786.6 80.9 %exchange_3.1 = bf16[8,128,2048]{2,1,0:T(8,128)(2,1)} custom-call(bf16[128,2048]{1,0:T(8,128)(2,1)} %fusion.91.refs_0_), custom_call_target="tpu_custom_call" | custom-call | tf_op jit(solution)/shard_map/exchange_3/pallas_call | solution.py:525
  867.5 4.6 convolution_convert_fusion.7.gm_ref
  872.2 20.8 %attend_back.1 = (f32[1024,256]{1,0:T(8,128)}, f32[1024,128]{1,0:T(8,128)}, f32[2048,512]{1,0:T(8,128)}, f32[2048,64]{1,0:T(8,128)}) custom-call(s32[1024,1]{1,0:T(8,128)} %copy-done.2, bf16[1024,256]{1,0:T(8,128)(2,1)} %copy-done.6, bf16[1024,128]{1,0:T(8,128)(2,1)} %copy.246.qr_ref, bf16[2048,512]{1,0:T(8,128)(2,1)} %convolution_convert_fusion.2.ex_ref, ...), custom_call_target="tpu_custom_call" | custom-call | flops 4362076160 | bytes 8388608 | tf_op jit(solution)/shard_map/attend_back/pallas_call | solution.py:192
  903.8 4.7 convolution_convert_fusion.4
  909.7 4.3 fusion.8
  914.0 89.1 %exchange_4.1 = (f32[256,576]{1,0:T(8,128)}, f32[128,2048]{1,0:T(8,128)}, f32[64,2048]{1,0:T(8,128)}) custom-call(bf16[8,256,576]{2,1,0:T(8,128)(2,1)} %bitcast.230, bf16[8,128,2048]{2,1,0:T(8,128)(2,1)} %bitcast.229, bf16[4,64,2048]{2,1,0:T(8,128)(2,1)} %bitcast.261), custom_call_target="tpu_custom_call" | custom-call | tf_op jit(solution)/shard_map/exchange_4/pallas_call | solution.py:525
  1014.6 5.0 copy.263
  1025.8 4.1 fusion.40
  1030.1 61.1 %exchange_5.1 = (bf16[8,64,384]{2,1,0:T(8,128)(2,1)}, bf16[8,16,512]{2,1,0:T(8,128)(2,1)}, bf16[8,128,576]{2,1,0:T(8,128)(2,1)}) custom-call(bf16[4,8,64,384]{3,2,1,0:T(8,128)(2,1)} %convert_element_type.296.refs_0_, bf16[4,8,16,512]{3,2,1,0:T(8,128)(2,1)} %bitcast.269, bf16[128,576]{1,0:T(8,128)(2,1)} %copy-done.38), custom_call_target="tpu_custom_call" | custom-call | tf_op jit(solution)/shard_map/exchange_5/pallas_call | solution.py:525
  1095.1 19.8 %exchange_6.1 = (f32[64,576]{1,0:T(8,128)}, f32[16,128]{1,0:T(8,128)}) custom-call(bf16[4,64,576]{2,1,0:T(8,128)(2,1)} %bitcast.259, f32[4,8,16,128]{3,2,1,0:T(8,128)} %copy.291), custom_call_target="tpu_custom_call" | custom-call | tf_op jit(solution)/shard_map/exchange_6/pallas_call | solution.py:525
  1129.4 4.0 fusion.36
  (331 shorter events, 140.4 us)
Async XLA Ops:
  7.2 435.2 %copy-start = (bf16[1,704,2048]{2,1,0:T(8,128)(2,1)S(1)}, bf16[1,704,2048]{2,1,0:T(8,128)(2,1)}, u32[]{:S(2)}) copy-start(bf16[1,704,2048]{2,1,0:T(8,128)(2,1)} %param.32) | copy-start | bytes 8650756
  7.2 232.4 %all-gather.4.cloned.1.call-start = ((), (), s32[]{:S(2)}) async-start(), calls=%async_computation.6 | async-start | bytes 8650752 | tf_op jit(solution)/shard_map/all_gather | solution.py:542
  7.9 254.5 %all-gather.6.cloned.1.call-start = ((), (), s32[]{:S(2)}) async-start(), calls=%async_computation.7 | async-start | bytes 17301504 | tf_op jit(solution)/shard_map/all_gather | solution.py:542
  8.7 375.5 %all-gather.8.cloned.1.call-start = ((), (), s32[]{:S(2)}) async-start(), calls=%async_computation.8 | async-start | bytes 17301504 | tf_op jit(solution)/shard_map/all_gather | solution.py:542
  111.3 15.3 %copy-start.59 = (f32[512]{0:T(512)}, f32[512]{0:T(512)S(1)}, u32[]{:S(2)}) copy-start(f32[512]{0:T(512)S(1)} %reshape.558) | copy-start | bytes 6148
  179.8 65.2 %copy-start.52 = (f32[2048]{0:T(1024)}, f32[2048]{0:T(1024)S(1)}, u32[]{:S(2)}) copy-start(f32[2048]{0:T(1024)S(1)} %reshape.559) | copy-start | bytes 24580
  180.0 24.1 %copy-start.2 = (s32[1024,1]{1,0:T(8,128)}, s32[1024,1]{1,0:T(8,128)S(1)}, u32[]{:S(2)}) copy-start(s32[1024,1]{1,0:T(8,128)S(1)} %copy.245.low_ref) | copy-start | bytes 12292
  204.2 11.4 %copy-start.6 = (bf16[1024,256]{1,0:T(8,128)(2,1)}, bf16[1024,256]{1,0:T(8,128)(2,1)S(1)}, u32[]{:S(2)}) copy-start(bf16[1024,256]{1,0:T(8,128)(2,1)S(1)} %convolution_convert_fusion.8.qn_ref) | copy-start | bytes 1572868
  245.0 10.4 copy-start.72
  255.4 40.0 %all-to-all-start = ((bf16[1,64,32,176]{3,1,0,2:T(8,128)(2,1)}), bf16[1,64,32,176]{3,1,0,2:T(8,128)(2,1)}, u32[]{:S(2)}, u32[]{:S(2)}) async-start(bf16[1,64,32,176]{3,1,0,2:T(8,128)(2,1)} %copy.251), calls=%async_computation | async-start | bytes 2097152 | tf_op jit(solution)/shard_map/all_to_all | solution.py:687
  258.7 480.0 %reduce-scatter.3.cloned.1.call-start = ((), (), s32[]{:S(2)}) async-start(), calls=%async_computation.9 | async-start | bytes 17301504 | tf_op jit(solution)/shard_map/reduce_scatter | solution.py:734
  262.4 121.8 %copy-start.22 = (bf16[2048,16]{1,0:T(8,128)(2,1)}, bf16[2048,16]{1,0:T(8,128)(2,1)S(1)}, u32[]{:S(2)}) copy-start(bf16[2048,16]{1,0:T(8,128)(2,1)S(1)} %reshape.531) | copy-start | bytes 196612
  415.2 15.7 %copy-start.9 = (bf16[32,96,2048]{2,1,0:T(8,128)(2,1)S(1)}, bf16[32,96,2048]{2,1,0:T(8,128)(2,1)}, u32[]{:S(2)}) copy-start(bf16[32,96,2048]{2,1,0:T(8,128)(2,1)} %convolution_convert_fusion) | copy-start | bytes 37748740
  415.2 15.7 %copy-start.78 = (bf16[1,2048,704]{1,2,0:T(8,128)(2,1)S(1)}, bf16[1,2048,704]{1,2,0:T(8,128)(2,1)}, u32[]{:S(2)}) copy-start(bf16[1,2048,704]{1,2,0:T(8,128)(2,1)} %param.31) | copy-start | bytes 8650756
  503.3 20.2 %copy-start.50 = (bf16[88,2048]{1,0:T(8,128)(2,1)S(1)}, bf16[88,2048]{1,0:T(8,128)(2,1)}, u32[]{:S(2)}) copy-start(bf16[88,2048]{1,0:T(8,128)(2,1)} %param.29) | copy-start | bytes 1081348
  564.6 119.2 %all-to-all-start.1 = ((f32[32,1,128]{2,1,0:T(1,128)}), f32[32,1,128]{2,1,0:T(1,128)S(1)}, u32[]{:S(2)}, u32[]{:S(2)}) async-start(f32[32,1,128]{2,1,0:T(1,128)} %bitcast.39), calls=%async_computation.2 | async-start | bytes 32768 | tf_op jit(solution)/shard_map/all_to_all | solution.py:750
  567.4 562.0 %reduce-scatter.5.cloned.1.call-start = ((), (), s32[]{:S(2)}) async-start(), calls=%async_computation.10 | async-start | bytes 17301504 | tf_op jit(solution)/shard_map/reduce_scatter | solution.py:734
  567.4 25.8 %slice-start.3 = ((s8[12582912]{0:T(1024)(128)(4,1)}), s8[4194304]{0:T(1024)(128)(4,1)S(1)}, s32[]{:S(2)}) async-start(s8[12582912]{0:T(1024)(128)(4,1)} %bitcast.224), calls=%async_computation.14 | async-start | bytes 8388608
  578.2 15.0 %slice-start.4 = ((s8[12582912]{0:T(1024)(128)(4,1)}), s8[4194304]{0:T(1024)(128)(4,1)S(1)}, s32[]{:S(2)}) async-start(s8[12582912]{0:T(1024)(128)(4,1)} %bitcast.224), calls=%async_computation.15 | async-start | bytes 8388608
  578.2 15.0 %slice-start.5 = ((s8[12582912]{0:T(1024)(128)(4,1)}), s8[4194304]{0:T(1024)(128)(4,1)S(1)}, s32[]{:S(2)}) async-start(s8[12582912]{0:T(1024)(128)(4,1)} %bitcast.224), calls=%async_computation.16 | async-start | bytes 8388608
  593.2 27.8 %slice-start = ((s8[12582912]{0:T(1024)(128)(4,1)}), s8[4194304]{0:T(1024)(128)(4,1)S(1)}, s32[]{:S(2)}) async-start(s8[12582912]{0:T(1024)(128)(4,1)} %bitcast.218), calls=%async_computation.11 | async-start | bytes 8388608
  593.2 27.8 %slice-start.1 = ((s8[12582912]{0:T(1024)(128)(4,1)}), s8[4194304]{0:T(1024)(128)(4,1)S(1)}, s32[]{:S(2)}) async-start(s8[12582912]{0:T(1024)(128)(4,1)} %bitcast.218), calls=%async_computation.12 | async-start | bytes 8388608
  605.9 15.2 %slice-start.2 = ((s8[12582912]{0:T(1024)(128)(4,1)}), s8[4194304]{0:T(1024)(128)(4,1)S(1)}, s32[]{:S(2)}) async-start(s8[12582912]{0:T(1024)(128)(4,1)} %bitcast.218), calls=%async_computation.13 | async-start | bytes 8388608
  634.2 20.8 %copy-start.19 = (bf16[4096,88]{0,1:T(8,128)(2,1)S(1)}, bf16[4096,88]{0,1:T(8,128)(2,1)}, u32[]{:S(2)}) copy-start(bf16[4096,88]{0,1:T(8,128)(2,1)} %get-tuple-element.56) | copy-start | bytes 2162692
  740.6 27.8 %all-to-all-start.2 = ((bf16[1,128,8,4,64]{1,4,3,0,2:T(8,128)(2,1)}), bf16[1,128,8,4,64]{1,4,3,0,2:T(8,128)(2,1)S(1)}, u32[]{:S(2)}, u32[]{:S(2)}) async-start(bf16[1,128,8,4,64]{1,4,3,0,2:T(8,128)(2,1)} %copy.258), calls=%async_computation.4 | async-start | bytes 1048576 | tf_op jit(solution)/shard_map/all_to_all | solution.py:813
  745.4 7.3 copy-start.36
  753.5 11.4 copy-start.13
  753.6 12.7 %copy-start.63 = (f32[1024]{0:T(1024)S(1)}, f32[1024]{0:T(1024)}, u32[]{:S(2)}) copy-start(f32[1024]{0:T(1024)} %get-tuple-element.212) | copy-start | bytes 12292
  753.6 16.0 %copy-start.15 = (bf16[128,2048]{1,0:T(8,128)(2,1)S(1)}, bf16[128,2048]{1,0:T(8,128)(2,1)}, u32[]{:S(2)}) copy-start(bf16[128,2048]{1,0:T(8,128)(2,1)} %multiply_convert_fusion.9) | copy-start | bytes 1572868
  753.6 16.0 %copy-start.23 = (bf16[2048,16]{1,0:T(8,128)(2,1)S(1)}, bf16[2048,16]{1,0:T(8,128)(2,1)}, u32[]{:S(2)}) copy-start(bf16[2048,16]{1,0:T(8,128)(2,1)} %copy-done.22) | copy-start | bytes 196612
  771.7 13.8 %copy-start.14 = (f32[128,2048]{1,0:T(8,128)}, f32[128,2048]{1,0:T(8,128)S(1)}, u32[]{:S(2)}) copy-start(f32[128,2048]{1,0:T(8,128)S(1)} %get-tuple-element.219) | copy-start | bytes 3145732
  773.8 11.6 %copy-start.73 = (f32[128]{0:T(128)S(1)}, f32[128]{0:T(128)}, u32[]{:S(2)}) copy-start(f32[128]{0:T(128)} %copy-done.72) | copy-start | bytes 1540
  773.8 11.6 %copy-start.20 = (bf16[128,2048]{1,0:T(8,128)(2,1)S(1)}, bf16[128,2048]{1,0:T(8,128)(2,1)}, u32[]{:S(2)}) copy-start(bf16[128,2048]{1,0:T(8,128)(2,1)} %param.35) | copy-start | bytes 1572868
  778.6 342.1 %all-to-all-start.3 = ((f32[32,64,1,176]{3,1,2,0:T(8,128)}), f32[32,64,1,176]{3,1,2,0:T(8,128)}, u32[]{:S(2)}, u32[]{:S(2)}) async-start(f32[32,64,1,176]{3,1,2,0:T(8,128)} %bitcast.231), calls=%async_computation.5 | async-start | bytes 4194304 | tf_op jit(solution)/shard_map/all_to_all | solution.py:888
  785.4 86.7 %copy-start.69 = (f32[128]{0:T(128)}, f32[128]{0:T(128)S(1)}, u32[]{:S(2)}) copy-start(f32[128]{0:T(128)S(1)} %multiply_multiply_fusion.2) | copy-start | bytes 1540
  1005.0 16.5 %collective-permute-start = (bf16[128,576]{1,0:T(8,128)(2,1)}, bf16[128,576]{1,0:T(8,128)(2,1)}, u32[]{:S(2)}, u32[]{:S(2)}) collective-permute-start(bf16[128,576]{1,0:T(8,128)(2,1)} %slice.234), channel_id=1, source_target_pairs={{8,0},{16,8},{24,16},{9,1},{17,9},{25,17},{10,2},{18,10},{26,18},{... | collective-permute-start | bytes 442376 | tf_op jit(solution)/shard_map/ppermute | solution.py:840
  1014.6 7.0 copy-start.49
  1014.6 7.9 copy-start.60
  1014.6 7.9 copy-start.71
  1014.6 9.0 copy-start.77
  1014.6 11.2 copy-start.56
  1014.6 11.2 copy-start.67
  1025.7 65.6 %copy-start.37 = (bf16[1024,4,1,64]{0,3,2,1:T(8,128)(2,1)S(1)}, bf16[1024,4,1,64]{0,3,2,1:T(8,128)(2,1)}, u32[]{:S(2)}) copy-start(bf16[1024,4,1,64]{0,3,2,1:T(8,128)(2,1)} %fusion.42) | copy-start | bytes 1572868
  1025.8 68.3 %copy-start.58 = (f32[32,64]{1,0:T(8,128)S(1)}, f32[32,64]{1,0:T(8,128)}, u32[]{:S(2)}) copy-start(f32[32,64]{1,0:T(8,128)} %reshape.549) | copy-start | bytes 24580
  1091.2 26.3 %copy-start.57 = (bf16[8,16,512]{2,1,0:T(8,128)(2,1)S(1)}, bf16[8,16,512]{2,1,0:T(8,128)(2,1)}, u32[]{:S(2)}) copy-start(bf16[8,16,512]{2,1,0:T(8,128)(2,1)} %get-tuple-element.75) | copy-start | bytes 393220
  1091.2 27.1 %copy-start.48 = (bf16[8,64,384]{2,1,0:T(8,128)(2,1)S(1)}, bf16[8,64,384]{2,1,0:T(8,128)(2,1)}, u32[]{:S(2)}) copy-start(bf16[8,64,384]{2,1,0:T(8,128)(2,1)} %get-tuple-element.73) | copy-start | bytes 1179652
  1091.2 28.1 %copy-start.75 = (f32[128]{0:T(128)S(1)}, f32[128]{0:T(128)}, u32[]{:S(2)}) copy-start(f32[128]{0:T(128)} %copy-done.74) | copy-start | bytes 1540
  1126.6 8.3 copy-start.1
  (48 other events, 196.0 us)
Sparse Core Ops, SparseCore 0:
  10.9 124.2 all-gather.3
  138.0 122.6 all-gather.5
  263.6 120.5 all-gather.7
  557.4 181.2 reduce-scatter.2
  740.9 271.0 reduce-scatter.4

commit v2 on v1

--- a/solution.py
+++ b/solution.py
@@ -413,6 +413,24 @@
     yield from group_sum(w, total, out, parts)
 
 
+def whole_swap(w, src, out, mid):
+    first = []
+    for d in range(1, w.n_plane):
+        to = w.plane_peer(d)
+        first.append(w.start(src.at[:, to], mid.at[w.j], w.at_plane(to)))
+    mid[w.j] = src[:, w.j]
+    yield
+    wait_received(first)
+    second = []
+    for d in range(1, w.n_groups):
+        to = w.group_peer(d)
+        second.append(w.start(mid.at[:, to], out.at[w.g], w.at_group(to)))
+    out[w.g] = mid[:, w.g]
+    yield
+    wait_sent(first)
+    wait_all(second)
+
+
 def group_sum(w, src, out, parts):
     copies = []
     for d in range(1, w.n_groups):
@@ -456,6 +474,7 @@
     "plane_sum": plane_sum,
     "group_sum": group_sum,
     "whole_sum": whole_sum,
+    "whole_swap": whole_swap,
     "group_sum_swap": group_sum_swap,
 }
 
@@ -508,6 +527,9 @@
         elif kind == "group_sum":
             out = shape[1:]
             own = [(n_groups - 1,) + out]
+        elif kind == "whole_swap":
+            out = shape
+            own = [(n_plane, n_groups) + shape[2:]]
         elif kind == "whole_sum":
             out = shape[2:]
             own = [(n_plane - 1, n_groups) + out, (n_groups,) + out, (n_groups - 1,) + out]
@@ -542,67 +564,203 @@
     return lax.all_gather(x, ALL, axis=0, tiled=True)
 
 
-def experts_chunk(h2, cot, expert_id, slots, expert_w, shared_w, router_weight):
+def moe_kernel(
+    first_logit, experts, slot_count, id_ref, h2_ref, cot_ref, place_ref, wg_ref, wu_ref, wd_ref,
+    sc_ref, sd_ref,
+    gh2_ref, rows_ref, gin_ref, act_ref, gg_ref, gu_ref, rw_ref, pg_ref, sact_ref, sgrad_ref,
+):
+    blocks = h2_ref.shape[0] // 128
+    step = pl.program_id(0)
+    half = sc_ref.shape[1] // 2
+    h2, cot = h2_ref[...], cot_ref[...]
+
+    pre = jnp.dot(h2, sc_ref[...], preferred_element_type=F32)
+    back = dot_nt(cot, sd_ref[...])
+    gate, up = pre[:, :half], pre[:, half:]
+    lane = lax.broadcasted_iota(jnp.int32, gate.shape, 1)
+    logits = jnp.where((lane >= first_logit) & (lane < first_logit + experts), gate, -1e30)
+    exps = jnp.exp(logits - jnp.max(logits, axis=1, keepdims=True))
+    chosen = jnp.where(lane == first_logit + id_ref[0], exps, 0.0)
+    weight = jnp.sum(chosen, axis=1, keepdims=True) / jnp.sum(exps, axis=1, keepdims=True)
+    act, grad_gate, grad_up = swiglu_both(gate, up, back)
+    sact_ref[...] = act.astype(BF)
+    shared_grad = jnp.concatenate([grad_gate.astype(BF), grad_up.astype(BF)], axis=1)
+    sgrad_ref[...] = shared_grad
+
+    hots, weights = [], []
+    for b in range(blocks):
+        place = place_ref[pl.ds(step * blocks + b, 1), :]
+        hot = lax.broadcasted_iota(jnp.int32, (slot_count, 128), 0) == place
+        hots.append(hot.astype(F32).astype(BF))
+        tokens = slice(b * 128, (b + 1) * 128)
+        slots = slice(b * slot_count, (b + 1) * slot_count)
+        rows_ref[slots, :] = jnp.dot(hots[b], h2[tokens], preferred_element_type=F32).astype(BF)
+        gin_ref[slots, :] = jnp.dot(hots[b], cot[tokens], preferred_element_type=F32).astype(BF)
+        spread = jnp.broadcast_to(weight[tokens], (128, 128))
+        weights.append(
+            jnp.dot(
+                hot.astype(F32),
+                spread,
+                preferred_element_type=F32,
+                precision=lax.Precision.HIGHEST,
+            )[:, :1]
+        )
+    row_weight = jnp.concatenate(weights, axis=0)
+    rw_ref[...] = row_weight
+    rows = rows_ref[...]
+    picked_cot = gin_ref[...]
+    back = dot_nt(picked_cot, wd_ref[...])
+    gin_ref[...] = (picked_cot.astype(F32) * row_weight).astype(BF)
+    gate = jnp.dot(rows, wg_ref[...], preferred_element_type=F32)
+    up = jnp.dot(rows, wu_ref[...], preferred_element_type=F32)
+    act, grad_gate, grad_up = swiglu_both(gate, up, back * row_weight)
+    act_low, grad_gate, grad_up = act.astype(BF), grad_gate.astype(BF), grad_up.astype(BF)
+    act_ref[...] = act_low
+    gg_ref[...] = grad_gate
+    gu_ref[...] = grad_up
+    pg_ref[...] = jnp.sum(act_low.astype(F32) * back, axis=1, keepdims=True)
+    grad_rows = (dot_nt(grad_gate, wg_ref[...]) + dot_nt(grad_up, wu_ref[...])).astype(BF)
+    for b in range(blocks):
+        tokens = slice(b * 128, (b + 1) * 128)
+        slots = slice(b * slot_count, (b + 1) * slot_count)
+        total = dot_tn(hots[b], grad_rows[slots]) + dot_nt(shared_grad[tokens], sc_ref[...])
+        gh2_ref[tokens, :] = total.astype(BF)
+
+
+def swiglu_both(gate, up, grad):
+    sigmoid = 1.0 / (1.0 + jnp.exp(-gate))
+    silu = gate * sigmoid
+    return silu * up, grad * up * (sigmoid * (1.0 + gate * (1.0 - sigmoid))), grad * silu
+
+
+def out_kernel(slot_count, act_ref, rw_ref, place_ref, sact_ref, wd_ref, sd_ref, out_ref):
+    blocks = out_ref.shape[0] // 128
+    step = pl.program_id(0)
+    rows = (jnp.dot(act_ref[...], wd_ref[...], preferred_element_type=F32) * rw_ref[...]).astype(BF)
+    for b in range(blocks):
+        place = place_ref[pl.ds(step * blocks + b, 1), :]
+        hot = lax.broadcasted_iota(jnp.int32, (slot_count, 128), 0) == place
+        tokens = slice(b * 128, (b + 1) * 128)
+        slots = slice(b * slot_count, (b + 1) * slot_count)
+        total = dot_tn(hot.astype(F32).astype(BF), rows[slots]) + jnp.dot(
+            sact_ref[tokens, :], sd_ref[...], preferred_element_type=F32
+        )
+        out_ref[tokens, :] = total.astype(BF)
+
+
+def experts_chunk(h2, cot, expert_id, place, slot_count, expert_w, shared_w, router_weight):
     w_gate, w_up, w_down = expert_w
     s_both, s_down = shared_w
-    blocks, rows, width = h2.shape
-    per_block = slots.shape[1]
-    hidden_s = s_down.shape[0]
-    flat_h2 = h2.reshape(blocks * rows, width)
-    flat_cot = cot.reshape(blocks * rows, width)
-
-    def pick(table):
-        return (
-            jnp.einsum("bst,btd->bsd", slots, table, preferred_element_type=F32)
-            .astype(BF)
-            .reshape(blocks * per_block, width)
-        )
-
-    def place(table):
-        return jnp.einsum(
-            "bst,bsd->btd",
-            slots,
-            table.astype(BF).reshape(blocks, per_block, width),
-            preferred_element_type=F32,
-        ).reshape(blocks * rows, width)
-
-    cot_rows = pick(cot)
-    back_act = dot_nt(cot_rows, w_down)
-    shared_back = dot_nt(flat_cot, s_down)
-    shared_pre = matmul(flat_h2, jnp.concatenate([s_both, router_weight], axis=1))
-    probs = softmax_rows(shared_pre[:, 2 * hidden_s :])
-    chosen = jnp.arange(probs.shape[1], dtype=jnp.int32) == expert_id
-    weight = jnp.sum(jnp.where(chosen, probs, 0.0), axis=1).reshape(blocks, 1, rows)
-    row_weight = jnp.sum(slots.astype(F32) * weight, axis=2).reshape(-1, 1)
-    rows_in = pick(h2)
-    gate_pre = matmul(rows_in, w_gate)
-    up_pre = matmul(rows_in, w_up)
-    act, act_vjp = jax.vjp(swiglu, gate_pre, up_pre)
-    act_low = act.astype(BF)
-    grad_gate, grad_up = act_vjp(back_act * row_weight)
-    grad_gate = grad_gate.astype(BF)
-    grad_up = grad_up.astype(BF)
-    grad_rows = dot_nt(grad_gate, w_gate) + dot_nt(grad_up, w_up)
-    s_act, s_vjp = jax.vjp(swiglu, shared_pre[:, :hidden_s], shared_pre[:, hidden_s : 2 * hidden_s])
-    s_act = s_act.astype(BF)
-    s_grad = jnp.concatenate(s_vjp(shared_back), axis=1).astype(BF)
-    grad_h2 = (place(grad_rows) + dot_nt(s_grad, s_both)).astype(BF)
-
-    grad_h2, act_low, back_act, grad_gate, grad_up, s_act, s_grad = lax.optimization_barrier(
-        (grad_h2, act_low, back_act, grad_gate, grad_up, s_act, s_grad)
-    )
-    picked_grad = jnp.sum(act_low.astype(F32) * back_act, axis=1).reshape(blocks, per_block, 1)
-    token_grad = jnp.sum(slots.astype(F32) * picked_grad, axis=1)
-    out_rows = matmul(act_low, w_down) * row_weight
-    out = (place(out_rows) + matmul(s_act, s_down)).astype(BF)
-
-    grad_in = (cot_rows.astype(F32) * row_weight).astype(BF)
+    tokens, width = h2.shape
+    hidden, hidden_s = w_down.shape[0], s_down.shape[0]
+    experts = router_weight.shape[1]
+    blocks = 4
+    steps = tokens // (128 * blocks)
+    step_slots = slot_count * blocks
+    all_slots = step_slots * steps
+    half = 128
+    s_cat = jnp.concatenate(
+        [
+            s_both[:, :hidden_s],
+            router_weight,
+            jnp.zeros((width, half - hidden_s - experts), BF),
+            s_both[:, hidden_s:],
+            jnp.zeros((width, half - hidden_s), BF),
+        ],
+        axis=1,
+    )
+    s_tall = jnp.pad(s_down, ((0, half - hidden_s), (0, 0)))
+
+    def whole(array):
+        return pl.BlockSpec(array.shape, lambda i: (0, 0), pipeline_mode=pl.Buffered(1))
+
+    def blocked(rows, cols):
+        return pl.BlockSpec((rows, cols), lambda i: (i, 0))
+
+    token_rows = blocked(128 * blocks, width)
+    shape = jax.ShapeDtypeStruct
+    flops = 2 * all_slots * width * hidden * 5 + 2 * tokens * width * (4 * half + 4 * slot_count)
+    grad_h2, rows_in, grad_in, act, grad_gate, grad_up, row_weight, picked, s_act, s_grad = (
+        pl.pallas_call(
+            functools.partial(moe_kernel, hidden_s, experts, slot_count),
+            grid=(steps,),
+            in_specs=[
+                pl.BlockSpec(memory_space=pltpu.SMEM),
+                token_rows,
+                token_rows,
+                whole(place),
+                whole(w_gate),
+                whole(w_up),
+                whole(w_down),
+                whole(s_cat),
+                whole(s_tall),
+            ],
+            out_specs=[
+                token_rows,
+                blocked(step_slots, width),
+                blocked(step_slots, width),
+                blocked(step_slots, hidden),
+                blocked(step_slots, hidden),
+                blocked(step_slots, hidden),
+                blocked(step_slots, 1),
+                blocked(step_slots, 1),
+                blocked(128 * blocks, half),
+                blocked(128 * blocks, 2 * half),
+            ],
+            out_shape=[
+                shape((tokens, width), BF),
+                shape((all_slots, width), BF),
+                shape((all_slots, width), BF),
+                shape((all_slots, hidden), BF),
+                shape((all_slots, hidden), BF),
+                shape((all_slots, hidden), BF),
+                shape((all_slots, 1), F32),
+                shape((all_slots, 1), F32),
+                shape((tokens, half), BF),
+                shape((tokens, 2 * half), BF),
+            ],
+            cost_estimate=pl.CostEstimate(
+                flops=flops, bytes_accessed=12 * tokens * width, transcendentals=tokens * 1024
+            ),
+            compiler_params=pltpu.CompilerParams(vmem_limit_bytes=63 * 1024 * 1024),
+            name="experts",
+        )(expert_id.reshape(1), h2, cot, place, w_gate, w_up, w_down, s_cat, s_tall)
+    )
+
+    grad_h2, act, rows_in, grad_in, s_act, s_grad = lax.optimization_barrier(
+        (grad_h2, act, rows_in, grad_in, s_act, s_grad)
+    )
+    hot = jnp.arange(slot_count, dtype=jnp.int32)[None, :, None] == place[:, None, :]
+    token_grad = jnp.sum(jnp.where(hot, picked.reshape(-1, slot_count, 1), 0.0), axis=1)
+    out = pl.pallas_call(
+        functools.partial(out_kernel, slot_count),
+        grid=(steps,),
+        in_specs=[
+            blocked(step_slots, hidden),
+            blocked(step_slots, 1),
+            whole(place),
+            blocked(128 * blocks, half),
+            whole(w_down),
+            whole(s_tall),
+        ],
+        out_specs=token_rows,
+        out_shape=shape((tokens, width), BF),
+        cost_estimate=pl.CostEstimate(
+            flops=2 * width * (all_slots * hidden + tokens * (half + slot_count)),
+            bytes_accessed=4 * tokens * width,
+            transcendentals=0,
+        ),
+        compiler_params=pltpu.CompilerParams(vmem_limit_bytes=56 * 1024 * 1024),
+        name="expert_out",
+    )(act, row_weight, place, s_act, w_down, s_tall)
+    g_both = dot_tn(h2, s_grad)
+    g_both = jnp.concatenate([g_both[:, :hidden_s], g_both[:, half : half + hidden_s]], axis=1)
     grads = (
         dot_tn(rows_in, grad_gate),
         dot_tn(rows_in, grad_up),
-        dot_tn(act_low, grad_in),
-        dot_tn(flat_h2, s_grad),
-        dot_tn(s_act, flat_cot),
+        dot_tn(act, grad_in),
+        g_both,
+        dot_tn(s_act, cot)[:hidden_s],
     )
     return out, grad_h2, token_grad, grads
 
@@ -735,18 +893,25 @@
 
     def on_rows(h2, cot_gathered, routes_here):
         rows = h2.shape[0]
-        h2_all = gather_all(h2).reshape(devices, rows, width)
+        h2_all = gather_all(h2)
         slot_count = min(slot_limit, rows)
         member = jnp.any(routes_here == expert_id, axis=2)
         member_int = member.astype(jnp.int32)
         rank = jnp.cumsum(member_int, axis=1) - member_int
-        slots = (
-            (rank[:, None, :] == jnp.arange(slot_count, dtype=jnp.int32)[None, :, None])
-            & member[:, None, :]
-        ).astype(BF)
+        merged = 128 // rows
+        first_slot = jnp.arange(devices, dtype=jnp.int32) % merged * slot_count
+        place = jnp.where(member, rank + first_slot[:, None], -1).reshape(-1, 128)
         out, grad_h2, token_grad, grads = experts_chunk(
-            h2_all, cot_gathered, expert_id, slots, expert_w, shared_w, router_weight
+            h2_all,
+            cot_gathered,
+            expert_id,
+            place,
+            merged * slot_count,
+            expert_w,
+            shared_w,
+            router_weight,
         )
+        token_grad = token_grad.reshape(devices, rows)
         picked = lax.all_to_all(token_grad, ALL, split_axis=0, concat_axis=0, tiled=True)
         picked = jnp.sum(picked.reshape(experts, devices // experts, rows), axis=1).T
         grad_h2, out, grads, picked = lax.optimization_barrier(
@@ -756,7 +921,7 @@
 
     parts = max(1, devices * tok // 4096)
     if parts == 1:
-        cot_all = gather_all(cotangent).reshape(devices, tok, width)
+        cot_all = gather_all(cotangent)
         out_own, grad_h2_own, grad_router_probs, grads = on_rows(
             h_two, cot_all, routes_all
         )
@@ -765,7 +930,7 @@
 
         def step(total, inputs):
             h2, cot, routes_here = inputs
-            cot_part = gather_all(cot).reshape(devices, rows, width)
+            cot_part = gather_all(cot)
             out, grad_h2, picked, grads = on_rows(h2, cot_part, routes_here)
             total = tuple(a + b for a, b in zip(total, grads))
             return total, (out, grad_h2, picked)
@@ -803,16 +968,7 @@
         low_bound, q_nope, q_rope, expanded, key_rope, lse, grad_mixed, scale
     )
 
-    def own_columns(table):
-        rows = table.shape[0]
-        split = table.reshape(rows, n_groups, n_plane, rows_w)
-        mine = lax.dynamic_index_in_dim(split, place_in, 2, keepdims=False)
-        return mine.reshape(rows, n_groups * rows_w)
-
-    mixed_split = mixed.reshape(tok, n_groups, n_plane, rows_w).transpose(0, 2, 1, 3)
-    mixed_cols = lax.all_to_all(mixed_split, PLANE, split_axis=1, concat_axis=0)
-    mixed_cols = mixed_cols.reshape(plane_tok, n_groups * rows_w)
-    g_output = dot_tn(mixed_cols, plane_grad).astype(BF).reshape(n_groups, rows_w, width)
+    g_output = dot_tn(mixed_heads, plane_grad).astype(BF).reshape(n_groups, rows_w, width)
 
     grad_expanded = dex.astype(BF)
     grad_expand = dot_tn(compressed, grad_expanded)
@@ -831,12 +987,17 @@
         .astype(BF)
     )
     grad_hidden = (dot_nt(gq_nope, wq_nope) + dot_nt(gq_rope, wq_rope)).astype(BF)
-    key_grads, grad_hidden, grad_output_weight = swap(
+    key_grads, grad_hidden, grad_output_weight, g_shared = swap(
         4,
         ("plane_sum", key_grads),
         ("plane_sum", grad_hidden.reshape(n_plane, tok, width)),
         ("group_sum", g_output),
-    )
+        ("whole_swap", g_both.astype(BF).reshape(n_groups, n_plane, rows_w, 2 * shared_n)),
+    )
+    row_pairs = [
+        (g * n_plane + j, n_groups * j + g) for g in range(n_groups) for j in range(n_plane)
+    ]
+    grad_output_weight = lax.ppermute(grad_output_weight, ALL, row_pairs)
     later = lax.ppermute(key_grads[:tok].astype(BF), "g", down_pairs).astype(F32)
     key_grad = key_grads[tok:] + later
     latent_own = own_rows(latent)
@@ -865,7 +1026,9 @@
     grad_expand_weight = g_expand.transpose(1, 0, 2).reshape(kv_n, -1).astype(F32)
 
     latent_grads = latent_grads.reshape(plane_tok, RANK + ROPE)
-    g_latent = dot_tn(own_columns(hidden), latent_grads).astype(BF)
+    g_latent = dot_tn(hidden, latent_grads).astype(BF)
+    g_latent = g_latent.reshape(n_groups, n_plane, rows_w, RANK + ROPE)
+    g_latent = lax.dynamic_index_in_dim(g_latent, place_in, 1, keepdims=False)
     grad_hidden = grad_hidden + dot_nt(grad_latent, latent_weight)
     norm_one_back = jax.vjp(rms_norm, input_float, gain_one)[1]
     grad_x_norm, grad_gain_one = norm_one_back(grad_hidden)
@@ -881,13 +1044,11 @@
     small_grads = jnp.pad(small_grads, ((0, 0), (0, -small_grads.shape[1] % 1024)))
     grad_latent_weight, small_grads = swap(
         6,
-        ("group_sum", g_latent.reshape(n_groups, rows_w, RANK + ROPE)),
+        ("group_sum", g_latent),
         ("whole_sum", small_grads.reshape(n_groups, n_plane, -1, 128)),
     )
     small_grads = small_grads.reshape(-1)
-    g_shared = lax.all_to_all(
-        g_both.reshape(devices, rows_w, 2 * shared_n), ALL, split_axis=0, concat_axis=1
-    )
+    g_shared = g_shared.transpose(2, 0, 1, 3).reshape(rows_w, devices, 2 * shared_n).astype(F32)
     grad_shared_gate = g_shared[:, :, :shared_n].reshape(rows_w, devices * shared_n)
     grad_shared_up = g_shared[:, :, shared_n:].reshape(rows_w, devices * shared_n)
     return (

time: 1150 us -> 1070 us (0.930)
  matrix products: 349 us -> 121 us
  Pallas kernels: 441 us -> 550 us
  waiting for transfers between devices: 164 us -> 212 us
    pallas_call x0 -> x2, Pallas kernels: none -> 116 us  [the longest x1 92.3 us: experts_chunk(): pl.pallas_call(functools.partial(moe_kernel, hidden_s, experts, slot_coun...]
    dot_general x11 -> x6, matrix products: 111 us -> 17.9 us  [dot_nt(): lax.dot_general(left, right, (((1,), (1,)), ((), ())), preferred_element_...]
    dot_general x11 -> x6, matrix products: 93.3 us -> 18.2 us  [matmul(): return jnp.dot(left, right, preferred_element_type=F32)]
    dot_general x4 -> x0, matrix products: 68.9 us -> none  [the longest x2 41.1 us: place(): jnp.einsum('bst,bsd->btd', slots, table.astype(BF).reshape(blocks, per_bl...]
    reduce_scatter x2, waiting for transfers between devices: 54.9 us -> 87.4 us  [scatter_all(): return lax.psum_scatter(x, ALL, scatter_dimension=0, tiled=True)]
    all_gather x3, waiting for transfers between devices: 88.9 us -> 104 us  [gather_all(): return lax.all_gather(x, ALL, axis=0, tiled=True)]
  transfers between devices with their start and end apart: 10 -> 9, of which waited for: 3 -> 3; matrix products, arithmetic and copies ran while one was open for 28% -> 24% of each run, Pallas kernels for 39% -> 43%
where the time goes in v2:
time: 1070 us; the launch traced here: 1060 us
  Pallas kernels  550 us (51%)
  waiting for transfers between devices  212 us (20%)
  matrix products  121 us (11%)
  local copies, waits for them, and re-layouts  102 us (10%)
  other arithmetic  43.1 us (4%)
  between operations  15.3 us (1%)
  starting transfers between devices  13.8 us (1%)
    pallas_call x7, Pallas kernels, exchange(): pl.pallas_call(functools.partial(exchange_kernel, n_groups, n_plane, kind...  401 us
    all_gather x3, waiting for transfers between devices, gather_all(): return lax.all_gather(x, ALL, axis=0, tiled=True)  104 us
    pallas_call x1, Pallas kernels, experts_chunk(): pl.pallas_call(functools.partial(moe_kernel, hidden_s, experts, slot_coun...  92.3 us
    reduce_scatter x2, waiting for transfers between devices, scatter_all(): return lax.psum_scatter(x, ALL, scatter_dimension=0, tiled=True)  87.4 us
    dot_general x11, matrix products, dot_tn(): lax.dot_general(left, right, (((0,), (0,)), ((), ())), preferred_element_...  84.6 us
    pallas_call x1, Pallas kernels, experts_chunk(): pl.pallas_call(functools.partial(out_kernel, slot_count), grid=(steps,),...  23.9 us
  transfers between devices with their start and end apart: 9, of which 3 were waited for; matrix products, arithmetic and copies ran while one was open for 24% of the time, Pallas kernels for 43%

profile of v2, /device:TPU:1, one launch (start us, length us, event | category | flops | bytes accessed | tf_op | source)
XLA Modules:
  0.0 1056.2 jit_solution(1891823523791717218)
XLA Ops:
  16.8 89.8 %exchange_0.1 = (bf16[8,128,2048]{2,1,0:T(8,128)(2,1)}, bf16[4,8,32,128]{3,2,1,0:T(8,128)(2,1)}, bf16[4,8,64,576]{3,2,1,0:T(8,128)(2,1)}, bf16[4,8,64,512]{3,2,1,0:T(8,128)(2,1)}) custom-call(bf16[128,2048]{1,0:T(8,128)(2,1)} %refs_0_.1, bf16[32,128]{1,0:T(8,128)(2,1)} %pad_bitcast_fusion.1.refs_1_, bf16[64,576]{1,0:T(8,128)(2,1)} %refs_2_.1, ...), custom_call_target="tpu_custom_call" | custom-call | tf_op jit(solution)/shard_map/exchange_0/pallas_call | solution.py:547
  107.8 2.9 slice.158
  111.2 3.2 fusion
  116.3 3.4 fusion.50
  121.8 3.4 fusion.15
  127.2 47.5 %exchange_1.1 = bf16[8,128,576]{2,1,0:T(8,128)(2,1)} custom-call(bf16[128,576]{1,0:T(8,128)(2,1)} %fusion.32.refs_0_), custom_call_target="tpu_custom_call" | custom-call | tf_op jit(solution)/shard_map/exchange_1/pallas_call | solution.py:547
  185.9 3.8 fusion.22
  191.4 4.5 convolution_convert_fusion.ex_ref
  197.2 11.5 %attend.1 = (bf16[1024,256]{1,0:T(8,128)(2,1)S(1)}, f32[1024,2]{1,0:T(8,128)S(1)}) custom-call(s32[1024,1]{1,0:T(8,128)S(1)} %copy.213.low_ref, bf16[1024,256]{1,0:T(8,128)(2,1)S(1)} %convolution_convert_fusion.6.qn_ref, bf16[1024,128]{1,0:T(8,128)(2,1)S(1)} %copy.214.qr_ref, bf16[2048,512]{1,0:T(8,128)(2,1)} %convolution_convert_fusion.ex_ref, ...), custom_call_target="tpu_custom_call" | custom-call | flops 1677721600 | bytes 4194304 | tf_op jit(solution)/shard_map/attend/pallas_call | solution.py:117
  210.3 20.4 %exchange_2.1 = bf16[8,128,256]{2,1,0:T(8,128)(2,1)} custom-call(bf16[8,128,256]{2,1,0:T(8,128)(2,1)} %bitcast.150), custom_call_target="tpu_custom_call" | custom-call | tf_op jit(solution)/shard_map/exchange_2/pallas_call | solution.py:547
  232.1 4.9 multiply_reduce_fusion.3
  243.6 3.6 all-to-all-start
  248.2 4.8 copy.219
  253.0 4.7 copy.220
  261.5 18.9 %all-to-all-done = bf16[1,64,32,176]{3,1,0,2:T(8,128)(2,1)S(1)} async-done(((bf16[1,64,32,176]{3,1,0,2:T(8,128)(2,1)}), bf16[1,64,32,176]{3,1,0,2:T(8,128)(2,1)S(1)}, u32[]{:S(2)}, u32[]{:S(2)}) %all-to-all-start) | async-done | bytes 720928 | tf_op jit(solution)/shard_map/all_to_all | solution.py:845
  283.0 104.2 %all-gather.6.cloned.1.call-done.h2_ref = bf16[4096,2048]{1,0:T(8,128)(2,1)} async-done(((bf16[128,2048]{1,0:T(8,128)(2,1)}), bf16[4096,2048]{1,0:T(8,128)(2,1)}) %all-gather.6.cloned.1.call-update) | async-done | bytes 16777232 | tf_op jit(solution)/shard_map/all_gather | solution.py:564
  387.2 92.3 %experts.1 = (bf16[4096,2048]{1,0:T(8,128)(2,1)}, bf16[3072,2048]{1,0:T(8,128)(2,1)}, bf16[3072,2048]{1,0:T(8,128)(2,1)}, bf16[3072,704]{1,0:T(8,128)(2,1)}, bf1...) custom-call(s32[1]{0:T(128)} %bitcast.21.id_ref, ...), custom_call_target="tpu_custom_call" | custom-call | flops 59324235776 | bytes 100663296 | tf_op jit(solution)/shard_map/experts/pallas_call | solution.py:684
  482.6 2.9 all-to-all-start.1
  485.5 11.1 %fusion.54 = bf16[2048,256]{0,1:T(8,128)(2,1)S(1)} fusion(bf16[4096,2048]{1,0:T(8,128)(2,1)} %all-gather.6.cloned.1.call-done.h2_ref, bf16[4096,256]{1,0:T(8,128)(2,1)} %get-tuple-element.78), kind=kOutput, calls=%fused_computation.142 | convolution fusion | flops 4294967296 | bytes 19922944 | tf_op jit(solution)/shard_map/dot_general | solution.py:54
  496.7 9.7 fusion.12
  506.4 23.9 %expert_out.1 = bf16[4096,2048]{1,0:T(8,128)(2,1)} custom-call(bf16[3072,704]{1,0:T(8,128)(2,1)} %get-tuple-element.71.act_ref, f32[3072,1]{1,0:T(8,128)} %get-tuple-element.72.rw_ref, s32[32,128]{1,0:T(8,128)} %subtract_select_fusion.place_ref, bf16[4096,128]{1,0:T(8,128)(2,1)} %get-tuple-element.73.sact_ref, bf16[704,2048]{1,0:T(8,128)(2,1)} %bitcast.203, ...), custom_call_target="tpu_custom_call" | custom-call | flops 12616466432 | bytes 33554432 | tf_op jit(solution)/shard_map/expert_out/pallas_call | solution.py:735
  530.4 15.4 %fusion.52 = f32[2048,704]{0,1:T(8,128)} fusion(bf16[3072,2048]{1,0:T(8,128)(2,1)} %get-tuple-element.74, bf16[3072,704]{1,0:T(8,128)(2,1)} %get-tuple-element.76), kind=kOutput, calls=%fused_computation.140 | convolution fusion | flops 8858370048 | bytes 22675456 | tf_op jit(solution)/shard_map/dot_general | solution.py:54
  545.8 15.4 %fusion.51 = f32[2048,704]{0,1:T(8,128)} fusion(bf16[3072,2048]{1,0:T(8,128)(2,1)} %get-tuple-element.74, bf16[3072,704]{1,0:T(8,128)(2,1)} %get-tuple-element.75), kind=kOutput, calls=%fused_computation.139 | convolution fusion | flops 8858370048 | bytes 22675456 | tf_op jit(solution)/shard_map/dot_general | solution.py:54
  561.2 11.5 %fusion.53 = f32[704,2048]{1,0:T(8,128)} fusion(bf16[3072,704]{1,0:T(8,128)(2,1)S(1)} %bitcast.210, bf16[3072,2048]{1,0:T(8,128)(2,1)S(1)} %bitcast.208), kind=kOutput, calls=%fused_computation.141 | convolution fusion | flops 8858370048 | bytes 22675456 | tf_op jit(solution)/shard_map/dot_general | solution.py:54
  573.6 87.4 %reduce-scatter.3.cloned.1.call-done = bf16[128,2048]{1,0:T(8,128)(2,1)} async-done(((bf16[4096,2048]{1,0:T(8,128)(2,1)}), bf16[128,2048]{1,0:T(8,128)(2,1)}) %reduce-scatter.3.cloned.1.call-update) | async-done | bytes 524304 | tf_op jit(solution)/shard_map/reduce_scatter | solution.py:892
  661.0 2.3 reshape.514
  671.7 2.5 reshape.501
  678.6 56.6 %exchange_3.1 = bf16[8,128,2048]{2,1,0:T(8,128)(2,1)} custom-call(bf16[128,2048]{1,0:T(8,128)(2,1)} %fusion.44.refs_0_), custom_call_target="tpu_custom_call" | custom-call | tf_op jit(solution)/shard_map/exchange_3/pallas_call | solution.py:547
  735.2 4.6 convolution_convert_fusion.5.gm_ref
  739.9 21.0 %attend_back.1 = (f32[1024,256]{1,0:T(8,128)}, f32[1024,128]{1,0:T(8,128)}, f32[2048,512]{1,0:T(8,128)}, f32[2048,64]{1,0:T(8,128)}) custom-call(s32[1024,1]{1,0:T(8,128)} %copy-done.2, bf16[1024,256]{1,0:T(8,128)(2,1)} %copy-done.5, bf16[1024,128]{1,0:T(8,128)(2,1)} %copy-done.4, bf16[2048,512]{1,0:T(8,128)(2,1)} %convolution_convert_fusion.ex_ref, ...), custom_call_target="tpu_custom_call" | custom-call | flops 4362076160 | bytes 8388608 | tf_op jit(solution)/shard_map/attend_back/pallas_call | solution.py:192
  760.9 2.6 convert_element_type.219
  771.5 3.3 convolution_convert_fusion.3
  777.4 6.1 copy.231
  783.5 5.6 convert_element_type.227.refs_0_
  789.2 4.7 convolution_convert_fusion.2
  795.1 4.3 fusion.3
  799.4 110.4 %exchange_4.1 = (f32[256,576]{1,0:T(8,128)}, f32[128,2048]{1,0:T(8,128)}, f32[64,2048]{1,0:T(8,128)}, bf16[4,8,64,176]{3,2,1,0:T(8,128)(2,1)}) custom-call(bf16[8,256,576]{2,1,0:T(8,128)(2,1)} %bitcast.152, bf16[8,128,2048]{2,1,0:T(8,128)(2,1)} %bitcast.151, bf16[4,64,2048]{2,1,0:T(8,128)(2,1)} %bitcast.183, bf16[4,8,64,176]{3,2,1,0:T(8,128)(2,1)} %bitcast.159), custom_call_target="tpu_custom_call" | custom-call | tf_op jit(solution)/shard_map/exchange_4/pallas_call | solution.py:547
  912.1 5.9 collective-permute-start.1
  919.5 4.3 fusion.5
  926.7 2.7 reshape.505
  929.4 2.8 copy.237
  932.2 2.7 reshape.504
  939.2 4.6 fusion.11
  944.9 57.0 %exchange_5.1 = (bf16[8,64,384]{2,1,0:T(8,128)(2,1)}, bf16[8,16,512]{2,1,0:T(8,128)(2,1)}, bf16[8,128,576]{2,1,0:T(8,128)(2,1)}) custom-call(bf16[4,8,64,384]{3,2,1,0:T(8,128)(2,1)} %convert_element_type.227.refs_0_, bf16[4,8,16,512]{3,2,1,0:T(8,128)(2,1)} %bitcast.191, bf16[128,576]{1,0:T(8,128)(2,1)} %copy-done.30), custom_call_target="tpu_custom_call" | custom-call | tf_op jit(solution)/shard_map/exchange_5/pallas_call | solution.py:547
  1001.9 6.7 bitcast_convert_fusion
  1008.6 4.4 copy.233
  1017.6 19.3 %exchange_6.1 = (f32[64,576]{1,0:T(8,128)}, f32[16,128]{1,0:T(8,128)}) custom-call(bf16[4,64,576]{2,1,0:T(8,128)(2,1)} %dynamic-slice_bitcast_fusion.refs_0_, f32[4,8,16,128]{3,2,1,0:T(8,128)} %copy.254), custom_call_target="tpu_custom_call" | custom-call | tf_op jit(solution)/shard_map/exchange_6/pallas_call | solution.py:547
  1043.8 3.1 fusion.7
  (289 shorter events, 102.5 us)
Async XLA Ops:
  7.2 224.9 %all-gather.4.cloned.1.call-start = ((), (), s32[]{:S(2)}) async-start(), calls=%async_computation.4 | async-start | bytes 8650752 | tf_op jit(solution)/shard_map/all_gather | solution.py:564
  7.9 275.1 %all-gather.8.cloned.1.call-start = ((), (), s32[]{:S(2)}) async-start(), calls=%async_computation.6 | async-start | bytes 17301504 | tf_op jit(solution)/shard_map/all_gather | solution.py:564
  8.7 378.5 %all-gather.6.cloned.1.call-start = ((), (), s32[]{:S(2)}) async-start(), calls=%async_computation.5 | async-start | bytes 17301504 | tf_op jit(solution)/shard_map/all_gather | solution.py:564
  107.8 73.2 %copy-start.18 = (bf16[2048,128]{1,0:T(8,128)(2,1)}, bf16[2048,128]{1,0:T(8,128)(2,1)S(1)}, u32[]{:S(2)}) copy-start(bf16[2048,128]{1,0:T(8,128)(2,1)S(1)} %slice.168) | copy-start | bytes 1572868
  110.9 14.4 %copy-start.51 = (f32[512]{0:T(512)}, f32[512]{0:T(512)S(1)}, u32[]{:S(2)}) copy-start(f32[512]{0:T(512)S(1)} %reshape.508) | copy-start | bytes 6148
  125.3 53.5 %copy-start.26 = (bf16[1024,32]{1,0:T(8,128)(2,1)}, bf16[1024,32]{1,0:T(8,128)(2,1)S(1)}, u32[]{:S(2)}) copy-start(bf16[1024,32]{1,0:T(8,128)(2,1)S(1)} %get-tuple-element.211) | copy-start | bytes 196612
  178.8 58.3 %copy-start.44 = (f32[2048]{0:T(1024)}, f32[2048]{0:T(1024)S(1)}, u32[]{:S(2)}) copy-start(f32[2048]{0:T(1024)S(1)} %reshape.509) | copy-start | bytes 24580
  179.0 18.1 %copy-start.2 = (s32[1024,1]{1,0:T(8,128)}, s32[1024,1]{1,0:T(8,128)S(1)}, u32[]{:S(2)}) copy-start(s32[1024,1]{1,0:T(8,128)S(1)} %copy.213.low_ref) | copy-start | bytes 12292
  181.0 8.7 copy-start.15
  182.4 13.5 %copy-start.19 = (bf16[2048,2,128]{0,2,1:T(8,128)(2,1)}, bf16[2048,2,128]{0,2,1:T(8,128)(2,1)S(1)}, u32[]{:S(2)}) copy-start(bf16[2048,2,128]{0,2,1:T(8,128)(2,1)S(1)} %slice.159) | copy-start | bytes 3145732
  190.0 7.1 copy-start.4
  197.2 11.5 %copy-start.5 = (bf16[1024,256]{1,0:T(8,128)(2,1)}, bf16[1024,256]{1,0:T(8,128)(2,1)S(1)}, u32[]{:S(2)}) copy-start(bf16[1024,256]{1,0:T(8,128)(2,1)S(1)} %convolution_convert_fusion.6.qn_ref) | copy-start | bytes 1572868
  197.2 34.9 %copy-start.11 = (bf16[128,2048]{1,0:T(8,128)(2,1)S(1)}, bf16[128,2048]{1,0:T(8,128)(2,1)}, u32[]{:S(2)}) copy-start(bf16[128,2048]{1,0:T(8,128)(2,1)} %refs_0_.1) | copy-start | bytes 1572868
  232.1 6.9 copy-start.40
  232.1 8.2 copy-start.41
  237.0 6.6 copy-start.55
  243.6 36.7 %all-to-all-start = ((bf16[1,64,32,176]{3,1,0,2:T(8,128)(2,1)}), bf16[1,64,32,176]{3,1,0,2:T(8,128)(2,1)S(1)}, u32[]{:S(2)}, u32[]{:S(2)}) async-start(bf16[1,64,32,176]{3,1,0,2:T(8,128)(2,1)} %copy.221), calls=%async_computation | async-start | bytes 2097152 | tf_op jit(solution)/shard_map/all_to_all | solution.py:845
  247.2 413.8 %reduce-scatter.3.cloned.1.call-start = ((), (), s32[]{:S(2)}) async-start(), calls=%async_computation.7 | async-start | bytes 17301504 | tf_op jit(solution)/shard_map/reduce_scatter | solution.py:892
  253.0 6.9 copy-start.42
  260.0 407.6 %copy-start.14 = (bf16[2048,16]{1,0:T(8,128)(2,1)}, bf16[2048,16]{1,0:T(8,128)(2,1)S(1)}, u32[]{:S(2)}) copy-start(bf16[2048,16]{1,0:T(8,128)(2,1)S(1)} %reshape.488) | copy-start | bytes 196612
  482.6 91.0 %all-to-all-start.1 = ((f32[32,1,128]{2,1,0:T(1,128)}), f32[32,1,128]{2,1,0:T(1,128)S(1)}, u32[]{:S(2)}, u32[]{:S(2)}) async-start(f32[32,1,128]{2,1,0:T(1,128)} %bitcast.32), calls=%async_computation.2 | async-start | bytes 32768 | tf_op jit(solution)/shard_map/all_to_all | solution.py:915
  485.5 11.2 %copy-start.28 = (bf16[4096,128]{1,0:T(8,128)(2,1)S(1)}, bf16[4096,128]{1,0:T(8,128)(2,1)}, u32[]{:S(2)}) copy-start(bf16[4096,128]{1,0:T(8,128)(2,1)} %get-tuple-element.73.sact_ref) | copy-start | bytes 3145732
  485.5 558.3 %reduce-scatter.5.cloned.1.call-start = ((), (), s32[]{:S(2)}) async-start(), calls=%async_computation.8 | async-start | bytes 17301504 | tf_op jit(solution)/shard_map/reduce_scatter | solution.py:892
  530.4 30.8 %slice-start = ((s8[12582912]{0:T(1024)(128)(4,1)}), s8[4194304]{0:T(1024)(128)(4,1)S(1)}, s32[]{:S(2)}) async-start(s8[12582912]{0:T(1024)(128)(4,1)} %bitcast.207), calls=%async_computation.10 | async-start | bytes 8388608
  530.4 30.8 %slice-start.1 = ((s8[12582912]{0:T(1024)(128)(4,1)}), s8[4194304]{0:T(1024)(128)(4,1)S(1)}, s32[]{:S(2)}) async-start(s8[12582912]{0:T(1024)(128)(4,1)} %bitcast.207), calls=%async_computation.11 | async-start | bytes 8388608
  530.4 30.8 %slice-start.3 = ((s8[4718592]{0:T(1024)(128)(4,1)}), s8[4194304]{0:T(1024)(128)(4,1)S(1)}, s32[]{:S(2)}) async-start(s8[4718592]{0:T(1024)(128)(4,1)} %bitcast.209), calls=%async_computation.13 | async-start | bytes 8388608
  545.8 15.4 %slice-start.4 = ((s8[4718592]{0:T(1024)(128)(4,1)}), s8[524288]{0:T(1024)(128)(4,1)S(1)}, s32[]{:S(2)}) async-start(s8[4718592]{0:T(1024)(128)(4,1)} %bitcast.209), calls=%async_computation.14 | async-start | bytes 1048576
  545.8 15.4 %slice-start.2 = ((s8[12582912]{0:T(1024)(128)(4,1)}), s8[4194304]{0:T(1024)(128)(4,1)S(1)}, s32[]{:S(2)}) async-start(s8[12582912]{0:T(1024)(128)(4,1)} %bitcast.207), calls=%async_computation.12 | async-start | bytes 8388608
  661.0 6.6 copy-start.13
  661.0 6.9 copy-start.45
  661.0 7.0 copy-start.56
  661.0 6.9 copy-start.8
  667.6 8.9 copy-start.61
  676.4 63.4 %copy-start.57 = (f32[128]{0:T(128)}, f32[128]{0:T(128)S(1)}, u32[]{:S(2)}) copy-start(f32[128]{0:T(128)S(1)} %multiply_multiply_fusion.2) | copy-start | bytes 1540
  777.4 11.7 %copy-start.1 = (bf16[1024,256]{1,0:T(8,128)(2,1)S(1)}, bf16[1024,256]{1,0:T(8,128)(2,1)}, u32[]{:S(2)}) copy-start(bf16[1024,256]{1,0:T(8,128)(2,1)} %copy-done) | copy-start | bytes 1572868
  910.8 24.0 %collective-permute-start = (bf16[128,576]{1,0:T(8,128)(2,1)S(1)}, bf16[128,576]{1,0:T(8,128)(2,1)S(1)}, u32[]{:S(2)}, u32[]{:S(2)}) collective-permute-start(bf16[128,576]{1,0:T(8,128)(2,1)S(1)} %slice.230), channel_id=1, source_target_pairs={{8,0},{16,8},{24,16},{9,1},{17,9},{25,17},{10,2},{18,10},{26,18},{... | collective-permute-start | bytes 442376 | tf_op jit(solution)/shard_map/ppermute | solution.py:1001
  912.1 131.7 %collective-permute-start.1 = (f32[64,2048]{1,0:T(8,128)}, f32[64,2048]{1,0:T(8,128)}, u32[]{:S(2)}, u32[]{:S(2)}) collective-permute-start(f32[64,2048]{1,0:T(8,128)} %get-tuple-element.96), channel_id=1, source_target_pairs={{0,0},{1,4},{2,8},{3,12},{4,16},{5,20},{6,24},{7,28},{8,1},{9,5},{... | collective-permute-start | bytes 1572872 | tf_op jit(solution)/shard_map/ppermute | solution.py:1000
  925.1 10.8 %copy-start.52 = (f32[512]{0:T(512)S(1)}, f32[512]{0:T(512)}, u32[]{:S(2)}) copy-start(f32[512]{0:T(512)} %copy-done.51) | copy-start | bytes 6148
  925.1 10.8 %copy-start.59 = (f32[128]{0:T(128)S(1)}, f32[128]{0:T(128)}, u32[]{:S(2)}) copy-start(f32[128]{0:T(128)} %fusion.38) | copy-start | bytes 1540
  925.1 11.9 %copy-start.65 = (f32[128]{0:T(128)S(1)}, f32[128]{0:T(128)}, u32[]{:S(2)}) copy-start(f32[128]{0:T(128)} %copy-done.64) | copy-start | bytes 1540
  926.7 12.5 %copy-start.48 = (f32[2048]{0:T(1024)S(1)}, f32[2048]{0:T(1024)}, u32[]{:S(2)}) copy-start(f32[2048]{0:T(1024)} %copy-done.47) | copy-start | bytes 24580
  934.8 9.1 copy-start.35
  934.8 9.1 copy-start.50
  1008.6 33.9 %copy-start.63 = (f32[128]{0:T(128)S(1)}, f32[128]{0:T(128)}, u32[]{:S(2)}) copy-start(f32[128]{0:T(128)} %copy-done.62) | copy-start | bytes 1540
  1008.6 33.9 %copy-start.66 = (f32[128]{0:T(128)S(1)}, f32[128]{0:T(128)}, u32[]{:S(2)}) copy-start(f32[128]{0:T(128)} %get-tuple-element.187) | copy-start | bytes 1540
  1008.6 35.2 %copy-start.17 = (bf16[128,2048]{1,0:T(8,128)(2,1)S(1)}, bf16[128,2048]{1,0:T(8,128)(2,1)}, u32[]{:S(2)}) copy-start(bf16[128,2048]{1,0:T(8,128)(2,1)} %param.35) | copy-start | bytes 1572868
  1008.6 35.2 %copy-start.58 = (f32[128]{0:T(128)S(1)}, f32[128]{0:T(128)}, u32[]{:S(2)}) copy-start(f32[128]{0:T(128)} %copy-done.57) | copy-start | bytes 1540
  1040.3 6.6 copy-start.46
  (34 other events, 113.4 us)
Sparse Core Ops, SparseCore 0:
  10.8 124.2 all-gather.3
  138.0 131.7 all-gather.7
  272.7 114.4 all-gather.5
  479.7 181.2 reduce-scatter.2
  663.1 255.4 reduce-scatter.4

commit v3 on v2

--- a/solution.py
+++ b/solution.py
@@ -564,15 +564,209 @@
     return lax.all_gather(x, ALL, axis=0, tiled=True)
 
 
+class StreamSum:
+    def __init__(self, w, steps, stage, from_core, pairs, from_chips, totals, parts, sems, credit):
+        self.w, self.steps = w, steps
+        self.stage, self.from_core, self.pairs = stage, from_core, pairs
+        self.from_chips, self.totals, self.parts = from_chips, totals, parts
+        self.core_sems, self.chip_sems, self.chip_recv, self.group_sems = sems
+        self.credit = credit
+
+    @staticmethod
+    def distances(step):
+        half = lax.rem(step, 2)
+        return 1 + 2 * half, 2 - 2 * half
+
+    def core_copy(self, step, i):
+        slot = lax.rem(step, 2)
+        return pltpu.make_async_remote_copy(
+            src_ref=self.stage.at[slot, 2 * i + 1 - self.w.c],
+            dst_ref=self.from_core.at[slot, i],
+            send_sem=self.core_sems.at[0, slot, i],
+            recv_sem=self.core_sems.at[1, slot, i],
+            device_id=self.w.partner(),
+            device_id_type=MESH,
+        )
+
+    def chip_copy(self, step, i):
+        slot, distance = lax.rem(step, 2), self.distances(step)[i]
+        group_at = step // 2
+        return pltpu.make_async_remote_copy(
+            src_ref=self.pairs.at[slot, i],
+            dst_ref=self.from_chips.at[group_at, distance - 1],
+            send_sem=self.chip_sems.at[slot, i],
+            recv_sem=self.chip_recv.at[group_at, distance - 1],
+            device_id=self.w.at_chip(lax.rem(self.w.p + distance, 4)),
+            device_id_type=MESH,
+        )
+
+    def chip_arrival(self, group_at, distance):
+        return pltpu.make_async_remote_copy(
+            src_ref=self.pairs.at[0, 0],
+            dst_ref=self.from_chips.at[group_at, distance - 1],
+            send_sem=self.chip_sems.at[0, 0],
+            recv_sem=self.chip_recv.at[group_at, distance - 1],
+            device_id=self.w.at_chip(lax.rem(self.w.p + distance, 4)),
+            device_id_type=MESH,
+        )
+
+    def group_copy(self, group_at):
+        return pltpu.make_async_remote_copy(
+            src_ref=self.totals.at[group_at],
+            dst_ref=self.parts.at[group_at],
+            send_sem=self.group_sems.at[0, group_at],
+            recv_sem=self.group_sems.at[1, group_at],
+            device_id=self.w.at_group(self.w.group_peer(group_at + 1)),
+            device_id_type=MESH,
+        )
+
+    def open_stage(self, step):
+        @pl.when(step >= 2)
+        def _():
+            for i in range(2):
+                self.core_copy(step, i).wait_send()
+
+    def push(self, step):
+        @pl.when(step >= 2)
+        def _():
+            pl.semaphore_wait(self.credit, 1)
+
+        for i in range(2):
+            self.core_copy(step, i).start()
+
+    def merge(self, step):
+        slot = lax.rem(step, 2)
+        for i in range(2):
+            self.core_copy(step, i).wait_recv()
+            sends = slot == 0 if i else slot >= 0
+
+            @pl.when(sends & (step >= 2))
+            def _():
+                self.chip_copy(step, i).wait_send()
+
+            sum_rows(
+                self.pairs.at[slot, i],
+                [self.stage.at[slot, 2 * i + self.w.c], self.from_core.at[slot, i]],
+            )
+
+            @pl.when(sends)
+            def _():
+                self.chip_copy(step, i).start()
+
+        @pl.when(step + 2 < self.steps)
+        def _():
+            pl.semaphore_signal(
+                self.credit, inc=1, device_id=self.w.partner(), device_id_type=MESH
+            )
+
+    def plane_total(self, group_at):
+        for distance in (1, 2, 3):
+            self.chip_arrival(group_at, distance).wait_recv()
+        return [self.pairs.at[1, 1]] + [self.from_chips.at[group_at, d] for d in range(3)]
+
+    def advance(self, step):
+        @pl.when(step >= 1)
+        def _():
+            last = step - 1
+
+            @pl.when((lax.rem(last, 2) == 0) & (last >= 2))
+            def _():
+                group_at = last // 2 - 1
+                sum_rows(self.totals.at[group_at], self.plane_total(group_at))
+                self.group_copy(group_at).start()
+
+            self.merge(last)
+
+    def finish(self, out):
+        steps = self.steps
+        self.merge(steps - 1)
+        sources = self.plane_total(steps // 2 - 1)
+        groups = steps // 2 - 1
+        for d in range(groups):
+            self.group_copy(d).wait_recv()
+            sources.append(self.parts.at[d])
+        sum_rows(out, sources)
+        for d in range(groups):
+            self.group_copy(d).wait_send()
+        for i in range(2):
+            self.core_copy(steps - 2, i).wait_send()
+            self.core_copy(steps - 1, i).wait_send()
+            self.chip_copy(steps - 2, i).wait_send()
+        self.chip_copy(steps - 1, 0).wait_send()
+
+    @staticmethod
+    def scratch(n_groups, rows, width):
+        dma = pltpu.SemaphoreType.DMA
+        return [
+            pltpu.VMEM((2, 4, rows, width), BF),
+            pltpu.VMEM((2, 2, rows, width), BF),
+            pltpu.VMEM((2, 2, rows, width), BF),
+            pltpu.VMEM((n_groups, 3, rows, width), BF),
+            pltpu.VMEM((n_groups - 1, rows, width), BF),
+            pltpu.VMEM((n_groups - 1, rows, width), BF),
+            dma((2, 2, 2)),
+            dma((2, 2)),
+            dma((n_groups, 3)),
+            dma((2, n_groups - 1)),
+            pltpu.SemaphoreType.REGULAR,
+        ]
+
+
+def swiglu_both(gate, up, grad):
+    sigmoid = 1.0 / (1.0 + jnp.exp(-gate))
+    silu = gate * sigmoid
+    return silu * up, grad * up * (sigmoid * (1.0 + gate * (1.0 - sigmoid))), grad * silu
+
+
+def step_chips(w, step):
+    group = lax.rem(w.g + 1 + step // 2, w.n_groups)
+    return [group * 4 + lax.rem(w.p + d, 4) for d in StreamSum.distances(step)]
+
+
+def hot_rows(place, rows, core, slot_count):
+    mine = place[:, core * rows : (core + 1) * rows]
+    return lax.broadcasted_iota(jnp.int32, (slot_count, rows), 0) == mine
+
+
 def moe_kernel(
-    first_logit, experts, slot_count, id_ref, h2_ref, cot_ref, place_ref, wg_ref, wu_ref, wd_ref,
-    sc_ref, sd_ref,
-    gh2_ref, rows_ref, gin_ref, act_ref, gg_ref, gu_ref, rw_ref, pg_ref, sact_ref, sgrad_ref,
+    n_groups, experts, first_logit, slot_count,
+    h2_hbm, cot_hbm, place_ref, wg_ref, wu_ref, wd_ref, sc_ref, sd_ref,
+    sum_ref, rows_ref, gin_ref, act_ref, gg_ref, gu_ref, rw_ref, sact_ref, sgrad_ref, tok_ref,
+    h2_buf, cot_buf, load_sems, *comm,
 ):
-    blocks = h2_ref.shape[0] // 128
-    step = pl.program_id(0)
+    rows = sum_ref.shape[0]
+    step, steps = pl.program_id(0), 2 * n_groups
+    w = Wires(n_groups, 8, None, None)
+    stream = StreamSum(w, steps, *comm[:6], comm[6:10], comm[10])
+    expert_id = w.g * 4 + w.p
     half = sc_ref.shape[1] // 2
-    h2, cot = h2_ref[...], cot_ref[...]
+
+    def loads(at):
+        slot = lax.rem(at, 2)
+        for i, chip in enumerate(step_chips(w, at)):
+            source = pl.ds(pl.multiple_of(chip * 2 * rows, 2 * rows), 2 * rows)
+            target = pl.ds(i * 2 * rows, 2 * rows)
+            for k, (hbm, buf) in enumerate(((h2_hbm, h2_buf), (cot_hbm, cot_buf))):
+                yield pltpu.make_async_copy(
+                    hbm.at[source], buf.at[slot, target], load_sems.at[slot, i, k]
+                )
+
+    @pl.when(step == 0)
+    def _():
+        for copy in loads(step):
+            copy.start()
+        w.meet()
+
+    @pl.when(step + 1 < steps)
+    def _():
+        for copy in loads(step + 1):
+            copy.start()
+
+    for copy in loads(step):
+        copy.wait()
+    slot = lax.rem(step, 2)
+    h2, cot = h2_buf[slot], cot_buf[slot]
+    chips = step_chips(w, step)
 
     pre = jnp.dot(h2, sc_ref[...], preferred_element_type=F32)
     back = dot_nt(cot, sd_ref[...])
@@ -580,83 +774,110 @@
     lane = lax.broadcasted_iota(jnp.int32, gate.shape, 1)
     logits = jnp.where((lane >= first_logit) & (lane < first_logit + experts), gate, -1e30)
     exps = jnp.exp(logits - jnp.max(logits, axis=1, keepdims=True))
-    chosen = jnp.where(lane == first_logit + id_ref[0], exps, 0.0)
+    chosen = jnp.where(lane == first_logit + expert_id, exps, 0.0)
     weight = jnp.sum(chosen, axis=1, keepdims=True) / jnp.sum(exps, axis=1, keepdims=True)
     act, grad_gate, grad_up = swiglu_both(gate, up, back)
-    sact_ref[...] = act.astype(BF)
+    shared_act = act.astype(BF)
     shared_grad = jnp.concatenate([grad_gate.astype(BF), grad_up.astype(BF)], axis=1)
-    sgrad_ref[...] = shared_grad
+    for i, chip in enumerate(chips):
+        at = pl.ds(pl.multiple_of(chip * 2 * rows, 2 * rows), 2 * rows)
+        sact_ref[at, :] = shared_act[i * 2 * rows : (i + 1) * 2 * rows]
+        sgrad_ref[at, :] = shared_grad[i * 2 * rows : (i + 1) * 2 * rows]
 
     hots, weights = [], []
-    for b in range(blocks):
-        place = place_ref[pl.ds(step * blocks + b, 1), :]
-        hot = lax.broadcasted_iota(jnp.int32, (slot_count, 128), 0) == place
-        hots.append(hot.astype(F32).astype(BF))
-        tokens = slice(b * 128, (b + 1) * 128)
-        slots = slice(b * slot_count, (b + 1) * slot_count)
-        rows_ref[slots, :] = jnp.dot(hots[b], h2[tokens], preferred_element_type=F32).astype(BF)
-        gin_ref[slots, :] = jnp.dot(hots[b], cot[tokens], preferred_element_type=F32).astype(BF)
-        spread = jnp.broadcast_to(weight[tokens], (128, 128))
+    for q in range(4):
+        place = place_ref[pl.ds(chips[q // 2], 1), :]
+        hot = hot_rows(place, rows, q % 2, slot_count).astype(F32)
+        hots.append(hot)
+        tokens = slice(q * rows, (q + 1) * rows)
+        slots = slice(q * slot_count, (q + 1) * slot_count)
+        low = hot.astype(BF)
+        rows_ref[slots, :] = jnp.dot(low, h2[tokens], preferred_element_type=F32).astype(BF)
+        gin_ref[slots, :] = jnp.dot(low, cot[tokens], preferred_element_type=F32).astype(BF)
+        spread = jnp.broadcast_to(weight[tokens], (rows, 128))
         weights.append(
-            jnp.dot(
-                hot.astype(F32),
-                spread,
-                preferred_element_type=F32,
-                precision=lax.Precision.HIGHEST,
-            )[:, :1]
+            jnp.dot(hot, spread, preferred_element_type=F32, precision=lax.Precision.HIGHEST)[:, :1]
         )
     row_weight = jnp.concatenate(weights, axis=0)
     rw_ref[...] = row_weight
-    rows = rows_ref[...]
+    expert_rows = rows_ref[...]
     picked_cot = gin_ref[...]
     back = dot_nt(picked_cot, wd_ref[...])
     gin_ref[...] = (picked_cot.astype(F32) * row_weight).astype(BF)
-    gate = jnp.dot(rows, wg_ref[...], preferred_element_type=F32)
-    up = jnp.dot(rows, wu_ref[...], preferred_element_type=F32)
+    gate = jnp.dot(expert_rows, wg_ref[...], preferred_element_type=F32)
+    up = jnp.dot(expert_rows, wu_ref[...], preferred_element_type=F32)
     act, grad_gate, grad_up = swiglu_both(gate, up, back * row_weight)
     act_low, grad_gate, grad_up = act.astype(BF), grad_gate.astype(BF), grad_up.astype(BF)
     act_ref[...] = act_low
     gg_ref[...] = grad_gate
     gu_ref[...] = grad_up
-    pg_ref[...] = jnp.sum(act_low.astype(F32) * back, axis=1, keepdims=True)
+    picked = jnp.sum(act_low.astype(F32) * back, axis=1, keepdims=True)
     grad_rows = (dot_nt(grad_gate, wg_ref[...]) + dot_nt(grad_up, wu_ref[...])).astype(BF)
-    for b in range(blocks):
-        tokens = slice(b * 128, (b + 1) * 128)
-        slots = slice(b * slot_count, (b + 1) * slot_count)
-        total = dot_tn(hots[b], grad_rows[slots]) + dot_nt(shared_grad[tokens], sc_ref[...])
-        gh2_ref[tokens, :] = total.astype(BF)
-
-
-def swiglu_both(gate, up, grad):
-    sigmoid = 1.0 / (1.0 + jnp.exp(-gate))
-    silu = gate * sigmoid
-    return silu * up, grad * up * (sigmoid * (1.0 + gate * (1.0 - sigmoid))), grad * silu
-
-
-def out_kernel(slot_count, act_ref, rw_ref, place_ref, sact_ref, wd_ref, sd_ref, out_ref):
-    blocks = out_ref.shape[0] // 128
-    step = pl.program_id(0)
-    rows = (jnp.dot(act_ref[...], wd_ref[...], preferred_element_type=F32) * rw_ref[...]).astype(BF)
-    for b in range(blocks):
-        place = place_ref[pl.ds(step * blocks + b, 1), :]
-        hot = lax.broadcasted_iota(jnp.int32, (slot_count, 128), 0) == place
-        tokens = slice(b * 128, (b + 1) * 128)
-        slots = slice(b * slot_count, (b + 1) * slot_count)
-        total = dot_tn(hot.astype(F32).astype(BF), rows[slots]) + jnp.dot(
-            sact_ref[tokens, :], sd_ref[...], preferred_element_type=F32
-        )
-        out_ref[tokens, :] = total.astype(BF)
-
-
-def experts_chunk(h2, cot, expert_id, place, slot_count, expert_w, shared_w, router_weight):
+    stream.open_stage(step)
+    for q in range(4):
+        tokens = slice(q * rows, (q + 1) * rows)
+        slots = slice(q * slot_count, (q + 1) * slot_count)
+        tok_ref[pl.ds(chips[q // 2] * 2 + q % 2, 1), :] = jnp.sum(
+            hots[q] * picked[slots], axis=0, keepdims=True
+        )
+        total = dot_tn(hots[q].astype(BF), grad_rows[slots]) + dot_nt(
+            shared_grad[tokens], sc_ref[...]
+        )
+        stream.stage[slot, q] = total.astype(BF)
+    stream.push(step)
+    stream.advance(step)
+
+    @pl.when(step == steps - 1)
+    def _():
+        stream.finish(sum_ref)
+
+
+def out_kernel(
+    n_groups, slot_count, act_ref, rw_ref, place_ref, sact_ref, wd_ref, sd_ref, sum_ref, *comm
+):
+    rows = sum_ref.shape[0]
+    step, steps = pl.program_id(0), 2 * n_groups
+    w = Wires(n_groups, 8, None, None)
+    stream = StreamSum(w, steps, *comm[:6], comm[6:10], comm[10])
+
+    @pl.when(step == 0)
+    def _():
+        w.meet()
+
+    slot = lax.rem(step, 2)
+    chips = step_chips(w, step)
+    out_rows = jnp.dot(act_ref[...], wd_ref[...], preferred_element_type=F32) * rw_ref[...]
+    out_rows = out_rows.astype(BF)
+    stream.open_stage(step)
+    for q in range(4):
+        chip = chips[q // 2]
+        place = place_ref[pl.ds(chip, 1), :]
+        low = hot_rows(place, rows, q % 2, slot_count).astype(F32).astype(BF)
+        slots = slice(q * slot_count, (q + 1) * slot_count)
+        shared = sact_ref[pl.ds(pl.multiple_of((chip * 2 + q % 2) * rows, rows), rows), :]
+        total = dot_tn(low, out_rows[slots]) + jnp.dot(
+            shared, sd_ref[...], preferred_element_type=F32
+        )
+        stream.stage[slot, q] = total.astype(BF)
+    stream.push(step)
+    stream.advance(step)
+
+    @pl.when(step == steps - 1)
+    def _():
+        stream.finish(sum_ref)
+
+
+def experts_sums(
+    n_groups, rows, h2, cot, place, slot_count, expert_w, shared_w, router_weight, first_id
+):
     w_gate, w_up, w_down = expert_w
     s_both, s_down = shared_w
     tokens, width = h2.shape
     hidden, hidden_s = w_down.shape[0], s_down.shape[0]
     experts = router_weight.shape[1]
-    blocks = 4
-    steps = tokens // (128 * blocks)
-    step_slots = slot_count * blocks
+    steps = 2 * n_groups
+    devices = tokens // rows
+    step_slots = slot_count * 4
     all_slots = step_slots * steps
     half = 128
     s_cat = jnp.concatenate(
@@ -677,17 +898,31 @@
     def blocked(rows, cols):
         return pl.BlockSpec((rows, cols), lambda i: (i, 0))
 
-    token_rows = blocked(128 * blocks, width)
     shape = jax.ShapeDtypeStruct
-    flops = 2 * all_slots * width * hidden * 5 + 2 * tokens * width * (4 * half + 4 * slot_count)
-    grad_h2, rows_in, grad_in, act, grad_gate, grad_up, row_weight, picked, s_act, s_grad = (
+    flops = 2 * all_slots * width * hidden * 5 + 2 * tokens * width * (4 * half + 3 * slot_count)
+    shapes = [
+        shape((rows, width), F32),
+        shape((all_slots, width), BF),
+        shape((all_slots, width), BF),
+        shape((all_slots, hidden), BF),
+        shape((all_slots, hidden), BF),
+        shape((all_slots, hidden), BF),
+        shape((all_slots, 1), F32),
+        shape((tokens, half), BF),
+        shape((tokens, 2 * half), BF),
+        shape((devices, rows), F32),
+    ]
+    specs = [
+        blocked(step_slots, s.shape[1]) if s.shape[0] == all_slots else whole(s) for s in shapes
+    ]
+    hbm = pl.BlockSpec(memory_space=pl.ANY)
+    grad_h2, rows_in, grad_in, act, grad_gate, grad_up, row_weight, s_act, s_grad, token_grad = (
         pl.pallas_call(
-            functools.partial(moe_kernel, hidden_s, experts, slot_count),
+            functools.partial(moe_kernel, n_groups, experts, hidden_s, slot_count),
             grid=(steps,),
             in_specs=[
-                pl.BlockSpec(memory_space=pltpu.SMEM),
-                token_rows,
-                token_rows,
+                hbm,
+                hbm,
                 whole(place),
                 whole(w_gate),
                 whole(w_up),
@@ -695,62 +930,49 @@
                 whole(s_cat),
                 whole(s_tall),
             ],
-            out_specs=[
-                token_rows,
-                blocked(step_slots, width),
-                blocked(step_slots, width),
-                blocked(step_slots, hidden),
-                blocked(step_slots, hidden),
-                blocked(step_slots, hidden),
-                blocked(step_slots, 1),
-                blocked(step_slots, 1),
-                blocked(128 * blocks, half),
-                blocked(128 * blocks, 2 * half),
-            ],
-            out_shape=[
-                shape((tokens, width), BF),
-                shape((all_slots, width), BF),
-                shape((all_slots, width), BF),
-                shape((all_slots, hidden), BF),
-                shape((all_slots, hidden), BF),
-                shape((all_slots, hidden), BF),
-                shape((all_slots, 1), F32),
-                shape((all_slots, 1), F32),
-                shape((tokens, half), BF),
-                shape((tokens, 2 * half), BF),
-            ],
+            out_specs=specs,
+            out_shape=shapes,
+            scratch_shapes=[
+                pltpu.VMEM((2, 4 * rows, width), BF),
+                pltpu.VMEM((2, 4 * rows, width), BF),
+                pltpu.SemaphoreType.DMA((2, 2, 2)),
+            ]
+            + StreamSum.scratch(n_groups, rows, width),
             cost_estimate=pl.CostEstimate(
                 flops=flops, bytes_accessed=12 * tokens * width, transcendentals=tokens * 1024
             ),
-            compiler_params=pltpu.CompilerParams(vmem_limit_bytes=63 * 1024 * 1024),
+            compiler_params=pltpu.CompilerParams(
+                collective_id=first_id,
+                has_side_effects=True,
+                vmem_limit_bytes=67043328,
+            ),
             name="experts",
-        )(expert_id.reshape(1), h2, cot, place, w_gate, w_up, w_down, s_cat, s_tall)
-    )
-
-    grad_h2, act, rows_in, grad_in, s_act, s_grad = lax.optimization_barrier(
-        (grad_h2, act, rows_in, grad_in, s_act, s_grad)
-    )
-    hot = jnp.arange(slot_count, dtype=jnp.int32)[None, :, None] == place[:, None, :]
-    token_grad = jnp.sum(jnp.where(hot, picked.reshape(-1, slot_count, 1), 0.0), axis=1)
+        )(h2, cot, place, w_gate, w_up, w_down, s_cat, s_tall)
+    )
     out = pl.pallas_call(
-        functools.partial(out_kernel, slot_count),
+        functools.partial(out_kernel, n_groups, slot_count),
         grid=(steps,),
         in_specs=[
             blocked(step_slots, hidden),
             blocked(step_slots, 1),
             whole(place),
-            blocked(128 * blocks, half),
+            whole(s_act),
             whole(w_down),
             whole(s_tall),
         ],
-        out_specs=token_rows,
-        out_shape=shape((tokens, width), BF),
+        out_specs=whole(grad_h2),
+        out_shape=shape((rows, width), F32),
+        scratch_shapes=StreamSum.scratch(n_groups, rows, width),
         cost_estimate=pl.CostEstimate(
             flops=2 * width * (all_slots * hidden + tokens * (half + slot_count)),
             bytes_accessed=4 * tokens * width,
             transcendentals=0,
         ),
-        compiler_params=pltpu.CompilerParams(vmem_limit_bytes=56 * 1024 * 1024),
+        compiler_params=pltpu.CompilerParams(
+            collective_id=first_id + 1,
+            has_side_effects=True,
+            vmem_limit_bytes=56 * 1024 * 1024,
+        ),
         name="expert_out",
     )(act, row_weight, place, s_act, w_down, s_tall)
     g_both = dot_tn(h2, s_grad)
@@ -888,9 +1110,6 @@
     shared_w = (s_both, shared_down)
     slot_limit = 2 * tok * TOP // experts
 
-    def scatter_all(x):
-        return lax.psum_scatter(x, ALL, scatter_dimension=0, tiled=True)
-
     def on_rows(h2, cot_gathered, routes_here):
         rows = h2.shape[0]
         h2_all = gather_all(h2)
@@ -898,26 +1117,22 @@
         member = jnp.any(routes_here == expert_id, axis=2)
         member_int = member.astype(jnp.int32)
         rank = jnp.cumsum(member_int, axis=1) - member_int
-        merged = 128 // rows
-        first_slot = jnp.arange(devices, dtype=jnp.int32) % merged * slot_count
-        place = jnp.where(member, rank + first_slot[:, None], -1).reshape(-1, 128)
-        out, grad_h2, token_grad, grads = experts_chunk(
+        place = jnp.where(member, rank, -1).reshape(devices // 2, 2 * rows)
+        out, grad_h2, token_grad, grads = experts_sums(
+            n_groups,
+            rows,
             h2_all,
             cot_gathered,
-            expert_id,
             place,
-            merged * slot_count,
+            slot_count,
             expert_w,
             shared_w,
             router_weight,
-        )
-        token_grad = token_grad.reshape(devices, rows)
+            8,
+        )
         picked = lax.all_to_all(token_grad, ALL, split_axis=0, concat_axis=0, tiled=True)
         picked = jnp.sum(picked.reshape(experts, devices // experts, rows), axis=1).T
-        grad_h2, out, grads, picked = lax.optimization_barrier(
-            (scatter_all(grad_h2), out, grads, picked)
-        )
-        return scatter_all(out), grad_h2, picked, grads
+        return out, grad_h2, picked, grads
 
     parts = max(1, devices * tok // 4096)
     if parts == 1:
@@ -954,8 +1169,8 @@
     )
     grad_logits = grad_logits.astype(BF)
     grad_router = dot_tn(h_two, grad_logits)
-    grad_h_two = grad_h2_own.astype(F32) + dot_nt(grad_logits, router_weight)
-    output = residual_one + out_own.astype(F32)
+    grad_h_two = grad_h2_own + dot_nt(grad_logits, router_weight)
+    output = residual_one + out_own
 
     grad_x_one, grad_gain_two = norm_two_back(grad_h_two)
     grad_x_one = grad_x_one + cotangent.astype(F32)

time: 1070 us -> 1030 us (0.963)
  waiting for transfers between devices: 212 us -> 99.9 us
  Pallas kernels: 550 us -> 609 us
  local copies, waits for them, and re-layouts: 102 us -> 113 us
    pallas_call x2, Pallas kernels: 116 us -> 244 us  [the longest x1 132 us: experts_sums(): pl.pallas_call(functools.partial(moe_kernel, n_groups, experts, hidden_s,...]
    reduce_scatter x2 -> x0, waiting for transfers between devices: 87.4 us -> none  [scatter_all(): return lax.psum_scatter(x, ALL, scatter_dimension=0, tiled=True)]
    pallas_call x7, Pallas kernels: 401 us -> 333 us  [exchange(): pl.pallas_call(functools.partial(exchange_kernel, n_groups, n_plane, kind...]
    all_gather x3, waiting for transfers between devices: 104 us -> 82.1 us  [gather_all(): return lax.all_gather(x, ALL, axis=0, tiled=True)]
  transfers between devices with their start and end apart: 9 -> 7, of which waited for: 3 -> 2; matrix products, arithmetic and copies ran while one was open for 24% -> 20% of each run, Pallas kernels for 43% -> 36%
where the time goes in v3:
time: 1030 us; the launch traced here: 1010 us
  Pallas kernels  609 us (59%)
  matrix products  122 us (12%)
  local copies, waits for them, and re-layouts  113 us (11%)
  waiting for transfers between devices  99.9 us (10%)
  other arithmetic  42.1 us (4%)
  between operations  15.4 us (1%)
  starting transfers between devices  12.5 us (1%)
    pallas_call x7, Pallas kernels, exchange(): pl.pallas_call(functools.partial(exchange_kernel, n_groups, n_plane, kind...  333 us
    pallas_call x1, Pallas kernels, experts_sums(): pl.pallas_call(functools.partial(moe_kernel, n_groups, experts, hidden_s,...  132 us
    pallas_call x1, Pallas kernels, experts_sums(): pl.pallas_call(functools.partial(out_kernel, n_groups, slot_count), grid=...  111 us
    all_gather x3, waiting for transfers between devices, gather_all(): return lax.all_gather(x, ALL, axis=0, tiled=True)  82.1 us
    dot_general x11, matrix products, dot_tn(): lax.dot_general(left, right, (((0,), (0,)), ((), ())), preferred_element_...  81.8 us
    dot_general x6, matrix products, dot_nt(): lax.dot_general(left, right, (((1,), (1,)), ((), ())), preferred_element_...  21.6 us
    pallas_call x1, Pallas kernels, attend_back(): pl.pallas_call(functools.partial(attend_back_kernel, heads, scale), grid=...  20.8 us
  transfers between devices with their start and end apart: 7, of which 2 were waited for; matrix products, arithmetic and copies ran while one was open for 20% of the time, Pallas kernels for 36%

profile of v3, /device:TPU:1, one launch (start us, length us, event | category | flops | bytes accessed | tf_op | source)
XLA Modules:
  0.0 1014.1 jit_solution(344537955396094560)
XLA Ops:
  16.8 89.6 %exchange_0.1 = (bf16[8,128,2048]{2,1,0:T(8,128)(2,1)}, bf16[4,8,32,128]{3,2,1,0:T(8,128)(2,1)}, bf16[4,8,64,576]{3,2,1,0:T(8,128)(2,1)}, bf16[4,8,64,512]{3,2,1,0:T(8,128)(2,1)}) custom-call(bf16[128,2048]{1,0:T(8,128)(2,1)} %refs_0_.1, bf16[32,128]{1,0:T(8,128)(2,1)} %pad_bitcast_fusion.1.refs_1_, bf16[64,576]{1,0:T(8,128)(2,1)} %refs_2_.1, ...), custom_call_target="tpu_custom_call" | custom-call | tf_op jit(solution)/shard_map/exchange_0/pallas_call | solution.py:547
  108.4 2.7 slice.160
  111.6 3.2 fusion
  116.7 3.4 fusion.53
  122.2 3.5 fusion.15
  127.7 47.4 %exchange_1.1 = bf16[8,128,576]{2,1,0:T(8,128)(2,1)} custom-call(bf16[128,576]{1,0:T(8,128)(2,1)} %fusion.32.refs_0_), custom_call_target="tpu_custom_call" | custom-call | tf_op jit(solution)/shard_map/exchange_1/pallas_call | solution.py:547
  179.3 2.9 copy.213
  189.1 3.8 fusion.22
  196.4 4.5 convolution_convert_fusion.ex_ref
  202.2 12.4 %attend.1 = (bf16[1024,256]{1,0:T(8,128)(2,1)S(1)}, f32[1024,2]{1,0:T(8,128)S(1)}) custom-call(s32[1024,1]{1,0:T(8,128)S(1)} %copy.220.low_ref, bf16[1024,256]{1,0:T(8,128)(2,1)S(1)} %convolution_convert_fusion.7.qn_ref, bf16[1024,128]{1,0:T(8,128)(2,1)S(1)} %copy.221.qr_ref, bf16[2048,512]{1,0:T(8,128)(2,1)} %convolution_convert_fusion.ex_ref, ...), custom_call_target="tpu_custom_call" | custom-call | flops 1677721600 | bytes 4194304 | tf_op jit(solution)/shard_map/attend/pallas_call | solution.py:117
  216.2 20.2 %exchange_2.1 = bf16[8,128,256]{2,1,0:T(8,128)(2,1)} custom-call(bf16[8,128,256]{2,1,0:T(8,128)(2,1)} %bitcast.161), custom_call_target="tpu_custom_call" | custom-call | tf_op jit(solution)/shard_map/exchange_2/pallas_call | solution.py:547
  237.8 5.2 multiply_reduce_fusion.3
  245.1 3.1 reshape.473
  248.1 3.0 reshape.474
  254.4 3.8 all-to-all-start
  261.9 4.6 copy.226
  266.5 4.7 copy.227
  278.4 16.4 %all-to-all-done = bf16[1,64,32,176]{3,1,0,2:T(8,128)(2,1)} async-done(((bf16[1,64,32,176]{3,1,0,2:T(8,128)(2,1)}), bf16[1,64,32,176]{3,1,0,2:T(8,128)(2,1)}, u32[]{:S(2)}, u32[]{:S(2)}) %all-to-all-start) | async-done | bytes 720928 | tf_op jit(solution)/shard_map/all_to_all | solution.py:1067
  296.5 3.8 concatenate.68.sc_ref
  301.7 82.1 %all-gather.6.cloned.1.call-done.h2_hbm = bf16[4096,2048]{1,0:T(8,128)(2,1)} async-done(((bf16[128,2048]{1,0:T(8,128)(2,1)}), bf16[4096,2048]{1,0:T(8,128)(2,1)}) %all-gather.6.cloned.1.call-update) | async-done | bytes 16777232 | tf_op jit(solution)/shard_map/all_gather | solution.py:564
  383.8 132.3 %experts.1 = (f32[128,2048]{1,0:T(8,128)}, bf16[3072,2048]{1,0:T(8,128)(2,1)}, bf16[3072,2048]{1,0:T(8,128)(2,1)}, bf16[3072,704]{1,0:T(8,128)(2,1)}, bf16[3072,...) custom-call(bf16[4096,2048]{1,0:T(8,128)(2,1)} %all-gather.6.cloned., ...), custom_call_target="tpu_custom_call" | custom-call | flops 57713623040 | bytes 100663296 | tf_op jit(solution)/shard_map/experts/pallas_call | solution.py:920
  516.1 10.9 %convolution_convert_fusion.1 = bf16[2048,256]{0,1:T(8,128)(2,1)S(1)} fusion(bf16[4096,2048]{1,0:T(8,128)(2,1)} %all-gather.6.cloned.1.call-done.h2_hbm, bf16[4096,256]{1,0:T(8,128)(2,1)} %get-tuple-element.60), kind=kOutput, calls=%fused_computation.14 | convolution fusion | flops 4295491584 | bytes 19922944 | tf_op jit(solution)/shard_map/dot_general | solution.py:54
  527.1 3.5 all-to-all-start.1
  531.9 15.3 %convolution_bitcast_fusion.2 = f32[1,2048,704]{1,2,0:T(8,128)} fusion(bf16[3072,2048]{1,0:T(8,128)(2,1)} %get-tuple-element.70, bf16[3072,704]{1,0:T(8,128)(2,1)} %get-tuple-element.71), kind=kOutput, calls=%fused_computation.11 | convolution fusion | flops 8858370048 | bytes 22675456 | tf_op jit(solution)/shard_map/dot_general | solution.py:54
  547.2 15.3 %convolution_bitcast_fusion.1 = f32[1,2048,704]{1,2,0:T(8,128)} fusion(bf16[3072,2048]{1,0:T(8,128)(2,1)} %get-tuple-element.70, bf16[3072,704]{1,0:T(8,128)(2,1)} %get-tuple-element.72), kind=kOutput, calls=%fused_computation.10 | convolution fusion | flops 8858370048 | bytes 22675456 | tf_op jit(solution)/shard_map/dot_general | solution.py:54
  562.5 11.6 %convolution_bitcast_fusion = f32[1,704,2048]{2,1,0:T(8,128)} fusion(bf16[3072,704]{1,0:T(8,128)(2,1)S(1)} %bitcast.216, bf16[3072,2048]{1,0:T(8,128)(2,1)S(1)} %bitcast.214), kind=kOutput, calls=%fused_computation.9 | convolution fusion | flops 8858370048 | bytes 22675456 | tf_op jit(solution)/shard_map/dot_general | solution.py:54
  574.1 111.3 %expert_out.1 = f32[128,2048]{1,0:T(8,128)} custom-call(bf16[3072,704]{1,0:T(8,128)(2,1)} %get-tuple-element.50.act_ref, f32[3072,1]{1,0:T(8,128)} %get-tuple-element.51.rw_ref, s32[16,256]{1,0:T(8,128)} %subtract_select_fusion.place_ref, bf16[4096,128]{1,0:T(8,128)(2,1)} %get-tuple-element.52.sact_ref, bf16[704,2048]{1,0:T(8,128)(2,1)} %bitcast.212, ...), custom_call_target="tpu_custom_call" | custom-call | flops 12616466432 | bytes 33554432 | tf_op jit(solution)/shard_map/expert_out/pallas_call | solution.py:952
  685.5 9.6 fusion.12
  701.0 34.1 %exchange_3.1 = bf16[8,128,2048]{2,1,0:T(8,128)(2,1)} custom-call(bf16[128,2048]{1,0:T(8,128)(2,1)} %fusion.47.refs_0_), custom_call_target="tpu_custom_call" | custom-call | tf_op jit(solution)/shard_map/exchange_3/pallas_call | solution.py:547
  735.2 4.6 convolution_convert_fusion.3
  739.7 3.3 convolution_convert_fusion.6.gm_ref
  743.0 20.8 %attend_back.1 = (f32[1024,256]{1,0:T(8,128)}, f32[1024,128]{1,0:T(8,128)}, f32[2048,512]{1,0:T(8,128)}, f32[2048,64]{1,0:T(8,128)}) custom-call(s32[1024,1]{1,0:T(8,128)} %copy-done, bf16[1024,256]{1,0:T(8,128)(2,1)} %copy-done.5, bf16[1024,128]{1,0:T(8,128)(2,1)} %copy-done.4, bf16[2048,512]{1,0:T(8,128)(2,1)} %convolution_convert_fusion.ex_ref, ...), custom_call_target="tpu_custom_call" | custom-call | flops 4362076160 | bytes 8388608 | tf_op jit(solution)/shard_map/attend_back/pallas_call | solution.py:192
  765.9 5.8 fusion.29
  774.2 2.6 convert_element_type.210
  785.5 3.7 convolution_convert_fusion.2
  791.4 6.0 copy.239
  797.4 5.4 convert_element_type.217.refs_0_
  802.9 6.9 fusion.3
  809.8 60.5 %exchange_4.1 = (f32[256,576]{1,0:T(8,128)}, f32[128,2048]{1,0:T(8,128)}, f32[64,2048]{1,0:T(8,128)}, bf16[4,8,64,176]{3,2,1,0:T(8,128)(2,1)}) custom-call(bf16[8,256,576]{2,1,0:T(8,128)(2,1)} %bitcast.163, bf16[8,128,2048]{2,1,0:T(8,128)(2,1)} %bitcast.162, bf16[4,64,2048]{2,1,0:T(8,128)(2,1)} %bitcast.194, bf16[4,8,64,176]{3,2,1,0:T(8,128)(2,1)} %pad_maximum_fusion.6.refs_3_), custom_call_target="tpu_custom_call" | custom-call | tf_op jit(solution)/shard_map/exchange_4/pallas_call | solution.py:547
  872.6 3.8 collective-permute-start.1
  880.8 2.7 reshape.491
  883.4 2.8 copy.245
  886.2 2.7 reshape.490
  893.8 59.1 %exchange_5.1 = (bf16[8,64,384]{2,1,0:T(8,128)(2,1)}, bf16[8,16,512]{2,1,0:T(8,128)(2,1)}, bf16[8,128,576]{2,1,0:T(8,128)(2,1)}) custom-call(bf16[4,8,64,384]{3,2,1,0:T(8,128)(2,1)} %convert_element_type.217.refs_0_, bf16[4,8,16,512]{3,2,1,0:T(8,128)(2,1)} %bitcast.202, bf16[128,576]{1,0:T(8,128)(2,1)} %pad_maximum_fusion.9.refs_2_), custom_call_target="tpu_custom_call" | custom-call | tf_op jit(solution)/shard_map/exchange_5/pallas_call | solution.py:547
  953.0 6.8 bitcast_convert_fusion
  959.9 2.5 fusion.11
  963.5 4.4 copy.241
  969.6 21.7 %exchange_6.1 = (f32[64,576]{1,0:T(8,128)}, f32[16,128]{1,0:T(8,128)}) custom-call(bf16[4,64,576]{2,1,0:T(8,128)(2,1)} %dynamic-slice_bitcast_fusion.refs_0_, f32[4,8,16,128]{3,2,1,0:T(8,128)} %copy.262), custom_call_target="tpu_custom_call" | custom-call | tf_op jit(solution)/shard_map/exchange_6/pallas_call | solution.py:547
  (295 shorter events, 108.4 us)
Async XLA Ops:
  7.2 230.6 %all-gather.4.cloned.1.call-start = ((), (), s32[]{:S(2)}) async-start(), calls=%async_computation.2 | async-start | bytes 8650752 | tf_op jit(solution)/shard_map/all_gather | solution.py:564
  7.9 293.8 %all-gather.8.cloned.1.call-start = ((), (), s32[]{:S(2)}) async-start(), calls=%async_computation.4 | async-start | bytes 17301504 | tf_op jit(solution)/shard_map/all_gather | solution.py:564
  8.7 375.2 %all-gather.6.cloned.1.call-start = ((), (), s32[]{:S(2)}) async-start(), calls=%async_computation.3 | async-start | bytes 17301504 | tf_op jit(solution)/shard_map/all_gather | solution.py:564
  111.3 14.3 %copy-start.56 = (f32[512]{0:T(512)}, f32[512]{0:T(512)S(1)}, u32[]{:S(2)}) copy-start(f32[512]{0:T(512)S(1)} %reshape.494) | copy-start | bytes 6148
  120.1 156.2 %copy-start.10 = (f32[1024,576]{1,0:T(8,128)}, f32[1024,576]{1,0:T(8,128)S(1)}, u32[]{:S(2)}) copy-start(f32[1024,576]{1,0:T(8,128)S(1)} %fusion.53) | copy-start | bytes 7077892
  179.1 64.0 %copy-start.48 = (f32[2048]{0:T(1024)}, f32[2048]{0:T(1024)S(1)}, u32[]{:S(2)}) copy-start(f32[2048]{0:T(1024)S(1)} %reshape.495) | copy-start | bytes 24580
  179.3 22.9 %copy-start = (s32[1024,1]{1,0:T(8,128)}, s32[1024,1]{1,0:T(8,128)S(1)}, u32[]{:S(2)}) copy-start(s32[1024,1]{1,0:T(8,128)S(1)} %copy.220.low_ref) | copy-start | bytes 12292
  194.9 7.3 copy-start.4
  196.3 5.9 copy-start.1
  202.2 12.4 %copy-start.5 = (bf16[1024,256]{1,0:T(8,128)(2,1)}, bf16[1024,256]{1,0:T(8,128)(2,1)S(1)}, u32[]{:S(2)}) copy-start(bf16[1024,256]{1,0:T(8,128)(2,1)S(1)} %convolution_convert_fusion.7.qn_ref) | copy-start | bytes 1572868
  243.0 11.4 %copy-start.68 = (f32[128]{0:T(128)}, f32[128]{0:T(128)S(1)}, u32[]{:S(2)}) copy-start(f32[128]{0:T(128)S(1)} %get-tuple-element.185) | copy-start | bytes 1540
  245.1 15.7 %copy-start.17 = (bf16[2048,128]{1,0:T(8,128)(2,1)S(1)}, bf16[2048,128]{1,0:T(8,128)(2,1)}, u32[]{:S(2)}) copy-start(bf16[2048,128]{1,0:T(8,128)(2,1)} %slice.170) | copy-start | bytes 1572868
  254.4 40.4 %all-to-all-start = ((bf16[1,64,32,176]{3,1,0,2:T(8,128)(2,1)}), bf16[1,64,32,176]{3,1,0,2:T(8,128)(2,1)}, u32[]{:S(2)}, u32[]{:S(2)}) async-start(bf16[1,64,32,176]{3,1,0,2:T(8,128)(2,1)} %copy.228), calls=%async_computation | async-start | bytes 2097152 | tf_op jit(solution)/shard_map/all_to_all | solution.py:1067
  266.5 10.0 copy-start.11
  276.5 24.1 %copy-start.71 = (f32[128]{0:T(128)}, f32[128]{0:T(128)S(1)}, u32[]{:S(2)}) copy-start(f32[128]{0:T(128)S(1)} %multiply_reduce_fusion.6) | copy-start | bytes 1540
  276.5 23.8 %copy-start.13 = (bf16[2048,16]{1,0:T(8,128)(2,1)S(1)}, bf16[2048,16]{1,0:T(8,128)(2,1)}, u32[]{:S(2)}) copy-start(bf16[2048,16]{1,0:T(8,128)(2,1)} %reshape.475) | copy-start | bytes 196612
  276.5 23.8 %copy-start.15 = (bf16[128,2048]{1,0:T(8,128)(2,1)S(1)}, bf16[128,2048]{1,0:T(8,128)(2,1)}, u32[]{:S(2)}) copy-start(bf16[128,2048]{1,0:T(8,128)(2,1)} %multiply_convert_fusion.1) | copy-start | bytes 1572868
  276.7 19.7 %copy-start.70 = (f32[128]{0:T(128)}, f32[128]{0:T(128)S(1)}, u32[]{:S(2)}) copy-start(f32[128]{0:T(128)S(1)} %fusion.8) | copy-start | bytes 1540
  527.1 169.5 %all-to-all-start.1 = ((f32[32,1,128]{2,1,0:T(1,128)}), f32[32,1,128]{2,1,0:T(1,128)S(1)}, u32[]{:S(2)}, u32[]{:S(2)}) async-start(f32[32,1,128]{2,1,0:T(1,128)} %bitcast.31), calls=%async_computation.1 | async-start | bytes 32768 | tf_op jit(solution)/shard_map/all_to_all | solution.py:1133
  531.9 30.6 %slice-start = ((s8[12582912]{0:T(1024)(128)(4,1)}), s8[4194304]{0:T(1024)(128)(4,1)S(1)}, s32[]{:S(2)}) async-start(s8[12582912]{0:T(1024)(128)(4,1)} %bitcast.213), calls=%async_computation.6 | async-start | bytes 8388608
  531.9 30.6 %slice-start.1 = ((s8[12582912]{0:T(1024)(128)(4,1)}), s8[4194304]{0:T(1024)(128)(4,1)S(1)}, s32[]{:S(2)}) async-start(s8[12582912]{0:T(1024)(128)(4,1)} %bitcast.213), calls=%async_computation.7 | async-start | bytes 8388608
  531.9 30.6 %slice-start.3 = ((s8[4718592]{0:T(1024)(128)(4,1)}), s8[4194304]{0:T(1024)(128)(4,1)S(1)}, s32[]{:S(2)}) async-start(s8[4718592]{0:T(1024)(128)(4,1)} %bitcast.215), calls=%async_computation.9 | async-start | bytes 8388608
  547.2 15.3 %slice-start.2 = ((s8[12582912]{0:T(1024)(128)(4,1)}), s8[4194304]{0:T(1024)(128)(4,1)S(1)}, s32[]{:S(2)}) async-start(s8[12582912]{0:T(1024)(128)(4,1)} %bitcast.213), calls=%async_computation.8 | async-start | bytes 8388608
  547.2 15.3 %slice-start.4 = ((s8[4718592]{0:T(1024)(128)(4,1)}), s8[524288]{0:T(1024)(128)(4,1)S(1)}, s32[]{:S(2)}) async-start(s8[4718592]{0:T(1024)(128)(4,1)} %bitcast.215), calls=%async_computation.10 | async-start | bytes 1048576
  574.1 111.4 %copy-start.35 = (bf16[4096,128]{1,0:T(8,128)(2,1)S(1)}, bf16[4096,128]{1,0:T(8,128)(2,1)}, u32[]{:S(2)}) copy-start(bf16[4096,128]{1,0:T(8,128)(2,1)} %get-tuple-element.52.sact_ref) | copy-start | bytes 3145732
  685.5 9.7 copy-start.33
  685.5 11.2 %copy-start.52 = (f32[128,16]{0,1:T(8,128)S(1)}, f32[128,16]{0,1:T(8,128)}, u32[]{:S(2)}) copy-start(f32[128,16]{0,1:T(8,128)} %copy-done.51) | copy-start | bytes 24580
  685.5 11.2 %copy-start.63 = (f32[128]{0:T(128)S(1)}, f32[128]{0:T(128)}, u32[]{:S(2)}) copy-start(f32[128]{0:T(128)} %copy-done.62) | copy-start | bytes 1540
  685.5 11.2 %copy-start.64 = (f32[128]{0:T(128)S(1)}, f32[128]{0:T(128)}, u32[]{:S(2)}) copy-start(f32[128]{0:T(128)} %fusion.38) | copy-start | bytes 1540
  685.5 11.2 %copy-start.16 = (bf16[128,2048]{1,0:T(8,128)(2,1)S(1)}, bf16[128,2048]{1,0:T(8,128)(2,1)}, u32[]{:S(2)}) copy-start(bf16[128,2048]{1,0:T(8,128)(2,1)} %multiply_convert_fusion.1) | copy-start | bytes 1572868
  685.5 12.6 %copy-start.14 = (bf16[2048,16]{1,0:T(8,128)(2,1)S(1)}, bf16[2048,16]{1,0:T(8,128)(2,1)}, u32[]{:S(2)}) copy-start(bf16[2048,16]{1,0:T(8,128)(2,1)} %reshape.475) | copy-start | bytes 196612
  685.5 12.6 %copy-start.49 = (f32[2048]{0:T(1024)S(1)}, f32[2048]{0:T(1024)}, u32[]{:S(2)}) copy-start(f32[2048]{0:T(1024)} %copy-done.48) | copy-start | bytes 24580
  685.5 12.6 %copy-start.61 = (f32[128]{0:T(128)S(1)}, f32[128]{0:T(128)}, u32[]{:S(2)}) copy-start(f32[128]{0:T(128)} %copy-done.60) | copy-start | bytes 1540
  699.8 35.3 %copy-start.3 = (bf16[1024,256]{1,0:T(8,128)(2,1)S(1)}, bf16[1024,256]{1,0:T(8,128)(2,1)}, u32[]{:S(2)}) copy-start(bf16[1024,256]{1,0:T(8,128)(2,1)} %copy-done.2) | copy-start | bytes 1572868
  699.9 39.8 %copy-start.66 = (f32[128]{0:T(128)}, f32[128]{0:T(128)S(1)}, u32[]{:S(2)}) copy-start(f32[128]{0:T(128)S(1)} %multiply_multiply_fusion.2) | copy-start | bytes 1540
  743.0 22.8 %copy-start.20 = (bf16[2048,2,128]{0,2,1:T(8,128)(2,1)S(1)}, bf16[2048,2,128]{0,2,1:T(8,128)(2,1)}, u32[]{:S(2)}) copy-start(bf16[2048,2,128]{0,2,1:T(8,128)(2,1)} %slice.161) | copy-start | bytes 3145732
  871.3 17.6 %collective-permute-start = (bf16[128,576]{1,0:T(8,128)(2,1)S(1)}, bf16[128,576]{1,0:T(8,128)(2,1)S(1)}, u32[]{:S(2)}, u32[]{:S(2)}) collective-permute-start(bf16[128,576]{1,0:T(8,128)(2,1)S(1)} %slice.232), channel_id=1, source_target_pairs={{8,0},{16,8},{24,16},{9,1},{17,9},{25,17},{10,2},{18,10},{26,18},{... | collective-permute-start | bytes 442376 | tf_op jit(solution)/shard_map/ppermute | solution.py:1216
  872.6 132.0 %collective-permute-start.1 = (f32[64,2048]{1,0:T(8,128)}, f32[64,2048]{1,0:T(8,128)}, u32[]{:S(2)}, u32[]{:S(2)}) collective-permute-start(f32[64,2048]{1,0:T(8,128)} %get-tuple-element.68), channel_id=1, source_target_pairs={{0,0},{1,4},{2,8},{3,12},{4,16},{5,20},{6,24},{7,28},{8,1},{9,5},{... | collective-permute-start | bytes 1572872 | tf_op jit(solution)/shard_map/ppermute | solution.py:1215
  879.2 11.7 %copy-start.57 = (f32[512]{0:T(512)S(1)}, f32[512]{0:T(512)}, u32[]{:S(2)}) copy-start(f32[512]{0:T(512)} %copy-done.56) | copy-start | bytes 6148
  879.2 11.7 %copy-start.67 = (f32[128]{0:T(128)S(1)}, f32[128]{0:T(128)}, u32[]{:S(2)}) copy-start(f32[128]{0:T(128)} %fusion.41) | copy-start | bytes 1540
  879.2 12.8 %copy-start.72 = (f32[128]{0:T(128)S(1)}, f32[128]{0:T(128)}, u32[]{:S(2)}) copy-start(f32[128]{0:T(128)} %copy-done.71) | copy-start | bytes 1540
  953.0 6.9 copy-start.12
  953.0 6.9 copy-start.29
  953.0 6.9 copy-start.36
  953.0 6.9 copy-start.42
  953.0 6.9 copy-start.54
  953.0 6.9 copy-start.65
  962.8 38.3 %copy-start.46 = (bf16[8,64,384]{2,1,0:T(8,128)(2,1)S(1)}, bf16[8,64,384]{2,1,0:T(8,128)(2,1)}, u32[]{:S(2)}) copy-start(bf16[8,64,384]{2,1,0:T(8,128)(2,1)} %get-tuple-element.65) | copy-start | bytes 1179652
  (38 other events, 113.9 us)
Sparse Core Ops, SparseCore 0:
  10.8 124.2 all-gather.3
  138.0 122.5 all-gather.7
  263.5 120.3 all-gather.5

commit v4 on v3

--- a/solution.py
+++ b/solution.py
@@ -263,8 +263,26 @@
         copy.start()
         return copy
 
-    def meet(self):
+    def at_device(self, index):
+        return {"g": index // self.n_plane, **self.on_plane(lax.rem(index, self.n_plane))}
+
+    def on_plane(self, j):
+        return {"p": j // self.cores, "c": j % self.cores}
+
+    def meet(self, heads=False):
         barrier = pltpu.get_barrier_semaphore()
+        waits = self.n_plane - 1 + self.n_groups - 1
+        if heads:
+            mine = self.head_owner() == self.j
+            part = lax.rem(self.g * self.n_plane + self.j, self.n_groups)
+            for r in range(self.n_groups):
+
+                @pl.when(jnp.logical_not(mine) | (part != r))
+                def _():
+                    source = self.at_device(self.n_groups * self.j + r)
+                    pl.semaphore_signal(barrier, inc=1, device_id=source, device_id_type=MESH)
+
+            waits = waits + jnp.where(mine, self.n_groups - 1, self.n_groups)
         for d in range(1, self.n_plane):
             pl.semaphore_signal(
                 barrier, inc=1, device_id=self.at_plane(self.plane_peer(d)), device_id_type=MESH
@@ -273,7 +291,10 @@
             pl.semaphore_signal(
                 barrier, inc=1, device_id=self.at_group(self.group_peer(d)), device_id_type=MESH
             )
-        pl.semaphore_wait(barrier, self.n_plane - 1 + self.n_groups - 1)
+        pl.semaphore_wait(barrier, waits)
+
+    def head_owner(self):
+        return (self.g * self.n_plane + self.j) // self.n_groups
 
 
 def sum_rows(dst, sources):
@@ -363,6 +384,57 @@
     wait_all(second)
 
 
+def head_rows(w, src, out):
+    index = w.g * w.n_plane + w.j
+    owner, part = w.head_owner(), lax.rem(index, w.n_groups)
+    mine = owner == w.j
+
+    def to(d):
+        return pltpu.make_async_remote_copy(
+            src_ref=src,
+            dst_ref=out.at[part],
+            send_sem=w.send.at[base + d],
+            recv_sem=w.recv.at[base + part],
+            device_id={"g": w.group_peer(d), **w.on_plane(owner)},
+            device_id_type=MESH,
+        )
+
+    def arrival(r):
+        return pltpu.make_async_remote_copy(
+            src_ref=src,
+            dst_ref=out.at[r],
+            send_sem=w.send.at[base],
+            recv_sem=w.recv.at[base + r],
+            device_id=w.at_device(w.n_groups * w.j + r),
+            device_id_type=MESH,
+        )
+
+    base = w.used
+    w.used += w.n_groups
+    for d in range(w.n_groups):
+
+        @pl.when((d > 0) | jnp.logical_not(mine))
+        def _():
+            to(d).start()
+
+    @pl.when(mine)
+    def _():
+        out[part] = src[...]
+
+    yield
+    for r in range(w.n_groups):
+
+        @pl.when(jnp.logical_not(mine) | (part != r))
+        def _():
+            arrival(r).wait_recv()
+
+    for d in range(w.n_groups):
+
+        @pl.when((d > 0) | jnp.logical_not(mine))
+        def _():
+            to(d).wait_send()
+
+
 def plane_swap(w, src, out):
     copies = []
     for d in range(1, w.n_plane):
@@ -431,6 +503,18 @@
     wait_all(second)
 
 
+def plane_sum_shift(w, src, out, from_core, pairs, from_chips, low, later):
+    rows = out.shape[0]
+    yield from plane_sum(w, src, low, from_core, pairs, from_chips)
+    copy = w.start(
+        low.at[pl.ds(0, rows)], later, w.at_group(lax.rem(w.g + w.n_groups - 1, w.n_groups))
+    )
+    yield
+    copy.wait()
+    keep = jnp.where(w.g == w.n_groups - 1, 0.0, 1.0)
+    out[...] = low[rows:, :].astype(F32) + later[...].astype(F32) * keep
+
+
 def group_sum(w, src, out, parts):
     copies = []
     for d in range(1, w.n_groups):
@@ -472,6 +556,8 @@
     "plane_swap_gather": plane_swap_gather,
     "plane_swap": plane_swap,
     "plane_sum": plane_sum,
+    "plane_sum_shift": plane_sum_shift,
+    "head_rows": head_rows,
     "group_sum": group_sum,
     "whole_sum": whole_sum,
     "whole_swap": whole_swap,
@@ -484,7 +570,7 @@
     sources, outs = refs[:count], refs[count : 2 * count]
     scratch = list(refs[2 * count : -2])
     w = Wires(n_groups, n_plane, refs[-2], refs[-1])
-    w.meet()
+    w.meet("head_rows" in kinds)
     running = []
     for kind, source, out, number in zip(kinds, sources, outs, extra):
         mine, scratch = scratch[:number], scratch[number:]
@@ -521,6 +607,12 @@
             out = (n_groups,) + shape
         elif kind == "plane_swap":
             out = shape
+        elif kind == "head_rows":
+            out = (n_groups,) + shape
+        elif kind == "plane_sum_shift":
+            pair = shape[1:]
+            out = (shape[1] // 2, shape[2])
+            own = [(chips,) + pair, (chips,) + pair, (chips - 1,) + pair, pair, out]
         elif kind == "plane_sum":
             out = shape[1:]
             own = [(chips,) + out, (chips,) + out, (chips - 1,) + out]
@@ -536,7 +628,7 @@
         elif kind == "group_sum_swap":
             out = shape[1:]
             own = [out, (n_groups - 1,) + out]
-        if kind in ("plane_sum", "group_sum", "whole_sum"):
+        if kind in ("plane_sum", "plane_sum_shift", "group_sum", "whole_sum"):
             shapes.append(jax.ShapeDtypeStruct(out, F32))
         else:
             shapes.append(jax.ShapeDtypeStruct(out, dtype))
@@ -833,7 +925,9 @@
 
 
 def out_kernel(
-    n_groups, slot_count, act_ref, rw_ref, place_ref, sact_ref, wd_ref, sd_ref, sum_ref, *comm
+    n_groups, slot_count,
+    act_ref, rw_ref, rows_ref, gin_ref, gg_ref, gu_ref, place_ref, sact_ref, wd_ref, sd_ref,
+    sum_ref, dg_ref, du_ref, dd_ref, *comm,
 ):
     rows = sum_ref.shape[0]
     step, steps = pl.program_id(0), 2 * n_groups
@@ -843,6 +937,8 @@
     @pl.when(step == 0)
     def _():
         w.meet()
+        for ref in (dg_ref, du_ref, dd_ref):
+            ref[...] = jnp.zeros_like(ref)
 
     slot = lax.rem(step, 2)
     chips = step_chips(w, step)
@@ -861,6 +957,18 @@
         stream.stage[slot, q] = total.astype(BF)
     stream.push(step)
     stream.advance(step)
+
+    width = rows_ref.shape[1]
+    piece = width // 4
+    for k in range(4):
+        cols = slice(k * piece, (k + 1) * piece)
+        turned = rows_ref[:, cols].T
+        dg_ref[cols, :] += jnp.dot(turned, gg_ref[...], preferred_element_type=F32)
+        du_ref[cols, :] += jnp.dot(turned, gu_ref[...], preferred_element_type=F32)
+    turned = act_ref[...].T
+    for k in range(4):
+        cols = slice(k * piece, (k + 1) * piece)
+        dd_ref[:, cols] += jnp.dot(turned, gin_ref[:, cols], preferred_element_type=F32)
 
     @pl.when(step == steps - 1)
     def _():
@@ -949,38 +1057,43 @@
             name="experts",
         )(h2, cot, place, w_gate, w_up, w_down, s_cat, s_tall)
     )
-    out = pl.pallas_call(
+    shapes = [grad_h2] + [shape(x.shape, F32) for x in expert_w]
+    out, d_gate, d_up, d_down = pl.pallas_call(
         functools.partial(out_kernel, n_groups, slot_count),
         grid=(steps,),
         in_specs=[
             blocked(step_slots, hidden),
             blocked(step_slots, 1),
+            blocked(step_slots, width),
+            blocked(step_slots, width),
+            blocked(step_slots, hidden),
+            blocked(step_slots, hidden),
             whole(place),
             whole(s_act),
             whole(w_down),
             whole(s_tall),
         ],
-        out_specs=whole(grad_h2),
-        out_shape=shape((rows, width), F32),
+        out_specs=[whole(x) for x in shapes],
+        out_shape=[shape(x.shape, F32) for x in shapes],
         scratch_shapes=StreamSum.scratch(n_groups, rows, width),
         cost_estimate=pl.CostEstimate(
-            flops=2 * width * (all_slots * hidden + tokens * (half + slot_count)),
+            flops=2 * width * (4 * all_slots * hidden + tokens * (half + slot_count)),
             bytes_accessed=4 * tokens * width,
             transcendentals=0,
         ),
         compiler_params=pltpu.CompilerParams(
             collective_id=first_id + 1,
             has_side_effects=True,
-            vmem_limit_bytes=56 * 1024 * 1024,
+            vmem_limit_bytes=67043328,
         ),
         name="expert_out",
-    )(act, row_weight, place, s_act, w_down, s_tall)
+    )(act, row_weight, rows_in, grad_in, grad_gate, grad_up, place, s_act, w_down, s_tall)
     g_both = dot_tn(h2, s_grad)
     g_both = jnp.concatenate([g_both[:, :hidden_s], g_both[:, half : half + hidden_s]], axis=1)
     grads = (
-        dot_tn(rows_in, grad_gate),
-        dot_tn(rows_in, grad_up),
-        dot_tn(act, grad_in),
+        d_gate,
+        d_up,
+        d_down,
         g_both,
         dot_tn(s_act, cot)[:hidden_s],
     )
@@ -1054,7 +1167,7 @@
     wq_nope = query_weight[:, :, :NOPE].reshape(width, local_heads * NOPE)
     wq_rope = query_weight[:, :, NOPE:].reshape(width, local_heads * ROPE)
     expand_weight = pair[:, head_cols:].reshape(RANK, kv_cols)
-    output_weight = gather_all(w_output)
+    cotangent_later = lax.optimization_barrier((cotangent, x_plane))[0]
 
     shared_n = shared_down.shape[0]
     s_both = jnp.concatenate(
@@ -1081,9 +1194,10 @@
     def own_rows(table):
         return lax.dynamic_slice_in_dim(table, place_in * tok, tok, 0)
 
-    down_pairs = [(i + 1, i) for i in range(n_groups - 1)]
     piece = own_rows(jnp.concatenate([compressed_own, key_rope_own], axis=1))
-    before = swap(1, ("shift_gather", piece))[0].reshape(plane_tok, RANK + ROPE)
+    before, own_output = swap(1, ("shift_gather", piece), ("head_rows", w_output))
+    before = before.reshape(plane_tok, RANK + ROPE)
+    own_output = own_output.reshape(local_heads * VDIM, width)
     compressed = jnp.concatenate([before[:, :RANK], compressed_own], axis=0)
     key_rope = jnp.concatenate([before[:, RANK:], key_rope_own], axis=0)
     q_nope = matmul(hidden, wq_nope).astype(BF)
@@ -1097,11 +1211,10 @@
     )
     low_bound = doc_start - plane_start + DOC_MAX
     mixed_heads, lse = attend(low_bound, q_nope, q_rope, expanded, key_rope, scale)
-    mixed = swap(2, ("plane_swap", mixed_heads.reshape(n_plane, tok, local_heads * VDIM)))[0]
-    mixed = mixed.transpose(1, 0, 2).reshape(tok, width)
-
+    attn_out = matmul(mixed_heads, own_output).astype(BF)
+    attn_out = swap(2, ("plane_sum", attn_out.reshape(n_plane, tok, width)))[0]
     input_float = layer_input.astype(F32)
-    residual_one = input_float + matmul(mixed, output_weight)
+    residual_one = input_float + attn_out
     h_two_f, norm_two_back = jax.vjp(rms_norm, residual_one, gain_two)
     h_two = h_two_f.astype(BF)
     router_probs = softmax_rows(matmul(h_two, router_weight))
@@ -1136,7 +1249,7 @@
 
     parts = max(1, devices * tok // 4096)
     if parts == 1:
-        cot_all = gather_all(cotangent)
+        cot_all = gather_all(cotangent_later)
         out_own, grad_h2_own, grad_router_probs, grads = on_rows(
             h_two, cot_all, routes_all
         )
@@ -1147,6 +1260,7 @@
             h2, cot, routes_here = inputs
             cot_part = gather_all(cot)
             out, grad_h2, picked, grads = on_rows(h2, cot_part, routes_here)
+            grads = lax.optimization_barrier(grads)
             total = tuple(a + b for a, b in zip(total, grads))
             return total, (out, grad_h2, picked)
 
@@ -1175,9 +1289,12 @@
     grad_x_one, grad_gain_two = norm_two_back(grad_h_two)
     grad_x_one = grad_x_one + cotangent.astype(F32)
     grad_attn_out = grad_x_one.astype(BF)
-    plane_grad = swap(3, ("plane_gather", grad_attn_out))[0].reshape(plane_tok, width)
-    head_rows = local_heads * VDIM
-    own_output = lax.dynamic_slice_in_dim(output_weight, place_in * head_rows, head_rows, 0)
+    plane_grad, g_shared = swap(
+        3,
+        ("plane_gather", grad_attn_out),
+        ("whole_swap", g_both.astype(BF).reshape(n_groups, n_plane, rows_w, 2 * shared_n)),
+    )
+    plane_grad = plane_grad.reshape(plane_tok, width)
     grad_mixed = dot_nt(plane_grad, own_output).astype(BF)
     dqn, dqr, dex, dkr = attend_back(
         low_bound, q_nope, q_rope, expanded, key_rope, lse, grad_mixed, scale
@@ -1202,42 +1319,31 @@
         .astype(BF)
     )
     grad_hidden = (dot_nt(gq_nope, wq_nope) + dot_nt(gq_rope, wq_rope)).astype(BF)
-    key_grads, grad_hidden, grad_output_weight, g_shared = swap(
+    gw_nope = dot_tn(hidden, gq_nope).astype(BF).reshape(n_groups, n_plane, rows_w, -1)
+    gw_rope = dot_tn(hidden, gq_rope).astype(BF).reshape(n_groups, n_plane, rows_w, -1)
+    g_expand = grad_expand.astype(BF).reshape(n_groups, n_plane, kv_n, kv_cols)
+    key_grad, grad_hidden, gw_nope, gw_rope, g_expand = swap(
         4,
-        ("plane_sum", key_grads),
+        ("plane_sum_shift", key_grads),
         ("plane_sum", grad_hidden.reshape(n_plane, tok, width)),
-        ("group_sum", g_output),
-        ("whole_swap", g_both.astype(BF).reshape(n_groups, n_plane, rows_w, 2 * shared_n)),
-    )
-    row_pairs = [
-        (g * n_plane + j, n_groups * j + g) for g in range(n_groups) for j in range(n_plane)
-    ]
-    grad_output_weight = lax.ppermute(grad_output_weight, ALL, row_pairs)
-    later = lax.ppermute(key_grads[:tok].astype(BF), "g", down_pairs).astype(F32)
-    key_grad = key_grads[tok:] + later
+        ("group_sum_swap", gw_nope),
+        ("group_sum_swap", gw_rope),
+        ("group_sum_swap", g_expand),
+    )
     latent_own = own_rows(latent)
     kv_norm_back = jax.vjp(rms_norm, latent_own[:, :RANK], gain_kv)[1]
     grad_comp_in, grad_gain_kv = kv_norm_back(key_grad[:, :RANK])
     grad_rope_in = unrotate(key_grad[:, RANK:], own_rows(cosine), own_rows(sine_part))
     grad_latent = jnp.concatenate([grad_comp_in, grad_rope_in], axis=1).astype(BF)
 
-    g_query = jnp.concatenate(
-        [
-            dot_tn(hidden, gq_nope).reshape(width, local_heads, NOPE),
-            dot_tn(hidden, gq_rope).reshape(width, local_heads, ROPE),
-        ],
-        axis=2,
-    ).reshape(width, local_heads * (NOPE + ROPE))
-
-    g_query = g_query.astype(BF).reshape(n_groups, n_plane, rows_w, head_cols)
-    g_expand = grad_expand.astype(BF).reshape(n_groups, n_plane, kv_n, kv_cols)
-    g_query, g_expand, latent_grads = swap(
-        5,
-        ("group_sum_swap", g_query),
-        ("group_sum_swap", g_expand),
-        ("plane_gather", grad_latent),
-    )
-    grad_query_weight = g_query.transpose(1, 0, 2).reshape(rows_w, -1).astype(F32)
+    latent_grads = swap(5, ("plane_gather", grad_latent))[0]
+
+    def per_head(table, cols):
+        return table.transpose(1, 0, 2).reshape(rows_w, HEADS, cols)
+
+    grad_query_weight = jnp.concatenate(
+        [per_head(gw_nope, NOPE), per_head(gw_rope, ROPE)], axis=2
+    ).reshape(rows_w, -1).astype(F32)
     grad_expand_weight = g_expand.transpose(1, 0, 2).reshape(kv_n, -1).astype(F32)
 
     latent_grads = latent_grads.reshape(plane_tok, RANK + ROPE)
@@ -1257,12 +1363,17 @@
         axis=1,
     )
     small_grads = jnp.pad(small_grads, ((0, 0), (0, -small_grads.shape[1] % 1024)))
-    grad_latent_weight, small_grads = swap(
+    grad_latent_weight, grad_output_weight, small_grads = swap(
         6,
         ("group_sum", g_latent),
+        ("group_sum", g_output),
         ("whole_sum", small_grads.reshape(n_groups, n_plane, -1, 128)),
     )
     small_grads = small_grads.reshape(-1)
+    row_pairs = [
+        (g * n_plane + j, n_groups * j + g) for g in range(n_groups) for j in range(n_plane)
+    ]
+    grad_output_weight = lax.ppermute(grad_output_weight, ALL, row_pairs)
     g_shared = g_shared.transpose(2, 0, 1, 3).reshape(rows_w, devices, 2 * shared_n).astype(F32)
     grad_shared_gate = g_shared[:, :, :shared_n].reshape(rows_w, devices * shared_n)
     grad_shared_up = g_shared[:, :, shared_n:].reshape(rows_w, devices * shared_n)

time: 1030 us -> 1070 us (1.039)
  Pallas kernels: 609 us -> 662 us
  matrix products: 122 us -> 85.6 us
  waiting for transfers between devices: 99.9 us -> 119 us
    pallas_call x7, Pallas kernels: 333 us -> 372 us  [exchange(): pl.pallas_call(functools.partial(exchange_kernel, n_groups, n_plane, kind...]
    dot_general x11 -> x8, matrix products: 81.8 us -> 43.4 us  [dot_tn(): lax.dot_general(left, right, (((0,), (0,)), ((), ())), preferred_element_...]
    ppermute x1, waiting for transfers between devices: 0.01 us -> 30.9 us  [body(): grad_output_weight = lax.ppermute(grad_output_weight, ALL, row_pairs)]
    unnamed x165 -> x156, local copies, waits for them, and re-layouts: 20.3 us -> 37.3 us
    pallas_call x1, Pallas kernels: 111 us -> 125 us  [experts_sums(): pl.pallas_call(functools.partial(out_kernel, n_groups, slot_count), grid=...]
    all_gather x3 -> x2, waiting for transfers between devices: 82.1 us -> 69 us  [gather_all(): return lax.all_gather(x, ALL, axis=0, tiled=True)]
  transfers between devices with their start and end apart: 7 -> 5, of which waited for: 2 -> 3; matrix products, arithmetic and copies ran while one was open for 20% -> 11% of each run, Pallas kernels for 36% -> 23%
where the time goes in v4:
time: 1070 us; the launch traced here: 1060 us
  Pallas kernels  662 us (62%)
  waiting for transfers between devices  119 us (11%)
  local copies, waits for them, and re-layouts  113 us (11%)
  matrix products  85.6 us (8%)
  other arithmetic  47.7 us (4%)
  between operations  15.7 us (1%)
  starting transfers between devices  14.9 us (1%)
    pallas_call x7, Pallas kernels, exchange(): pl.pallas_call(functools.partial(exchange_kernel, n_groups, n_plane, kind...  372 us
    pallas_call x1, Pallas kernels, experts_sums(): pl.pallas_call(functools.partial(moe_kernel, n_groups, experts, hidden_s,...  132 us
    pallas_call x1, Pallas kernels, experts_sums(): pl.pallas_call(functools.partial(out_kernel, n_groups, slot_count), grid=...  125 us
    all_gather x2, waiting for transfers between devices, gather_all(): return lax.all_gather(x, ALL, axis=0, tiled=True)  69 us
    dot_general x8, matrix products, dot_tn(): lax.dot_general(left, right, (((0,), (0,)), ((), ())), preferred_element_...  43.4 us
    unnamed x156, local copies, waits for them, and re-layouts  37.3 us
    ppermute x1, waiting for transfers between devices, body(): grad_output_weight = lax.ppermute(grad_output_weight, ALL, row_pairs)  30.9 us
    dot_general x6, matrix products, dot_nt(): lax.dot_general(left, right, (((1,), (1,)), ((), ())), preferred_element_...  24.6 us
  transfers between devices with their start and end apart: 5, of which 3 were waited for; matrix products, arithmetic and copies ran while one was open for 11% of the time, Pallas kernels for 23%

profile of v4, /device:TPU:1, one launch (start us, length us, event | category | flops | bytes accessed | tf_op | source)
XLA Modules:
  0.0 1057.5 jit_solution(7129039938894384388)
XLA Ops:
  15.4 79.3 %exchange_0.1 = (bf16[8,128,2048]{2,1,0:T(8,128)(2,1)}, bf16[4,8,32,128]{3,2,1,0:T(8,128)(2,1)}, bf16[4,8,64,576]{3,2,1,0:T(8,128)(2,1)}, bf16[4,8,64,512]{3,2,1,0:T(8,128)(2,1)}) custom-call(bf16[128,2048]{1,0:T(8,128)(2,1)} %refs_0_.1, bf16[32,128]{1,0:T(8,128)(2,1)} %pad_bitcast_fusion.1.refs_1_, bf16[64,576]{1,0:T(8,128)(2,1)} %refs_2_.1, ...), custom_call_target="tpu_custom_call" | custom-call | tf_op jit(solution)/shard_map/exchange_0/pallas_call | solution.py:639
  94.6 6.6 bitcast_convert_fusion.1
  104.0 3.2 multiply_reduce_fusion
  109.6 3.4 fusion.51
  115.0 3.3 fusion.15
  120.3 51.8 %exchange_1.1 = (bf16[8,128,576]{2,1,0:T(8,128)(2,1)}, bf16[4,64,2048]{2,1,0:T(8,128)(2,1)}) custom-call(bf16[128,576]{1,0:T(8,128)(2,1)} %fusion.32.refs_0_, bf16[64,2048]{1,0:T(8,128)(2,1)} %refs_1_.1), custom_call_target="tpu_custom_call" | custom-call | tf_op jit(solution)/shard_map/exchange_1/pallas_call | solution.py:639
  176.4 2.8 copy.213
  181.3 2.3 slice.152
  186.1 3.8 fusion.22
  193.4 4.5 convolution_convert_fusion.1.ex_ref
  199.3 11.5 %attend.1 = (bf16[1024,256]{1,0:T(8,128)(2,1)S(1)}, f32[1024,2]{1,0:T(8,128)S(1)}) custom-call(s32[1024,1]{1,0:T(8,128)S(1)} %copy.220.low_ref, bf16[1024,256]{1,0:T(8,128)(2,1)S(1)} %convolution_convert_fusion.7.qn_ref, bf16[1024,128]{1,0:T(8,128)(2,1)S(1)} %copy.221.qr_ref, bf16[2048,512]{1,0:T(8,128)(2,1)} %convolution_convert_fusion.1.ex_ref, ...), custom_call_target="tpu_custom_call" | custom-call | flops 1677721600 | bytes 4194304 | tf_op jit(solution)/shard_map/attend/pallas_call | solution.py:117
  211.6 3.3 convolution_convert_fusion
  214.8 51.9 %exchange_2.1 = f32[128,2048]{1,0:T(8,128)} custom-call(bf16[8,128,2048]{2,1,0:T(8,128)(2,1)} %bitcast.147), custom_call_target="tpu_custom_call" | custom-call | tf_op jit(solution)/shard_map/exchange_2/pallas_call | solution.py:639
  270.2 3.1 reshape.480
  273.3 3.0 reshape.481
  279.6 6.4 all-to-all-start
  289.7 4.6 copy.225
  294.3 4.6 copy.226
  307.7 18.7 %all-to-all-done = bf16[1,64,32,176]{3,1,0,2:T(8,128)(2,1)} async-done(((bf16[1,64,32,176]{3,1,0,2:T(8,128)(2,1)}), bf16[1,64,32,176]{3,1,0,2:T(8,128)(2,1)}, u32[]{:S(2)}, u32[]{:S(2)}) %all-to-all-start) | async-done | bytes 720928 | tf_op jit(solution)/shard_map/all_to_all | solution.py:1180
  330.4 69.0 %all-gather.3.cloned.1.call-done.h2_hbm = bf16[4096,2048]{1,0:T(8,128)(2,1)} async-done(((bf16[128,2048]{1,0:T(8,128)(2,1)}), bf16[4096,2048]{1,0:T(8,128)(2,1)}) %all-gather.3.cloned.1.call-update) | async-done | bytes 16777232 | tf_op jit(solution)/shard_map/all_gather | solution.py:656
  399.4 132.5 %experts.1 = (f32[128,2048]{1,0:T(8,128)}, bf16[3072,2048]{1,0:T(8,128)(2,1)}, bf16[3072,2048]{1,0:T(8,128)(2,1)}, bf16[3072,704]{1,0:T(8,128)(2,1)}, bf16[3072,...) custom-call(bf16[4096,2048]{1,0:T(8,128)(2,1)} %all-gather.3.cloned., ...), custom_call_target="tpu_custom_call" | custom-call | flops 57713623040 | bytes 100663296 | tf_op jit(solution)/shard_map/experts/pallas_call | solution.py:1028
  531.9 10.9 %convolution_convert_fusion.2 = bf16[2048,256]{0,1:T(8,128)(2,1)S(1)} fusion(bf16[4096,2048]{1,0:T(8,128)(2,1)} %all-gather.3.cloned.1.call-done.h2_hbm, bf16[4096,256]{1,0:T(8,128)(2,1)} %get-tuple-element.72), kind=kOutput, calls=%fused_computation.13 | convolution fusion | flops 4295491584 | bytes 19922944 | tf_op jit(solution)/shard_map/dot_general | solution.py:54
  542.8 3.8 all-to-all-start.1
  548.6 124.9 %expert_out.1 = (f32[128,2048]{1,0:T(8,128)}, f32[2048,704]{1,0:T(8,128)}, f32[2048,704]{1,0:T(8,128)}, f32[704,2048]{1,0:T(8,128)}) custom-call(bf16[3072,704]{1,0:T(8,128)(2,1)} %get-tuple-element.61.act_ref, f32[3072,1]{1,0:T(8,128)} %get-tuple-element.62.rw_ref, bf16[3072,2048]{1,0:T(8,128)(2,1)} %get-tuple-element.63.rows_ref, ...), custom_call_target="tpu_custom_call" | custom-call | flops 39191576576 | bytes 33554432 | tf_op jit(solution)/shard_map/expert_out/pallas_call | solution.py:1061
  673.6 9.9 fusion.13
  685.0 6.4 copy.246
  691.4 6.7 copy.247
  703.2 62.6 %exchange_3.1 = (bf16[8,128,2048]{2,1,0:T(8,128)(2,1)}, bf16[4,8,64,176]{3,2,1,0:T(8,128)(2,1)}) custom-call(bf16[128,2048]{1,0:T(8,128)(2,1)} %fusion.45.refs_0_, bf16[4,8,64,176]{3,2,1,0:T(8,128)(2,1)} %pad_maximum_fusion.5.refs_1_), custom_call_target="tpu_custom_call" | custom-call | tf_op jit(solution)/shard_map/exchange_3/pallas_call | solution.py:639
  765.9 4.7 convolution_convert_fusion.6.gm_ref
  774.8 20.8 %attend_back.1 = (f32[1024,256]{1,0:T(8,128)}, f32[1024,128]{1,0:T(8,128)}, f32[2048,512]{1,0:T(8,128)}, f32[2048,64]{1,0:T(8,128)}) custom-call(s32[1024,1]{1,0:T(8,128)} %copy-done.2, bf16[1024,256]{1,0:T(8,128)(2,1)} %copy-done.5, bf16[1024,128]{1,0:T(8,128)(2,1)} %copy-done.4, bf16[2048,512]{1,0:T(8,128)(2,1)} %convolution_convert_fusion.1.ex_ref, ...), custom_call_target="tpu_custom_call" | custom-call | flops 4362076160 | bytes 8388608 | tf_op jit(solution)/shard_map/attend_back/pallas_call | solution.py:192
  795.6 5.9 fusion.29
  801.5 6.1 fusion.4
  816.9 4.3 convolution_convert_fusion.4
  821.2 6.9 fusion
  828.1 64.7 %exchange_4.1 = (f32[128,576]{1,0:T(8,128)}, f32[128,2048]{1,0:T(8,128)}, bf16[8,64,256]{2,1,0:T(8,128)(2,1)}, bf16[8,64,128]{2,1,0:T(8,128)(2,1)}, bf16[8,16,512]{2,1,0:T(8,128)(2,1)}) custom-call(bf16[8,256,576]{2,1,0:T(8,128)(2,1)} %bitcast.149, bf16[8,128,2048]{2,1,0:T(8,128)(2,1)} %bitcast.148, bf16[4,8,64,256]{3,2,1,0:T(8,128)(2,1)} %bitcast.178, ...), custom_call_target="tpu_custom_call" | custom-call | tf_op jit(solution)/shard_map/exchange_4/pallas_call | solution.py:639
  896.9 20.7 %exchange_5.1 = bf16[8,128,576]{2,1,0:T(8,128)(2,1)} custom-call(bf16[128,576]{1,0:T(8,128)(2,1)} %pad_maximum_fusion.9.refs_0_), custom_call_target="tpu_custom_call" | custom-call | tf_op jit(solution)/shard_map/exchange_5/pallas_call | solution.py:639
  917.7 4.1 fusion.12
  922.8 6.6 bitcast_convert_fusion
  929.5 4.3 copy.238
  935.5 41.4 %exchange_6.1 = (f32[64,576]{1,0:T(8,128)}, f32[64,2048]{1,0:T(8,128)}, f32[16,128]{1,0:T(8,128)}) custom-call(bf16[4,64,576]{2,1,0:T(8,128)(2,1)} %dynamic-slice_bitcast_fusion.refs_0_, bf16[4,64,2048]{2,1,0:T(8,128)(2,1)} %bitcast.179, f32[4,8,16,128]{3,2,1,0:T(8,128)} %copy.260), custom_call_target="tpu_custom_call" | custom-call | tf_op jit(solution)/shard_map/exchange_6/pallas_call | solution.py:639
  985.3 2.7 reshape.502
  988.0 2.8 copy.243
  990.8 2.7 reshape.501
  1000.8 2.5 reshape.508
  1003.9 4.6 collective-permute-start
  1008.6 3.3 fusion.8
  1011.9 30.9 %collective-permute-done = f32[64,2048]{1,0:T(8,128)S(1)} collective-permute-done((f32[64,2048]{1,0:T(8,128)}, f32[64,2048]{1,0:T(8,128)S(1)}, u32[]{:S(2)}, u32[]{:S(2)}) %collective-permute-start) | collective-permute-done | bytes 524320 | tf_op jit(solution)/shard_map/ppermute | solution.py:1376
  1044.3 5.9 copy.267
  (274 shorter events, 101.3 us)
Async XLA Ops:
  7.2 323.2 %all-gather.5.cloned.1.call-start = ((), (), s32[]{:S(2)}) async-start(), calls=%async_computation.3 | async-start | bytes 17301504 | tf_op jit(solution)/shard_map/all_gather | solution.py:656
  94.6 6.7 copy-start.28
  101.3 298.1 %all-gather.3.cloned.1.call-start = ((), (), s32[]{:S(2)}) async-start(), calls=%async_computation.2 | async-start | bytes 17301504 | tf_op jit(solution)/shard_map/all_gather | solution.py:656
  103.7 14.6 %copy-start.48 = (f32[512]{0:T(512)}, f32[512]{0:T(512)S(1)}, u32[]{:S(2)}) copy-start(f32[512]{0:T(512)S(1)} %reshape.505) | copy-start | bytes 6148
  113.0 190.4 %copy-start.10 = (f32[1024,576]{1,0:T(8,128)}, f32[1024,576]{1,0:T(8,128)S(1)}, u32[]{:S(2)}) copy-start(f32[1024,576]{1,0:T(8,128)S(1)} %fusion.51) | copy-start | bytes 7077892
  176.1 92.2 %copy-start.40 = (f32[2048]{0:T(1024)}, f32[2048]{0:T(1024)S(1)}, u32[]{:S(2)}) copy-start(f32[2048]{0:T(1024)S(1)} %reshape.506) | copy-start | bytes 24580
  176.4 22.8 %copy-start.2 = (s32[1024,1]{1,0:T(8,128)}, s32[1024,1]{1,0:T(8,128)S(1)}, u32[]{:S(2)}) copy-start(s32[1024,1]{1,0:T(8,128)S(1)} %copy.220.low_ref) | copy-start | bytes 12292
  192.0 7.2 copy-start.4
  199.2 15.6 %copy-start.5 = (bf16[1024,256]{1,0:T(8,128)(2,1)}, bf16[1024,256]{1,0:T(8,128)(2,1)S(1)}, u32[]{:S(2)}) copy-start(bf16[1024,256]{1,0:T(8,128)(2,1)S(1)} %convolution_convert_fusion.7.qn_ref) | copy-start | bytes 1572868
  199.2 12.3 %copy-start.36 = (bf16[4,64,2048]{2,1,0:T(8,128)(2,1)S(1)}, bf16[4,64,2048]{2,1,0:T(8,128)(2,1)}, u32[]{:S(2)}) copy-start(bf16[4,64,2048]{2,1,0:T(8,128)(2,1)} %get-tuple-element.59) | copy-start | bytes 3145732
  214.8 51.9 %copy-start.14 = (bf16[128,2048]{1,0:T(8,128)(2,1)S(1)}, bf16[128,2048]{1,0:T(8,128)(2,1)}, u32[]{:S(2)}) copy-start(bf16[128,2048]{1,0:T(8,128)(2,1)} %refs_0_.1) | copy-start | bytes 1572868
  268.2 11.3 %copy-start.68 = (f32[128]{0:T(128)}, f32[128]{0:T(128)S(1)}, u32[]{:S(2)}) copy-start(f32[128]{0:T(128)S(1)} %get-tuple-element.192) | copy-start | bytes 1540
  268.2 38.3 %copy-start.64 = (f32[128]{0:T(128)}, f32[128]{0:T(128)S(1)}, u32[]{:S(2)}) copy-start(f32[128]{0:T(128)S(1)} %get-tuple-element.210) | copy-start | bytes 1540
  270.2 18.4 %copy-start.16 = (bf16[2048,128]{1,0:T(8,128)(2,1)S(1)}, bf16[2048,128]{1,0:T(8,128)(2,1)}, u32[]{:S(2)}) copy-start(bf16[2048,128]{1,0:T(8,128)(2,1)} %slice.161) | copy-start | bytes 1572868
  279.6 46.8 %all-to-all-start = ((bf16[1,64,32,176]{3,1,0,2:T(8,128)(2,1)}), bf16[1,64,32,176]{3,1,0,2:T(8,128)(2,1)}, u32[]{:S(2)}, u32[]{:S(2)}) async-start(bf16[1,64,32,176]{3,1,0,2:T(8,128)(2,1)} %copy.227), calls=%async_computation | async-start | bytes 2097152 | tf_op jit(solution)/shard_map/all_to_all | solution.py:1180
  299.5 30.9 %copy-start.11 = (bf16[2048,16]{1,0:T(8,128)(2,1)}, bf16[2048,16]{1,0:T(8,128)(2,1)S(1)}, u32[]{:S(2)}) copy-start(bf16[2048,16]{1,0:T(8,128)(2,1)S(1)} %reshape.482) | copy-start | bytes 196612
  303.5 24.4 %copy-start.66 = (f32[128]{0:T(128)}, f32[128]{0:T(128)S(1)}, u32[]{:S(2)}) copy-start(f32[128]{0:T(128)S(1)} %multiply_reduce_fusion.7) | copy-start | bytes 1540
  304.9 23.1 %copy-start.55 = (f32[128]{0:T(128)}, f32[128]{0:T(128)S(1)}, u32[]{:S(2)}) copy-start(f32[128]{0:T(128)S(1)} %get-tuple-element.222) | copy-start | bytes 1540
  542.8 155.2 %all-to-all-start.1 = ((f32[32,1,128]{2,1,0:T(1,128)}), f32[32,1,128]{2,1,0:T(1,128)}, u32[]{:S(2)}, u32[]{:S(2)}) async-start(f32[32,1,128]{2,1,0:T(1,128)} %bitcast.31), calls=%async_computation.1 | async-start | bytes 32768 | tf_op jit(solution)/shard_map/all_to_all | solution.py:1246
  673.5 9.9 copy-start.29
  673.6 9.9 copy-start.30
  691.3 7.6 copy-start.45
  691.3 7.6 copy-start.56
  691.3 7.6 copy-start.57
  691.3 7.6 copy-start.13
  691.3 8.9 copy-start.9
  691.3 8.9 copy-start.12
  691.3 8.9 copy-start.41
  691.3 8.9 copy-start.53
  702.1 68.5 %copy-start.61 = (f32[128]{0:T(128)}, f32[128]{0:T(128)S(1)}, u32[]{:S(2)}) copy-start(f32[128]{0:T(128)S(1)} %multiply_multiply_fusion.2) | copy-start | bytes 1540
  774.8 20.8 %copy-start.19 = (bf16[2048,2,128]{0,2,1:T(8,128)(2,1)S(1)}, bf16[2048,2,128]{0,2,1:T(8,128)(2,1)}, u32[]{:S(2)}) copy-start(bf16[2048,2,128]{0,2,1:T(8,128)(2,1)} %slice.152) | copy-start | bytes 3145732
  795.6 5.9 copy-start.31
  795.6 5.9 copy-start.47
  795.6 5.9 copy-start.58
  801.5 6.1 copy-start.20
  828.1 65.8 %copy-start.49 = (f32[512]{0:T(512)S(1)}, f32[512]{0:T(512)}, u32[]{:S(2)}) copy-start(f32[512]{0:T(512)} %copy-done.48) | copy-start | bytes 6148
  828.1 65.8 %copy-start.63 = (f32[128]{0:T(128)S(1)}, f32[128]{0:T(128)}, u32[]{:S(2)}) copy-start(f32[128]{0:T(128)} %fusion.40) | copy-start | bytes 1540
  828.1 66.9 %copy-start.67 = (f32[128]{0:T(128)S(1)}, f32[128]{0:T(128)}, u32[]{:S(2)}) copy-start(f32[128]{0:T(128)} %copy-done.66) | copy-start | bytes 1540
  828.1 89.6 %copy-start.15 = (bf16[128,2048]{1,0:T(8,128)(2,1)S(1)}, bf16[128,2048]{1,0:T(8,128)(2,1)}, u32[]{:S(2)}) copy-start(bf16[128,2048]{1,0:T(8,128)(2,1)} %refs_0_.1) | copy-start | bytes 1572868
  828.1 89.6 %copy-start.59 = (f32[128]{0:T(128)S(1)}, f32[128]{0:T(128)}, u32[]{:S(2)}) copy-start(f32[128]{0:T(128)} %fusion.41) | copy-start | bytes 1540
  983.7 11.6 %copy-start.65 = (f32[128]{0:T(128)S(1)}, f32[128]{0:T(128)}, u32[]{:S(2)}) copy-start(f32[128]{0:T(128)} %copy-done.64) | copy-start | bytes 1540
  997.0 6.3 copy-start.43
  997.0 11.6 %copy-start.54 = (f32[128]{0:T(128)S(1)}, f32[128]{0:T(128)}, u32[]{:S(2)}) copy-start(f32[128]{0:T(128)} %copy-done.52) | copy-start | bytes 1540
  997.0 11.6 %copy-start.60 = (f32[128]{0:T(128)S(1)}, f32[128]{0:T(128)}, u32[]{:S(2)}) copy-start(f32[128]{0:T(128)} %fusion.41) | copy-start | bytes 1540
  997.0 11.6 %copy-start.62 = (f32[128]{0:T(128)S(1)}, f32[128]{0:T(128)}, u32[]{:S(2)}) copy-start(f32[128]{0:T(128)} %copy-done.61) | copy-start | bytes 1540
  997.0 11.6 %copy-start.70 = (f32[128]{0:T(128)S(1)}, f32[128]{0:T(128)}, u32[]{:S(2)}) copy-start(f32[128]{0:T(128)} %multiply_multiply_fusion) | copy-start | bytes 1540
  1003.3 39.6 %copy-start.42 = (f32[64,576]{1,0:T(8,128)S(1)}, f32[64,576]{1,0:T(8,128)}, u32[]{:S(2)}) copy-start(f32[64,576]{1,0:T(8,128)} %get-tuple-element.248) | copy-start | bytes 442372
  1003.9 38.9 %collective-permute-start = (f32[64,2048]{1,0:T(8,128)}, f32[64,2048]{1,0:T(8,128)S(1)}, u32[]{:S(2)}, u32[]{:S(2)}) collective-permute-start(f32[64,2048]{1,0:T(8,128)} %get-tuple-element.85), channel_id=1, source_target_pairs={{0,0},{1,4},{2,8},{3,12},{4,16},{5,20},{6,24},{7,28},{8,1},{9,5},{... | collective-permute-start | bytes 1572872 | tf_op jit(solution)/shard_map/ppermute | solution.py:1376
  (30 other events, 91.8 us)
Sparse Core Ops, SparseCore 0:
  101.4 141.9 all-gather.4
  270.3 129.0 all-gather.2

commit v5 on v4

--- a/solution.py
+++ b/solution.py
@@ -269,7 +269,7 @@
     def on_plane(self, j):
         return {"p": j // self.cores, "c": j % self.cores}
 
-    def meet(self, heads=False):
+    def meet(self, heads=False, home=False):
         barrier = pltpu.get_barrier_semaphore()
         waits = self.n_plane - 1 + self.n_groups - 1
         if heads:
@@ -283,6 +283,17 @@
                     pl.semaphore_signal(barrier, inc=1, device_id=source, device_id_type=MESH)
 
             waits = waits + jnp.where(mine, self.n_groups - 1, self.n_groups)
+        if home:
+            source = self.home_source()
+            stays = source == self.g * self.n_plane + self.j
+
+            @pl.when(jnp.logical_not(stays))
+            def _():
+                pl.semaphore_signal(
+                    barrier, inc=1, device_id=self.at_device(source), device_id_type=MESH
+                )
+
+            waits = waits + jnp.where(stays, 0, 1)
         for d in range(1, self.n_plane):
             pl.semaphore_signal(
                 barrier, inc=1, device_id=self.at_plane(self.plane_peer(d)), device_id_type=MESH
@@ -293,6 +304,10 @@
             )
         pl.semaphore_wait(barrier, waits)
 
+    def home_source(self):
+        index = self.g * self.n_plane + self.j
+        return lax.rem(index, self.n_groups) * self.n_plane + index // self.n_groups
+
     def head_owner(self):
         return (self.g * self.n_plane + self.j) // self.n_groups
 
@@ -487,20 +502,57 @@
 
 def whole_swap(w, src, out, mid):
     first = []
+    for d in range(1, w.n_groups):
+        to = w.group_peer(d)
+        first.append(w.start(src.at[to], mid.at[w.g], w.at_group(to)))
+    mid[w.g] = src[w.g]
+    yield
+    wait_received(first)
+    second = []
     for d in range(1, w.n_plane):
         to = w.plane_peer(d)
-        first.append(w.start(src.at[:, to], mid.at[w.j], w.at_plane(to)))
-    mid[w.j] = src[:, w.j]
-    yield
-    wait_received(first)
-    second = []
+        second.append(w.start(mid.at[:, to], out.at[:, w.j], w.at_plane(to)))
+    out[:, w.j] = mid[:, w.j]
+    yield
+    wait_sent(first)
+    wait_all(second)
+
+
+def group_sum_home(w, src, out, parts, low, home):
+    copies = []
     for d in range(1, w.n_groups):
         to = w.group_peer(d)
-        second.append(w.start(mid.at[:, to], out.at[w.g], w.at_group(to)))
-    out[w.g] = mid[:, w.g]
-    yield
-    wait_sent(first)
-    wait_all(second)
+        copies.append(w.start(src.at[to], parts.at[d - 1], w.at_group(to)))
+    yield
+    wait_received(copies)
+    sum_rows(low, [src.at[w.g]] + [parts.at[d] for d in range(w.n_groups - 1)])
+    stays = w.home_source() == w.g * w.n_plane + w.j
+    copy = pltpu.make_async_remote_copy(
+        src_ref=low,
+        dst_ref=home,
+        send_sem=w.send.at[w.used],
+        recv_sem=w.recv.at[w.used],
+        device_id=w.at_device(w.n_groups * w.j + w.g),
+        device_id_type=MESH,
+    )
+    w.used += 1
+
+    @pl.when(jnp.logical_not(stays))
+    def _():
+        copy.start()
+
+    @pl.when(stays)
+    def _():
+        home[...] = low[...]
+
+    yield
+
+    @pl.when(jnp.logical_not(stays))
+    def _():
+        copy.wait()
+
+    out[...] = home[...].astype(F32)
+    wait_sent(copies)
 
 
 def plane_sum_shift(w, src, out, from_core, pairs, from_chips, low, later):
@@ -561,6 +613,7 @@
     "group_sum": group_sum,
     "whole_sum": whole_sum,
     "whole_swap": whole_swap,
+    "group_sum_home": group_sum_home,
     "group_sum_swap": group_sum_swap,
 }
 
@@ -570,7 +623,7 @@
     sources, outs = refs[:count], refs[count : 2 * count]
     scratch = list(refs[2 * count : -2])
     w = Wires(n_groups, n_plane, refs[-2], refs[-1])
-    w.meet("head_rows" in kinds)
+    w.meet("head_rows" in kinds, "group_sum_home" in kinds)
     running = []
     for kind, source, out, number in zip(kinds, sources, outs, extra):
         mine, scratch = scratch[:number], scratch[number:]
@@ -616,19 +669,22 @@
         elif kind == "plane_sum":
             out = shape[1:]
             own = [(chips,) + out, (chips,) + out, (chips - 1,) + out]
+        elif kind == "group_sum_home":
+            out = shape[1:]
+            own = [(n_groups - 1,) + out, out, out]
         elif kind == "group_sum":
             out = shape[1:]
             own = [(n_groups - 1,) + out]
         elif kind == "whole_swap":
             out = shape
-            own = [(n_plane, n_groups) + shape[2:]]
+            own = [shape]
         elif kind == "whole_sum":
             out = shape[2:]
             own = [(n_plane - 1, n_groups) + out, (n_groups,) + out, (n_groups - 1,) + out]
         elif kind == "group_sum_swap":
             out = shape[1:]
             own = [out, (n_groups - 1,) + out]
-        if kind in ("plane_sum", "plane_sum_shift", "group_sum", "whole_sum"):
+        if kind in ("plane_sum", "plane_sum_shift", "group_sum", "group_sum_home", "whole_sum"):
             shapes.append(jax.ShapeDtypeStruct(out, F32))
         else:
             shapes.append(jax.ShapeDtypeStruct(out, dtype))
@@ -665,9 +721,11 @@
         self.credit = credit
 
     @staticmethod
-    def distances(step):
+    def chips(w, step):
         half = lax.rem(step, 2)
-        return 1 + 2 * half, 2 - 2 * half
+        beside = w.p + 1 - 2 * lax.rem(w.p, 2)
+        above = w.p + 2 - 4 * (w.p // 2)
+        return beside + half * (above - beside), 3 - w.p + half * (2 * w.p - 3)
 
     def core_copy(self, step, i):
         slot = lax.rem(step, 2)
@@ -680,25 +738,27 @@
             device_id_type=MESH,
         )
 
-    def chip_copy(self, step, i):
-        slot, distance = lax.rem(step, 2), self.distances(step)[i]
-        group_at = step // 2
+    def part(self, ref, upper):
+        rows = ref.shape[0] // 2
+        return ref.at[pl.ds(rows, rows)] if upper else ref.at[pl.ds(0, rows)]
+
+    def chip_copy(self, group_at, which):
+        slot, i, upper, up = (
+            (0, 0, False, False),
+            (0, 1, False, False),
+            (0, 1, True, True),
+            (1, 0, True, True),
+            (1, 0, False, True),
+            (0, 0, True, False),
+        )[which]
+        p = self.w.p
+        to = p + 2 - 4 * (p // 2) if up else p + 1 - 2 * lax.rem(p, 2)
         return pltpu.make_async_remote_copy(
-            src_ref=self.pairs.at[slot, i],
-            dst_ref=self.from_chips.at[group_at, distance - 1],
-            send_sem=self.chip_sems.at[slot, i],
-            recv_sem=self.chip_recv.at[group_at, distance - 1],
-            device_id=self.w.at_chip(lax.rem(self.w.p + distance, 4)),
-            device_id_type=MESH,
-        )
-
-    def chip_arrival(self, group_at, distance):
-        return pltpu.make_async_remote_copy(
-            src_ref=self.pairs.at[0, 0],
-            dst_ref=self.from_chips.at[group_at, distance - 1],
-            send_sem=self.chip_sems.at[0, 0],
-            recv_sem=self.chip_recv.at[group_at, distance - 1],
-            device_id=self.w.at_chip(lax.rem(self.w.p + distance, 4)),
+            src_ref=self.part(self.pairs.at[slot, i], upper),
+            dst_ref=self.from_chips.at[group_at, which],
+            send_sem=self.chip_sems.at[which],
+            recv_sem=self.chip_recv.at[group_at, which],
+            device_id=self.w.at_chip(to),
             device_id_type=MESH,
         )
 
@@ -727,23 +787,20 @@
             self.core_copy(step, i).start()
 
     def merge(self, step):
-        slot = lax.rem(step, 2)
+        slot, group_at = lax.rem(step, 2), step // 2
+        for half, sends in ((0, (0, 1, 2, 5)), (1, (3, 4))):
+
+            @pl.when((slot == half) & (step >= 2))
+            def _():
+                for which in sends:
+                    self.chip_copy(group_at, which).wait_send()
+
         for i in range(2):
             self.core_copy(step, i).wait_recv()
-            sends = slot == 0 if i else slot >= 0
-
-            @pl.when(sends & (step >= 2))
-            def _():
-                self.chip_copy(step, i).wait_send()
-
             sum_rows(
                 self.pairs.at[slot, i],
                 [self.stage.at[slot, 2 * i + self.w.c], self.from_core.at[slot, i]],
             )
-
-            @pl.when(sends)
-            def _():
-                self.chip_copy(step, i).start()
 
         @pl.when(step + 2 < self.steps)
         def _():
@@ -751,10 +808,28 @@
                 self.credit, inc=1, device_id=self.w.partner(), device_id_type=MESH
             )
 
+        @pl.when(slot == 0)
+        def _():
+            for which in (0, 1, 2):
+                self.chip_copy(group_at, which).start()
+
+        @pl.when(slot == 1)
+        def _():
+            self.chip_copy(group_at, 3).start()
+            for source, i, upper, which in ((1, (1, 0), False, 4), (2, (0, 0), True, 5)):
+                self.chip_copy(group_at, source).wait_recv()
+                target = self.part(self.pairs.at[i], upper)
+                sum_rows(target, [target, self.from_chips.at[group_at, source]])
+                self.chip_copy(group_at, which).start()
+
     def plane_total(self, group_at):
-        for distance in (1, 2, 3):
-            self.chip_arrival(group_at, distance).wait_recv()
-        return [self.pairs.at[1, 1]] + [self.from_chips.at[group_at, d] for d in range(3)]
+        for which in (0, 3, 4, 5):
+            self.chip_copy(group_at, which).wait_recv()
+        return [
+            [self.part(self.pairs.at[1, 1], upper)]
+            + [self.from_chips.at[group_at, which] for which in arrived]
+            for upper, arrived in ((False, (0, 4)), (True, (3, 5)))
+        ]
 
     def advance(self, step):
         @pl.when(step >= 1)
@@ -764,7 +839,8 @@
             @pl.when((lax.rem(last, 2) == 0) & (last >= 2))
             def _():
                 group_at = last // 2 - 1
-                sum_rows(self.totals.at[group_at], self.plane_total(group_at))
+                for upper, sources in enumerate(self.plane_total(group_at)):
+                    sum_rows(self.part(self.totals.at[group_at], upper), sources)
                 self.group_copy(group_at).start()
 
             self.merge(last)
@@ -772,19 +848,20 @@
     def finish(self, out):
         steps = self.steps
         self.merge(steps - 1)
-        sources = self.plane_total(steps // 2 - 1)
         groups = steps // 2 - 1
+        halves = self.plane_total(groups)
         for d in range(groups):
             self.group_copy(d).wait_recv()
-            sources.append(self.parts.at[d])
-        sum_rows(out, sources)
+        for upper, sources in enumerate(halves):
+            parts = [self.part(self.parts.at[d], upper) for d in range(groups)]
+            sum_rows(self.part(out, upper), sources + parts)
         for d in range(groups):
             self.group_copy(d).wait_send()
         for i in range(2):
             self.core_copy(steps - 2, i).wait_send()
             self.core_copy(steps - 1, i).wait_send()
-            self.chip_copy(steps - 2, i).wait_send()
-        self.chip_copy(steps - 1, 0).wait_send()
+        for which in range(6):
+            self.chip_copy(groups, which).wait_send()
 
     @staticmethod
     def scratch(n_groups, rows, width):
@@ -793,12 +870,12 @@
             pltpu.VMEM((2, 4, rows, width), BF),
             pltpu.VMEM((2, 2, rows, width), BF),
             pltpu.VMEM((2, 2, rows, width), BF),
-            pltpu.VMEM((n_groups, 3, rows, width), BF),
+            pltpu.VMEM((n_groups, 6, rows // 2, width), BF),
             pltpu.VMEM((n_groups - 1, rows, width), BF),
             pltpu.VMEM((n_groups - 1, rows, width), BF),
             dma((2, 2, 2)),
-            dma((2, 2)),
-            dma((n_groups, 3)),
+            dma((6,)),
+            dma((n_groups, 6)),
             dma((2, n_groups - 1)),
             pltpu.SemaphoreType.REGULAR,
         ]
@@ -812,7 +889,7 @@
 
 def step_chips(w, step):
     group = lax.rem(w.g + 1 + step // 2, w.n_groups)
-    return [group * 4 + lax.rem(w.p + d, 4) for d in StreamSum.distances(step)]
+    return [group * 4 + chip for chip in StreamSum.chips(w, step)]
 
 
 def hot_rows(place, rows, core, slot_count):
@@ -1336,8 +1413,6 @@
     grad_rope_in = unrotate(key_grad[:, RANK:], own_rows(cosine), own_rows(sine_part))
     grad_latent = jnp.concatenate([grad_comp_in, grad_rope_in], axis=1).astype(BF)
 
-    latent_grads = swap(5, ("plane_gather", grad_latent))[0]
-
     def per_head(table, cols):
         return table.transpose(1, 0, 2).reshape(rows_w, HEADS, cols)
 
@@ -1346,10 +1421,8 @@
     ).reshape(rows_w, -1).astype(F32)
     grad_expand_weight = g_expand.transpose(1, 0, 2).reshape(kv_n, -1).astype(F32)
 
-    latent_grads = latent_grads.reshape(plane_tok, RANK + ROPE)
-    g_latent = dot_tn(hidden, latent_grads).astype(BF)
+    g_latent = dot_tn(own_rows(hidden), grad_latent).astype(BF)
     g_latent = g_latent.reshape(n_groups, n_plane, rows_w, RANK + ROPE)
-    g_latent = lax.dynamic_index_in_dim(g_latent, place_in, 1, keepdims=False)
     grad_hidden = grad_hidden + dot_nt(grad_latent, latent_weight)
     norm_one_back = jax.vjp(rms_norm, input_float, gain_one)[1]
     grad_x_norm, grad_gain_one = norm_one_back(grad_hidden)
@@ -1365,15 +1438,11 @@
     small_grads = jnp.pad(small_grads, ((0, 0), (0, -small_grads.shape[1] % 1024)))
     grad_latent_weight, grad_output_weight, small_grads = swap(
         6,
-        ("group_sum", g_latent),
-        ("group_sum", g_output),
+        ("whole_sum", g_latent),
+        ("group_sum_home", g_output),
         ("whole_sum", small_grads.reshape(n_groups, n_plane, -1, 128)),
     )
     small_grads = small_grads.reshape(-1)
-    row_pairs = [
-        (g * n_plane + j, n_groups * j + g) for g in range(n_groups) for j in range(n_plane)
-    ]
-    grad_output_weight = lax.ppermute(grad_output_weight, ALL, row_pairs)
     g_shared = g_shared.transpose(2, 0, 1, 3).reshape(rows_w, devices, 2 * shared_n).astype(F32)
     grad_shared_gate = g_shared[:, :, :shared_n].reshape(rows_w, devices * shared_n)
     grad_shared_up = g_shared[:, :, shared_n:].reshape(rows_w, devices * shared_n)

time: 1070 us -> 989 us (0.924)
  waiting for transfers between devices: 119 us -> 83.7 us
  Pallas kernels: 662 us -> 643 us
  matrix products: 85.6 us -> 68.4 us
    ppermute x1 -> x0, waiting for transfers between devices: 30.9 us -> none  [body(): grad_output_weight = lax.ppermute(grad_output_weight, ALL, row_pairs)]
    pallas_call x1, Pallas kernels: 125 us -> 105 us  [experts_sums(): pl.pallas_call(functools.partial(out_kernel, n_groups, slot_count), grid=...]
    pallas_call x7 -> x6, Pallas kernels: 372 us -> 382 us  [exchange(): pl.pallas_call(functools.partial(exchange_kernel, n_groups, n_plane, kind...]
    unnamed x156 -> x180, local copies, waits for them, and re-layouts: 37.3 us -> 39 us
  transfers between devices with their start and end apart: 5 -> 4, of which waited for: 3 -> 2; matrix products, arithmetic and copies ran while one was open for 11% -> 13% of each run, Pallas kernels for 23% -> 33%
where the time goes in v5:
time: 989 us; the launch traced here: 979 us
  Pallas kernels  643 us (65%)
  local copies, waits for them, and re-layouts  112 us (11%)
  waiting for transfers between devices  83.7 us (8%)
  matrix products  68.4 us (7%)
  other arithmetic  46.1 us (5%)
  between operations  15.6 us (2%)
    pallas_call x6, Pallas kernels, exchange(): pl.pallas_call(functools.partial(exchange_kernel, n_groups, n_plane, kind...  382 us
    pallas_call x1, Pallas kernels, experts_sums(): pl.pallas_call(functools.partial(moe_kernel, n_groups, experts, hidden_s,...  123 us
    pallas_call x1, Pallas kernels, experts_sums(): pl.pallas_call(functools.partial(out_kernel, n_groups, slot_count), grid=...  105 us
    all_gather x2, waiting for transfers between devices, gather_all(): return lax.all_gather(x, ALL, axis=0, tiled=True)  68.3 us
    unnamed x180, local copies, waits for them, and re-layouts  39 us
    dot_general x8, matrix products, dot_tn(): lax.dot_general(left, right, (((0,), (0,)), ((), ())), preferred_element_...  35.1 us
    pallas_call x1, Pallas kernels, attend_back(): pl.pallas_call(functools.partial(attend_back_kernel, heads, scale), grid=...  20.6 us
  transfers between devices with their start and end apart: 4, of which 2 were waited for; matrix products, arithmetic and copies ran while one was open for 13% of the time, Pallas kernels for 33%

profile of v5, /device:TPU:1, one launch (start us, length us, event | category | flops | bytes accessed | tf_op | source)
XLA Modules:
  0.0 978.8 jit_solution(740019805973572794)
XLA Ops:
  12.6 2.1 concatenate.60
  16.1 104.8 %exchange_0.1 = (bf16[8,128,2048]{2,1,0:T(8,128)(2,1)}, bf16[4,8,32,128]{3,2,1,0:T(8,128)(2,1)}, bf16[4,8,64,576]{3,2,1,0:T(8,128)(2,1)}, bf16[4,8,64,512]{3,2,1,0:T(8,128)(2,1)}) custom-call(bf16[128,2048]{1,0:T(8,128)(2,1)} %refs_0_.1, bf16[32,128]{1,0:T(8,128)(2,1)} %pad_bitcast_fusion.1.refs_1_, bf16[64,576]{1,0:T(8,128)(2,1)} %refs_2_.1, ...), custom_call_target="tpu_custom_call" | custom-call | tf_op jit(solution)/shard_map/exchange_0/pallas_call | solution.py:695
  122.8 3.2 slice.151
  126.5 3.2 multiply_reduce_fusion
  131.7 3.4 fusion.51
  137.2 3.3 fusion.11
  142.4 54.4 %exchange_1.1 = (bf16[8,128,576]{2,1,0:T(8,128)(2,1)}, bf16[4,64,2048]{2,1,0:T(8,128)(2,1)}) custom-call(bf16[128,576]{1,0:T(8,128)(2,1)} %fusion.29.refs_0_, bf16[64,2048]{1,0:T(8,128)(2,1)} %refs_1_.1), custom_call_target="tpu_custom_call" | custom-call | tf_op jit(solution)/shard_map/exchange_1/pallas_call | solution.py:695
  198.6 2.3 slice.160
  201.1 2.8 copy.208
  204.0 2.1 reshape.465
  206.1 2.3 slice.152
  210.9 3.8 fusion.18
  218.1 4.5 convolution_convert_fusion.2.ex_ref
  224.0 11.4 %attend.1 = (bf16[1024,256]{1,0:T(8,128)(2,1)S(1)}, f32[1024,2]{1,0:T(8,128)S(1)}) custom-call(s32[1024,1]{1,0:T(8,128)S(1)} %copy.215.low_ref, bf16[1024,256]{1,0:T(8,128)(2,1)S(1)} %convolution_convert_fusion.9.qn_ref, bf16[1024,128]{1,0:T(8,128)(2,1)S(1)} %copy.216.qr_ref, bf16[2048,512]{1,0:T(8,128)(2,1)} %convolution_convert_fusion.2.ex_ref, ...), custom_call_target="tpu_custom_call" | custom-call | flops 1677721600 | bytes 4194304 | tf_op jit(solution)/shard_map/attend/pallas_call | solution.py:117
  236.2 3.3 convolution_convert_fusion
  239.5 51.2 %exchange_2.1 = f32[128,2048]{1,0:T(8,128)} custom-call(bf16[8,128,2048]{2,1,0:T(8,128)(2,1)} %bitcast.141), custom_call_target="tpu_custom_call" | custom-call | tf_op jit(solution)/shard_map/exchange_2/pallas_call | solution.py:695
  296.3 3.0 reshape.469
  302.6 3.4 all-to-all-start
  310.2 4.6 copy.220
  314.8 4.6 copy.221
  327.7 5.2 multiply_convert_fusion
  332.8 14.8 %all-to-all-done = bf16[1,64,32,176]{3,1,0,2:T(8,128)(2,1)} async-done(((bf16[1,64,32,176]{3,1,0,2:T(8,128)(2,1)}), bf16[1,64,32,176]{3,1,0,2:T(8,128)(2,1)}, u32[]{:S(2)}, u32[]{:S(2)}) %all-to-all-start) | async-done | bytes 720928 | tf_op jit(solution)/shard_map/all_to_all | solution.py:1257
  349.4 2.2 concatenate.68.sc_ref
  351.6 68.3 %all-gather.3.cloned.1.call-done.h2_hbm = bf16[4096,2048]{1,0:T(8,128)(2,1)} async-done(((bf16[128,2048]{1,0:T(8,128)(2,1)}), bf16[4096,2048]{1,0:T(8,128)(2,1)}) %all-gather.3.cloned.1.call-update) | async-done | bytes 16777232 | tf_op jit(solution)/shard_map/all_gather | solution.py:712
  419.8 123.3 %experts.1 = (f32[128,2048]{1,0:T(8,128)}, bf16[3072,2048]{1,0:T(8,128)(2,1)}, bf16[3072,2048]{1,0:T(8,128)(2,1)}, bf16[3072,704]{1,0:T(8,128)(2,1)}, bf16[3072,...) custom-call(bf16[4096,2048]{1,0:T(8,128)(2,1)} %all-gather.3.cloned., ...), custom_call_target="tpu_custom_call" | custom-call | flops 57713623040 | bytes 100663296 | tf_op jit(solution)/shard_map/experts/pallas_call | solution.py:1105
  543.2 10.9 %convolution_convert_fusion.3 = bf16[2048,256]{0,1:T(8,128)(2,1)S(1)} fusion(bf16[4096,2048]{1,0:T(8,128)(2,1)} %all-gather.3.cloned.1.call-done.h2_hbm, bf16[4096,256]{1,0:T(8,128)(2,1)} %get-tuple-element.72), kind=kOutput, calls=%fused_computation.10 | convolution fusion | flops 4295491584 | bytes 19922944 | tf_op jit(solution)/shard_map/dot_general | solution.py:54
  554.2 6.4 all-to-all-start.1
  562.6 104.9 %expert_out.1 = (f32[128,2048]{1,0:T(8,128)}, f32[2048,704]{1,0:T(8,128)}, f32[2048,704]{1,0:T(8,128)}, f32[704,2048]{1,0:T(8,128)}) custom-call(bf16[3072,704]{1,0:T(8,128)(2,1)} %get-tuple-element.61.act_ref, f32[3072,1]{1,0:T(8,128)} %get-tuple-element.62.rw_ref, bf16[3072,2048]{1,0:T(8,128)(2,1)} %get-tuple-element.63.rows_ref, ...), custom_call_target="tpu_custom_call" | custom-call | flops 39191576576 | bytes 33554432 | tf_op jit(solution)/shard_map/expert_out/pallas_call | solution.py:1138
  667.6 9.9 %fusion.9 = f32[88,2048]{1,0:T(8,128)} fusion(bf16[4096,2048]{1,0:T(8,128)(2,1)} %all-gather.5.cloned.1.call-done.cot_hbm, bf16[4096,128]{1,0:T(8,128)(2,1)} %get-tuple-element.67.sact_ref), kind=kOutput, calls=%fused_computation.42 | convolution fusion | flops 1476395008 | bytes 18546688 | tf_op jit(solution)/shard_map/dot_general | solution.py:54
  678.9 6.4 copy.240
  685.3 6.9 copy.241
  698.4 47.2 %exchange_3.1 = (bf16[8,128,2048]{2,1,0:T(8,128)(2,1)}, bf16[4,8,64,176]{3,2,1,0:T(8,128)(2,1)}) custom-call(bf16[128,2048]{1,0:T(8,128)(2,1)} %fusion.45.refs_0_, bf16[4,8,64,176]{3,2,1,0:T(8,128)(2,1)} %pad_maximum_fusion.5.refs_1_), custom_call_target="tpu_custom_call" | custom-call | tf_op jit(solution)/shard_map/exchange_3/pallas_call | solution.py:695
  745.6 4.4 convolution_convert_fusion.8.gm_ref
  750.1 2.2 convolution_convert_fusion.4
  753.6 20.6 %attend_back.1 = (f32[1024,256]{1,0:T(8,128)}, f32[1024,128]{1,0:T(8,128)}, f32[2048,512]{1,0:T(8,128)}, f32[2048,64]{1,0:T(8,128)}) custom-call(s32[1024,1]{1,0:T(8,128)} %copy-done.2, bf16[1024,256]{1,0:T(8,128)(2,1)} %copy-done.5, bf16[1024,128]{1,0:T(8,128)(2,1)} %copy-done.4, bf16[2048,512]{1,0:T(8,128)(2,1)} %convolution_convert_fusion.2.ex_ref, ...), custom_call_target="tpu_custom_call" | custom-call | flops 4362076160 | bytes 8388608 | tf_op jit(solution)/shard_map/attend_back/pallas_call | solution.py:192
  774.3 2.6 convert_element_type.217
  777.0 2.1 fusion.2
  782.9 4.5 convolution_convert_fusion.6
  789.5 2.3 convolution_convert_fusion.5
  791.9 4.3 fusion
  796.2 61.0 %exchange_4.1 = (f32[128,576]{1,0:T(8,128)}, f32[128,2048]{1,0:T(8,128)}, bf16[8,64,256]{2,1,0:T(8,128)(2,1)}, bf16[8,64,128]{2,1,0:T(8,128)(2,1)}, bf16[8,16,512]{2,1,0:T(8,128)(2,1)}) custom-call(bf16[8,256,576]{2,1,0:T(8,128)(2,1)} %bitcast.144, bf16[8,128,2048]{2,1,0:T(8,128)(2,1)} %bitcast.142, bf16[4,8,64,256]{3,2,1,0:T(8,128)(2,1)} %bitcast.172, ...), custom_call_target="tpu_custom_call" | custom-call | tf_op jit(solution)/shard_map/exchange_4/pallas_call | solution.py:695
  863.5 2.6 fusion.8
  872.1 2.7 copy.232
  874.8 63.8 %exchange_6.1 = (f32[64,576]{1,0:T(8,128)}, f32[64,2048]{1,0:T(8,128)}, f32[16,128]{1,0:T(8,128)}) custom-call(bf16[4,8,64,576]{3,2,1,0:T(8,128)(2,1)} %bitcast.143, bf16[4,64,2048]{2,1,0:T(8,128)(2,1)} %bitcast.174, f32[4,8,16,128]{3,2,1,0:T(8,128)} %copy.253), custom_call_target="tpu_custom_call" | custom-call | tf_op jit(solution)/shard_map/exchange_6/pallas_call | solution.py:695
  946.9 2.8 reshape.489
  958.5 2.5 reshape.496
  961.0 3.4 fusion.4
  965.9 5.9 copy.260
  (293 shorter events, 95.3 us)
Async XLA Ops:
  7.2 344.4 %all-gather.5.cloned.1.call-start = ((), (), s32[]{:S(2)}) async-start(), calls=%async_computation.3 | async-start | bytes 17301504 | tf_op jit(solution)/shard_map/all_gather | solution.py:712
  7.9 411.9 %all-gather.3.cloned.1.call-start = ((), (), s32[]{:S(2)}) async-start(), calls=%async_computation.2 | async-start | bytes 17301504 | tf_op jit(solution)/shard_map/all_gather | solution.py:712
  126.2 14.2 %copy-start.60 = (f32[512]{0:T(512)}, f32[512]{0:T(512)S(1)}, u32[]{:S(2)}) copy-start(f32[512]{0:T(512)S(1)} %reshape.493) | copy-start | bytes 6148
  126.4 201.3 %copy-start.53 = (f32[2048]{0:T(1024)}, f32[2048]{0:T(1024)S(1)}, u32[]{:S(2)}) copy-start(f32[2048]{0:T(1024)S(1)} %reshape.492) | copy-start | bytes 24580
  135.1 188.8 %copy-start.10 = (f32[1024,576]{1,0:T(8,128)}, f32[1024,576]{1,0:T(8,128)S(1)}, u32[]{:S(2)}) copy-start(f32[1024,576]{1,0:T(8,128)S(1)} %fusion.51) | copy-start | bytes 7077892
  200.9 91.3 %copy-start.55 = (f32[2048]{0:T(1024)}, f32[2048]{0:T(1024)S(1)}, u32[]{:S(2)}) copy-start(f32[2048]{0:T(1024)S(1)} %reshape.494) | copy-start | bytes 24580
  201.1 22.8 %copy-start.2 = (s32[1024,1]{1,0:T(8,128)}, s32[1024,1]{1,0:T(8,128)S(1)}, u32[]{:S(2)}) copy-start(s32[1024,1]{1,0:T(8,128)S(1)} %copy.215.low_ref) | copy-start | bytes 12292
  216.7 7.2 copy-start.4
  223.9 15.5 %copy-start.5 = (bf16[1024,256]{1,0:T(8,128)(2,1)}, bf16[1024,256]{1,0:T(8,128)(2,1)S(1)}, u32[]{:S(2)}) copy-start(bf16[1024,256]{1,0:T(8,128)(2,1)S(1)} %convolution_convert_fusion.9.qn_ref) | copy-start | bytes 1572868
  223.9 12.3 %copy-start.43 = (bf16[4,64,2048]{2,1,0:T(8,128)(2,1)S(1)}, bf16[4,64,2048]{2,1,0:T(8,128)(2,1)}, u32[]{:S(2)}) copy-start(bf16[4,64,2048]{2,1,0:T(8,128)(2,1)} %get-tuple-element.59) | copy-start | bytes 3145732
  239.5 51.2 %copy-start.16 = (bf16[128,2048]{1,0:T(8,128)(2,1)S(1)}, bf16[128,2048]{1,0:T(8,128)(2,1)}, u32[]{:S(2)}) copy-start(bf16[128,2048]{1,0:T(8,128)(2,1)} %refs_0_.1) | copy-start | bytes 1572868
  239.5 54.7 %copy-start.50 = (bf16[64,2816]{1,0:T(8,128)(2,1)S(1)}, bf16[64,2816]{1,0:T(8,128)(2,1)}, u32[]{:S(2)}) copy-start(bf16[64,2816]{1,0:T(8,128)(2,1)} %param.27) | copy-start | bytes 1081348
  292.2 10.4 %copy-start.79 = (f32[128]{0:T(128)}, f32[128]{0:T(128)S(1)}, u32[]{:S(2)}) copy-start(f32[128]{0:T(128)S(1)} %get-tuple-element.192) | copy-start | bytes 1540
  292.2 34.3 %copy-start.75 = (f32[128]{0:T(128)}, f32[128]{0:T(128)S(1)}, u32[]{:S(2)}) copy-start(f32[128]{0:T(128)S(1)} %get-tuple-element.210) | copy-start | bytes 1540
  292.2 10.4 %copy-start.64 = (f32[128]{0:T(128)}, f32[128]{0:T(128)S(1)}, u32[]{:S(2)}) copy-start(f32[128]{0:T(128)S(1)} %fusion.37) | copy-start | bytes 1540
  294.2 14.9 %copy-start.20 = (bf16[2048,128]{1,0:T(8,128)(2,1)S(1)}, bf16[2048,128]{1,0:T(8,128)(2,1)}, u32[]{:S(2)}) copy-start(bf16[2048,128]{1,0:T(8,128)(2,1)} %slice.161) | copy-start | bytes 1572868
  302.6 45.0 %all-to-all-start = ((bf16[1,64,32,176]{3,1,0,2:T(8,128)(2,1)}), bf16[1,64,32,176]{3,1,0,2:T(8,128)(2,1)}, u32[]{:S(2)}, u32[]{:S(2)}) async-start(bf16[1,64,32,176]{3,1,0,2:T(8,128)(2,1)} %copy.222), calls=%async_computation | async-start | bytes 2097152 | tf_op jit(solution)/shard_map/all_to_all | solution.py:1257
  314.8 8.3 copy-start.51
  321.0 28.4 %copy-start.13 = (bf16[2048,16]{1,0:T(8,128)(2,1)}, bf16[2048,16]{1,0:T(8,128)(2,1)S(1)}, u32[]{:S(2)}) copy-start(bf16[2048,16]{1,0:T(8,128)(2,1)S(1)} %reshape.470) | copy-start | bytes 196612
  324.0 8.8 copy-start.77
  325.4 7.5 copy-start.58
  325.4 7.5 copy-start.67
  554.2 138.1 %all-to-all-start.1 = ((f32[32,1,128]{2,1,0:T(1,128)}), f32[32,1,128]{2,1,0:T(1,128)}, u32[]{:S(2)}, u32[]{:S(2)}) async-start(f32[32,1,128]{2,1,0:T(1,128)} %bitcast.31), calls=%async_computation.1 | async-start | bytes 32768 | tf_op jit(solution)/shard_map/all_to_all | solution.py:1323
  667.6 9.9 %copy-start.34 = (bf16[2048,88]{1,0:T(8,128)(2,1)S(1)}, bf16[2048,88]{1,0:T(8,128)(2,1)}, u32[]{:S(2)}) copy-start(bf16[2048,88]{1,0:T(8,128)(2,1)} %copy.224) | copy-start | bytes 1081348
  667.6 9.9 %copy-start.35 = (bf16[2048,88]{1,0:T(8,128)(2,1)S(1)}, bf16[2048,88]{1,0:T(8,128)(2,1)}, u32[]{:S(2)}) copy-start(bf16[2048,88]{1,0:T(8,128)(2,1)} %copy.225) | copy-start | bytes 1081348
  685.3 7.8 copy-start.59
  685.3 7.8 copy-start.68
  685.3 7.8 copy-start.69
  685.3 7.9 copy-start.15
  685.3 9.2 copy-start.9
  685.3 9.2 copy-start.14
  685.3 9.2 copy-start.56
  685.3 9.1 copy-start.65
  696.3 49.3 %copy-start.44 = (bf16[4,64,2048]{2,1,0:T(8,128)(2,1)S(1)}, bf16[4,64,2048]{2,1,0:T(8,128)(2,1)}, u32[]{:S(2)}) copy-start(bf16[4,64,2048]{2,1,0:T(8,128)(2,1)} %get-tuple-element.59) | copy-start | bytes 3145732
  696.3 53.8 %copy-start.72 = (f32[128]{0:T(128)}, f32[128]{0:T(128)S(1)}, u32[]{:S(2)}) copy-start(f32[128]{0:T(128)S(1)} %multiply_multiply_fusion.2) | copy-start | bytes 1540
  796.2 62.3 %copy-start.61 = (f32[512]{0:T(512)S(1)}, f32[512]{0:T(512)}, u32[]{:S(2)}) copy-start(f32[512]{0:T(512)} %copy-done.60) | copy-start | bytes 6148
  796.2 62.3 %copy-start.74 = (f32[128]{0:T(128)S(1)}, f32[128]{0:T(128)}, u32[]{:S(2)}) copy-start(f32[128]{0:T(128)} %fusion.38) | copy-start | bytes 1540
  796.2 64.2 %copy-start.78 = (f32[128]{0:T(128)S(1)}, f32[128]{0:T(128)}, u32[]{:S(2)}) copy-start(f32[128]{0:T(128)} %copy-done.77) | copy-start | bytes 1540
  874.8 67.8 %copy-start.39 = (bf16[4,8,64,176]{3,2,1,0:T(8,128)(2,1)S(1)}, bf16[4,8,64,176]{3,2,1,0:T(8,128)(2,1)}, u32[]{:S(2)}) copy-start(bf16[4,8,64,176]{3,2,1,0:T(8,128)(2,1)} %get-tuple-element.86) | copy-start | bytes 2162692
  943.2 8.4 copy-start.76
  943.2 8.4 copy-start.81
  946.9 14.1 %copy-start.12 = (f32[128,2048]{1,0:T(8,128)S(1)}, f32[128,2048]{1,0:T(8,128)}, u32[]{:S(2)}) copy-start(f32[128,2048]{1,0:T(8,128)} %copy-done.11) | copy-start | bytes 3145732
  946.9 14.1 %copy-start.18 = (bf16[128,2048]{1,0:T(8,128)(2,1)S(1)}, bf16[128,2048]{1,0:T(8,128)(2,1)}, u32[]{:S(2)}) copy-start(bf16[128,2048]{1,0:T(8,128)(2,1)} %refs_0_.1) | copy-start | bytes 1572868
  946.9 14.1 %copy-start.22 = (bf16[128,2048]{1,0:T(8,128)(2,1)S(1)}, bf16[128,2048]{1,0:T(8,128)(2,1)}, u32[]{:S(2)}) copy-start(bf16[128,2048]{1,0:T(8,128)(2,1)} %param.35) | copy-start | bytes 1572868
  953.3 7.8 copy-start.66
  953.3 7.8 copy-start.71
  953.3 7.8 copy-start.73
  953.3 7.8 copy-start.82
  (41 other events, 149.7 us)
Sparse Core Ops, SparseCore 0:
  10.8 188.0 all-gather.4
  294.3 125.4 all-gather.2

commit v6 on v5

--- a/solution.py
+++ b/solution.py
@@ -244,6 +244,15 @@
     def partner(self):
         return {"g": self.g, "p": self.p, "c": 1 - self.c}
 
+    def beside(self):
+        return self.p + 1 - 2 * lax.rem(self.p, 2)
+
+    def above(self):
+        return self.p + 2 - 4 * (self.p // 2)
+
+    def core_of(self, p):
+        return p * self.cores + self.c
+
     def plane_peer(self, d):
         return lax.rem(self.j + d, self.n_plane)
 
@@ -342,21 +351,59 @@
         copy.wait_send()
 
 
+def part_of(ref, upper):
+    rows = ref.shape[0] // 2
+    return ref.at[pl.ds(rows, rows)] if upper else ref.at[pl.ds(0, rows)]
+
+
+def spread(w, own, at):
+    beside, above = w.at_chip(w.beside()), w.at_chip(w.above())
+    mine = at(w.j)
+    halves = [(part_of(own, u), part_of(mine, u)) for u in (0, 1)]
+    lower = w.start(*halves[0], beside)
+    upper = w.start(*halves[1], above)
+    rest = [w.start(*halves[1], beside), w.start(*halves[0], above)]
+    on_chip = [w.start(own, mine, w.partner())]
+    yield
+    lower.wait_recv()
+    block = part_of(at(w.core_of(w.beside())), 0)
+    rest.append(w.start(block, block, above))
+    upper.wait_recv()
+    block = part_of(at(w.core_of(w.above())), 1)
+    rest.append(w.start(block, block, beside))
+    yield
+    wait_received(rest)
+    for p in (w.beside(), w.above(), 3 - w.p):
+        block = at(w.core_of(p))
+        on_chip.append(w.start(block, block, w.partner()))
+    yield
+    wait_sent([lower, upper] + rest)
+    wait_all(on_chip)
+
+
 def plane_gather(w, src, out):
-    chips = w.n_plane // w.cores
-    first = [
-        w.start(src, out.at[w.j], w.at_chip(lax.rem(w.p + d, chips))) for d in range(1, chips)
-    ]
-    second = [w.start(src, out.at[w.j], w.partner())]
     out[w.j] = src[...]
-    yield
-    for d in range(1, chips):
-        first[d - 1].wait_recv()
-        at = lax.rem(w.p + chips - d, chips) * w.cores + w.c
-        second.append(w.start(out.at[at], out.at[at], w.partner()))
-    yield
-    wait_sent(first)
-    wait_all(second)
+    yield from spread(w, src, lambda j: out.at[j])
+
+
+def far_gather(w, src, out, sem):
+    mine = out.at[w.g, w.j]
+    away = [w.start(src, mine, w.at_group(w.group_peer(d))) for d in range(1, w.n_groups)]
+    local = pltpu.make_async_copy(src, mine, sem)
+    local.start()
+    running = [spread(w, src, lambda j: out.at[w.g, j])]
+    next(running[0])
+    for d in range(1, w.n_groups):
+        away[d - 1].wait_recv()
+        g = w.group_peer(w.n_groups - d)
+        running.append(spread(w, out.at[g, w.j], lambda j, g=g: out.at[g, j]))
+        next(running[d])
+    for _ in range(3):
+        for routine in running:
+            next(routine, None)
+        yield
+    local.wait()
+    wait_sent(away)
 
 
 def shift_gather(w, src, mid, out):
@@ -367,19 +414,25 @@
 
 
 def whole_gather(w, src, out):
+    chips = w.n_plane // w.cores
     first = [
         w.start(src, out.at[w.g, w.j], w.at_group(w.group_peer(d))) for d in range(1, w.n_groups)
     ]
     out[w.g, w.j] = src[...]
     yield
     wait_received(first)
-    second = [
-        w.start(out.at[:, w.j], out.at[:, w.j], w.at_plane(w.plane_peer(d)))
-        for d in range(1, w.n_plane)
-    ]
+    mine = out.at[:, w.j]
+    second = [w.start(mine, mine, w.at_chip(lax.rem(w.p + d, chips))) for d in range(1, chips)]
+    third = [w.start(mine, mine, w.partner())]
+    yield
+    for d in range(1, chips):
+        second[d - 1].wait_recv()
+        block = out.at[:, w.core_of(lax.rem(w.p + chips - d, chips))]
+        third.append(w.start(block, block, w.partner()))
     yield
     wait_sent(first)
-    wait_all(second)
+    wait_sent(second)
+    wait_all(third)
 
 
 def plane_swap_gather(w, src, out):
@@ -461,42 +514,74 @@
 
 
 def plane_sum(w, src, out, from_core, pairs, from_chips):
+    to = (w.beside(), 3 - w.p, w.above(), w.p)
+    beside, above = w.at_chip(w.beside()), w.at_chip(w.above())
+    first = [
+        w.start(src.at[p * w.cores + 1 - w.c], from_core.at[i], w.partner())
+        for i, p in enumerate(to)
+    ]
+    yield
+    sent = []
+
+    def send(i, upper, slot, device):
+        sent.append(w.start(part_of(pairs.at[i], upper), from_chips.at[slot], device))
+
+    for i, p in enumerate(to):
+        first[i].wait_recv()
+        sum_rows(pairs.at[i], [src.at[w.core_of(p)], from_core.at[i]])
+        if i < 2:
+            send(i, 0, i, beside)
+        if i == 1:
+            send(1, 1, 2, above)
+        if i == 2:
+            send(2, 1, 3, above)
+    yield
+    for wire, i, upper, slot, device in ((1, 2, 0, 4, above), (2, 0, 1, 5, beside)):
+        sent[wire].wait_recv()
+        target = part_of(pairs.at[i], upper)
+        sum_rows(target, [target, from_chips.at[wire]])
+        send(i, upper, slot, device)
+    yield
+    for wire in (0, 3, 4, 5):
+        sent[wire].wait_recv()
+    for upper, arrived in ((0, (0, 4)), (1, (3, 5))):
+        sum_rows(
+            part_of(out, upper),
+            [part_of(pairs.at[3], upper)] + [from_chips.at[slot] for slot in arrived],
+        )
+    wait_sent(first)
+    wait_sent(sent)
+
+
+def whole_sum(w, src, out, from_core, pairs, from_chips, total, parts):
     chips = w.n_plane // w.cores
-    first = []
-    for d in range(chips):
-        p = lax.rem(w.p + d, chips)
-        first.append(w.start(src.at[p * w.cores + 1 - w.c], from_core.at[d], w.partner()))
+    to = [lax.rem(w.p + d, chips) for d in range(chips)]
+    first = [
+        w.start(src.at[:, p * w.cores + 1 - w.c], from_core.at[d], w.partner())
+        for d, p in enumerate(to)
+    ]
     yield
     second = []
     for d in list(range(1, chips)) + [0]:
-        p = lax.rem(w.p + d, chips)
         first[d].wait_recv()
-        sum_rows(pairs.at[d], [src.at[p * w.cores + w.c], from_core.at[d]])
+
+        def step(i, carry):
+            sum_rows(pairs.at[d, i], [src.at[i, w.core_of(to[d])], from_core.at[d, i]])
+            return carry
+
+        lax.fori_loop(0, w.n_groups, step, 0)
         if d:
-            second.append(w.start(pairs.at[d], from_chips.at[d - 1], w.at_chip(p)))
+            second.append(w.start(pairs.at[d], from_chips.at[d - 1], w.at_chip(to[d])))
     yield
     wait_received(second)
-    sum_rows(out, [pairs.at[0]] + [from_chips.at[d] for d in range(chips - 1)])
+
+    def step(i, carry):
+        sum_rows(total.at[i], [pairs.at[0, i]] + [from_chips.at[d, i] for d in range(chips - 1)])
+        return carry
+
+    lax.fori_loop(0, w.n_groups, step, 0)
     wait_sent(first)
     wait_sent(second)
-
-
-def whole_sum(w, src, out, from_plane, total, parts):
-    first = []
-    for d in range(1, w.n_plane):
-        to = w.plane_peer(d)
-        first.append(w.start(src.at[:, to], from_plane.at[d - 1], w.at_plane(to)))
-    yield
-    wait_received(first)
-
-    def step(i, carry):
-        sum_rows(
-            total.at[i], [src.at[i, w.j]] + [from_plane.at[d, i] for d in range(w.n_plane - 1)]
-        )
-        return carry
-
-    lax.fori_loop(0, w.n_groups, step, 0)
-    wait_sent(first)
     yield from group_sum(w, total, out, parts)
 
 
@@ -605,6 +690,7 @@
     "plane_gather": plane_gather,
     "shift_gather": shift_gather,
     "whole_gather": whole_gather,
+    "far_gather": far_gather,
     "plane_swap_gather": plane_swap_gather,
     "plane_swap": plane_swap,
     "plane_sum": plane_sum,
@@ -654,7 +740,7 @@
             out = (n_plane,) + shape
             if kind == "shift_gather":
                 own = [shape]
-        elif kind == "whole_gather":
+        elif kind in ("whole_gather", "far_gather"):
             out = (n_groups, n_plane) + shape
         elif kind == "plane_swap_gather":
             out = (n_groups,) + shape
@@ -665,10 +751,11 @@
         elif kind == "plane_sum_shift":
             pair = shape[1:]
             out = (shape[1] // 2, shape[2])
-            own = [(chips,) + pair, (chips,) + pair, (chips - 1,) + pair, pair, out]
+            half = (pair[0] // 2, pair[1])
+            own = [(chips,) + pair, (chips,) + pair, (6,) + half, pair, out]
         elif kind == "plane_sum":
             out = shape[1:]
-            own = [(chips,) + out, (chips,) + out, (chips - 1,) + out]
+            own = [(chips,) + out, (chips,) + out, (6, out[0] // 2, out[1])]
         elif kind == "group_sum_home":
             out = shape[1:]
             own = [(n_groups - 1,) + out, out, out]
@@ -680,7 +767,9 @@
             own = [shape]
         elif kind == "whole_sum":
             out = shape[2:]
-            own = [(n_plane - 1, n_groups) + out, (n_groups,) + out, (n_groups - 1,) + out]
+            full = (n_groups,) + out
+            own = [(chips,) + full, (chips,) + full, (chips - 1,) + full, full]
+            own = own + [(n_groups - 1,) + out]
         elif kind == "group_sum_swap":
             out = shape[1:]
             own = [out, (n_groups - 1,) + out]
@@ -689,6 +778,9 @@
         else:
             shapes.append(jax.ShapeDtypeStruct(out, dtype))
         scratch += [pltpu.VMEM(s, dtype) for s in own]
+        if kind == "far_gather":
+            own = [None]
+            scratch.append(pltpu.SemaphoreType.DMA)
         extra.append(len(own))
     copies = 64 + 32 * len(items)
     vmem = pl.BlockSpec(memory_space=pltpu.VMEM)
@@ -696,7 +788,9 @@
         functools.partial(exchange_kernel, n_groups, n_plane, kinds, extra),
         out_shape=shapes,
         in_specs=[vmem] * len(items),
-        out_specs=[vmem] * len(items),
+        out_specs=[
+            pl.BlockSpec(memory_space=pl.ANY) if kind == "far_gather" else vmem for kind in kinds
+        ],
         scratch_shapes=scratch
         + [pltpu.SemaphoreType.DMA((copies,)), pltpu.SemaphoreType.DMA((copies,))],
         compiler_params=pltpu.CompilerParams(
@@ -1220,12 +1314,12 @@
         axis=2,
     )
     swap = functools.partial(exchange, n_groups, n_plane)
-    x_plane, small, latent_weight, pair = swap(
+    pair, latent_weight, small, x_plane = swap(
         0,
+        ("plane_swap_gather", pair),
+        ("whole_gather", w_latent),
+        ("whole_gather", small),
         ("plane_gather", layer_input),
-        ("whole_gather", small),
-        ("whole_gather", w_latent),
-        ("plane_swap_gather", pair),
     )
     x_plane = x_plane.reshape(plane_tok, width).astype(F32)
     latent_weight = latent_weight.reshape(width, RANK + ROPE)
@@ -1300,9 +1394,8 @@
     shared_w = (s_both, shared_down)
     slot_limit = 2 * tok * TOP // experts
 
-    def on_rows(h2, cot_gathered, routes_here):
+    def on_rows(h2, h2_all, cot_gathered, routes_here):
         rows = h2.shape[0]
-        h2_all = gather_all(h2)
         slot_count = min(slot_limit, rows)
         member = jnp.any(routes_here == expert_id, axis=2)
         member_int = member.astype(jnp.int32)
@@ -1328,7 +1421,7 @@
     if parts == 1:
         cot_all = gather_all(cotangent_later)
         out_own, grad_h2_own, grad_router_probs, grads = on_rows(
-            h_two, cot_all, routes_all
+            h_two, swap(5, ("far_gather", h_two))[0].reshape(-1, width), cot_all, routes_all
         )
     else:
         rows = tok // parts
@@ -1336,7 +1429,7 @@
         def step(total, inputs):
             h2, cot, routes_here = inputs
             cot_part = gather_all(cot)
-            out, grad_h2, picked, grads = on_rows(h2, cot_part, routes_here)
+            out, grad_h2, picked, grads = on_rows(h2, gather_all(h2), cot_part, routes_here)
             grads = lax.optimization_barrier(grads)
             total = tuple(a + b for a, b in zip(total, grads))
             return total, (out, grad_h2, picked)
@@ -1366,10 +1459,10 @@
     grad_x_one, grad_gain_two = norm_two_back(grad_h_two)
     grad_x_one = grad_x_one + cotangent.astype(F32)
     grad_attn_out = grad_x_one.astype(BF)
-    plane_grad, g_shared = swap(
+    g_shared, plane_grad = swap(
         3,
+        ("whole_swap", g_both.astype(BF).reshape(n_groups, n_plane, rows_w, 2 * shared_n)),
         ("plane_gather", grad_attn_out),
-        ("whole_swap", g_both.astype(BF).reshape(n_groups, n_plane, rows_w, 2 * shared_n)),
     )
     plane_grad = plane_grad.reshape(plane_tok, width)
     grad_mixed = dot_nt(plane_grad, own_output).astype(BF)

time: 989 us -> 1020 us (1.031)
  Pallas kernels: 643 us -> 766 us
  waiting for transfers between devices: 83.7 us -> 0.69 us
    pallas_call x6 -> x7, Pallas kernels: 382 us -> 495 us  [exchange(): pl.pallas_call(functools.partial(exchange_kernel, n_groups, n_plane, kind...]
    all_gather x2 -> x1, waiting for transfers between devices: 68.3 us -> 0.01 us  [gather_all(): return lax.all_gather(x, ALL, axis=0, tiled=True)]
    all_to_all x1, waiting for transfers between devices: 14.8 us -> 0.01 us  [body(): lax.all_to_all(s_both, ALL, split_axis=1, concat_axis=0)]
    pallas_call x1, Pallas kernels: 123 us -> 134 us  [experts_sums(): pl.pallas_call(functools.partial(moe_kernel, n_groups, experts, hidden_s,...]
    unnamed x180 -> x188, local copies, waits for them, and re-layouts: 39 us -> 39.6 us
  transfers between devices with their start and end apart: 4 -> 3, of which waited for: 2 -> 0; matrix products, arithmetic and copies ran while one was open for 13% -> 11% of each run, Pallas kernels for 33% -> 42%
where the time goes in v6:
time: 1020 us; the launch traced here: 1010 us
  Pallas kernels  766 us (75%)
  local copies, waits for them, and re-layouts  105 us (10%)
  matrix products  67.4 us (7%)
  other arithmetic  42.7 us (4%)
  between operations  15.7 us (2%)
  starting transfers between devices  15 us (1%)
    pallas_call x7, Pallas kernels, exchange(): pl.pallas_call(functools.partial(exchange_kernel, n_groups, n_plane, kind...  495 us
    pallas_call x1, Pallas kernels, experts_sums(): pl.pallas_call(functools.partial(moe_kernel, n_groups, experts, hidden_s,...  134 us
    pallas_call x1, Pallas kernels, experts_sums(): pl.pallas_call(functools.partial(out_kernel, n_groups, slot_count), grid=...  105 us
    unnamed x188, local copies, waits for them, and re-layouts  39.6 us
    dot_general x8, matrix products, dot_tn(): lax.dot_general(left, right, (((0,), (0,)), ((), ())), preferred_element_...  35.1 us
    pallas_call x1, Pallas kernels, attend_back(): pl.pallas_call(functools.partial(attend_back_kernel, heads, scale), grid=...  20.6 us
  transfers between devices with their start and end apart: 3, of which 0 were waited for; matrix products, arithmetic and copies ran while one was open for 11% of the time, Pallas kernels for 42%

profile of v6, /device:TPU:1, one launch (start us, length us, event | category | flops | bytes accessed | tf_op | source)
XLA Modules:
  0.0 1012.6 jit_solution(18232748437044441618)
XLA Ops:
  8.0 2.3 reshape.472
  10.3 2.2 reshape.473
  14.5 7.6 all-to-all-start
  24.5 114.0 %exchange_0.1 = (bf16[4,8,64,512]{3,2,1,0:T(8,128)(2,1)}, bf16[4,8,64,576]{3,2,1,0:T(8,128)(2,1)}, bf16[4,8,32,128]{3,2,1,0:T(8,128)(2,1)}, bf16[8,128,2048]{2,1,0:T(8,128)(2,1)}) custom-call(bf16[8,64,512]{2,1,0:T(8,128)(2,1)} %pad_maximum_fusion.6.refs_0_, bf16[64,576]{1,0:T(8,128)(2,1)} %refs_1_.2, bf16[32,128]{1,0:T(8,128)(2,1)} %pad_bitcast_fusion.1.refs_2_, ...), custom_call_target="tpu_custom_call" | custom-call | tf_op jit(solution)/shard_map/exchange_0/pallas_call | solution.py:787
  141.5 2.7 slice.151
  146.8 3.3 multiply_reduce_fusion
  152.0 3.4 fusion.51
  157.5 3.3 fusion.11
  162.8 76.5 %exchange_1.1 = (bf16[8,128,576]{2,1,0:T(8,128)(2,1)}, bf16[4,64,2048]{2,1,0:T(8,128)(2,1)}) custom-call(bf16[128,576]{1,0:T(8,128)(2,1)} %fusion.29.refs_0_, bf16[64,2048]{1,0:T(8,128)(2,1)} %refs_1_.3), custom_call_target="tpu_custom_call" | custom-call | tf_op jit(solution)/shard_map/exchange_1/pallas_call | solution.py:787
  240.9 2.3 slice.160
  243.2 4.6 copy.220
  247.8 4.6 copy.221
  254.2 2.9 copy.208
  257.0 2.3 slice.152
  263.7 3.8 fusion.18
  270.9 4.5 convolution_convert_fusion.2.ex_ref
  276.8 11.4 %attend.1 = (bf16[1024,256]{1,0:T(8,128)(2,1)S(1)}, f32[1024,2]{1,0:T(8,128)S(1)}) custom-call(s32[1024,1]{1,0:T(8,128)S(1)} %copy.215.low_ref, bf16[1024,256]{1,0:T(8,128)(2,1)S(1)} %convolution_convert_fusion.9.qn_ref, bf16[1024,128]{1,0:T(8,128)(2,1)S(1)} %copy.216.qr_ref, bf16[2048,512]{1,0:T(8,128)(2,1)} %convolution_convert_fusion.2.ex_ref, ...), custom_call_target="tpu_custom_call" | custom-call | flops 1677721600 | bytes 4194304 | tf_op jit(solution)/shard_map/attend/pallas_call | solution.py:117
  289.0 3.3 convolution_convert_fusion
  292.3 32.0 %exchange_2.1 = f32[128,2048]{1,0:T(8,128)} custom-call(bf16[8,128,2048]{2,1,0:T(8,128)(2,1)} %bitcast.142), custom_call_target="tpu_custom_call" | custom-call | tf_op jit(solution)/shard_map/exchange_2/pallas_call | solution.py:787
  327.9 91.3 %exchange_5.1 = bf16[4,8,128,2048]{3,2,1,0:T(8,128)(2,1)} custom-call(bf16[128,2048]{1,0:T(8,128)(2,1)} %multiply_convert_fusion.3.refs_0_), custom_call_target="tpu_custom_call" | custom-call | tf_op jit(solution)/shard_map/exchange_5/pallas_call | solution.py:787
  424.4 5.2 multiply_convert_fusion
  431.3 2.2 concatenate.68.sc_ref
  433.5 134.4 %experts.1 = (f32[128,2048]{1,0:T(8,128)}, bf16[3072,2048]{1,0:T(8,128)(2,1)}, bf16[3072,2048]{1,0:T(8,128)(2,1)}, bf16[3072,704]{1,0:T(8,128)(2,1)}, bf16[3072,...) custom-call(bf16[4096,2048]{1,0:T(8,128)(2,1)} %bitcast.144, ...), custom_call_target="tpu_custom_call" | custom-call | flops 57713623040 | bytes 100663296 | tf_op jit(solution)/shard_map/experts/pallas_call | solution.py:1199
  567.9 10.9 %convolution_convert_fusion.3 = bf16[2048,256]{0,1:T(8,128)(2,1)S(1)} fusion(bf16[4096,2048]{1,0:T(8,128)(2,1)} %bitcast.145, bf16[4096,256]{1,0:T(8,128)(2,1)} %get-tuple-element.72), kind=kOutput, calls=%fused_computation.10 | convolution fusion | flops 4295491584 | bytes 19922944 | tf_op jit(solution)/shard_map/dot_general | solution.py:54
  578.9 7.3 all-to-all-start.1
  588.2 104.8 %expert_out.1 = (f32[128,2048]{1,0:T(8,128)}, f32[2048,704]{1,0:T(8,128)}, f32[2048,704]{1,0:T(8,128)}, f32[704,2048]{1,0:T(8,128)}) custom-call(bf16[3072,704]{1,0:T(8,128)(2,1)} %get-tuple-element.61.act_ref, f32[3072,1]{1,0:T(8,128)} %get-tuple-element.62.rw_ref, bf16[3072,2048]{1,0:T(8,128)(2,1)} %get-tuple-element.63.rows_ref, ...), custom_call_target="tpu_custom_call" | custom-call | flops 39191576576 | bytes 33554432 | tf_op jit(solution)/shard_map/expert_out/pallas_call | solution.py:1232
  693.1 9.9 fusion.9
  704.4 6.4 copy.240
  710.8 6.7 copy.241
  723.6 51.0 %exchange_3.1 = (bf16[4,8,64,176]{3,2,1,0:T(8,128)(2,1)}, bf16[8,128,2048]{2,1,0:T(8,128)(2,1)}) custom-call(bf16[4,8,64,176]{3,2,1,0:T(8,128)(2,1)} %pad_maximum_fusion.5.refs_0_, bf16[128,2048]{1,0:T(8,128)(2,1)} %fusion.45.refs_1_), custom_call_target="tpu_custom_call" | custom-call | tf_op jit(solution)/shard_map/exchange_3/pallas_call | solution.py:787
  774.6 4.4 convolution_convert_fusion.8.gm_ref
  779.1 2.2 convolution_convert_fusion.4
  782.6 20.6 %attend_back.1 = (f32[1024,256]{1,0:T(8,128)}, f32[1024,128]{1,0:T(8,128)}, f32[2048,512]{1,0:T(8,128)}, f32[2048,64]{1,0:T(8,128)}) custom-call(s32[1024,1]{1,0:T(8,128)} %copy-done.2, bf16[1024,256]{1,0:T(8,128)(2,1)} %copy-done.5, bf16[1024,128]{1,0:T(8,128)(2,1)} %copy-done.4, bf16[2048,512]{1,0:T(8,128)(2,1)} %convolution_convert_fusion.2.ex_ref, ...), custom_call_target="tpu_custom_call" | custom-call | flops 4362076160 | bytes 8388608 | tf_op jit(solution)/shard_map/attend_back/pallas_call | solution.py:192
  803.3 2.6 convert_element_type.217
  806.1 2.1 fusion.2
  811.9 4.5 convolution_convert_fusion.6
  818.6 2.4 convolution_convert_fusion.5
  820.9 4.3 fusion
  825.3 71.4 %exchange_4.1 = (f32[128,576]{1,0:T(8,128)}, f32[128,2048]{1,0:T(8,128)}, bf16[8,64,256]{2,1,0:T(8,128)(2,1)}, bf16[8,64,128]{2,1,0:T(8,128)(2,1)}, bf16[8,16,512]{2,1,0:T(8,128)(2,1)}) custom-call(bf16[8,256,576]{2,1,0:T(8,128)(2,1)} %bitcast.147, bf16[8,128,2048]{2,1,0:T(8,128)(2,1)} %bitcast.143, bf16[4,8,64,256]{3,2,1,0:T(8,128)(2,1)} %bitcast.175, ...), custom_call_target="tpu_custom_call" | custom-call | tf_op jit(solution)/shard_map/exchange_4/pallas_call | solution.py:787
  898.0 1.9 multiply_reduce_fusion.5
  902.9 2.6 fusion.8
  911.5 2.6 copy.232
  914.1 58.3 %exchange_6.1 = (f32[64,576]{1,0:T(8,128)}, f32[64,2048]{1,0:T(8,128)}, f32[16,128]{1,0:T(8,128)}) custom-call(bf16[4,8,64,576]{3,2,1,0:T(8,128)(2,1)} %bitcast.146, bf16[4,64,2048]{2,1,0:T(8,128)(2,1)} %bitcast.177, f32[4,8,16,128]{3,2,1,0:T(8,128)} %copy.253), custom_call_target="tpu_custom_call" | custom-call | tf_op jit(solution)/shard_map/exchange_6/pallas_call | solution.py:787
  980.6 2.8 reshape.493
  990.1 2.1 maximum_convert_fusion
  992.2 2.5 reshape.500
  994.8 3.4 fusion.4
  999.6 5.9 copy.260
  (299 shorter events, 83.3 us)
Async XLA Ops:
  7.2 15.0 %copy-start.87 = (s32[128]{0:T(128)S(1)}, s32[128]{0:T(128)}, u32[]{:S(2)}) copy-start(s32[128]{0:T(128)} %param.34) | copy-start | bytes 1540
  7.2 15.0 %copy-start.69 = (s32[128,6]{0,1:T(8,128)S(1)}, s32[128,6]{0,1:T(8,128)}, u32[]{:S(2)}) copy-start(s32[128,6]{0,1:T(8,128)} %param.33) | copy-start | bytes 9220
  7.2 15.0 %copy-start.68 = (bf16[64,16]{0,1:T(8,128)(2,1)S(1)}, bf16[64,16]{0,1:T(8,128)(2,1)}, u32[]{:S(2)}) copy-start(bf16[64,16]{0,1:T(8,128)(2,1)} %param.26) | copy-start | bytes 6148
  7.2 426.3 %all-gather.2.cloned.1.call-start = ((), (), s32[]{:S(2)}) async-start(), calls=%async_computation.2 | async-start | bytes 17301504 | tf_op jit(solution)/shard_map/all_gather | solution.py:806
  7.9 14.8 %copy-start.57 = (bf16[16,4096]{1,0:T(8,128)(2,1)S(1)}, bf16[16,4096]{1,0:T(8,128)(2,1)}, u32[]{:S(2)}) copy-start(bf16[16,4096]{1,0:T(8,128)(2,1)} %param.23) | copy-start | bytes 393220
  8.0 14.9 %copy-start.49 = (bf16[64,3072]{1,0:T(8,128)(2,1)S(1)}, bf16[64,3072]{1,0:T(8,128)(2,1)}, u32[]{:S(2)}) copy-start(bf16[64,3072]{1,0:T(8,128)(2,1)} %param.20) | copy-start | bytes 1179652
  10.2 12.7 %copy-start.83 = (bf16[64]{0:T(256)(128)(2,1)S(1)}, bf16[64]{0:T(256)(128)(2,1)}, u32[]{:S(2)}) copy-start(bf16[64]{0:T(256)(128)(2,1)} %param.19) | copy-start | bytes 388
  10.3 12.7 %copy-start.84 = (bf16[64]{0:T(256)(128)(2,1)S(1)}, bf16[64]{0:T(256)(128)(2,1)}, u32[]{:S(2)}) copy-start(bf16[64]{0:T(256)(128)(2,1)} %param.25) | copy-start | bytes 388
  10.3 12.7 %copy-start.85 = (bf16[16]{0:T(256)(128)(2,1)S(1)}, bf16[16]{0:T(256)(128)(2,1)}, u32[]{:S(2)}) copy-start(bf16[16]{0:T(256)(128)(2,1)} %param.22) | copy-start | bytes 100
  14.5 415.0 %all-to-all-start = ((bf16[1,64,32,176]{3,1,0,2:T(8,128)(2,1)}), bf16[1,64,32,176]{3,1,0,2:T(8,128)(2,1)}, u32[]{:S(2)}, u32[]{:S(2)}) async-start(bf16[1,64,32,176]{3,1,0,2:T(8,128)(2,1)} %copy.222), calls=%async_computation | async-start | bytes 2097152 | tf_op jit(solution)/shard_map/all_to_all | solution.py:1351
  146.5 14.2 %copy-start.58 = (f32[512]{0:T(512)}, f32[512]{0:T(512)S(1)}, u32[]{:S(2)}) copy-start(f32[512]{0:T(512)S(1)} %reshape.497) | copy-start | bytes 6148
  146.7 277.7 %copy-start.50 = (f32[2048]{0:T(1024)}, f32[2048]{0:T(1024)S(1)}, u32[]{:S(2)}) copy-start(f32[2048]{0:T(1024)S(1)} %reshape.496) | copy-start | bytes 24580
  155.5 265.6 %copy-start.10 = (f32[1024,576]{1,0:T(8,128)}, f32[1024,576]{1,0:T(8,128)S(1)}, u32[]{:S(2)}) copy-start(f32[1024,576]{1,0:T(8,128)S(1)} %fusion.51) | copy-start | bytes 7077892
  252.5 73.5 %copy-start.52 = (f32[2048]{0:T(1024)}, f32[2048]{0:T(1024)S(1)}, u32[]{:S(2)}) copy-start(f32[2048]{0:T(1024)S(1)} %reshape.498) | copy-start | bytes 24580
  254.2 22.5 %copy-start.2 = (s32[1024,1]{1,0:T(8,128)}, s32[1024,1]{1,0:T(8,128)S(1)}, u32[]{:S(2)}) copy-start(s32[1024,1]{1,0:T(8,128)S(1)} %copy.215.low_ref) | copy-start | bytes 12292
  276.7 15.6 %copy-start.5 = (bf16[1024,256]{1,0:T(8,128)(2,1)}, bf16[1024,256]{1,0:T(8,128)(2,1)S(1)}, u32[]{:S(2)}) copy-start(bf16[1024,256]{1,0:T(8,128)(2,1)S(1)} %convolution_convert_fusion.9.qn_ref) | copy-start | bytes 1572868
  276.8 12.3 %copy-start.43 = (bf16[4,64,2048]{2,1,0:T(8,128)(2,1)S(1)}, bf16[4,64,2048]{2,1,0:T(8,128)(2,1)}, u32[]{:S(2)}) copy-start(bf16[4,64,2048]{2,1,0:T(8,128)(2,1)} %get-tuple-element.59) | copy-start | bytes 3145732
  292.3 32.0 %copy-start.17 = (bf16[128,2048]{1,0:T(8,128)(2,1)S(1)}, bf16[128,2048]{1,0:T(8,128)(2,1)}, u32[]{:S(2)}) copy-start(bf16[128,2048]{1,0:T(8,128)(2,1)} %refs_3_.1) | copy-start | bytes 1572868
  325.9 93.3 %copy-start.79 = (f32[128]{0:T(128)}, f32[128]{0:T(128)S(1)}, u32[]{:S(2)}) copy-start(f32[128]{0:T(128)S(1)} %get-tuple-element.192) | copy-start | bytes 1540
  325.9 97.3 %copy-start.75 = (f32[128]{0:T(128)}, f32[128]{0:T(128)S(1)}, u32[]{:S(2)}) copy-start(f32[128]{0:T(128)S(1)} %get-tuple-element.210) | copy-start | bytes 1540
  325.9 93.3 %copy-start.62 = (f32[128]{0:T(128)}, f32[128]{0:T(128)S(1)}, u32[]{:S(2)}) copy-start(f32[128]{0:T(128)S(1)} %fusion.37) | copy-start | bytes 1540
  327.8 93.3 %copy-start.13 = (bf16[2048,16]{1,0:T(8,128)(2,1)S(1)}, bf16[2048,16]{1,0:T(8,128)(2,1)}, u32[]{:S(2)}) copy-start(bf16[2048,16]{1,0:T(8,128)(2,1)} %reshape.474) | copy-start | bytes 196612
  327.8 93.3 %copy-start.15 = (bf16[128,2048]{1,0:T(8,128)(2,1)S(1)}, bf16[128,2048]{1,0:T(8,128)(2,1)}, u32[]{:S(2)}) copy-start(bf16[128,2048]{1,0:T(8,128)(2,1)} %multiply_convert_fusion.3.refs_0_) | copy-start | bytes 1572868
  421.2 8.4 copy-start.77
  421.5 8.0 copy-start.65
  578.9 138.6 %all-to-all-start.1 = ((f32[32,1,128]{2,1,0:T(1,128)}), f32[32,1,128]{2,1,0:T(1,128)}, u32[]{:S(2)}, u32[]{:S(2)}) async-start(f32[32,1,128]{2,1,0:T(1,128)} %bitcast.32), calls=%async_computation.1 | async-start | bytes 32768 | tf_op jit(solution)/shard_map/all_to_all | solution.py:1416
  693.0 9.9 copy-start.34
  693.1 9.9 copy-start.35
  710.8 7.6 copy-start.16
  710.8 8.9 copy-start.9
  710.8 8.9 copy-start.14
  710.8 8.9 copy-start.53
  710.8 8.9 copy-start.63
  721.5 53.1 %copy-start.44 = (bf16[4,64,2048]{2,1,0:T(8,128)(2,1)S(1)}, bf16[4,64,2048]{2,1,0:T(8,128)(2,1)}, u32[]{:S(2)}) copy-start(bf16[4,64,2048]{2,1,0:T(8,128)(2,1)} %get-tuple-element.59) | copy-start | bytes 3145732
  721.5 57.5 %copy-start.72 = (f32[128]{0:T(128)}, f32[128]{0:T(128)S(1)}, u32[]{:S(2)}) copy-start(f32[128]{0:T(128)S(1)} %multiply_multiply_fusion.2) | copy-start | bytes 1540
  825.2 72.7 %copy-start.59 = (f32[512]{0:T(512)S(1)}, f32[512]{0:T(512)}, u32[]{:S(2)}) copy-start(f32[512]{0:T(512)} %copy-done.58) | copy-start | bytes 6148
  825.2 72.7 %copy-start.74 = (f32[128]{0:T(128)S(1)}, f32[128]{0:T(128)}, u32[]{:S(2)}) copy-start(f32[128]{0:T(128)} %fusion.38) | copy-start | bytes 1540
  825.2 74.6 %copy-start.78 = (f32[128]{0:T(128)S(1)}, f32[128]{0:T(128)}, u32[]{:S(2)}) copy-start(f32[128]{0:T(128)} %copy-done.77) | copy-start | bytes 1540
  914.1 62.3 %copy-start.39 = (bf16[4,8,64,176]{3,2,1,0:T(8,128)(2,1)S(1)}, bf16[4,8,64,176]{3,2,1,0:T(8,128)(2,1)}, u32[]{:S(2)}) copy-start(bf16[4,8,64,176]{3,2,1,0:T(8,128)(2,1)} %get-tuple-element.86) | copy-start | bytes 2162692
  977.0 8.4 copy-start.76
  977.0 8.4 copy-start.81
  980.6 14.1 %copy-start.12 = (f32[128,2048]{1,0:T(8,128)S(1)}, f32[128,2048]{1,0:T(8,128)}, u32[]{:S(2)}) copy-start(f32[128,2048]{1,0:T(8,128)} %copy-done.11) | copy-start | bytes 3145732
  980.6 14.1 %copy-start.19 = (bf16[128,2048]{1,0:T(8,128)(2,1)S(1)}, bf16[128,2048]{1,0:T(8,128)(2,1)}, u32[]{:S(2)}) copy-start(bf16[128,2048]{1,0:T(8,128)(2,1)} %refs_3_.1) | copy-start | bytes 1572868
  980.6 14.1 %copy-start.22 = (bf16[128,2048]{1,0:T(8,128)(2,1)S(1)}, bf16[128,2048]{1,0:T(8,128)(2,1)}, u32[]{:S(2)}) copy-start(bf16[128,2048]{1,0:T(8,128)(2,1)} %param.35) | copy-start | bytes 1572868
  987.0 7.8 copy-start.64
  987.0 7.8 copy-start.71
  987.0 7.8 copy-start.73
  987.0 7.8 copy-start.82
  (44 other events, 170.3 us)
Sparse Core Ops, SparseCore 0:
  10.9 172.5 all-gather.1

commit v7 on v6

--- a/solution.py
+++ b/solution.py
@@ -224,6 +224,11 @@
 MESH = pl.DeviceIdType.MESH
 
 
+def pause(rounds):
+    for _ in range(rounds):
+        yield
+
+
 class Wires:
     def __init__(self, n_groups, n_plane, send, recv):
         self.n_groups, self.n_plane, self.send, self.recv = n_groups, n_plane, send, recv
@@ -447,7 +452,7 @@
         w.start(out.at[w.g], out.at[w.g], w.at_group(w.group_peer(d)))
         for d in range(1, w.n_groups)
     ]
-    yield
+    yield from pause(4)
     wait_sent(first)
     wait_all(second)
 
@@ -477,6 +482,7 @@
             device_id_type=MESH,
         )
 
+    yield from pause(3)
     base = w.used
     w.used += w.n_groups
     for d in range(w.n_groups):
@@ -489,7 +495,7 @@
     def _():
         out[part] = src[...]
 
-    yield
+    yield from pause(2)
     for r in range(w.n_groups):
 
         @pl.when(jnp.logical_not(mine) | (part != r))
@@ -591,7 +597,7 @@
         to = w.group_peer(d)
         first.append(w.start(src.at[to], mid.at[w.g], w.at_group(to)))
     mid[w.g] = src[w.g]
-    yield
+    yield from pause(3)
     wait_received(first)
     second = []
     for d in range(1, w.n_plane):
@@ -608,7 +614,7 @@
     for d in range(1, w.n_groups):
         to = w.group_peer(d)
         copies.append(w.start(src.at[to], parts.at[d - 1], w.at_group(to)))
-    yield
+    yield from pause(3)
     wait_received(copies)
     sum_rows(low, [src.at[w.g]] + [parts.at[d] for d in range(w.n_groups - 1)])
     stays = w.home_source() == w.g * w.n_plane + w.j
@@ -668,7 +674,7 @@
     for d in range(1, w.n_groups):
         to = w.group_peer(d)
         copies.append(w.start(src.at[to], parts.at[d - 1], w.at_group(to)))
-    yield
+    yield from pause(4)
     wait_received(copies)
 
     def step(i, carry):
@@ -1338,7 +1344,7 @@
     wq_nope = query_weight[:, :, :NOPE].reshape(width, local_heads * NOPE)
     wq_rope = query_weight[:, :, NOPE:].reshape(width, local_heads * ROPE)
     expand_weight = pair[:, head_cols:].reshape(RANK, kv_cols)
-    cotangent_later = lax.optimization_barrier((cotangent, x_plane))[0]
+    cotangent_later = jnp.where(x_plane[0, 0] < 1e6, cotangent, jnp.zeros_like(cotangent))
 
     shared_n = shared_down.shape[0]
     s_both = jnp.concatenate(

time: 1020 us -> 958 us (0.939)
  Pallas kernels: 766 us -> 694 us
    pallas_call x7, Pallas kernels: 495 us -> 423 us  [exchange(): pl.pallas_call(functools.partial(exchange_kernel, n_groups, n_plane, kind...]
    unnamed x188 -> x180, local copies, waits for them, and re-layouts: 39.6 us -> 39.3 us
  transfers between devices with their start and end apart: 3 -> 3, of which waited for: 0 -> 0; matrix products, arithmetic and copies ran while one was open for 11% -> 11% of each run, Pallas kernels for 42% -> 33%
where the time goes in v7:
time: 958 us; the launch traced here: 951 us
  Pallas kernels  694 us (72%)
  local copies, waits for them, and re-layouts  106 us (11%)
  matrix products  67.4 us (7%)
  other arithmetic  46 us (5%)
  starting transfers between devices  21.9 us (2%)
  between operations  16.3 us (2%)
    pallas_call x7, Pallas kernels, exchange(): pl.pallas_call(functools.partial(exchange_kernel, n_groups, n_plane, kind...  423 us
    pallas_call x1, Pallas kernels, experts_sums(): pl.pallas_call(functools.partial(moe_kernel, n_groups, experts, hidden_s,...  134 us
    pallas_call x1, Pallas kernels, experts_sums(): pl.pallas_call(functools.partial(out_kernel, n_groups, slot_count), grid=...  105 us
    unnamed x180, local copies, waits for them, and re-layouts  39.3 us
    dot_general x8, matrix products, dot_tn(): lax.dot_general(left, right, (((0,), (0,)), ((), ())), preferred_element_...  35.1 us
    pallas_call x1, Pallas kernels, attend_back(): pl.pallas_call(functools.partial(attend_back_kernel, heads, scale), grid=...  20.6 us
  transfers between devices with their start and end apart: 3, of which 0 were waited for; matrix products, arithmetic and copies ran while one was open for 11% of the time, Pallas kernels for 33%

profile of v7, /device:TPU:1, one launch (start us, length us, event | category | flops | bytes accessed | tf_op | source)
XLA Modules:
  0.0 951.2 jit_solution(7268209621529859287)
XLA Ops:
  9.8 2.1 concatenate.61
  15.4 56.9 %exchange_0.1 = (bf16[4,8,64,512]{3,2,1,0:T(8,128)(2,1)}, bf16[4,8,64,576]{3,2,1,0:T(8,128)(2,1)}, bf16[4,8,32,128]{3,2,1,0:T(8,128)(2,1)}, bf16[8,128,2048]{2,1,0:T(8,128)(2,1)}) custom-call(bf16[8,64,512]{2,1,0:T(8,128)(2,1)} %pad_maximum_fusion.6.refs_0_, bf16[64,576]{1,0:T(8,128)(2,1)} %refs_1_.2, bf16[32,128]{1,0:T(8,128)(2,1)} %pad_bitcast_fusion.1.refs_2_, ...), custom_call_target="tpu_custom_call" | custom-call | tf_op jit(solution)/shard_map/exchange_0/pallas_call | solution.py:793
  74.1 1.9 broadcast_select_fusion
  80.6 14.6 %all-to-all-start = ((bf16[1,64,32,176]{3,1,0,2:T(8,128)(2,1)}), bf16[1,64,32,176]{3,1,0,2:T(8,128)(2,1)}, u32[]{:S(2)}, u32[]{:S(2)}) async-start(bf16[1,64,32,176]{3,1,0,2:T(8,128)(2,1)} %copy.222), calls=%async_computation | async-start | bytes 2097152 | tf_op jit(solution)/shard_map/all_to_all | solution.py:1357
  100.2 3.2 multiply_reduce_fusion
  105.3 3.4 fusion.51
  110.8 3.3 fusion.11
  116.0 56.3 %exchange_1.1 = (bf16[8,128,576]{2,1,0:T(8,128)(2,1)}, bf16[4,64,2048]{2,1,0:T(8,128)(2,1)}) custom-call(bf16[128,576]{1,0:T(8,128)(2,1)} %fusion.29.refs_0_, bf16[64,2048]{1,0:T(8,128)(2,1)} %refs_1_.3), custom_call_target="tpu_custom_call" | custom-call | tf_op jit(solution)/shard_map/exchange_1/pallas_call | solution.py:793
  174.1 2.3 slice.164
  176.4 4.6 copy.220
  180.9 4.6 copy.221
  187.3 2.9 copy.208
  190.2 2.3 slice.156
  192.5 1.9 copy.230
  196.9 3.8 fusion.18
  204.1 4.5 convolution_convert_fusion.2.ex_ref
  209.9 11.4 %attend.1 = (bf16[1024,256]{1,0:T(8,128)(2,1)S(1)}, f32[1024,2]{1,0:T(8,128)S(1)}) custom-call(s32[1024,1]{1,0:T(8,128)S(1)} %copy.215.low_ref, bf16[1024,256]{1,0:T(8,128)(2,1)S(1)} %convolution_convert_fusion.9.qn_ref, bf16[1024,128]{1,0:T(8,128)(2,1)S(1)} %copy.216.qr_ref, bf16[2048,512]{1,0:T(8,128)(2,1)} %convolution_convert_fusion.2.ex_ref, ...), custom_call_target="tpu_custom_call" | custom-call | flops 1677721600 | bytes 4194304 | tf_op jit(solution)/shard_map/attend/pallas_call | solution.py:117
  222.2 3.3 convolution_convert_fusion
  225.5 46.7 %exchange_2.1 = f32[128,2048]{1,0:T(8,128)} custom-call(bf16[8,128,2048]{2,1,0:T(8,128)(2,1)} %bitcast.144), custom_call_target="tpu_custom_call" | custom-call | tf_op jit(solution)/shard_map/exchange_2/pallas_call | solution.py:793
  275.7 91.9 %exchange_5.1 = bf16[4,8,128,2048]{3,2,1,0:T(8,128)(2,1)} custom-call(bf16[128,2048]{1,0:T(8,128)(2,1)} %multiply_convert_fusion.3.refs_0_), custom_call_target="tpu_custom_call" | custom-call | tf_op jit(solution)/shard_map/exchange_5/pallas_call | solution.py:793
  372.7 5.2 multiply_convert_fusion
  379.6 2.2 concatenate.68.sc_ref
  381.9 134.4 %experts.1 = (f32[128,2048]{1,0:T(8,128)}, bf16[3072,2048]{1,0:T(8,128)(2,1)}, bf16[3072,2048]{1,0:T(8,128)(2,1)}, bf16[3072,704]{1,0:T(8,128)(2,1)}, bf16[3072,...) custom-call(bf16[4096,2048]{1,0:T(8,128)(2,1)} %bitcast.146, ...), custom_call_target="tpu_custom_call" | custom-call | flops 57713623040 | bytes 100663296 | tf_op jit(solution)/shard_map/experts/pallas_call | solution.py:1205
  516.2 10.9 %convolution_convert_fusion.3 = bf16[2048,256]{0,1:T(8,128)(2,1)S(1)} fusion(bf16[4096,2048]{1,0:T(8,128)(2,1)} %bitcast.147, bf16[4096,256]{1,0:T(8,128)(2,1)} %get-tuple-element.70), kind=kOutput, calls=%fused_computation.10 | convolution fusion | flops 4295491584 | bytes 19922944 | tf_op jit(solution)/shard_map/dot_general | solution.py:54
  527.2 7.2 all-to-all-start.1
  536.4 104.8 %expert_out.1 = (f32[128,2048]{1,0:T(8,128)}, f32[2048,704]{1,0:T(8,128)}, f32[2048,704]{1,0:T(8,128)}, f32[704,2048]{1,0:T(8,128)}) custom-call(bf16[3072,704]{1,0:T(8,128)(2,1)} %get-tuple-element.59.act_ref, f32[3072,1]{1,0:T(8,128)} %get-tuple-element.60.rw_ref, bf16[3072,2048]{1,0:T(8,128)(2,1)} %get-tuple-element.61.rows_ref, ...), custom_call_target="tpu_custom_call" | custom-call | flops 39191576576 | bytes 33554432 | tf_op jit(solution)/shard_map/expert_out/pallas_call | solution.py:1238
  641.3 9.9 %fusion.9 = f32[88,2048]{1,0:T(8,128)} fusion(bf16[4096,2048]{1,0:T(8,128)(2,1)} %all-gather.2.cloned.1.call-done.cot_hbm, bf16[4096,128]{1,0:T(8,128)(2,1)} %get-tuple-element.65.sact_ref), kind=kOutput, calls=%fused_computation.42 | convolution fusion | flops 1476395008 | bytes 18546688 | tf_op jit(solution)/shard_map/dot_general | solution.py:54
  652.7 6.4 copy.240
  659.1 6.7 copy.241
  671.9 41.8 %exchange_3.1 = (bf16[4,8,64,176]{3,2,1,0:T(8,128)(2,1)}, bf16[8,128,2048]{2,1,0:T(8,128)(2,1)}) custom-call(bf16[4,8,64,176]{3,2,1,0:T(8,128)(2,1)} %pad_maximum_fusion.5.refs_0_, bf16[128,2048]{1,0:T(8,128)(2,1)} %fusion.45.refs_1_), custom_call_target="tpu_custom_call" | custom-call | tf_op jit(solution)/shard_map/exchange_3/pallas_call | solution.py:793
  713.7 4.4 convolution_convert_fusion.8.gm_ref
  718.2 2.3 convolution_convert_fusion.4
  721.7 20.6 %attend_back.1 = (f32[1024,256]{1,0:T(8,128)}, f32[1024,128]{1,0:T(8,128)}, f32[2048,512]{1,0:T(8,128)}, f32[2048,64]{1,0:T(8,128)}) custom-call(s32[1024,1]{1,0:T(8,128)} %copy-done.2, bf16[1024,256]{1,0:T(8,128)(2,1)} %copy-done.5, bf16[1024,128]{1,0:T(8,128)(2,1)} %copy-done.4, bf16[2048,512]{1,0:T(8,128)(2,1)} %convolution_convert_fusion.2.ex_ref, ...), custom_call_target="tpu_custom_call" | custom-call | flops 4362076160 | bytes 8388608 | tf_op jit(solution)/shard_map/attend_back/pallas_call | solution.py:192
  742.4 2.6 convert_element_type.217
  745.2 2.1 fusion.2
  751.0 4.5 convolution_convert_fusion.6
  757.6 2.3 convolution_convert_fusion.5
  760.0 4.3 fusion
  764.3 63.1 %exchange_4.1 = (f32[128,576]{1,0:T(8,128)}, f32[128,2048]{1,0:T(8,128)}, bf16[8,64,256]{2,1,0:T(8,128)(2,1)}, bf16[8,64,128]{2,1,0:T(8,128)(2,1)}, bf16[8,16,512]{2,1,0:T(8,128)(2,1)}) custom-call(bf16[8,256,576]{2,1,0:T(8,128)(2,1)} %bitcast.149, bf16[8,128,2048]{2,1,0:T(8,128)(2,1)} %bitcast.145, bf16[4,8,64,256]{3,2,1,0:T(8,128)(2,1)} %bitcast.177, ...), custom_call_target="tpu_custom_call" | custom-call | tf_op jit(solution)/shard_map/exchange_4/pallas_call | solution.py:793
  828.7 1.9 multiply_reduce_fusion.5
  833.6 2.6 fusion.8
  842.2 2.6 copy.232
  844.8 66.2 %exchange_6.1 = (f32[64,576]{1,0:T(8,128)}, f32[64,2048]{1,0:T(8,128)}, f32[16,128]{1,0:T(8,128)}) custom-call(bf16[4,8,64,576]{3,2,1,0:T(8,128)(2,1)} %bitcast.148, bf16[4,64,2048]{2,1,0:T(8,128)(2,1)} %bitcast.179, f32[4,8,16,128]{3,2,1,0:T(8,128)} %copy.253), custom_call_target="tpu_custom_call" | custom-call | tf_op jit(solution)/shard_map/exchange_6/pallas_call | solution.py:793
  919.2 2.8 reshape.495
  928.7 2.1 maximum_convert_fusion
  930.8 2.5 reshape.502
  933.3 3.4 fusion.4
  938.2 5.9 copy.260
  (293 shorter events, 87.7 us)
Async XLA Ops:
  7.2 68.8 %copy-start.50 = (bf16[64,2816]{1,0:T(8,128)(2,1)S(1)}, bf16[64,2816]{1,0:T(8,128)(2,1)}, u32[]{:S(2)}) copy-start(bf16[64,2816]{1,0:T(8,128)(2,1)} %param.27) | copy-start | bytes 1081348
  7.2 70.1 %copy-start.51 = (bf16[64,2816]{1,0:T(8,128)(2,1)S(1)}, bf16[64,2816]{1,0:T(8,128)(2,1)}, u32[]{:S(2)}) copy-start(bf16[64,2816]{1,0:T(8,128)(2,1)} %param.28) | copy-start | bytes 1081348
  7.2 374.7 %all-gather.2.cloned.1.call-start = ((), (), s32[]{:S(2)}) async-start(), calls=%async_computation.2 | async-start | bytes 17301504 | tf_op jit(solution)/shard_map/all_gather | solution.py:812
  77.3 18.9 %copy-start.34 = (bf16[4,8,64,512]{3,2,1,0:T(8,128)(2,1)S(1)}, bf16[4,8,64,512]{3,2,1,0:T(8,128)(2,1)}, u32[]{:S(2)}) copy-start(bf16[4,8,64,512]{3,2,1,0:T(8,128)(2,1)} %get-tuple-element.54) | copy-start | bytes 6291460
  78.6 16.7 %copy-start.52 = (bf16[4,8,32,128]{3,2,1,0:T(8,128)(2,1)S(1)}, bf16[4,8,32,128]{3,2,1,0:T(8,128)(2,1)}, u32[]{:S(2)}) copy-start(bf16[4,8,32,128]{3,2,1,0:T(8,128)(2,1)} %get-tuple-element.52) | copy-start | bytes 786436
  80.6 297.3 %all-to-all-start = ((bf16[1,64,32,176]{3,1,0,2:T(8,128)(2,1)}), bf16[1,64,32,176]{3,1,0,2:T(8,128)(2,1)}, u32[]{:S(2)}, u32[]{:S(2)}) async-start(bf16[1,64,32,176]{3,1,0,2:T(8,128)(2,1)} %copy.222), calls=%async_computation | async-start | bytes 2097152 | tf_op jit(solution)/shard_map/all_to_all | solution.py:1357
  99.9 14.1 %copy-start.60 = (f32[512]{0:T(512)}, f32[512]{0:T(512)S(1)}, u32[]{:S(2)}) copy-start(f32[512]{0:T(512)S(1)} %reshape.499) | copy-start | bytes 6148
  100.1 272.7 %copy-start.53 = (f32[2048]{0:T(1024)}, f32[2048]{0:T(1024)S(1)}, u32[]{:S(2)}) copy-start(f32[2048]{0:T(1024)S(1)} %reshape.498) | copy-start | bytes 24580
  108.7 260.7 %copy-start.10 = (f32[1024,576]{1,0:T(8,128)}, f32[1024,576]{1,0:T(8,128)S(1)}, u32[]{:S(2)}) copy-start(f32[1024,576]{1,0:T(8,128)S(1)} %fusion.51) | copy-start | bytes 7077892
  185.6 88.1 %copy-start.55 = (f32[2048]{0:T(1024)}, f32[2048]{0:T(1024)S(1)}, u32[]{:S(2)}) copy-start(f32[2048]{0:T(1024)S(1)} %reshape.500) | copy-start | bytes 24580
  187.3 22.5 %copy-start.2 = (s32[1024,1]{1,0:T(8,128)}, s32[1024,1]{1,0:T(8,128)S(1)}, u32[]{:S(2)}) copy-start(s32[1024,1]{1,0:T(8,128)S(1)} %copy.215.low_ref) | copy-start | bytes 12292
  202.6 7.3 copy-start.4
  209.9 15.6 %copy-start.5 = (bf16[1024,256]{1,0:T(8,128)(2,1)}, bf16[1024,256]{1,0:T(8,128)(2,1)S(1)}, u32[]{:S(2)}) copy-start(bf16[1024,256]{1,0:T(8,128)(2,1)S(1)} %convolution_convert_fusion.9.qn_ref) | copy-start | bytes 1572868
  209.9 12.3 %copy-start.44 = (bf16[4,64,2048]{2,1,0:T(8,128)(2,1)S(1)}, bf16[4,64,2048]{2,1,0:T(8,128)(2,1)}, u32[]{:S(2)}) copy-start(bf16[4,64,2048]{2,1,0:T(8,128)(2,1)} %get-tuple-element.58) | copy-start | bytes 3145732
  225.5 46.7 %copy-start.17 = (bf16[128,2048]{1,0:T(8,128)(2,1)S(1)}, bf16[128,2048]{1,0:T(8,128)(2,1)}, u32[]{:S(2)}) copy-start(bf16[128,2048]{1,0:T(8,128)(2,1)} %refs_3_.1) | copy-start | bytes 1572868
  273.7 93.9 %copy-start.79 = (f32[128]{0:T(128)}, f32[128]{0:T(128)S(1)}, u32[]{:S(2)}) copy-start(f32[128]{0:T(128)S(1)} %get-tuple-element.190) | copy-start | bytes 1540
  273.7 97.9 %copy-start.75 = (f32[128]{0:T(128)}, f32[128]{0:T(128)S(1)}, u32[]{:S(2)}) copy-start(f32[128]{0:T(128)S(1)} %get-tuple-element.208) | copy-start | bytes 1540
  273.7 93.8 %copy-start.64 = (f32[128]{0:T(128)}, f32[128]{0:T(128)S(1)}, u32[]{:S(2)}) copy-start(f32[128]{0:T(128)S(1)} %fusion.37) | copy-start | bytes 1540
  275.7 93.8 %copy-start.13 = (bf16[2048,16]{1,0:T(8,128)(2,1)S(1)}, bf16[2048,16]{1,0:T(8,128)(2,1)}, u32[]{:S(2)}) copy-start(bf16[2048,16]{1,0:T(8,128)(2,1)} %reshape.476) | copy-start | bytes 196612
  275.7 93.8 %copy-start.15 = (bf16[128,2048]{1,0:T(8,128)(2,1)S(1)}, bf16[128,2048]{1,0:T(8,128)(2,1)}, u32[]{:S(2)}) copy-start(bf16[128,2048]{1,0:T(8,128)(2,1)} %multiply_convert_fusion.3.refs_0_) | copy-start | bytes 1572868
  369.5 8.4 copy-start.77
  369.8 8.1 copy-start.67
  527.2 138.6 %all-to-all-start.1 = ((f32[32,1,128]{2,1,0:T(1,128)}), f32[32,1,128]{2,1,0:T(1,128)}, u32[]{:S(2)}, u32[]{:S(2)}) async-start(f32[32,1,128]{2,1,0:T(1,128)} %bitcast.33), calls=%async_computation.1 | async-start | bytes 32768 | tf_op jit(solution)/shard_map/all_to_all | solution.py:1422
  641.3 9.9 %copy-start.35 = (bf16[2048,88]{1,0:T(8,128)(2,1)S(1)}, bf16[2048,88]{1,0:T(8,128)(2,1)}, u32[]{:S(2)}) copy-start(bf16[2048,88]{1,0:T(8,128)(2,1)} %copy.224) | copy-start | bytes 1081348
  641.3 9.9 %copy-start.36 = (bf16[2048,88]{1,0:T(8,128)(2,1)S(1)}, bf16[2048,88]{1,0:T(8,128)(2,1)}, u32[]{:S(2)}) copy-start(bf16[2048,88]{1,0:T(8,128)(2,1)} %copy.225) | copy-start | bytes 1081348
  659.0 7.6 copy-start.59
  659.0 7.6 copy-start.68
  659.0 7.6 copy-start.69
  659.0 7.6 copy-start.16
  659.1 8.9 copy-start.9
  659.1 8.9 copy-start.14
  659.1 8.9 copy-start.56
  659.1 8.9 copy-start.65
  669.8 43.9 %copy-start.45 = (bf16[4,64,2048]{2,1,0:T(8,128)(2,1)S(1)}, bf16[4,64,2048]{2,1,0:T(8,128)(2,1)}, u32[]{:S(2)}) copy-start(bf16[4,64,2048]{2,1,0:T(8,128)(2,1)} %get-tuple-element.58) | copy-start | bytes 3145732
  669.8 48.3 %copy-start.72 = (f32[128]{0:T(128)}, f32[128]{0:T(128)S(1)}, u32[]{:S(2)}) copy-start(f32[128]{0:T(128)S(1)} %multiply_multiply_fusion.2) | copy-start | bytes 1540
  764.3 64.3 %copy-start.61 = (f32[512]{0:T(512)S(1)}, f32[512]{0:T(512)}, u32[]{:S(2)}) copy-start(f32[512]{0:T(512)} %copy-done.60) | copy-start | bytes 6148
  764.3 64.3 %copy-start.74 = (f32[128]{0:T(128)S(1)}, f32[128]{0:T(128)}, u32[]{:S(2)}) copy-start(f32[128]{0:T(128)} %fusion.38) | copy-start | bytes 1540
  764.3 66.2 %copy-start.78 = (f32[128]{0:T(128)S(1)}, f32[128]{0:T(128)}, u32[]{:S(2)}) copy-start(f32[128]{0:T(128)} %copy-done.77) | copy-start | bytes 1540
  844.8 70.1 %copy-start.40 = (bf16[4,8,64,176]{3,2,1,0:T(8,128)(2,1)S(1)}, bf16[4,8,64,176]{3,2,1,0:T(8,128)(2,1)}, u32[]{:S(2)}) copy-start(bf16[4,8,64,176]{3,2,1,0:T(8,128)(2,1)} %get-tuple-element.84) | copy-start | bytes 2162692
  915.5 8.4 copy-start.76
  915.5 8.4 copy-start.81
  919.2 14.1 %copy-start.12 = (f32[128,2048]{1,0:T(8,128)S(1)}, f32[128,2048]{1,0:T(8,128)}, u32[]{:S(2)}) copy-start(f32[128,2048]{1,0:T(8,128)} %copy-done.11) | copy-start | bytes 3145732
  919.2 14.1 %copy-start.19 = (bf16[128,2048]{1,0:T(8,128)(2,1)S(1)}, bf16[128,2048]{1,0:T(8,128)(2,1)}, u32[]{:S(2)}) copy-start(bf16[128,2048]{1,0:T(8,128)(2,1)} %refs_3_.1) | copy-start | bytes 1572868
  919.2 14.1 %copy-start.22 = (bf16[128,2048]{1,0:T(8,128)(2,1)S(1)}, bf16[128,2048]{1,0:T(8,128)(2,1)}, u32[]{:S(2)}) copy-start(bf16[128,2048]{1,0:T(8,128)(2,1)} %param.35) | copy-start | bytes 1572868
  925.6 7.8 copy-start.66
  925.6 7.8 copy-start.71
  925.6 7.8 copy-start.73
  925.6 7.8 copy-start.82
  (40 other events, 140.2 us)
Sparse Core Ops, SparseCore 0:
  76.1 161.5 all-gather.1

commit v8 on v7

--- a/solution.py
+++ b/solution.py
@@ -332,10 +332,13 @@
 
     def step(i, carry):
         at = pl.ds(pl.multiple_of(i * tile, tile), tile)
-        total = sources[0][at, :].astype(F32)
-        for source in sources[1:]:
-            total = total + source[at, :].astype(F32)
-        dst[at, :] = total.astype(dst.dtype)
+        if len(sources) == 2 and all(r.dtype == BF for r in [dst] + sources):
+            dst[at, :] = sources[0][at, :] + sources[1][at, :]
+        else:
+            total = sources[0][at, :].astype(F32)
+            for source in sources[1:]:
+                total = total + source[at, :].astype(F32)
+            dst[at, :] = total.astype(dst.dtype)
         return carry
 
     lax.fori_loop(0, rows // tile, step, 0)
@@ -1073,15 +1076,17 @@
     picked_cot = gin_ref[...]
     back = dot_nt(picked_cot, wd_ref[...])
     gin_ref[...] = (picked_cot.astype(F32) * row_weight).astype(BF)
-    gate = jnp.dot(expert_rows, wg_ref[...], preferred_element_type=F32)
-    up = jnp.dot(expert_rows, wu_ref[...], preferred_element_type=F32)
+    gate = dot_nt(expert_rows, wg_ref[...])
+    up = dot_nt(expert_rows, wu_ref[...])
     act, grad_gate, grad_up = swiglu_both(gate, up, back * row_weight)
     act_low, grad_gate, grad_up = act.astype(BF), grad_gate.astype(BF), grad_up.astype(BF)
     act_ref[...] = act_low
     gg_ref[...] = grad_gate
     gu_ref[...] = grad_up
     picked = jnp.sum(act_low.astype(F32) * back, axis=1, keepdims=True)
-    grad_rows = (dot_nt(grad_gate, wg_ref[...]) + dot_nt(grad_up, wu_ref[...])).astype(BF)
+    grad_rows = jnp.dot(grad_gate, wg_ref[...], preferred_element_type=F32)
+    grad_rows = grad_rows + jnp.dot(grad_up, wu_ref[...], preferred_element_type=F32)
+    grad_rows = grad_rows.astype(BF)
     stream.open_stage(step)
     for q in range(4):
         tokens = slice(q * rows, (q + 1) * rows)
@@ -1137,15 +1142,17 @@
 
     width = rows_ref.shape[1]
     piece = width // 4
-    for k in range(4):
-        cols = slice(k * piece, (k + 1) * piece)
-        turned = rows_ref[:, cols].T
-        dg_ref[cols, :] += jnp.dot(turned, gg_ref[...], preferred_element_type=F32)
-        du_ref[cols, :] += jnp.dot(turned, gu_ref[...], preferred_element_type=F32)
-    turned = act_ref[...].T
-    for k in range(4):
-        cols = slice(k * piece, (k + 1) * piece)
-        dd_ref[:, cols] += jnp.dot(turned, gin_ref[:, cols], preferred_element_type=F32)
+    for left_ref, right_ref, total_ref in (
+        (gg_ref, rows_ref, dg_ref),
+        (gu_ref, rows_ref, du_ref),
+        (act_ref, gin_ref, dd_ref),
+    ):
+        turned = left_ref[...].T
+        for k in range(4):
+            cols = slice(k * piece, (k + 1) * piece)
+            total_ref[:, cols] += jnp.dot(
+                turned, right_ref[:, cols], preferred_element_type=F32
+            )
 
     @pl.when(step == steps - 1)
     def _():
@@ -1396,7 +1403,7 @@
     h_two = h_two_f.astype(BF)
     router_probs = softmax_rows(matmul(h_two, router_weight))
 
-    expert_w = (expert_gate[0], expert_up[0], expert_down[0])
+    expert_w = (expert_gate[0].T, expert_up[0].T, expert_down[0])
     shared_w = (s_both, shared_down)
     slot_limit = 2 * tok * TOP // experts
 
@@ -1559,8 +1566,8 @@
         grad_shared_gate,
         grad_shared_up,
         g_sdown,
-        g_gate[None],
-        g_up[None],
+        g_gate.T[None],
+        g_up.T[None],
         g_down[None],
     )
 

time: 958 us -> 943 us (0.984)
  local copies, waits for them, and re-layouts: 106 us -> 92.7 us
    unnamed x180 -> x182, local copies, waits for them, and re-layouts: 39.3 us -> 25.8 us
  transfers between devices with their start and end apart: 3 -> 3, of which waited for: 0 -> 0; matrix products, arithmetic and copies ran while one was open for 11% -> 9% of each run, Pallas kernels for 33% -> 33%
where the time goes in v8:
time: 943 us; the launch traced here: 934 us
  Pallas kernels  690 us (73%)
  local copies, waits for them, and re-layouts  92.7 us (10%)
  matrix products  67.6 us (7%)
  other arithmetic  45.8 us (5%)
  starting transfers between devices  21.9 us (2%)
  between operations  16.3 us (2%)
    pallas_call x7, Pallas kernels, exchange(): pl.pallas_call(functools.partial(exchange_kernel, n_groups, n_plane, kind...  422 us
    pallas_call x1, Pallas kernels, experts_sums(): pl.pallas_call(functools.partial(moe_kernel, n_groups, experts, hidden_s,...  133 us
    pallas_call x1, Pallas kernels, experts_sums(): pl.pallas_call(functools.partial(out_kernel, n_groups, slot_count), grid=...  103 us
    dot_general x8, matrix products, dot_tn(): lax.dot_general(left, right, (((0,), (0,)), ((), ())), preferred_element_...  35.2 us
    unnamed x182, local copies, waits for them, and re-layouts  25.8 us
    pallas_call x1, Pallas kernels, attend_back(): pl.pallas_call(functools.partial(attend_back_kernel, heads, scale), grid=...  20.7 us
  transfers between devices with their start and end apart: 3, of which 0 were waited for; matrix products, arithmetic and copies ran while one was open for 9% of the time, Pallas kernels for 33%

profile of v8, /device:TPU:1, one launch (start us, length us, event | category | flops | bytes accessed | tf_op | source)
XLA Modules:
  0.0 934.4 jit_solution(12386910966851876733)
XLA Ops:
  9.8 2.1 concatenate.61
  15.4 56.9 %exchange_0.1 = (bf16[4,8,64,512]{3,2,1,0:T(8,128)(2,1)}, bf16[4,8,64,576]{3,2,1,0:T(8,128)(2,1)}, bf16[4,8,32,128]{3,2,1,0:T(8,128)(2,1)}, bf16[8,128,2048]{2,1,0:T(8,128)(2,1)}) custom-call(bf16[8,64,512]{2,1,0:T(8,128)(2,1)} %pad_maximum_fusion.6.refs_0_, bf16[64,576]{1,0:T(8,128)(2,1)} %refs_1_.2, bf16[32,128]{1,0:T(8,128)(2,1)} %pad_bitcast_fusion.1.refs_2_, ...), custom_call_target="tpu_custom_call" | custom-call | tf_op jit(solution)/shard_map/exchange_0/pallas_call | solution.py:796
  74.2 1.9 broadcast_select_fusion
  80.7 14.5 %all-to-all-start = ((bf16[1,64,32,176]{3,1,0,2:T(8,128)(2,1)}), bf16[1,64,32,176]{3,1,0,2:T(8,128)(2,1)}, u32[]{:S(2)}, u32[]{:S(2)}) async-start(bf16[1,64,32,176]{3,1,0,2:T(8,128)(2,1)} %copy.200), calls=%async_computation | async-start | bytes 2097152 | tf_op jit(solution)/shard_map/all_to_all | solution.py:1364
  100.1 3.2 multiply_reduce_fusion
  105.2 3.4 fusion.51
  110.7 3.3 fusion.11
  116.0 56.9 %exchange_1.1 = (bf16[8,128,576]{2,1,0:T(8,128)(2,1)}, bf16[4,64,2048]{2,1,0:T(8,128)(2,1)}) custom-call(bf16[128,576]{1,0:T(8,128)(2,1)} %fusion.29.refs_0_, bf16[64,2048]{1,0:T(8,128)(2,1)} %refs_1_.3), custom_call_target="tpu_custom_call" | custom-call | tf_op jit(solution)/shard_map/exchange_1/pallas_call | solution.py:796
  174.6 2.3 slice.164
  178.6 3.0 copy.188
  181.7 2.3 slice.156
  184.0 2.0 copy.208
  188.6 3.9 fusion.18
  195.9 4.5 convolution_convert_fusion.2.ex_ref
  201.8 11.5 %attend.1 = (bf16[1024,256]{1,0:T(8,128)(2,1)S(1)}, f32[1024,2]{1,0:T(8,128)S(1)}) custom-call(s32[1024,1]{1,0:T(8,128)S(1)} %copy.195.low_ref, bf16[1024,256]{1,0:T(8,128)(2,1)S(1)} %convolution_convert_fusion.9.qn_ref, bf16[1024,128]{1,0:T(8,128)(2,1)S(1)} %copy.196.qr_ref, bf16[2048,512]{1,0:T(8,128)(2,1)} %convolution_convert_fusion.2.ex_ref, ...), custom_call_target="tpu_custom_call" | custom-call | flops 1677721600 | bytes 4194304 | tf_op jit(solution)/shard_map/attend/pallas_call | solution.py:117
  214.1 3.3 convolution_convert_fusion
  217.4 45.9 %exchange_2.1 = f32[128,2048]{1,0:T(8,128)} custom-call(bf16[8,128,2048]{2,1,0:T(8,128)(2,1)} %bitcast.152), custom_call_target="tpu_custom_call" | custom-call | tf_op jit(solution)/shard_map/exchange_2/pallas_call | solution.py:796
  266.8 91.9 %exchange_5.1 = bf16[4,8,128,2048]{3,2,1,0:T(8,128)(2,1)} custom-call(bf16[128,2048]{1,0:T(8,128)(2,1)} %multiply_convert_fusion.3.refs_0_), custom_call_target="tpu_custom_call" | custom-call | tf_op jit(solution)/shard_map/exchange_5/pallas_call | solution.py:796
  358.6 1.8 pad.13.sd_ref
  363.7 5.2 multiply_convert_fusion
  370.7 2.2 concatenate.68.sc_ref
  372.9 132.6 %experts.1 = (f32[128,2048]{1,0:T(8,128)}, bf16[3072,2048]{1,0:T(8,128)(2,1)}, bf16[3072,2048]{1,0:T(8,128)(2,1)}, bf16[3072,704]{1,0:T(8,128)(2,1)}, bf16[3072,...) custom-call(bf16[4096,2048]{1,0:T(8,128)(2,1)} %bitcast.154, ...), custom_call_target="tpu_custom_call" | custom-call | flops 57713623040 | bytes 100663296 | tf_op jit(solution)/shard_map/experts/pallas_call | solution.py:1212
  505.6 10.9 %convolution_convert_fusion.3 = bf16[2048,256]{0,1:T(8,128)(2,1)S(1)} fusion(bf16[4096,2048]{1,0:T(8,128)(2,1)} %bitcast.155, bf16[4096,256]{1,0:T(8,128)(2,1)} %get-tuple-element.70), kind=kOutput, calls=%fused_computation.10 | convolution fusion | flops 4295491584 | bytes 19922944 | tf_op jit(solution)/shard_map/dot_general | solution.py:54
  516.5 7.3 all-to-all-start.1
  525.9 103.0 %expert_out.1 = (f32[128,2048]{1,0:T(8,128)}, f32[704,2048]{1,0:T(8,128)}, f32[704,2048]{1,0:T(8,128)}, f32[704,2048]{1,0:T(8,128)}) custom-call(bf16[3072,704]{1,0:T(8,128)(2,1)} %get-tuple-element.59.act_ref, f32[3072,1]{1,0:T(8,128)} %get-tuple-element.60.rw_ref, bf16[3072,2048]{1,0:T(8,128)(2,1)} %get-tuple-element.61.rows_ref, ...), custom_call_target="tpu_custom_call" | custom-call | flops 39191576576 | bytes 33554432 | tf_op jit(solution)/shard_map/expert_out/pallas_call | solution.py:1245
  629.0 9.9 %fusion.9 = f32[88,2048]{1,0:T(8,128)} fusion(bf16[4096,2048]{1,0:T(8,128)(2,1)} %all-gather.2.cloned.1.call-done.cot_hbm, bf16[4096,128]{1,0:T(8,128)(2,1)} %get-tuple-element.65.sact_ref), kind=kOutput, calls=%fused_computation.42 | convolution fusion | flops 1476395008 | bytes 18546688 | tf_op jit(solution)/shard_map/dot_general | solution.py:54
  646.5 42.1 %exchange_3.1 = (bf16[4,8,64,176]{3,2,1,0:T(8,128)(2,1)}, bf16[8,128,2048]{2,1,0:T(8,128)(2,1)}) custom-call(bf16[4,8,64,176]{3,2,1,0:T(8,128)(2,1)} %pad_maximum_fusion.5.refs_0_, bf16[128,2048]{1,0:T(8,128)(2,1)} %fusion.45.refs_1_), custom_call_target="tpu_custom_call" | custom-call | tf_op jit(solution)/shard_map/exchange_3/pallas_call | solution.py:796
  688.6 4.4 convolution_convert_fusion.8.gm_ref
  693.1 2.3 convolution_convert_fusion.4
  696.7 20.7 %attend_back.1 = (f32[1024,256]{1,0:T(8,128)}, f32[1024,128]{1,0:T(8,128)}, f32[2048,512]{1,0:T(8,128)}, f32[2048,64]{1,0:T(8,128)}) custom-call(s32[1024,1]{1,0:T(8,128)} %copy-done.2, bf16[1024,256]{1,0:T(8,128)(2,1)} %copy-done.5, bf16[1024,128]{1,0:T(8,128)(2,1)} %copy-done.4, bf16[2048,512]{1,0:T(8,128)(2,1)} %convolution_convert_fusion.2.ex_ref, ...), custom_call_target="tpu_custom_call" | custom-call | flops 4362076160 | bytes 8388608 | tf_op jit(solution)/shard_map/attend_back/pallas_call | solution.py:192
  717.4 2.6 convert_element_type.217
  720.2 2.1 fusion.2
  726.0 4.5 convolution_convert_fusion.6
  732.7 2.4 convolution_convert_fusion.5
  735.0 4.3 fusion
  739.4 62.5 %exchange_4.1 = (f32[128,576]{1,0:T(8,128)}, f32[128,2048]{1,0:T(8,128)}, bf16[8,64,256]{2,1,0:T(8,128)(2,1)}, bf16[8,64,128]{2,1,0:T(8,128)(2,1)}, bf16[8,16,512]{2,1,0:T(8,128)(2,1)}) custom-call(bf16[8,256,576]{2,1,0:T(8,128)(2,1)} %bitcast.157, bf16[8,128,2048]{2,1,0:T(8,128)(2,1)} %bitcast.153, bf16[4,8,64,256]{3,2,1,0:T(8,128)(2,1)} %bitcast.185, ...), custom_call_target="tpu_custom_call" | custom-call | tf_op jit(solution)/shard_map/exchange_4/pallas_call | solution.py:796
  803.1 1.9 multiply_reduce_fusion.5
  806.2 1.9 convolution_convert_fusion.1
  808.1 2.6 fusion.8
  816.7 2.7 copy.210
  819.4 66.1 %exchange_6.1 = (f32[64,576]{1,0:T(8,128)}, f32[64,2048]{1,0:T(8,128)}, f32[16,128]{1,0:T(8,128)}) custom-call(bf16[4,8,64,576]{3,2,1,0:T(8,128)(2,1)} %bitcast.156, bf16[4,64,2048]{2,1,0:T(8,128)(2,1)} %bitcast.187, f32[4,8,16,128]{3,2,1,0:T(8,128)} %copy.229), custom_call_target="tpu_custom_call" | custom-call | tf_op jit(solution)/shard_map/exchange_6/pallas_call | solution.py:796
  893.8 2.8 reshape.495
  903.3 2.1 maximum_convert_fusion
  905.3 2.5 reshape.502
  907.9 3.4 fusion.4
  912.8 6.0 copy.238
  918.8 6.0 copy.239
  924.8 2.5 copy.240
  (296 shorter events, 83.9 us)
Async XLA Ops:
  7.2 68.9 %copy-start.50 = (bf16[64,2816]{1,0:T(8,128)(2,1)S(1)}, bf16[64,2816]{1,0:T(8,128)(2,1)}, u32[]{:S(2)}) copy-start(bf16[64,2816]{1,0:T(8,128)(2,1)} %param.27) | copy-start | bytes 1081348
  7.2 70.1 %copy-start.51 = (bf16[64,2816]{1,0:T(8,128)(2,1)S(1)}, bf16[64,2816]{1,0:T(8,128)(2,1)}, u32[]{:S(2)}) copy-start(bf16[64,2816]{1,0:T(8,128)(2,1)} %param.28) | copy-start | bytes 1081348
  7.2 365.7 %all-gather.2.cloned.1.call-start = ((), (), s32[]{:S(2)}) async-start(), calls=%async_computation.2 | async-start | bytes 17301504 | tf_op jit(solution)/shard_map/all_gather | solution.py:815
  77.3 18.8 %copy-start.34 = (bf16[4,8,64,512]{3,2,1,0:T(8,128)(2,1)S(1)}, bf16[4,8,64,512]{3,2,1,0:T(8,128)(2,1)}, u32[]{:S(2)}) copy-start(bf16[4,8,64,512]{3,2,1,0:T(8,128)(2,1)} %get-tuple-element.54) | copy-start | bytes 6291460
  78.6 16.6 %copy-start.52 = (bf16[4,8,32,128]{3,2,1,0:T(8,128)(2,1)S(1)}, bf16[4,8,32,128]{3,2,1,0:T(8,128)(2,1)}, u32[]{:S(2)}) copy-start(bf16[4,8,32,128]{3,2,1,0:T(8,128)(2,1)} %get-tuple-element.52) | copy-start | bytes 786436
  80.7 288.3 %all-to-all-start = ((bf16[1,64,32,176]{3,1,0,2:T(8,128)(2,1)}), bf16[1,64,32,176]{3,1,0,2:T(8,128)(2,1)}, u32[]{:S(2)}, u32[]{:S(2)}) async-start(bf16[1,64,32,176]{3,1,0,2:T(8,128)(2,1)} %copy.200), calls=%async_computation | async-start | bytes 2097152 | tf_op jit(solution)/shard_map/all_to_all | solution.py:1364
  99.9 14.1 %copy-start.60 = (f32[512]{0:T(512)}, f32[512]{0:T(512)S(1)}, u32[]{:S(2)}) copy-start(f32[512]{0:T(512)S(1)} %reshape.499) | copy-start | bytes 6148
  100.0 263.7 %copy-start.53 = (f32[2048]{0:T(1024)}, f32[2048]{0:T(1024)S(1)}, u32[]{:S(2)}) copy-start(f32[2048]{0:T(1024)S(1)} %reshape.498) | copy-start | bytes 24580
  108.7 251.8 %copy-start.10 = (f32[1024,576]{1,0:T(8,128)}, f32[1024,576]{1,0:T(8,128)S(1)}, u32[]{:S(2)}) copy-start(f32[1024,576]{1,0:T(8,128)S(1)} %fusion.51) | copy-start | bytes 7077892
  176.9 87.9 %copy-start.55 = (f32[2048]{0:T(1024)}, f32[2048]{0:T(1024)S(1)}, u32[]{:S(2)}) copy-start(f32[2048]{0:T(1024)S(1)} %reshape.500) | copy-start | bytes 24580
  178.6 23.1 %copy-start.2 = (s32[1024,1]{1,0:T(8,128)}, s32[1024,1]{1,0:T(8,128)S(1)}, u32[]{:S(2)}) copy-start(s32[1024,1]{1,0:T(8,128)S(1)} %copy.195.low_ref) | copy-start | bytes 12292
  194.5 7.3 copy-start.4
  201.7 15.6 %copy-start.5 = (bf16[1024,256]{1,0:T(8,128)(2,1)}, bf16[1024,256]{1,0:T(8,128)(2,1)S(1)}, u32[]{:S(2)}) copy-start(bf16[1024,256]{1,0:T(8,128)(2,1)S(1)} %convolution_convert_fusion.9.qn_ref) | copy-start | bytes 1572868
  201.8 12.3 %copy-start.44 = (bf16[4,64,2048]{2,1,0:T(8,128)(2,1)S(1)}, bf16[4,64,2048]{2,1,0:T(8,128)(2,1)}, u32[]{:S(2)}) copy-start(bf16[4,64,2048]{2,1,0:T(8,128)(2,1)} %get-tuple-element.58) | copy-start | bytes 3145732
  217.4 45.9 %copy-start.17 = (bf16[128,2048]{1,0:T(8,128)(2,1)S(1)}, bf16[128,2048]{1,0:T(8,128)(2,1)}, u32[]{:S(2)}) copy-start(bf16[128,2048]{1,0:T(8,128)(2,1)} %refs_3_.1) | copy-start | bytes 1572868
  264.8 93.8 %copy-start.79 = (f32[128]{0:T(128)}, f32[128]{0:T(128)S(1)}, u32[]{:S(2)}) copy-start(f32[128]{0:T(128)S(1)} %get-tuple-element.174) | copy-start | bytes 1540
  264.8 97.7 %copy-start.75 = (f32[128]{0:T(128)}, f32[128]{0:T(128)S(1)}, u32[]{:S(2)}) copy-start(f32[128]{0:T(128)S(1)} %get-tuple-element.192) | copy-start | bytes 1540
  264.8 93.8 %copy-start.64 = (f32[128]{0:T(128)}, f32[128]{0:T(128)S(1)}, u32[]{:S(2)}) copy-start(f32[128]{0:T(128)S(1)} %fusion.37) | copy-start | bytes 1540
  266.7 93.8 %copy-start.13 = (bf16[2048,16]{1,0:T(8,128)(2,1)S(1)}, bf16[2048,16]{1,0:T(8,128)(2,1)}, u32[]{:S(2)}) copy-start(bf16[2048,16]{1,0:T(8,128)(2,1)} %reshape.476) | copy-start | bytes 196612
  266.8 93.8 %copy-start.15 = (bf16[128,2048]{1,0:T(8,128)(2,1)S(1)}, bf16[128,2048]{1,0:T(8,128)(2,1)}, u32[]{:S(2)}) copy-start(bf16[128,2048]{1,0:T(8,128)(2,1)} %multiply_convert_fusion.3.refs_0_) | copy-start | bytes 1572868
  360.6 8.3 copy-start.77
  360.9 8.0 copy-start.67
  516.5 123.9 %all-to-all-start.1 = ((f32[32,1,128]{2,1,0:T(1,128)}), f32[32,1,128]{2,1,0:T(1,128)}, u32[]{:S(2)}, u32[]{:S(2)}) async-start(f32[32,1,128]{2,1,0:T(1,128)} %bitcast.35), calls=%async_computation.1 | async-start | bytes 32768 | tf_op jit(solution)/shard_map/all_to_all | solution.py:1429
  628.9 10.0 %copy-start.35 = (bf16[2048,88]{1,0:T(8,128)(2,1)S(1)}, bf16[2048,88]{1,0:T(8,128)(2,1)}, u32[]{:S(2)}) copy-start(bf16[2048,88]{1,0:T(8,128)(2,1)} %copy.202) | copy-start | bytes 1081348
  628.9 10.0 %copy-start.36 = (bf16[2048,88]{1,0:T(8,128)(2,1)S(1)}, bf16[2048,88]{1,0:T(8,128)(2,1)}, u32[]{:S(2)}) copy-start(bf16[2048,88]{1,0:T(8,128)(2,1)} %copy.203) | copy-start | bytes 1081348
  628.9 12.2 %copy-start.59 = (f32[128,16]{0,1:T(8,128)S(1)}, f32[128,16]{0,1:T(8,128)}, u32[]{:S(2)}) copy-start(f32[128,16]{0,1:T(8,128)} %copy-done.58) | copy-start | bytes 24580
  628.9 12.2 %copy-start.68 = (f32[128]{0:T(128)S(1)}, f32[128]{0:T(128)}, u32[]{:S(2)}) copy-start(f32[128]{0:T(128)} %copy-done.67) | copy-start | bytes 1540
  629.0 12.2 %copy-start.69 = (f32[128]{0:T(128)S(1)}, f32[128]{0:T(128)}, u32[]{:S(2)}) copy-start(f32[128]{0:T(128)} %fusion.35) | copy-start | bytes 1540
  629.0 12.3 %copy-start.16 = (bf16[128,2048]{1,0:T(8,128)(2,1)S(1)}, bf16[128,2048]{1,0:T(8,128)(2,1)}, u32[]{:S(2)}) copy-start(bf16[128,2048]{1,0:T(8,128)(2,1)} %multiply_convert_fusion.3.refs_0_) | copy-start | bytes 1572868
  629.0 13.6 %copy-start.14 = (bf16[2048,16]{1,0:T(8,128)(2,1)S(1)}, bf16[2048,16]{1,0:T(8,128)(2,1)}, u32[]{:S(2)}) copy-start(bf16[2048,16]{1,0:T(8,128)(2,1)} %reshape.476) | copy-start | bytes 196612
  629.0 13.6 %copy-start.56 = (f32[2048]{0:T(1024)S(1)}, f32[2048]{0:T(1024)}, u32[]{:S(2)}) copy-start(f32[2048]{0:T(1024)} %copy-done.55) | copy-start | bytes 24580
  629.0 13.6 %copy-start.65 = (f32[128]{0:T(128)S(1)}, f32[128]{0:T(128)}, u32[]{:S(2)}) copy-start(f32[128]{0:T(128)} %copy-done.64) | copy-start | bytes 1540
  644.4 44.2 %copy-start.45 = (bf16[4,64,2048]{2,1,0:T(8,128)(2,1)S(1)}, bf16[4,64,2048]{2,1,0:T(8,128)(2,1)}, u32[]{:S(2)}) copy-start(bf16[4,64,2048]{2,1,0:T(8,128)(2,1)} %get-tuple-element.58) | copy-start | bytes 3145732
  644.4 48.7 %copy-start.72 = (f32[128]{0:T(128)}, f32[128]{0:T(128)S(1)}, u32[]{:S(2)}) copy-start(f32[128]{0:T(128)S(1)} %multiply_multiply_fusion.2) | copy-start | bytes 1540
  739.3 63.7 %copy-start.61 = (f32[512]{0:T(512)S(1)}, f32[512]{0:T(512)}, u32[]{:S(2)}) copy-start(f32[512]{0:T(512)} %copy-done.60) | copy-start | bytes 6148
  739.3 63.7 %copy-start.74 = (f32[128]{0:T(128)S(1)}, f32[128]{0:T(128)}, u32[]{:S(2)}) copy-start(f32[128]{0:T(128)} %fusion.38) | copy-start | bytes 1540
  739.3 65.6 %copy-start.78 = (f32[128]{0:T(128)S(1)}, f32[128]{0:T(128)}, u32[]{:S(2)}) copy-start(f32[128]{0:T(128)} %copy-done.77) | copy-start | bytes 1540
  819.4 70.1 %copy-start.40 = (bf16[4,8,64,176]{3,2,1,0:T(8,128)(2,1)S(1)}, bf16[4,8,64,176]{3,2,1,0:T(8,128)(2,1)}, u32[]{:S(2)}) copy-start(bf16[4,8,64,176]{3,2,1,0:T(8,128)(2,1)} %get-tuple-element.84) | copy-start | bytes 2162692
  890.1 8.4 copy-start.76
  890.1 8.4 copy-start.81
  893.8 14.1 %copy-start.12 = (f32[128,2048]{1,0:T(8,128)S(1)}, f32[128,2048]{1,0:T(8,128)}, u32[]{:S(2)}) copy-start(f32[128,2048]{1,0:T(8,128)} %copy-done.11) | copy-start | bytes 3145732
  893.8 14.1 %copy-start.19 = (bf16[128,2048]{1,0:T(8,128)(2,1)S(1)}, bf16[128,2048]{1,0:T(8,128)(2,1)}, u32[]{:S(2)}) copy-start(bf16[128,2048]{1,0:T(8,128)(2,1)} %refs_3_.1) | copy-start | bytes 1572868
  893.8 14.1 %copy-start.22 = (bf16[128,2048]{1,0:T(8,128)(2,1)S(1)}, bf16[128,2048]{1,0:T(8,128)(2,1)}, u32[]{:S(2)}) copy-start(bf16[128,2048]{1,0:T(8,128)(2,1)} %param.35) | copy-start | bytes 1572868
  900.1 7.8 copy-start.66
  900.1 7.8 copy-start.71
  900.2 7.8 copy-start.73
  900.2 7.8 copy-start.82
  912.8 12.0 %slice-start = ((s8[5767168]{0:T(1024)(128)(4,1)}), s8[4194304]{0:T(1024)(128)(4,1)S(1)}, s32[]{:S(2)}) async-start(s8[5767168]{0:T(1024)(128)(4,1)} %bitcast.162), calls=%async_computation.3 | async-start | bytes 8388608
  (42 other events, 152.8 us)
Sparse Core Ops, SparseCore 0:
  76.2 161.4 all-gather.1

commit v9 on v8

--- a/solution.py
+++ b/solution.py
@@ -1003,7 +1003,8 @@
 def moe_kernel(
     n_groups, experts, first_logit, slot_count,
     h2_hbm, cot_hbm, place_ref, wg_ref, wu_ref, wd_ref, sc_ref, sd_ref,
-    sum_ref, rows_ref, gin_ref, act_ref, gg_ref, gu_ref, rw_ref, sact_ref, sgrad_ref, tok_ref,
+    sum_ref, rows_ref, gin_ref, act_ref, gg_ref, gu_ref, rw_ref, sact_ref, dboth_ref, dsd_ref,
+    tok_ref,
     h2_buf, cot_buf, load_sems, *comm,
 ):
     rows = sum_ref.shape[0]
@@ -1028,6 +1029,8 @@
         for copy in loads(step):
             copy.start()
         w.meet()
+        for ref in (dboth_ref, dsd_ref):
+            ref[...] = jnp.zeros_like(ref)
 
     @pl.when(step + 1 < steps)
     def _():
@@ -1054,7 +1057,6 @@
     for i, chip in enumerate(chips):
         at = pl.ds(pl.multiple_of(chip * 2 * rows, 2 * rows), 2 * rows)
         sact_ref[at, :] = shared_act[i * 2 * rows : (i + 1) * 2 * rows]
-        sgrad_ref[at, :] = shared_grad[i * 2 * rows : (i + 1) * 2 * rows]
 
     hots, weights = [], []
     for q in range(4):
@@ -1099,6 +1101,13 @@
         )
         stream.stage[slot, q] = total.astype(BF)
     stream.push(step)
+
+    piece = h2.shape[1] // 4
+    turned, turned_act = shared_grad.T, shared_act.T
+    for k in range(4):
+        cols = slice(k * piece, (k + 1) * piece)
+        dboth_ref[:, cols] += jnp.dot(turned, h2[:, cols], preferred_element_type=F32)
+        dsd_ref[:, cols] += jnp.dot(turned_act, cot[:, cols], preferred_element_type=F32)
     stream.advance(step)
 
     @pl.when(step == steps - 1)
@@ -1201,14 +1210,15 @@
         shape((all_slots, hidden), BF),
         shape((all_slots, 1), F32),
         shape((tokens, half), BF),
-        shape((tokens, 2 * half), BF),
+        shape((2 * half, width), F32),
+        shape((half, width), F32),
         shape((devices, rows), F32),
     ]
     specs = [
         blocked(step_slots, s.shape[1]) if s.shape[0] == all_slots else whole(s) for s in shapes
     ]
     hbm = pl.BlockSpec(memory_space=pl.ANY)
-    grad_h2, rows_in, grad_in, act, grad_gate, grad_up, row_weight, s_act, s_grad, token_grad = (
+    grad_h2, rows_in, grad_in, act, grad_gate, grad_up, row_weight, s_act, *d_shared, token_grad = (
         pl.pallas_call(
             functools.partial(moe_kernel, n_groups, experts, hidden_s, slot_count),
             grid=(steps,),
@@ -1272,15 +1282,9 @@
         ),
         name="expert_out",
     )(act, row_weight, rows_in, grad_in, grad_gate, grad_up, place, s_act, w_down, s_tall)
-    g_both = dot_tn(h2, s_grad)
-    g_both = jnp.concatenate([g_both[:, :hidden_s], g_both[:, half : half + hidden_s]], axis=1)
-    grads = (
-        d_gate,
-        d_up,
-        d_down,
-        g_both,
-        dot_tn(s_act, cot)[:hidden_s],
-    )
+    d_both, d_tall = d_shared
+    d_both = jnp.concatenate([d_both[:hidden_s], d_both[half : half + hidden_s]], axis=0)
+    grads = (d_gate, d_up, d_down, d_both.T, d_tall[:hidden_s])
     return out, grad_h2, token_grad, grads
 
 
@@ -1361,7 +1365,7 @@
         ],
         axis=2,
     )
-    s_both = lax.all_to_all(s_both, ALL, split_axis=1, concat_axis=0).reshape(width, 2 * shared_n)
+    s_both = s_both.transpose(1, 0, 2).reshape(n_groups, n_plane, rows_w, 2 * shared_n)
 
     hidden = rms_norm(x_plane, gain_one).astype(BF)
     rope_half = ROPE // 2
@@ -1404,7 +1408,12 @@
     router_probs = softmax_rows(matmul(h_two, router_weight))
 
     expert_w = (expert_gate[0].T, expert_up[0].T, expert_down[0])
-    shared_w = (s_both, shared_down)
+    parts = max(1, devices * tok // 4096)
+    if parts == 1:
+        h2_all, s_both = swap(5, ("far_gather", h_two), ("whole_swap", s_both))
+    else:
+        s_both = swap(7, ("whole_swap", s_both))[0]
+    shared_w = (s_both.reshape(width, 2 * shared_n), shared_down)
     slot_limit = 2 * tok * TOP // experts
 
     def on_rows(h2, h2_all, cot_gathered, routes_here):
@@ -1430,11 +1439,10 @@
         picked = jnp.sum(picked.reshape(experts, devices // experts, rows), axis=1).T
         return out, grad_h2, picked, grads
 
-    parts = max(1, devices * tok // 4096)
     if parts == 1:
         cot_all = gather_all(cotangent_later)
         out_own, grad_h2_own, grad_router_probs, grads = on_rows(
-            h_two, swap(5, ("far_gather", h_two))[0].reshape(-1, width), cot_all, routes_all
+            h_two, h2_all.reshape(-1, width), cot_all, routes_all
         )
     else:
         rows = tok // parts

time: 943 us -> 949 us (level)
  Pallas kernels: 690 us -> 715 us
  matrix products: 67.6 us -> 47.8 us
  starting transfers between devices: 21.9 us -> 5.52 us
  local copies, waits for them, and re-layouts: 92.7 us -> 104 us
    dot_general x8 -> x6, matrix products: 35.2 us -> 14.3 us  [dot_tn(): lax.dot_general(left, right, (((0,), (0,)), ((), ())), preferred_element_...]
    all_to_all x1 -> x0, starting transfers between devices: 14.5 us -> none  [body(): lax.all_to_all(s_both, ALL, split_axis=1, concat_axis=0)]
    pallas_call x7, Pallas kernels: 422 us -> 435 us  [exchange(): pl.pallas_call(functools.partial(exchange_kernel, n_groups, n_plane, kind...]
    pallas_call x1, Pallas kernels: 133 us -> 145 us  [experts_sums(): pl.pallas_call(functools.partial(moe_kernel, n_groups, experts, hidden_s,...]
    unnamed x182 -> x180, local copies, waits for them, and re-layouts: 25.8 us -> 26 us
  transfers between devices with their start and end apart: 3 -> 2, of which waited for: 0 -> 0; matrix products, arithmetic and copies ran while one was open for 9% -> 10% of each run, Pallas kernels for 33% -> 34%
where the time goes in v9:
time: 949 us; the launch traced here: 939 us
  Pallas kernels  715 us (75%)
  local copies, waits for them, and re-layouts  104 us (11%)
  other arithmetic  50.8 us (5%)
  matrix products  47.8 us (5%)
  between operations  16.2 us (2%)
    pallas_call x7, Pallas kernels, exchange(): pl.pallas_call(functools.partial(exchange_kernel, n_groups, n_plane, kind...  435 us
    pallas_call x1, Pallas kernels, experts_sums(): pl.pallas_call(functools.partial(moe_kernel, n_groups, experts, hidden_s,...  145 us
    pallas_call x1, Pallas kernels, experts_sums(): pl.pallas_call(functools.partial(out_kernel, n_groups, slot_count), grid=...  103 us
    unnamed x180, local copies, waits for them, and re-layouts  26 us
    pallas_call x1, Pallas kernels, attend_back(): pl.pallas_call(functools.partial(attend_back_kernel, heads, scale), grid=...  20.7 us
  transfers between devices with their start and end apart: 2, of which 0 were waited for; matrix products, arithmetic and copies ran while one was open for 10% of the time, Pallas kernels for 34%

profile of v9, /device:TPU:1, one launch (start us, length us, event | category | flops | bytes accessed | tf_op | source)
XLA Modules:
  0.0 938.9 jit_solution(14373937221368445103)
XLA Ops:
  9.7 2.1 concatenate.56
  15.4 56.8 %exchange_0.1 = (bf16[4,8,64,512]{3,2,1,0:T(8,128)(2,1)}, bf16[4,8,64,576]{3,2,1,0:T(8,128)(2,1)}, bf16[4,8,32,128]{3,2,1,0:T(8,128)(2,1)}, bf16[8,128,2048]{2,1,0:T(8,128)(2,1)}) custom-call(bf16[8,64,512]{2,1,0:T(8,128)(2,1)} %pad_maximum_fusion.6.refs_0_, bf16[64,576]{1,0:T(8,128)(2,1)} %refs_1_.2, bf16[32,128]{1,0:T(8,128)(2,1)} %pad_bitcast_fusion.1.refs_2_, ...), custom_call_target="tpu_custom_call" | custom-call | tf_op jit(solution)/shard_map/exchange_0/pallas_call | solution.py:796
  74.1 1.9 broadcast_select_fusion
  84.1 3.2 multiply_reduce_fusion
  89.7 3.4 fusion.49
  95.8 3.3 fusion.9
  101.0 59.7 %exchange_1.1 = (bf16[8,128,576]{2,1,0:T(8,128)(2,1)}, bf16[4,64,2048]{2,1,0:T(8,128)(2,1)}) custom-call(bf16[128,576]{1,0:T(8,128)(2,1)} %fusion.27.refs_0_, bf16[64,2048]{1,0:T(8,128)(2,1)} %refs_1_.3), custom_call_target="tpu_custom_call" | custom-call | tf_op jit(solution)/shard_map/exchange_1/pallas_call | solution.py:796
  162.4 2.3 slice.163
  166.9 2.2 reshape.477
  170.5 2.1 reshape.481
  173.5 2.9 copy.154
  176.4 2.3 slice.155
  178.7 1.9 copy.174
  183.0 3.8 fusion.16
  190.3 4.6 convolution_convert_fusion.2.ex_ref
  196.3 11.5 %attend.1 = (bf16[1024,256]{1,0:T(8,128)(2,1)S(1)}, f32[1024,2]{1,0:T(8,128)S(1)}) custom-call(s32[1024,1]{1,0:T(8,128)S(1)} %copy.161.low_ref, bf16[1024,256]{1,0:T(8,128)(2,1)S(1)} %convolution_convert_fusion.8.qn_ref, bf16[1024,128]{1,0:T(8,128)(2,1)S(1)} %copy.162.qr_ref, bf16[2048,512]{1,0:T(8,128)(2,1)} %convolution_convert_fusion.2.ex_ref, ...), custom_call_target="tpu_custom_call" | custom-call | flops 1677721600 | bytes 4194304 | tf_op jit(solution)/shard_map/attend/pallas_call | solution.py:117
  208.7 3.3 convolution_convert_fusion
  212.0 42.6 %exchange_2.1 = f32[128,2048]{1,0:T(8,128)} custom-call(bf16[8,128,2048]{2,1,0:T(8,128)(2,1)} %bitcast.147), custom_call_target="tpu_custom_call" | custom-call | tf_op jit(solution)/shard_map/exchange_2/pallas_call | solution.py:796
  255.4 2.5 pad_maximum_fusion.5
  261.4 105.4 %exchange_5.1 = (bf16[4,8,128,2048]{3,2,1,0:T(8,128)(2,1)}, bf16[4,8,64,176]{3,2,1,0:T(8,128)(2,1)}) custom-call(bf16[128,2048]{1,0:T(8,128)(2,1)} %multiply_convert_fusion.3.refs_0_, bf16[4,8,64,176]{3,2,1,0:T(8,128)(2,1)} %bitcast.167), custom_call_target="tpu_custom_call" | custom-call | tf_op jit(solution)/shard_map/exchange_5/pallas_call | solution.py:796
  366.9 2.5 fusion.46
  371.1 4.0 concatenate.63.sc_ref
  379.0 5.2 multiply_convert_fusion
  384.2 144.7 %experts.1 = (f32[128,2048]{1,0:T(8,128)}, bf16[3072,2048]{1,0:T(8,128)(2,1)}, bf16[3072,2048]{1,0:T(8,128)(2,1)}, bf16[3072,704]{1,0:T(8,128)(2,1)}, bf16[3072,...) custom-call(bf16[4096,2048]{1,0:T(8,128)(2,1)} %bitcast.201, ...), custom_call_target="tpu_custom_call" | custom-call | flops 57713623040 | bytes 100663296 | tf_op jit(solution)/shard_map/experts/pallas_call | solution.py:1222
  528.9 5.5 all-to-all-start
  537.1 102.7 %expert_out.1 = (f32[128,2048]{1,0:T(8,128)}, f32[704,2048]{1,0:T(8,128)}, f32[704,2048]{1,0:T(8,128)}, f32[704,2048]{1,0:T(8,128)}) custom-call(bf16[3072,704]{1,0:T(8,128)(2,1)} %get-tuple-element.64.act_ref, f32[3072,1]{1,0:T(8,128)} %get-tuple-element.65.rw_ref, bf16[3072,2048]{1,0:T(8,128)(2,1)} %get-tuple-element.66.rows_ref, ...), custom_call_target="tpu_custom_call" | custom-call | flops 39191576576 | bytes 33554432 | tf_op jit(solution)/shard_map/expert_out/pallas_call | solution.py:1255
  641.2 2.1 slice.151
  651.0 42.1 %exchange_3.1 = (bf16[4,8,64,176]{3,2,1,0:T(8,128)(2,1)}, bf16[8,128,2048]{2,1,0:T(8,128)(2,1)}) custom-call(bf16[4,8,64,176]{3,2,1,0:T(8,128)(2,1)} %bitcast.162, bf16[128,2048]{1,0:T(8,128)(2,1)} %fusion.43.refs_1_), custom_call_target="tpu_custom_call" | custom-call | tf_op jit(solution)/shard_map/exchange_3/pallas_call | solution.py:796
  693.1 4.4 convolution_convert_fusion.7.gm_ref
  697.5 2.2 convolution_convert_fusion.3
  701.1 20.7 %attend_back.1 = (f32[1024,256]{1,0:T(8,128)}, f32[1024,128]{1,0:T(8,128)}, f32[2048,512]{1,0:T(8,128)}, f32[2048,64]{1,0:T(8,128)}) custom-call(s32[1024,1]{1,0:T(8,128)} %copy-done.2, bf16[1024,256]{1,0:T(8,128)(2,1)} %copy-done.5, bf16[1024,128]{1,0:T(8,128)(2,1)} %copy-done.4, bf16[2048,512]{1,0:T(8,128)(2,1)} %convolution_convert_fusion.2.ex_ref, ...), custom_call_target="tpu_custom_call" | custom-call | flops 4362076160 | bytes 8388608 | tf_op jit(solution)/shard_map/attend_back/pallas_call | solution.py:192
  721.8 2.6 convert_element_type.220
  724.6 2.1 fusion.2
  730.4 4.5 convolution_convert_fusion.5
  737.0 2.4 convolution_convert_fusion.4
  739.4 4.3 fusion
  743.7 62.6 %exchange_4.1 = (f32[128,576]{1,0:T(8,128)}, f32[128,2048]{1,0:T(8,128)}, bf16[8,64,256]{2,1,0:T(8,128)(2,1)}, bf16[8,64,128]{2,1,0:T(8,128)(2,1)}, bf16[8,16,512]{2,1,0:T(8,128)(2,1)}) custom-call(bf16[8,256,576]{2,1,0:T(8,128)(2,1)} %bitcast.150, bf16[8,128,2048]{2,1,0:T(8,128)(2,1)} %bitcast.148, bf16[4,8,64,256]{3,2,1,0:T(8,128)(2,1)} %bitcast.178, ...), custom_call_target="tpu_custom_call" | custom-call | tf_op jit(solution)/shard_map/exchange_4/pallas_call | solution.py:796
  807.6 1.9 multiply_reduce_fusion.5
  812.6 2.6 fusion.8
  821.2 2.7 copy.176
  823.9 66.1 %exchange_6.1 = (f32[64,576]{1,0:T(8,128)}, f32[64,2048]{1,0:T(8,128)}, f32[16,128]{1,0:T(8,128)}) custom-call(bf16[4,8,64,576]{3,2,1,0:T(8,128)(2,1)} %bitcast.149, bf16[4,64,2048]{2,1,0:T(8,128)(2,1)} %bitcast.181, f32[4,8,16,128]{3,2,1,0:T(8,128)} %copy.195), custom_call_target="tpu_custom_call" | custom-call | tf_op jit(solution)/shard_map/exchange_6/pallas_call | solution.py:796
  898.3 2.8 reshape.501
  907.8 2.1 maximum_convert_fusion
  909.8 2.5 reshape.508
  912.4 3.4 fusion.4
  917.3 6.0 copy.204
  923.3 6.0 copy.205
  929.3 2.5 copy.206
  (292 shorter events, 91.8 us)
Async XLA Ops:
  7.2 377.0 %all-gather.2.cloned.1.call-start = ((), (), s32[]{:S(2)}) async-start(), calls=%async_computation.1 | async-start | bytes 17301504 | tf_op jit(solution)/shard_map/all_gather | solution.py:815
  72.2 8.0 copy-start.33
  83.9 15.2 %copy-start.57 = (f32[512]{0:T(512)}, f32[512]{0:T(512)S(1)}, u32[]{:S(2)}) copy-start(f32[512]{0:T(512)S(1)} %reshape.505) | copy-start | bytes 6148
  84.0 294.9 %copy-start.50 = (f32[2048]{0:T(1024)}, f32[2048]{0:T(1024)S(1)}, u32[]{:S(2)}) copy-start(f32[2048]{0:T(1024)S(1)} %reshape.504) | copy-start | bytes 24580
  93.1 282.0 %copy-start.10 = (f32[1024,576]{1,0:T(8,128)}, f32[1024,576]{1,0:T(8,128)S(1)}, u32[]{:S(2)}) copy-start(f32[1024,576]{1,0:T(8,128)S(1)} %fusion.49) | copy-start | bytes 7077892
  99.0 65.6 %copy-start.48 = (bf16[64,2816]{1,0:T(8,128)(2,1)S(1)}, bf16[64,2816]{1,0:T(8,128)(2,1)}, u32[]{:S(2)}) copy-start(bf16[64,2816]{1,0:T(8,128)(2,1)} %param.27) | copy-start | bytes 1081348
  170.2 89.3 %copy-start.52 = (f32[2048]{0:T(1024)}, f32[2048]{0:T(1024)S(1)}, u32[]{:S(2)}) copy-start(f32[2048]{0:T(1024)S(1)} %reshape.506) | copy-start | bytes 24580
  173.5 22.8 %copy-start.2 = (s32[1024,1]{1,0:T(8,128)}, s32[1024,1]{1,0:T(8,128)S(1)}, u32[]{:S(2)}) copy-start(s32[1024,1]{1,0:T(8,128)S(1)} %copy.161.low_ref) | copy-start | bytes 12292
  188.8 7.4 copy-start.4
  196.3 15.7 %copy-start.5 = (bf16[1024,256]{1,0:T(8,128)(2,1)}, bf16[1024,256]{1,0:T(8,128)(2,1)S(1)}, u32[]{:S(2)}) copy-start(bf16[1024,256]{1,0:T(8,128)(2,1)S(1)} %convolution_convert_fusion.8.qn_ref) | copy-start | bytes 1572868
  196.3 12.4 %copy-start.42 = (bf16[4,64,2048]{2,1,0:T(8,128)(2,1)S(1)}, bf16[4,64,2048]{2,1,0:T(8,128)(2,1)}, u32[]{:S(2)}) copy-start(bf16[4,64,2048]{2,1,0:T(8,128)(2,1)} %get-tuple-element.61) | copy-start | bytes 3145732
  211.9 42.6 %copy-start.49 = (bf16[88,2048]{1,0:T(8,128)(2,1)S(1)}, bf16[88,2048]{1,0:T(8,128)(2,1)}, u32[]{:S(2)}) copy-start(bf16[88,2048]{1,0:T(8,128)(2,1)} %param.29) | copy-start | bytes 1081348
  211.9 43.5 %copy-start.34 = (bf16[64,32,88]{2,0,1:T(8,128)(2,1)S(1)}, bf16[64,32,88]{2,0,1:T(8,128)(2,1)}, u32[]{:S(2)}) copy-start(bf16[64,32,88]{2,0,1:T(8,128)(2,1)} %copy.163) | copy-start | bytes 1081348
  211.9 46.0 %copy-start.16 = (bf16[128,2048]{1,0:T(8,128)(2,1)S(1)}, bf16[128,2048]{1,0:T(8,128)(2,1)}, u32[]{:S(2)}) copy-start(bf16[128,2048]{1,0:T(8,128)(2,1)} %refs_3_.1) | copy-start | bytes 1572868
  257.9 113.2 %copy-start.13 = (bf16[2048,16]{1,0:T(8,128)(2,1)S(1)}, bf16[2048,16]{1,0:T(8,128)(2,1)}, u32[]{:S(2)}) copy-start(bf16[2048,16]{1,0:T(8,128)(2,1)} %reshape.481) | copy-start | bytes 196612
  259.5 115.7 %copy-start.78 = (f32[128]{0:T(128)}, f32[128]{0:T(128)S(1)}, u32[]{:S(2)}) copy-start(f32[128]{0:T(128)S(1)} %get-tuple-element.164) | copy-start | bytes 1540
  259.5 118.3 %copy-start.74 = (f32[128]{0:T(128)}, f32[128]{0:T(128)S(1)}, u32[]{:S(2)}) copy-start(f32[128]{0:T(128)S(1)} %get-tuple-element.182) | copy-start | bytes 1540
  259.5 115.7 %copy-start.63 = (f32[128]{0:T(128)}, f32[128]{0:T(128)S(1)}, u32[]{:S(2)}) copy-start(f32[128]{0:T(128)S(1)} %fusion.35) | copy-start | bytes 1540
  366.9 11.5 %copy-start.62 = (pred[16,256]{1,0:T(8,128)(4,1)S(1)}, pred[16,256]{1,0:T(8,128)(4,1)}, u32[]{:S(2)}) copy-start(pred[16,256]{1,0:T(8,128)(4,1)} %reduce_or.12) | copy-start | bytes 12292
  366.9 12.1 %copy-start.61 = (f32[1024]{0:T(1024)S(1)}, f32[1024]{0:T(1024)}, u32[]{:S(2)}) copy-start(f32[1024]{0:T(1024)} %get-tuple-element.192) | copy-start | bytes 12292
  375.3 8.9 copy-start.76
  376.7 7.5 copy-start.55
  376.7 7.5 copy-start.66
  528.9 116.0 %all-to-all-start = ((f32[32,1,128]{2,1,0:T(1,128)}), f32[32,1,128]{2,1,0:T(1,128)}, u32[]{:S(2)}, u32[]{:S(2)}) async-start(f32[32,1,128]{2,1,0:T(1,128)} %bitcast.198), calls=%async_computation | async-start | bytes 32768 | tf_op jit(solution)/shard_map/all_to_all | solution.py:1438
  639.8 7.3 copy-start.9
  639.8 7.3 copy-start.14
  639.8 7.3 copy-start.53
  639.8 7.2 copy-start.64
  641.1 7.7 copy-start.79
  641.1 8.7 copy-start.20
  648.8 44.2 %copy-start.43 = (bf16[4,64,2048]{2,1,0:T(8,128)(2,1)S(1)}, bf16[4,64,2048]{2,1,0:T(8,128)(2,1)}, u32[]{:S(2)}) copy-start(bf16[4,64,2048]{2,1,0:T(8,128)(2,1)} %get-tuple-element.61) | copy-start | bytes 3145732
  648.9 48.6 %copy-start.71 = (f32[128]{0:T(128)}, f32[128]{0:T(128)S(1)}, u32[]{:S(2)}) copy-start(f32[128]{0:T(128)S(1)} %multiply_multiply_fusion.2) | copy-start | bytes 1540
  743.7 63.8 %copy-start.58 = (f32[512]{0:T(512)S(1)}, f32[512]{0:T(512)}, u32[]{:S(2)}) copy-start(f32[512]{0:T(512)} %copy-done.57) | copy-start | bytes 6148
  743.7 63.8 %copy-start.73 = (f32[128]{0:T(128)S(1)}, f32[128]{0:T(128)}, u32[]{:S(2)}) copy-start(f32[128]{0:T(128)} %fusion.36) | copy-start | bytes 1540
  743.7 65.7 %copy-start.77 = (f32[128]{0:T(128)S(1)}, f32[128]{0:T(128)}, u32[]{:S(2)}) copy-start(f32[128]{0:T(128)} %copy-done.76) | copy-start | bytes 1540
  806.3 6.2 copy-start.17
  806.3 6.2 copy-start.30
  823.9 70.1 %copy-start.38 = (bf16[4,8,64,176]{3,2,1,0:T(8,128)(2,1)S(1)}, bf16[4,8,64,176]{3,2,1,0:T(8,128)(2,1)}, u32[]{:S(2)}) copy-start(bf16[4,8,64,176]{3,2,1,0:T(8,128)(2,1)} %get-tuple-element.89) | copy-start | bytes 2162692
  894.6 8.4 copy-start.75
  894.6 8.4 copy-start.80
  898.3 14.1 %copy-start.12 = (f32[128,2048]{1,0:T(8,128)S(1)}, f32[128,2048]{1,0:T(8,128)}, u32[]{:S(2)}) copy-start(f32[128,2048]{1,0:T(8,128)} %copy-done.11) | copy-start | bytes 3145732
  898.3 14.1 %copy-start.18 = (bf16[128,2048]{1,0:T(8,128)(2,1)S(1)}, bf16[128,2048]{1,0:T(8,128)(2,1)}, u32[]{:S(2)}) copy-start(bf16[128,2048]{1,0:T(8,128)(2,1)} %refs_3_.1) | copy-start | bytes 1572868
  898.3 14.1 %copy-start.21 = (bf16[128,2048]{1,0:T(8,128)(2,1)S(1)}, bf16[128,2048]{1,0:T(8,128)(2,1)}, u32[]{:S(2)}) copy-start(bf16[128,2048]{1,0:T(8,128)(2,1)} %param.35) | copy-start | bytes 1572868
  904.6 7.8 copy-start.65
  904.6 7.8 copy-start.70
  904.6 7.8 copy-start.72
  904.7 7.8 copy-start.81
  917.3 12.0 %slice-start = ((s8[5767168]{0:T(1024)(128)(4,1)}), s8[4194304]{0:T(1024)(128)(4,1)S(1)}, s32[]{:S(2)}) async-start(s8[5767168]{0:T(1024)(128)(4,1)} %bitcast.155), calls=%async_computation.2 | async-start | bytes 8388608
  (40 other events, 149.1 us)
Sparse Core Ops, SparseCore 0:
  76.2 148.8 all-gather.1

commit v10 on v9

--- a/solution.py
+++ b/solution.py
@@ -1318,29 +1318,29 @@
         ]
     )
     small = jnp.pad(small, (0, -small.shape[0] % 4096)).reshape(-1, 128)
-    head_cols = local_heads * (NOPE + ROPE)
     kv_cols = local_heads * (NOPE + VDIM)
     fold = kv_n * kv_cols // rows_w
-    pair = jnp.concatenate(
-        [
-            w_query.reshape(rows_w, n_plane, head_cols).transpose(1, 0, 2),
-            w_expand.reshape(kv_n, n_plane, kv_cols // fold, fold)
-            .transpose(1, 0, 2, 3)
-            .reshape(n_plane, rows_w, fold),
-        ],
-        axis=2,
+    by_head = w_query.reshape(rows_w, n_plane, local_heads, NOPE + ROPE).transpose(1, 0, 2, 3)
+    folded = (
+        w_expand.reshape(kv_n, n_plane, kv_cols // fold, fold)
+        .transpose(1, 0, 2, 3)
+        .reshape(n_plane, rows_w, fold)
     )
     swap = functools.partial(exchange, n_groups, n_plane)
-    pair, latent_weight, small, x_plane = swap(
+    wq_nope, wq_rope, expand_weight, latent_weight, small, x_plane = swap(
         0,
-        ("plane_swap_gather", pair),
+        ("plane_swap_gather", by_head[..., :NOPE].reshape(n_plane, rows_w, local_heads * NOPE)),
+        ("plane_swap_gather", by_head[..., NOPE:].reshape(n_plane, rows_w, local_heads * ROPE)),
+        ("plane_swap_gather", folded),
         ("whole_gather", w_latent),
         ("whole_gather", small),
         ("plane_gather", layer_input),
     )
     x_plane = x_plane.reshape(plane_tok, width).astype(F32)
     latent_weight = latent_weight.reshape(width, RANK + ROPE)
-    pair = pair.reshape(width, head_cols + fold)
+    wq_nope = wq_nope.reshape(width, local_heads * NOPE)
+    wq_rope = wq_rope.reshape(width, local_heads * ROPE)
+    expand_weight = expand_weight.reshape(RANK, kv_cols)
     small = small.reshape(devices, -1)
     cuts = [rows_w, 2 * rows_w, 2 * rows_w + kv_n, 2 * rows_w + kv_n + rows_w * experts]
     cuts = cuts + [cuts[-1] + tok * TOP, cuts[-1] + tok * TOP + tok]
@@ -1351,10 +1351,6 @@
     routes_all = small[:, cuts[3] : cuts[4]].astype(jnp.int32).reshape(devices, tok, TOP)
     segments_all = small[:, cuts[4] : cuts[5]].astype(jnp.int32).reshape(-1)
 
-    query_weight = pair[:, :head_cols].reshape(width, local_heads, NOPE + ROPE)
-    wq_nope = query_weight[:, :, :NOPE].reshape(width, local_heads * NOPE)
-    wq_rope = query_weight[:, :, NOPE:].reshape(width, local_heads * ROPE)
-    expand_weight = pair[:, head_cols:].reshape(RANK, kv_cols)
     cotangent_later = jnp.where(x_plane[0, 0] < 1e6, cotangent, jnp.zeros_like(cotangent))
 
     shared_n = shared_down.shape[0]
@@ -1374,7 +1370,16 @@
     angles = positions.astype(F32)[:, None] * frequency[None, :]
     cosine = jnp.cos(angles)
     sine_part = jnp.sin(angles)
-    cos_h, sin_h = cosine[:, None, :], sine_part[:, None, :]
+    cos_h = jnp.tile(cosine, (1, 2 * local_heads))
+    sin_h = jnp.tile(jnp.concatenate([-sine_part, sine_part], axis=1), (1, local_heads))
+
+    def turn(rows, direction):
+        pieces = []
+        for h in range(local_heads):
+            at = h * ROPE
+            pieces += [rows[:, at + rope_half : at + ROPE], rows[:, at : at + rope_half]]
+        return rows * cos_h + jnp.concatenate(pieces, axis=1) * (direction * sin_h)
+
     latent = matmul(hidden, latent_weight)
     compressed_own = rms_norm(latent[:, :RANK], gain_kv).astype(BF)
     key_rope_own = rotate(latent[:, RANK:], cosine, sine_part).astype(BF)
@@ -1389,9 +1394,7 @@
     compressed = jnp.concatenate([before[:, :RANK], compressed_own], axis=0)
     key_rope = jnp.concatenate([before[:, RANK:], key_rope_own], axis=0)
     q_nope = matmul(hidden, wq_nope).astype(BF)
-    q_rope = rotate(
-        matmul(hidden, wq_rope).reshape(plane_tok, local_heads, ROPE), cos_h, sin_h
-    ).reshape(plane_tok, local_heads * ROPE).astype(BF)
+    q_rope = turn(matmul(hidden, wq_rope), 1.0).astype(BF)
     expanded = matmul(compressed, expand_weight).astype(BF)
     plane_segments = lax.dynamic_slice_in_dim(segments_all, plane_start, plane_tok, 0)
     doc_start = jnp.sum(
@@ -1420,8 +1423,8 @@
         rows = h2.shape[0]
         slot_count = min(slot_limit, rows)
         member = jnp.any(routes_here == expert_id, axis=2)
-        member_int = member.astype(jnp.int32)
-        rank = jnp.cumsum(member_int, axis=1) - member_int
+        before_it = jnp.arange(rows)[:, None] < jnp.arange(rows)[None, :]
+        rank = matmul(member.astype(BF), before_it.astype(BF)).astype(jnp.int32)
         place = jnp.where(member, rank, -1).reshape(devices // 2, 2 * rows)
         out, grad_h2, token_grad, grads = experts_sums(
             n_groups,
@@ -1504,11 +1507,7 @@
     )
 
     gq_nope = dqn.astype(BF)
-    gq_rope = (
-        unrotate(dqr.reshape(plane_tok, local_heads, ROPE), cos_h, sin_h)
-        .reshape(plane_tok, local_heads * ROPE)
-        .astype(BF)
-    )
+    gq_rope = turn(dqr, -1.0).astype(BF)
     grad_hidden = (dot_nt(gq_nope, wq_nope) + dot_nt(gq_rope, wq_rope)).astype(BF)
     gw_nope = dot_tn(hidden, gq_nope).astype(BF).reshape(n_groups, n_plane, rows_w, -1)
     gw_rope = dot_tn(hidden, gq_rope).astype(BF).reshape(n_groups, n_plane, rows_w, -1)

time: 949 us -> 950 us (level)
  Pallas kernels: 715 us -> 732 us
    pallas_call x7, Pallas kernels: 435 us -> 454 us  [exchange(): pl.pallas_call(functools.partial(exchange_kernel, n_groups, n_plane, kind...]
    unnamed x180 -> x198, local copies, waits for them, and re-layouts: 26 us -> 27.1 us
  transfers between devices with their start and end apart: 2 -> 2, of which waited for: 0 -> 0; matrix products, arithmetic and copies ran while one was open for 10% -> 9% of each run, Pallas kernels for 34% -> 35%
where the time goes in v10:
time: 950 us; the launch traced here: 947 us
  Pallas kernels  732 us (77%)
  local copies, waits for them, and re-layouts  103 us (11%)
  other arithmetic  47.1 us (5%)
  matrix products  43.7 us (5%)
  between operations  16.2 us (2%)
    pallas_call x7, Pallas kernels, exchange(): pl.pallas_call(functools.partial(exchange_kernel, n_groups, n_plane, kind...  454 us
    pallas_call x1, Pallas kernels, experts_sums(): pl.pallas_call(functools.partial(moe_kernel, n_groups, experts, hidden_s,...  143 us
    pallas_call x1, Pallas kernels, experts_sums(): pl.pallas_call(functools.partial(out_kernel, n_groups, slot_count), grid=...  103 us
    unnamed x198, local copies, waits for them, and re-layouts  27.1 us
    pallas_call x1, Pallas kernels, attend_back(): pl.pallas_call(functools.partial(attend_back_kernel, heads, scale), grid=...  20.9 us
  transfers between devices with their start and end apart: 2, of which 0 were waited for; matrix products, arithmetic and copies ran while one was open for 9% of the time, Pallas kernels for 35%

profile of v10, /device:TPU:1, one launch (start us, length us, event | category | flops | bytes accessed | tf_op | source)
XLA Modules:
  0.0 946.7 jit_solution(17616063524762389936)
XLA Ops:
  14.3 66.0 %exchange_0.1 = (bf16[4,8,64,256]{3,2,1,0:T(8,128)(2,1)}, bf16[4,8,64,128]{3,2,1,0:T(8,128)(2,1)}, bf16[4,8,64,128]{3,2,1,0:T(8,128)(2,1)}, bf16[4,8,64,576]{3,2...) custom-call(bf16[8,64,256]{2,1,0:T(8,128)(2,1)} %reshape.398.refs_0_, ...), custom_call_target="tpu_custom_call" | custom-call | tf_op jit(solution)/shard_map/exchange_0/pallas_call | solution.py:796
  85.0 3.2 multiply_reduce_fusion
  90.2 3.4 fusion.51
  95.7 3.2 fusion.13
  100.9 59.6 %exchange_1.1 = (bf16[8,128,576]{2,1,0:T(8,128)(2,1)}, bf16[4,64,2048]{2,1,0:T(8,128)(2,1)}) custom-call(bf16[128,576]{1,0:T(8,128)(2,1)} %fusion.26.refs_0_, bf16[64,2048]{1,0:T(8,128)(2,1)} %refs_1_.1), custom_call_target="tpu_custom_call" | custom-call | tf_op jit(solution)/shard_map/exchange_1/pallas_call | solution.py:796
  162.2 2.5 slice.172
  166.3 2.1 reshape.409
  168.4 2.2 reshape.447
  170.6 2.0 pad_maximum_fusion.6
  172.6 1.9 copy.171
  180.5 3.8 fusion.50
  186.0 2.6 convolution_convert_fusion.2.ex_ref
  190.7 11.5 %attend.1 = (bf16[1024,256]{1,0:T(8,128)(2,1)S(1)}, f32[1024,2]{1,0:T(8,128)S(1)}) custom-call(s32[1024,1]{1,0:T(8,128)S(1)} %copy.176.low_ref, bf16[1024,256]{1,0:T(8,128)(2,1)S(1)} %convolution_convert_fusion.8.qn_ref, bf16[1024,128]{1,0:T(8,128)(2,1)S(1)} %fusion.17.qr_ref, bf16[2048,512]{1,0:T(8,128)(2,1)} %convolution_convert_fusion.2.ex_ref, ...), custom_call_target="tpu_custom_call" | custom-call | flops 1677721600 | bytes 4194304 | tf_op jit(solution)/shard_map/attend/pallas_call | solution.py:117
  203.0 3.3 convolution_convert_fusion
  206.3 49.6 %exchange_2.1 = f32[128,2048]{1,0:T(8,128)} custom-call(bf16[8,128,2048]{2,1,0:T(8,128)(2,1)} %bitcast.136), custom_call_target="tpu_custom_call" | custom-call | tf_op jit(solution)/shard_map/exchange_2/pallas_call | solution.py:796
  258.2 2.2 reshape.413
  266.4 2.6 pad_maximum_fusion.5
  272.7 107.7 %exchange_5.1 = (bf16[4,8,128,2048]{3,2,1,0:T(8,128)(2,1)}, bf16[4,8,64,176]{3,2,1,0:T(8,128)(2,1)}) custom-call(bf16[128,2048]{1,0:T(8,128)(2,1)} %multiply_convert_fusion.3.refs_0_, bf16[4,8,64,176]{3,2,1,0:T(8,128)(2,1)} %bitcast.150), custom_call_target="tpu_custom_call" | custom-call | tf_op jit(solution)/shard_map/exchange_5/pallas_call | solution.py:796
  381.3 2.6 fusion.45
  385.6 4.0 concatenate.61.sc_ref
  392.8 5.2 multiply_convert_fusion
  398.1 142.8 %experts.1 = (f32[128,2048]{1,0:T(8,128)}, bf16[3072,2048]{1,0:T(8,128)(2,1)}, bf16[3072,2048]{1,0:T(8,128)(2,1)}, bf16[3072,704]{1,0:T(8,128)(2,1)}, bf16[3072,...) custom-call(bf16[4096,2048]{1,0:T(8,128)(2,1)} %bitcast.185, ...), custom_call_target="tpu_custom_call" | custom-call | flops 57713623040 | bytes 100663296 | tf_op jit(solution)/shard_map/experts/pallas_call | solution.py:1222
  540.9 5.2 all-to-all-start
  548.7 102.8 %expert_out.1 = (f32[128,2048]{1,0:T(8,128)}, f32[704,2048]{1,0:T(8,128)}, f32[704,2048]{1,0:T(8,128)}, f32[704,2048]{1,0:T(8,128)}) custom-call(bf16[3072,704]{1,0:T(8,128)(2,1)} %get-tuple-element.68.act_ref, f32[3072,1]{1,0:T(8,128)} %get-tuple-element.69.rw_ref, bf16[3072,2048]{1,0:T(8,128)(2,1)} %get-tuple-element.70.rows_ref, ...), custom_call_target="tpu_custom_call" | custom-call | flops 39191576576 | bytes 33554432 | tf_op jit(solution)/shard_map/expert_out/pallas_call | solution.py:1255
  654.5 2.0 slice.159
  658.6 2.4 multiply_reduce_fusion.2
  663.1 42.2 %exchange_3.1 = (bf16[4,8,64,176]{3,2,1,0:T(8,128)(2,1)}, bf16[8,128,2048]{2,1,0:T(8,128)(2,1)}) custom-call(bf16[4,8,64,176]{3,2,1,0:T(8,128)(2,1)} %bitcast.149, bf16[128,2048]{1,0:T(8,128)(2,1)} %fusion.42.refs_1_), custom_call_target="tpu_custom_call" | custom-call | tf_op jit(solution)/shard_map/exchange_3/pallas_call | solution.py:796
  705.4 4.4 convolution_convert_fusion.7.gm_ref
  709.8 2.3 convolution_convert_fusion.3
  712.1 20.9 %attend_back.1 = (f32[1024,256]{1,0:T(8,128)}, f32[1024,128]{1,0:T(8,128)}, f32[2048,512]{1,0:T(8,128)}, f32[2048,64]{1,0:T(8,128)}) custom-call(s32[1024,1]{1,0:T(8,128)} %copy-done.2, bf16[1024,256]{1,0:T(8,128)(2,1)} %copy-done.5, bf16[1024,128]{1,0:T(8,128)(2,1)} %copy-done.4, bf16[2048,512]{1,0:T(8,128)(2,1)} %convolution_convert_fusion.2.ex_ref, ...), custom_call_target="tpu_custom_call" | custom-call | flops 4362076160 | bytes 8388608 | tf_op jit(solution)/shard_map/attend_back/pallas_call | solution.py:192
  733.0 2.6 convert_element_type.208
  735.8 2.1 fusion.1
  741.1 2.1 convolution_convert_fusion.5
  743.2 2.4 convolution_convert_fusion.4
  745.6 3.3 add_convert_fusion
  752.4 62.7 %exchange_4.1 = (f32[128,576]{1,0:T(8,128)}, f32[128,2048]{1,0:T(8,128)}, bf16[8,64,256]{2,1,0:T(8,128)(2,1)}, bf16[8,64,128]{2,1,0:T(8,128)(2,1)}, bf16[8,16,512]{2,1,0:T(8,128)(2,1)}) custom-call(bf16[8,256,576]{2,1,0:T(8,128)(2,1)} %bitcast.142, bf16[8,128,2048]{2,1,0:T(8,128)(2,1)} %bitcast.140, bf16[4,8,64,256]{3,2,1,0:T(8,128)(2,1)} %bitcast.165, ...), custom_call_target="tpu_custom_call" | custom-call | tf_op jit(solution)/shard_map/exchange_4/pallas_call | solution.py:796
  818.8 1.9 convolution_convert_fusion.1
  820.7 2.5 fusion.8
  824.7 1.8 reshape.432
  831.1 2.6 copy.188
  833.7 66.0 %exchange_6.1 = (f32[64,576]{1,0:T(8,128)}, f32[64,2048]{1,0:T(8,128)}, f32[16,128]{1,0:T(8,128)}) custom-call(bf16[4,8,64,576]{3,2,1,0:T(8,128)(2,1)} %bitcast.141, bf16[4,64,2048]{2,1,0:T(8,128)(2,1)} %bitcast.167, f32[4,8,16,128]{3,2,1,0:T(8,128)} %copy.207), custom_call_target="tpu_custom_call" | custom-call | tf_op jit(solution)/shard_map/exchange_6/pallas_call | solution.py:796
  912.1 2.7 reshape.437
  914.7 2.8 copy.194
  917.6 2.7 reshape.438
  920.3 3.4 fusion.4
  925.1 6.0 copy.217
  931.2 6.0 copy.218
  937.2 2.5 copy.219
  (309 shorter events, 88.2 us)
Async XLA Ops:
  7.2 6.4 copy-start.87
  7.2 6.4 copy-start.89
  7.2 6.4 copy-start.88
  7.2 74.9 %copy-start.26 = (bf16[128,2048]{1,0:T(8,128)(2,1)S(1)}, bf16[128,2048]{1,0:T(8,128)(2,1)}, u32[]{:S(2)}) copy-start(bf16[128,2048]{1,0:T(8,128)(2,1)} %param.35) | copy-start | bytes 1572868
  7.3 390.8 %all-gather.2.cloned.1.call-start = ((), (), s32[]{:S(2)}) async-start(), calls=%async_computation.1 | async-start | bytes 17301504 | tf_op jit(solution)/shard_map/all_gather | solution.py:815
  84.9 307.9 %copy-start.54 = (f32[2048]{0:T(1024)}, f32[2048]{0:T(1024)S(1)}, u32[]{:S(2)}) copy-start(f32[2048]{0:T(1024)S(1)} %reshape.440) | copy-start | bytes 24580
  84.9 14.0 %copy-start.63 = (f32[512]{0:T(512)}, f32[512]{0:T(512)S(1)}, u32[]{:S(2)}) copy-start(f32[512]{0:T(512)S(1)} %reshape.441) | copy-start | bytes 6148
  93.7 296.0 %copy-start.12 = (f32[1024,576]{1,0:T(8,128)}, f32[1024,576]{1,0:T(8,128)S(1)}, u32[]{:S(2)}) copy-start(f32[1024,576]{1,0:T(8,128)S(1)} %fusion.51) | copy-start | bytes 7077892
  98.9 71.7 %copy-start.34 = (f32[1024,32]{1,0:T(8,128)}, f32[1024,32]{1,0:T(8,128)S(1)}, u32[]{:S(2)}) copy-start(f32[1024,32]{1,0:T(8,128)S(1)} %get-tuple-element.195) | copy-start | bytes 393220
  179.1 11.5 %copy-start.2 = (s32[1024,1]{1,0:T(8,128)}, s32[1024,1]{1,0:T(8,128)S(1)}, u32[]{:S(2)}) copy-start(s32[1024,1]{1,0:T(8,128)S(1)} %copy.176.low_ref) | copy-start | bytes 12292
  180.5 10.1 %copy-start.3 = (bf16[2048,64]{1,0:T(8,128)(2,1)}, bf16[2048,64]{1,0:T(8,128)(2,1)S(1)}, u32[]{:S(2)}) copy-start(bf16[2048,64]{1,0:T(8,128)(2,1)S(1)} %maximum_maximum_fusion.kr_ref) | copy-start | bytes 786436
  190.6 15.6 %copy-start.5 = (bf16[1024,256]{1,0:T(8,128)(2,1)}, bf16[1024,256]{1,0:T(8,128)(2,1)S(1)}, u32[]{:S(2)}) copy-start(bf16[1024,256]{1,0:T(8,128)(2,1)S(1)} %convolution_convert_fusion.8.qn_ref) | copy-start | bytes 1572868
  190.7 12.3 %copy-start.45 = (bf16[4,64,2048]{2,1,0:T(8,128)(2,1)S(1)}, bf16[4,64,2048]{2,1,0:T(8,128)(2,1)}, u32[]{:S(2)}) copy-start(bf16[4,64,2048]{2,1,0:T(8,128)(2,1)} %get-tuple-element.65) | copy-start | bytes 3145732
  206.2 49.6 %copy-start.62 = (f32[32,64]{1,0:T(8,128)S(1)}, f32[32,64]{1,0:T(8,128)}, u32[]{:S(2)}) copy-start(f32[32,64]{1,0:T(8,128)} %get-tuple-element.191) | copy-start | bytes 24580
  206.3 49.7 %copy-start.51 = (bf16[64,2816]{1,0:T(8,128)(2,1)S(1)}, bf16[64,2816]{1,0:T(8,128)(2,1)}, u32[]{:S(2)}) copy-start(bf16[64,2816]{1,0:T(8,128)(2,1)} %param.27) | copy-start | bytes 1081348
  255.9 14.9 %copy-start.56 = (f32[2048]{0:T(1024)}, f32[2048]{0:T(1024)S(1)}, u32[]{:S(2)}) copy-start(f32[2048]{0:T(1024)S(1)} %reshape.442) | copy-start | bytes 24580
  262.7 127.1 %copy-start.16 = (bf16[2048,16]{1,0:T(8,128)(2,1)}, bf16[2048,16]{1,0:T(8,128)(2,1)S(1)}, u32[]{:S(2)}) copy-start(bf16[2048,16]{1,0:T(8,128)(2,1)S(1)} %reshape.418) | copy-start | bytes 196612
  264.2 116.2 %copy-start.52 = (bf16[88,2048]{1,0:T(8,128)(2,1)S(1)}, bf16[88,2048]{1,0:T(8,128)(2,1)}, u32[]{:S(2)}) copy-start(bf16[88,2048]{1,0:T(8,128)(2,1)} %param.29) | copy-start | bytes 1081348
  270.7 114.9 %copy-start.84 = (f32[128]{0:T(128)}, f32[128]{0:T(128)S(1)}, u32[]{:S(2)}) copy-start(f32[128]{0:T(128)S(1)} %get-tuple-element.168) | copy-start | bytes 1540
  270.7 121.5 %copy-start.80 = (f32[128]{0:T(128)}, f32[128]{0:T(128)S(1)}, u32[]{:S(2)}) copy-start(f32[128]{0:T(128)S(1)} %get-tuple-element.182) | copy-start | bytes 1540
  270.8 118.9 %copy-start.67 = (f32[128]{0:T(128)}, f32[128]{0:T(128)S(1)}, u32[]{:S(2)}) copy-start(f32[128]{0:T(128)S(1)} %fusion.34) | copy-start | bytes 1540
  389.8 8.2 copy-start.82
  391.2 6.9 copy-start.59
  391.2 6.9 copy-start.70
  540.9 115.6 %all-to-all-start = ((f32[32,1,128]{2,1,0:T(1,128)}), f32[32,1,128]{2,1,0:T(1,128)}, u32[]{:S(2)}, u32[]{:S(2)}) async-start(f32[32,1,128]{2,1,0:T(1,128)} %bitcast.182), calls=%async_computation | async-start | bytes 32768 | tf_op jit(solution)/shard_map/all_to_all | solution.py:1441
  651.6 7.0 copy-start.9
  651.6 7.0 copy-start.17
  651.7 7.0 copy-start.57
  651.7 7.0 copy-start.68
  653.0 8.0 copy-start.85
  653.0 9.0 copy-start.27
  661.0 44.3 %copy-start.46 = (bf16[4,64,2048]{2,1,0:T(8,128)(2,1)S(1)}, bf16[4,64,2048]{2,1,0:T(8,128)(2,1)}, u32[]{:S(2)}) copy-start(bf16[4,64,2048]{2,1,0:T(8,128)(2,1)} %get-tuple-element.65) | copy-start | bytes 3145732
  661.0 48.8 %copy-start.77 = (f32[128]{0:T(128)}, f32[128]{0:T(128)S(1)}, u32[]{:S(2)}) copy-start(f32[128]{0:T(128)S(1)} %multiply_multiply_fusion.2) | copy-start | bytes 1540
  752.4 64.0 %copy-start.64 = (f32[512]{0:T(512)S(1)}, f32[512]{0:T(512)}, u32[]{:S(2)}) copy-start(f32[512]{0:T(512)} %copy-done.63) | copy-start | bytes 6148
  752.4 64.0 %copy-start.79 = (f32[128]{0:T(128)S(1)}, f32[128]{0:T(128)}, u32[]{:S(2)}) copy-start(f32[128]{0:T(128)} %fusion.35) | copy-start | bytes 1540
  752.4 65.3 %copy-start.83 = (f32[128]{0:T(128)S(1)}, f32[128]{0:T(128)}, u32[]{:S(2)}) copy-start(f32[128]{0:T(128)} %copy-done.82) | copy-start | bytes 1540
  833.6 69.3 %copy-start.53 = (bf16[8,64,256]{2,1,0:T(8,128)(2,1)S(1)}, bf16[8,64,256]{2,1,0:T(8,128)(2,1)}, u32[]{:S(2)}) copy-start(bf16[8,64,256]{2,1,0:T(8,128)(2,1)} %get-tuple-element.88) | copy-start | bytes 786436
  833.6 69.5 %copy-start.61 = (bf16[8,64,128]{2,1,0:T(8,128)(2,1)S(1)}, bf16[8,64,128]{2,1,0:T(8,128)(2,1)}, u32[]{:S(2)}) copy-start(bf16[8,64,128]{2,1,0:T(8,128)(2,1)} %get-tuple-element.89) | copy-start | bytes 393220
  833.6 73.5 %copy-start.81 = (f32[128]{0:T(128)S(1)}, f32[128]{0:T(128)}, u32[]{:S(2)}) copy-start(f32[128]{0:T(128)} %copy-done.80) | copy-start | bytes 1540
  833.6 73.5 %copy-start.86 = (f32[128]{0:T(128)S(1)}, f32[128]{0:T(128)}, u32[]{:S(2)}) copy-start(f32[128]{0:T(128)} %get-tuple-element.167) | copy-start | bytes 1540
  833.7 75.2 %copy-start.40 = (bf16[4,8,64,176]{3,2,1,0:T(8,128)(2,1)S(1)}, bf16[4,8,64,176]{3,2,1,0:T(8,128)(2,1)}, u32[]{:S(2)}) copy-start(bf16[4,8,64,176]{3,2,1,0:T(8,128)(2,1)} %get-tuple-element.93) | copy-start | bytes 2162692
  910.5 9.8 %copy-start.15 = (f32[128,2048]{1,0:T(8,128)S(1)}, f32[128,2048]{1,0:T(8,128)}, u32[]{:S(2)}) copy-start(f32[128,2048]{1,0:T(8,128)} %copy-done.14) | copy-start | bytes 3145732
  910.5 9.8 %copy-start.20 = (bf16[128,2048]{1,0:T(8,128)(2,1)S(1)}, bf16[128,2048]{1,0:T(8,128)(2,1)}, u32[]{:S(2)}) copy-start(bf16[128,2048]{1,0:T(8,128)(2,1)} %refs_5_.1) | copy-start | bytes 1572868
  910.5 9.8 %copy-start.28 = (bf16[128,2048]{1,0:T(8,128)(2,1)S(1)}, bf16[128,2048]{1,0:T(8,128)(2,1)}, u32[]{:S(2)}) copy-start(bf16[128,2048]{1,0:T(8,128)(2,1)} %param.35) | copy-start | bytes 1572868
  910.5 9.8 %copy-start.69 = (f32[128]{0:T(128)S(1)}, f32[128]{0:T(128)}, u32[]{:S(2)}) copy-start(f32[128]{0:T(128)} %copy-done.67) | copy-start | bytes 1540
  910.5 9.8 %copy-start.76 = (f32[128]{0:T(128)S(1)}, f32[128]{0:T(128)}, u32[]{:S(2)}) copy-start(f32[128]{0:T(128)} %fusion.36) | copy-start | bytes 1540
  910.5 9.8 %copy-start.78 = (f32[128]{0:T(128)S(1)}, f32[128]{0:T(128)}, u32[]{:S(2)}) copy-start(f32[128]{0:T(128)} %copy-done.77) | copy-start | bytes 1540
  925.1 12.0 %slice-start = ((s8[5767168]{0:T(1024)(128)(4,1)}), s8[4194304]{0:T(1024)(128)(4,1)S(1)}, s32[]{:S(2)}) async-start(s8[5767168]{0:T(1024)(128)(4,1)} %bitcast.144), calls=%async_computation.2 | async-start | bytes 8388608
  (49 other events, 180.3 us)
Sparse Core Ops, SparseCore 0:
  83.1 132.0 all-gather.1

commit v11 on v10

--- a/solution.py
+++ b/solution.py
@@ -1101,6 +1101,7 @@
         )
         stream.stage[slot, q] = total.astype(BF)
     stream.push(step)
+    stream.advance(step)
 
     piece = h2.shape[1] // 4
     turned, turned_act = shared_grad.T, shared_act.T
@@ -1108,7 +1109,6 @@
         cols = slice(k * piece, (k + 1) * piece)
         dboth_ref[:, cols] += jnp.dot(turned, h2[:, cols], preferred_element_type=F32)
         dsd_ref[:, cols] += jnp.dot(turned_act, cot[:, cols], preferred_element_type=F32)
-    stream.advance(step)
 
     @pl.when(step == steps - 1)
     def _():
@@ -1363,7 +1363,7 @@
     )
     s_both = s_both.transpose(1, 0, 2).reshape(n_groups, n_plane, rows_w, 2 * shared_n)
 
-    hidden = rms_norm(x_plane, gain_one).astype(BF)
+    hidden = lax.optimization_barrier(rms_norm(x_plane, gain_one).astype(BF))
     rope_half = ROPE // 2
     positions = plane_start + jnp.arange(plane_tok, dtype=jnp.int32)
     frequency = 10000.0 ** (-jnp.arange(rope_half, dtype=F32) / rope_half)
@@ -1403,7 +1403,12 @@
     low_bound = doc_start - plane_start + DOC_MAX
     mixed_heads, lse = attend(low_bound, q_nope, q_rope, expanded, key_rope, scale)
     attn_out = matmul(mixed_heads, own_output).astype(BF)
-    attn_out = swap(2, ("plane_sum", attn_out.reshape(n_plane, tok, width)))[0]
+    parts = max(1, devices * tok // 4096)
+    attn_out, s_both = swap(
+        2,
+        ("plane_sum", attn_out.reshape(n_plane, tok, width)),
+        ("whole_swap", s_both),
+    )
     input_float = layer_input.astype(F32)
     residual_one = input_float + attn_out
     h_two_f, norm_two_back = jax.vjp(rms_norm, residual_one, gain_two)
@@ -1411,11 +1416,8 @@
     router_probs = softmax_rows(matmul(h_two, router_weight))
 
     expert_w = (expert_gate[0].T, expert_up[0].T, expert_down[0])
-    parts = max(1, devices * tok // 4096)
     if parts == 1:
-        h2_all, s_both = swap(5, ("far_gather", h_two), ("whole_swap", s_both))
-    else:
-        s_both = swap(7, ("whole_swap", s_both))[0]
+        h2_all = swap(5, ("far_gather", h_two))[0]
     shared_w = (s_both.reshape(width, 2 * shared_n), shared_down)
     slot_limit = 2 * tok * TOP // experts
 

time: 950 us -> 950 us (level)
  Pallas kernels: 732 us -> 721 us
    unnamed x198 -> x186, local copies, waits for them, and re-layouts: 27.1 us -> 27.5 us
  transfers between devices with their start and end apart: 2 -> 2, of which waited for: 0 -> 0; matrix products, arithmetic and copies ran while one was open for 9% -> 9% of each run, Pallas kernels for 35% -> 34%
where the time goes in v11:
time: 950 us; the launch traced here: 940 us
  Pallas kernels  721 us (76%)
  local copies, waits for them, and re-layouts  107 us (11%)
  matrix products  47.3 us (5%)
  other arithmetic  41.4 us (4%)
  between operations  16.3 us (2%)
    pallas_call x7, Pallas kernels, exchange(): pl.pallas_call(functools.partial(exchange_kernel, n_groups, n_plane, kind...  446 us
    pallas_call x1, Pallas kernels, experts_sums(): pl.pallas_call(functools.partial(moe_kernel, n_groups, experts, hidden_s,...  139 us
    pallas_call x1, Pallas kernels, experts_sums(): pl.pallas_call(functools.partial(out_kernel, n_groups, slot_count), grid=...  103 us
    unnamed x186, local copies, waits for them, and re-layouts  27.5 us
    pallas_call x1, Pallas kernels, attend_back(): pl.pallas_call(functools.partial(attend_back_kernel, heads, scale), grid=...  20.7 us
  transfers between devices with their start and end apart: 2, of which 0 were waited for; matrix products, arithmetic and copies ran while one was open for 9% of the time, Pallas kernels for 34%

profile of v11, /device:TPU:1, one launch (start us, length us, event | category | flops | bytes accessed | tf_op | source)
XLA Modules:
  0.0 939.8 jit_solution(10511161249093798636)
XLA Ops:
  14.3 65.9 %exchange_0.1 = (bf16[4,8,64,256]{3,2,1,0:T(8,128)(2,1)}, bf16[4,8,64,128]{3,2,1,0:T(8,128)(2,1)}, bf16[4,8,64,128]{3,2,1,0:T(8,128)(2,1)}, bf16[4,8,64,576]{3,2...) custom-call(bf16[8,64,256]{2,1,0:T(8,128)(2,1)} %reshape.365.refs_0_, ...), custom_call_target="tpu_custom_call" | custom-call | tf_op jit(solution)/shard_map/exchange_0/pallas_call | solution.py:796
  81.4 3.2 multiply_reduce_fusion
  84.8 3.1 multiply_convert_fusion
  90.1 6.0 fusion.50
  98.1 3.3 fusion.13
  103.4 55.6 %exchange_1.1 = (bf16[8,128,576]{2,1,0:T(8,128)(2,1)}, bf16[4,64,2048]{2,1,0:T(8,128)(2,1)}) custom-call(bf16[128,576]{1,0:T(8,128)(2,1)} %fusion.26.refs_0_, bf16[64,2048]{1,0:T(8,128)(2,1)} %refs_1_.1), custom_call_target="tpu_custom_call" | custom-call | tf_op jit(solution)/shard_map/exchange_1/pallas_call | solution.py:796
  159.0 2.3 slice.172
  163.6 2.1 reshape.376
  165.8 2.1 reshape.414
  168.2 2.4 pad_maximum_fusion.6
  180.6 3.0 reshape.380
  183.6 2.0 copy.178
  185.6 3.0 reshape.379
  188.6 2.1 copy.177
  190.8 2.7 pad_maximum_fusion.5
  194.8 3.8 fusion.49
  200.2 2.6 convolution_convert_fusion.2.ex_ref
  205.0 11.7 %attend.1 = (bf16[1024,256]{1,0:T(8,128)(2,1)S(1)}, f32[1024,2]{1,0:T(8,128)S(1)}) custom-call(s32[1024,1]{1,0:T(8,128)S(1)} %copy.176.low_ref, bf16[1024,256]{1,0:T(8,128)(2,1)S(1)} %convolution_convert_fusion.8.qn_ref, bf16[1024,128]{1,0:T(8,128)(2,1)S(1)} %fusion.17.qr_ref, bf16[2048,512]{1,0:T(8,128)(2,1)} %convolution_convert_fusion.2.ex_ref, ...), custom_call_target="tpu_custom_call" | custom-call | flops 1677721600 | bytes 4194304 | tf_op jit(solution)/shard_map/attend/pallas_call | solution.py:117
  217.5 3.3 convolution_convert_fusion
  220.8 60.0 %exchange_2.1 = (f32[128,2048]{1,0:T(8,128)}, bf16[4,8,64,176]{3,2,1,0:T(8,128)(2,1)}) custom-call(bf16[8,128,2048]{2,1,0:T(8,128)(2,1)} %bitcast.133, bf16[4,8,64,176]{3,2,1,0:T(8,128)(2,1)} %bitcast.146), custom_call_target="tpu_custom_call" | custom-call | tf_op jit(solution)/shard_map/exchange_2/pallas_call | solution.py:796
  284.3 93.8 %exchange_5.1 = bf16[4,8,128,2048]{3,2,1,0:T(8,128)(2,1)} custom-call(bf16[128,2048]{1,0:T(8,128)(2,1)} %multiply_convert_fusion.2.refs_0_), custom_call_target="tpu_custom_call" | custom-call | tf_op jit(solution)/shard_map/exchange_5/pallas_call | solution.py:796
  380.5 2.1 reshape.385
  383.4 2.5 fusion.44
  387.7 4.1 concatenate.61.sc_ref
  395.5 139.5 %experts.1 = (f32[128,2048]{1,0:T(8,128)}, bf16[3072,2048]{1,0:T(8,128)(2,1)}, bf16[3072,2048]{1,0:T(8,128)(2,1)}, bf16[3072,704]{1,0:T(8,128)(2,1)}, bf16[3072,...) custom-call(bf16[4096,2048]{1,0:T(8,128)(2,1)} %bitcast.135, ...), custom_call_target="tpu_custom_call" | custom-call | flops 57713623040 | bytes 100663296 | tf_op jit(solution)/shard_map/experts/pallas_call | solution.py:1222
  537.6 6.7 all-to-all-start
  544.3 102.7 %expert_out.1 = (f32[128,2048]{1,0:T(8,128)}, f32[704,2048]{1,0:T(8,128)}, f32[704,2048]{1,0:T(8,128)}, f32[704,2048]{1,0:T(8,128)}) custom-call(bf16[3072,704]{1,0:T(8,128)(2,1)} %get-tuple-element.68.act_ref, f32[3072,1]{1,0:T(8,128)} %get-tuple-element.69.rw_ref, bf16[3072,2048]{1,0:T(8,128)(2,1)} %get-tuple-element.70.rows_ref, ...), custom_call_target="tpu_custom_call" | custom-call | flops 39191576576 | bytes 33554432 | tf_op jit(solution)/shard_map/expert_out/pallas_call | solution.py:1255
  652.6 2.4 multiply_reduce_fusion.2
  657.2 42.4 %exchange_3.1 = (bf16[4,8,64,176]{3,2,1,0:T(8,128)(2,1)}, bf16[8,128,2048]{2,1,0:T(8,128)(2,1)}) custom-call(bf16[4,8,64,176]{3,2,1,0:T(8,128)(2,1)} %bitcast.145, bf16[128,2048]{1,0:T(8,128)(2,1)} %fusion.41.refs_1_), custom_call_target="tpu_custom_call" | custom-call | tf_op jit(solution)/shard_map/exchange_3/pallas_call | solution.py:796
  699.6 4.3 convolution_convert_fusion.7.gm_ref
  703.9 20.7 %attend_back.1 = (f32[1024,256]{1,0:T(8,128)}, f32[1024,128]{1,0:T(8,128)}, f32[2048,512]{1,0:T(8,128)}, f32[2048,64]{1,0:T(8,128)}) custom-call(s32[1024,1]{1,0:T(8,128)} %copy-done.2, bf16[1024,256]{1,0:T(8,128)(2,1)} %copy-done.5, bf16[1024,128]{1,0:T(8,128)(2,1)} %copy-done.4, bf16[2048,512]{1,0:T(8,128)(2,1)} %convolution_convert_fusion.2.ex_ref, ...), custom_call_target="tpu_custom_call" | custom-call | flops 4362076160 | bytes 8388608 | tf_op jit(solution)/shard_map/attend_back/pallas_call | solution.py:192
  724.6 2.2 fusion.45
  729.6 2.1 convolution_convert_fusion.5
  732.1 2.2 convolution_convert_fusion.3
  737.2 2.1 fusion.1
  742.7 2.3 convolution_convert_fusion.4
  745.0 3.3 add_convert_fusion
  748.4 62.5 %exchange_4.1 = (f32[128,576]{1,0:T(8,128)}, f32[128,2048]{1,0:T(8,128)}, bf16[8,64,256]{2,1,0:T(8,128)(2,1)}, bf16[8,64,128]{2,1,0:T(8,128)(2,1)}, bf16[8,16,512]{2,1,0:T(8,128)(2,1)}) custom-call(bf16[8,256,576]{2,1,0:T(8,128)(2,1)} %bitcast.137, bf16[8,128,2048]{2,1,0:T(8,128)(2,1)} %bitcast.134, bf16[4,8,64,256]{3,2,1,0:T(8,128)(2,1)} %bitcast.161, ...), custom_call_target="tpu_custom_call" | custom-call | tf_op jit(solution)/shard_map/exchange_4/pallas_call | solution.py:796
  816.8 2.6 copy.188
  819.4 4.3 fusion.8
  825.5 66.1 %exchange_6.1 = (f32[64,576]{1,0:T(8,128)}, f32[64,2048]{1,0:T(8,128)}, f32[16,128]{1,0:T(8,128)}) custom-call(bf16[4,8,64,576]{3,2,1,0:T(8,128)(2,1)} %bitcast.136, bf16[4,64,2048]{2,1,0:T(8,128)(2,1)} %bitcast.163, f32[4,8,16,128]{3,2,1,0:T(8,128)} %copy.207), custom_call_target="tpu_custom_call" | custom-call | tf_op jit(solution)/shard_map/exchange_6/pallas_call | solution.py:796
  904.9 2.7 reshape.404
  907.6 2.8 copy.194
  910.4 2.7 reshape.405
  913.1 3.4 fusion.4
  918.0 6.0 copy.217
  924.0 6.0 copy.218
  930.0 2.5 copy.219
  (295 shorter events, 86.4 us)
Async XLA Ops:
  7.2 5.8 copy-start.69
  7.2 6.0 copy-start.70
  7.2 6.3 copy-start.85
  7.2 6.3 copy-start.81
  7.2 6.3 copy-start.82
  7.2 6.3 copy-start.83
  7.2 388.3 %all-gather.2.cloned.1.call-start = ((), (), s32[]{:S(2)}) async-start(), calls=%async_computation.1 | async-start | bytes 17301504 | tf_op jit(solution)/shard_map/all_gather | solution.py:815
  81.2 81.7 %copy-start.44 = (bf16[4,8,32,128]{3,1,2,0:T(8,128)(2,1)}, bf16[4,8,32,128]{3,1,2,0:T(8,128)(2,1)S(1)}, u32[]{:S(2)}) copy-start(bf16[4,8,32,128]{3,1,2,0:T(8,128)(2,1)S(1)} %copy.208) | copy-start | bytes 786436
  81.4 6.5 copy-start.57
  90.0 11.4 %copy-start.60 = (f32[512]{0:T(512)}, f32[512]{0:T(512)S(1)}, u32[]{:S(2)}) copy-start(f32[512]{0:T(512)S(1)} %reshape.409) | copy-start | bytes 6148
  96.1 295.7 %copy-start.12 = (f32[1024,576]{1,0:T(8,128)}, f32[1024,576]{1,0:T(8,128)S(1)}, u32[]{:S(2)}) copy-start(f32[1024,576]{1,0:T(8,128)S(1)} %fusion.50) | copy-start | bytes 7077892
  101.4 64.4 %copy-start.33 = (bf16[1024,32]{1,0:T(8,128)(2,1)}, bf16[1024,32]{1,0:T(8,128)(2,1)S(1)}, u32[]{:S(2)}) copy-start(bf16[1024,32]{1,0:T(8,128)(2,1)S(1)} %get-tuple-element.173) | copy-start | bytes 196612
  168.2 36.8 %copy-start.2 = (s32[1024,1]{1,0:T(8,128)}, s32[1024,1]{1,0:T(8,128)S(1)}, u32[]{:S(2)}) copy-start(s32[1024,1]{1,0:T(8,128)S(1)} %copy.176.low_ref) | copy-start | bytes 12292
  190.8 91.6 %copy-start.51 = (f32[2048]{0:T(1024)}, f32[2048]{0:T(1024)S(1)}, u32[]{:S(2)}) copy-start(f32[2048]{0:T(1024)S(1)} %reshape.410) | copy-start | bytes 24580
  194.8 10.2 %copy-start.3 = (bf16[2048,64]{1,0:T(8,128)(2,1)}, bf16[2048,64]{1,0:T(8,128)(2,1)S(1)}, u32[]{:S(2)}) copy-start(bf16[2048,64]{1,0:T(8,128)(2,1)S(1)} %maximum_maximum_fusion.kr_ref) | copy-start | bytes 786436
  205.0 15.8 %copy-start.5 = (bf16[1024,256]{1,0:T(8,128)(2,1)}, bf16[1024,256]{1,0:T(8,128)(2,1)S(1)}, u32[]{:S(2)}) copy-start(bf16[1024,256]{1,0:T(8,128)(2,1)S(1)} %convolution_convert_fusion.8.qn_ref) | copy-start | bytes 1572868
  205.0 12.5 %copy-start.42 = (bf16[4,64,2048]{2,1,0:T(8,128)(2,1)S(1)}, bf16[4,64,2048]{2,1,0:T(8,128)(2,1)}, u32[]{:S(2)}) copy-start(bf16[4,64,2048]{2,1,0:T(8,128)(2,1)} %get-tuple-element.65) | copy-start | bytes 3145732
  220.8 60.0 %copy-start.19 = (bf16[128,2048]{1,0:T(8,128)(2,1)S(1)}, bf16[128,2048]{1,0:T(8,128)(2,1)}, u32[]{:S(2)}) copy-start(bf16[128,2048]{1,0:T(8,128)(2,1)} %refs_5_.1) | copy-start | bytes 1572868
  282.3 112.1 %copy-start.75 = (f32[128]{0:T(128)}, f32[128]{0:T(128)S(1)}, u32[]{:S(2)}) copy-start(f32[128]{0:T(128)S(1)} %get-tuple-element.184) | copy-start | bytes 1540
  282.4 95.7 %copy-start.62 = (f32[128]{0:T(128)}, f32[128]{0:T(128)S(1)}, u32[]{:S(2)}) copy-start(f32[128]{0:T(128)S(1)} %fusion.34) | copy-start | bytes 1540
  284.3 98.2 %copy-start.48 = (bf16[88,2048]{1,0:T(8,128)(2,1)S(1)}, bf16[88,2048]{1,0:T(8,128)(2,1)}, u32[]{:S(2)}) copy-start(bf16[88,2048]{1,0:T(8,128)(2,1)} %param.29) | copy-start | bytes 1081348
  380.5 11.5 %copy-start.16 = (bf16[128,2048]{1,0:T(8,128)(2,1)S(1)}, bf16[128,2048]{1,0:T(8,128)(2,1)}, u32[]{:S(2)}) copy-start(bf16[128,2048]{1,0:T(8,128)(2,1)} %multiply_convert_fusion.2.refs_0_) | copy-start | bytes 1572868
  537.6 114.1 %all-to-all-start = ((f32[32,1,128]{2,1,0:T(1,128)}), f32[32,1,128]{2,1,0:T(1,128)}, u32[]{:S(2)}, u32[]{:S(2)}) async-start(f32[32,1,128]{2,1,0:T(1,128)} %bitcast.28), calls=%async_computation | async-start | bytes 32768 | tf_op jit(solution)/shard_map/all_to_all | solution.py:1443
  647.1 5.4 copy-start.55
  647.1 5.4 copy-start.67
  647.1 5.5 copy-start.8
  647.1 5.5 copy-start.18
  647.1 5.5 copy-start.52
  647.1 5.5 copy-start.63
  647.1 7.9 copy-start.80
  647.2 8.9 copy-start.26
  652.6 47.0 %copy-start.43 = (bf16[4,64,2048]{2,1,0:T(8,128)(2,1)S(1)}, bf16[4,64,2048]{2,1,0:T(8,128)(2,1)}, u32[]{:S(2)}) copy-start(bf16[4,64,2048]{2,1,0:T(8,128)(2,1)} %get-tuple-element.65) | copy-start | bytes 3145732
  655.1 48.8 %copy-start.72 = (f32[128]{0:T(128)}, f32[128]{0:T(128)S(1)}, u32[]{:S(2)}) copy-start(f32[128]{0:T(128)S(1)} %multiply_multiply_fusion.2) | copy-start | bytes 1540
  748.4 63.6 %copy-start.61 = (f32[512]{0:T(512)S(1)}, f32[512]{0:T(512)}, u32[]{:S(2)}) copy-start(f32[512]{0:T(512)} %copy-done.60) | copy-start | bytes 6148
  748.4 63.6 %copy-start.74 = (f32[128]{0:T(128)S(1)}, f32[128]{0:T(128)}, u32[]{:S(2)}) copy-start(f32[128]{0:T(128)} %fusion.35) | copy-start | bytes 1540
  748.4 65.4 %copy-start.78 = (f32[128]{0:T(128)S(1)}, f32[128]{0:T(128)}, u32[]{:S(2)}) copy-start(f32[128]{0:T(128)} %copy-done.77) | copy-start | bytes 1540
  823.7 71.2 %copy-start.76 = (f32[128]{0:T(128)S(1)}, f32[128]{0:T(128)}, u32[]{:S(2)}) copy-start(f32[128]{0:T(128)} %copy-done.75) | copy-start | bytes 1540
  823.7 71.2 %copy-start.56 = (bf16[8,64,128]{2,1,0:T(8,128)(2,1)S(1)}, bf16[8,64,128]{2,1,0:T(8,128)(2,1)}, u32[]{:S(2)}) copy-start(bf16[8,64,128]{2,1,0:T(8,128)(2,1)} %get-tuple-element.89) | copy-start | bytes 393220
  825.5 76.2 %copy-start.38 = (bf16[4,8,64,176]{3,2,1,0:T(8,128)(2,1)S(1)}, bf16[4,8,64,176]{3,2,1,0:T(8,128)(2,1)}, u32[]{:S(2)}) copy-start(bf16[4,8,64,176]{3,2,1,0:T(8,128)(2,1)} %get-tuple-element.93) | copy-start | bytes 2162692
  903.3 9.8 %copy-start.15 = (f32[128,2048]{1,0:T(8,128)S(1)}, f32[128,2048]{1,0:T(8,128)}, u32[]{:S(2)}) copy-start(f32[128,2048]{1,0:T(8,128)} %copy-done.14) | copy-start | bytes 3145732
  903.3 9.8 %copy-start.20 = (bf16[128,2048]{1,0:T(8,128)(2,1)S(1)}, bf16[128,2048]{1,0:T(8,128)(2,1)}, u32[]{:S(2)}) copy-start(bf16[128,2048]{1,0:T(8,128)(2,1)} %refs_5_.1) | copy-start | bytes 1572868
  903.3 9.8 %copy-start.27 = (bf16[128,2048]{1,0:T(8,128)(2,1)S(1)}, bf16[128,2048]{1,0:T(8,128)(2,1)}, u32[]{:S(2)}) copy-start(bf16[128,2048]{1,0:T(8,128)(2,1)} %param.35) | copy-start | bytes 1572868
  903.3 9.8 %copy-start.64 = (f32[128]{0:T(128)S(1)}, f32[128]{0:T(128)}, u32[]{:S(2)}) copy-start(f32[128]{0:T(128)} %copy-done.62) | copy-start | bytes 1540
  903.3 9.8 %copy-start.71 = (f32[128]{0:T(128)S(1)}, f32[128]{0:T(128)}, u32[]{:S(2)}) copy-start(f32[128]{0:T(128)} %fusion.36) | copy-start | bytes 1540
  903.4 9.8 %copy-start.73 = (f32[128]{0:T(128)S(1)}, f32[128]{0:T(128)}, u32[]{:S(2)}) copy-start(f32[128]{0:T(128)} %copy-done.72) | copy-start | bytes 1540
  910.4 6.1 copy-start.53
  918.0 12.0 %slice-start = ((s8[5767168]{0:T(1024)(128)(4,1)}), s8[4194304]{0:T(1024)(128)(4,1)S(1)}, s32[]{:S(2)}) async-start(s8[5767168]{0:T(1024)(128)(4,1)} %bitcast.140), calls=%async_computation.2 | async-start | bytes 8388608
  924.0 6.0 slice-start.1
  (42 other events, 114.6 us)
Sparse Core Ops, SparseCore 0:
  90.0 139.4 all-gather.1

commit v12 on v10

--- a/solution.py
+++ b/solution.py
@@ -1101,6 +1101,7 @@
         )
         stream.stage[slot, q] = total.astype(BF)
     stream.push(step)
+    stream.advance(step)
 
     piece = h2.shape[1] // 4
     turned, turned_act = shared_grad.T, shared_act.T
@@ -1108,7 +1109,6 @@
         cols = slice(k * piece, (k + 1) * piece)
         dboth_ref[:, cols] += jnp.dot(turned, h2[:, cols], preferred_element_type=F32)
         dsd_ref[:, cols] += jnp.dot(turned_act, cot[:, cols], preferred_element_type=F32)
-    stream.advance(step)
 
     @pl.when(step == steps - 1)
     def _():

time: 950 us -> 949 us (level)
  no operation moved by 1% of the time
where the time goes in v12:
time: 949 us; the launch traced here: 946 us
  Pallas kernels  731 us (77%)
  local copies, waits for them, and re-layouts  103 us (11%)
  other arithmetic  47.1 us (5%)
  matrix products  43.7 us (5%)
  between operations  16.2 us (2%)
    pallas_call x7, Pallas kernels, exchange(): pl.pallas_call(functools.partial(exchange_kernel, n_groups, n_plane, kind...  454 us
    pallas_call x1, Pallas kernels, experts_sums(): pl.pallas_call(functools.partial(moe_kernel, n_groups, experts, hidden_s,...  142 us
    pallas_call x1, Pallas kernels, experts_sums(): pl.pallas_call(functools.partial(out_kernel, n_groups, slot_count), grid=...  103 us
    unnamed x198, local copies, waits for them, and re-layouts  27.1 us
    pallas_call x1, Pallas kernels, attend_back(): pl.pallas_call(functools.partial(attend_back_kernel, heads, scale), grid=...  20.9 us
  transfers between devices with their start and end apart: 2, of which 0 were waited for; matrix products, arithmetic and copies ran while one was open for 9% of the time, Pallas kernels for 35%

profile of v12, /device:TPU:1, one launch (start us, length us, event | category | flops | bytes accessed | tf_op | source)
XLA Modules:
  0.0 945.7 jit_solution(14457067079978967022)
XLA Ops:
  14.3 66.0 %exchange_0.1 = (bf16[4,8,64,256]{3,2,1,0:T(8,128)(2,1)}, bf16[4,8,64,128]{3,2,1,0:T(8,128)(2,1)}, bf16[4,8,64,128]{3,2,1,0:T(8,128)(2,1)}, bf16[4,8,64,576]{3,2...) custom-call(bf16[8,64,256]{2,1,0:T(8,128)(2,1)} %reshape.398.refs_0_, ...), custom_call_target="tpu_custom_call" | custom-call | tf_op jit(solution)/shard_map/exchange_0/pallas_call | solution.py:796
  85.0 3.2 multiply_reduce_fusion
  90.2 3.4 fusion.51
  95.7 3.2 fusion.13
  100.9 59.6 %exchange_1.1 = (bf16[8,128,576]{2,1,0:T(8,128)(2,1)}, bf16[4,64,2048]{2,1,0:T(8,128)(2,1)}) custom-call(bf16[128,576]{1,0:T(8,128)(2,1)} %fusion.26.refs_0_, bf16[64,2048]{1,0:T(8,128)(2,1)} %refs_1_.1), custom_call_target="tpu_custom_call" | custom-call | tf_op jit(solution)/shard_map/exchange_1/pallas_call | solution.py:796
  162.2 2.5 slice.172
  166.3 2.1 reshape.409
  168.4 2.2 reshape.447
  170.6 2.0 pad_maximum_fusion.6
  172.6 1.9 copy.171
  180.5 3.8 fusion.50
  186.0 2.6 convolution_convert_fusion.2.ex_ref
  190.7 11.5 %attend.1 = (bf16[1024,256]{1,0:T(8,128)(2,1)S(1)}, f32[1024,2]{1,0:T(8,128)S(1)}) custom-call(s32[1024,1]{1,0:T(8,128)S(1)} %copy.176.low_ref, bf16[1024,256]{1,0:T(8,128)(2,1)S(1)} %convolution_convert_fusion.8.qn_ref, bf16[1024,128]{1,0:T(8,128)(2,1)S(1)} %fusion.17.qr_ref, bf16[2048,512]{1,0:T(8,128)(2,1)} %convolution_convert_fusion.2.ex_ref, ...), custom_call_target="tpu_custom_call" | custom-call | flops 1677721600 | bytes 4194304 | tf_op jit(solution)/shard_map/attend/pallas_call | solution.py:117
  203.0 3.3 convolution_convert_fusion
  206.3 49.6 %exchange_2.1 = f32[128,2048]{1,0:T(8,128)} custom-call(bf16[8,128,2048]{2,1,0:T(8,128)(2,1)} %bitcast.136), custom_call_target="tpu_custom_call" | custom-call | tf_op jit(solution)/shard_map/exchange_2/pallas_call | solution.py:796
  258.2 2.2 reshape.413
  266.4 2.6 pad_maximum_fusion.5
  272.7 107.7 %exchange_5.1 = (bf16[4,8,128,2048]{3,2,1,0:T(8,128)(2,1)}, bf16[4,8,64,176]{3,2,1,0:T(8,128)(2,1)}) custom-call(bf16[128,2048]{1,0:T(8,128)(2,1)} %multiply_convert_fusion.3.refs_0_, bf16[4,8,64,176]{3,2,1,0:T(8,128)(2,1)} %bitcast.150), custom_call_target="tpu_custom_call" | custom-call | tf_op jit(solution)/shard_map/exchange_5/pallas_call | solution.py:796
  381.3 2.6 fusion.45
  385.6 4.0 concatenate.61.sc_ref
  392.8 5.2 multiply_convert_fusion
  398.1 141.8 %experts.1 = (f32[128,2048]{1,0:T(8,128)}, bf16[3072,2048]{1,0:T(8,128)(2,1)}, bf16[3072,2048]{1,0:T(8,128)(2,1)}, bf16[3072,704]{1,0:T(8,128)(2,1)}, bf16[3072,...) custom-call(bf16[4096,2048]{1,0:T(8,128)(2,1)} %bitcast.185, ...), custom_call_target="tpu_custom_call" | custom-call | flops 57713623040 | bytes 100663296 | tf_op jit(solution)/shard_map/experts/pallas_call | solution.py:1222
  539.8 5.2 all-to-all-start
  547.7 102.9 %expert_out.1 = (f32[128,2048]{1,0:T(8,128)}, f32[704,2048]{1,0:T(8,128)}, f32[704,2048]{1,0:T(8,128)}, f32[704,2048]{1,0:T(8,128)}) custom-call(bf16[3072,704]{1,0:T(8,128)(2,1)} %get-tuple-element.68.act_ref, f32[3072,1]{1,0:T(8,128)} %get-tuple-element.69.rw_ref, bf16[3072,2048]{1,0:T(8,128)(2,1)} %get-tuple-element.70.rows_ref, ...), custom_call_target="tpu_custom_call" | custom-call | flops 39191576576 | bytes 33554432 | tf_op jit(solution)/shard_map/expert_out/pallas_call | solution.py:1255
  653.5 2.0 slice.159
  657.6 2.4 multiply_reduce_fusion.2
  662.1 42.2 %exchange_3.1 = (bf16[4,8,64,176]{3,2,1,0:T(8,128)(2,1)}, bf16[8,128,2048]{2,1,0:T(8,128)(2,1)}) custom-call(bf16[4,8,64,176]{3,2,1,0:T(8,128)(2,1)} %bitcast.149, bf16[128,2048]{1,0:T(8,128)(2,1)} %fusion.42.refs_1_), custom_call_target="tpu_custom_call" | custom-call | tf_op jit(solution)/shard_map/exchange_3/pallas_call | solution.py:796
  704.3 4.4 convolution_convert_fusion.7.gm_ref
  708.8 2.3 convolution_convert_fusion.3
  711.0 20.9 %attend_back.1 = (f32[1024,256]{1,0:T(8,128)}, f32[1024,128]{1,0:T(8,128)}, f32[2048,512]{1,0:T(8,128)}, f32[2048,64]{1,0:T(8,128)}) custom-call(s32[1024,1]{1,0:T(8,128)} %copy-done.2, bf16[1024,256]{1,0:T(8,128)(2,1)} %copy-done.5, bf16[1024,128]{1,0:T(8,128)(2,1)} %copy-done.4, bf16[2048,512]{1,0:T(8,128)(2,1)} %convolution_convert_fusion.2.ex_ref, ...), custom_call_target="tpu_custom_call" | custom-call | flops 4362076160 | bytes 8388608 | tf_op jit(solution)/shard_map/attend_back/pallas_call | solution.py:192
  732.0 2.6 convert_element_type.208
  734.8 2.1 fusion.1
  740.1 2.1 convolution_convert_fusion.5
  742.2 2.4 convolution_convert_fusion.4
  744.6 3.3 add_convert_fusion
  751.3 62.7 %exchange_4.1 = (f32[128,576]{1,0:T(8,128)}, f32[128,2048]{1,0:T(8,128)}, bf16[8,64,256]{2,1,0:T(8,128)(2,1)}, bf16[8,64,128]{2,1,0:T(8,128)(2,1)}, bf16[8,16,512]{2,1,0:T(8,128)(2,1)}) custom-call(bf16[8,256,576]{2,1,0:T(8,128)(2,1)} %bitcast.142, bf16[8,128,2048]{2,1,0:T(8,128)(2,1)} %bitcast.140, bf16[4,8,64,256]{3,2,1,0:T(8,128)(2,1)} %bitcast.165, ...), custom_call_target="tpu_custom_call" | custom-call | tf_op jit(solution)/shard_map/exchange_4/pallas_call | solution.py:796
  817.8 1.9 convolution_convert_fusion.1
  819.7 2.5 fusion.8
  823.6 1.8 reshape.432
  830.1 2.6 copy.188
  832.6 66.0 %exchange_6.1 = (f32[64,576]{1,0:T(8,128)}, f32[64,2048]{1,0:T(8,128)}, f32[16,128]{1,0:T(8,128)}) custom-call(bf16[4,8,64,576]{3,2,1,0:T(8,128)(2,1)} %bitcast.141, bf16[4,64,2048]{2,1,0:T(8,128)(2,1)} %bitcast.167, f32[4,8,16,128]{3,2,1,0:T(8,128)} %copy.207), custom_call_target="tpu_custom_call" | custom-call | tf_op jit(solution)/shard_map/exchange_6/pallas_call | solution.py:796
  911.1 2.7 reshape.437
  913.7 2.8 copy.194
  916.5 2.7 reshape.438
  919.3 3.4 fusion.4
  924.1 6.0 copy.217
  930.1 6.0 copy.218
  936.2 2.5 copy.219
  (309 shorter events, 88.2 us)
Async XLA Ops:
  7.2 6.4 copy-start.87
  7.2 6.4 copy-start.89
  7.2 6.4 copy-start.88
  7.2 74.9 %copy-start.26 = (bf16[128,2048]{1,0:T(8,128)(2,1)S(1)}, bf16[128,2048]{1,0:T(8,128)(2,1)}, u32[]{:S(2)}) copy-start(bf16[128,2048]{1,0:T(8,128)(2,1)} %param.35) | copy-start | bytes 1572868
  7.3 390.8 %all-gather.2.cloned.1.call-start = ((), (), s32[]{:S(2)}) async-start(), calls=%async_computation.1 | async-start | bytes 17301504 | tf_op jit(solution)/shard_map/all_gather | solution.py:815
  84.9 307.9 %copy-start.54 = (f32[2048]{0:T(1024)}, f32[2048]{0:T(1024)S(1)}, u32[]{:S(2)}) copy-start(f32[2048]{0:T(1024)S(1)} %reshape.440) | copy-start | bytes 24580
  84.9 14.0 %copy-start.63 = (f32[512]{0:T(512)}, f32[512]{0:T(512)S(1)}, u32[]{:S(2)}) copy-start(f32[512]{0:T(512)S(1)} %reshape.441) | copy-start | bytes 6148
  93.7 296.0 %copy-start.12 = (f32[1024,576]{1,0:T(8,128)}, f32[1024,576]{1,0:T(8,128)S(1)}, u32[]{:S(2)}) copy-start(f32[1024,576]{1,0:T(8,128)S(1)} %fusion.51) | copy-start | bytes 7077892
  98.9 71.7 %copy-start.34 = (f32[1024,32]{1,0:T(8,128)}, f32[1024,32]{1,0:T(8,128)S(1)}, u32[]{:S(2)}) copy-start(f32[1024,32]{1,0:T(8,128)S(1)} %get-tuple-element.195) | copy-start | bytes 393220
  179.1 11.5 %copy-start.2 = (s32[1024,1]{1,0:T(8,128)}, s32[1024,1]{1,0:T(8,128)S(1)}, u32[]{:S(2)}) copy-start(s32[1024,1]{1,0:T(8,128)S(1)} %copy.176.low_ref) | copy-start | bytes 12292
  180.5 10.1 %copy-start.3 = (bf16[2048,64]{1,0:T(8,128)(2,1)}, bf16[2048,64]{1,0:T(8,128)(2,1)S(1)}, u32[]{:S(2)}) copy-start(bf16[2048,64]{1,0:T(8,128)(2,1)S(1)} %maximum_maximum_fusion.kr_ref) | copy-start | bytes 786436
  190.6 15.6 %copy-start.5 = (bf16[1024,256]{1,0:T(8,128)(2,1)}, bf16[1024,256]{1,0:T(8,128)(2,1)S(1)}, u32[]{:S(2)}) copy-start(bf16[1024,256]{1,0:T(8,128)(2,1)S(1)} %convolution_convert_fusion.8.qn_ref) | copy-start | bytes 1572868
  190.7 12.3 %copy-start.45 = (bf16[4,64,2048]{2,1,0:T(8,128)(2,1)S(1)}, bf16[4,64,2048]{2,1,0:T(8,128)(2,1)}, u32[]{:S(2)}) copy-start(bf16[4,64,2048]{2,1,0:T(8,128)(2,1)} %get-tuple-element.65) | copy-start | bytes 3145732
  206.2 49.6 %copy-start.62 = (f32[32,64]{1,0:T(8,128)S(1)}, f32[32,64]{1,0:T(8,128)}, u32[]{:S(2)}) copy-start(f32[32,64]{1,0:T(8,128)} %get-tuple-element.191) | copy-start | bytes 24580
  206.3 49.7 %copy-start.51 = (bf16[64,2816]{1,0:T(8,128)(2,1)S(1)}, bf16[64,2816]{1,0:T(8,128)(2,1)}, u32[]{:S(2)}) copy-start(bf16[64,2816]{1,0:T(8,128)(2,1)} %param.27) | copy-start | bytes 1081348
  255.9 14.9 %copy-start.56 = (f32[2048]{0:T(1024)}, f32[2048]{0:T(1024)S(1)}, u32[]{:S(2)}) copy-start(f32[2048]{0:T(1024)S(1)} %reshape.442) | copy-start | bytes 24580
  262.7 127.1 %copy-start.16 = (bf16[2048,16]{1,0:T(8,128)(2,1)}, bf16[2048,16]{1,0:T(8,128)(2,1)S(1)}, u32[]{:S(2)}) copy-start(bf16[2048,16]{1,0:T(8,128)(2,1)S(1)} %reshape.418) | copy-start | bytes 196612
  264.2 116.2 %copy-start.52 = (bf16[88,2048]{1,0:T(8,128)(2,1)S(1)}, bf16[88,2048]{1,0:T(8,128)(2,1)}, u32[]{:S(2)}) copy-start(bf16[88,2048]{1,0:T(8,128)(2,1)} %param.29) | copy-start | bytes 1081348
  270.7 114.9 %copy-start.84 = (f32[128]{0:T(128)}, f32[128]{0:T(128)S(1)}, u32[]{:S(2)}) copy-start(f32[128]{0:T(128)S(1)} %get-tuple-element.168) | copy-start | bytes 1540
  270.7 121.5 %copy-start.80 = (f32[128]{0:T(128)}, f32[128]{0:T(128)S(1)}, u32[]{:S(2)}) copy-start(f32[128]{0:T(128)S(1)} %get-tuple-element.182) | copy-start | bytes 1540
  270.8 118.9 %copy-start.67 = (f32[128]{0:T(128)}, f32[128]{0:T(128)S(1)}, u32[]{:S(2)}) copy-start(f32[128]{0:T(128)S(1)} %fusion.34) | copy-start | bytes 1540
  389.8 8.2 copy-start.82
  391.2 6.9 copy-start.59
  391.2 6.9 copy-start.70
  539.8 115.7 %all-to-all-start = ((f32[32,1,128]{2,1,0:T(1,128)}), f32[32,1,128]{2,1,0:T(1,128)}, u32[]{:S(2)}, u32[]{:S(2)}) async-start(f32[32,1,128]{2,1,0:T(1,128)} %bitcast.182), calls=%async_computation | async-start | bytes 32768 | tf_op jit(solution)/shard_map/all_to_all | solution.py:1441
  650.6 7.0 copy-start.9
  650.6 7.0 copy-start.17
  650.7 7.0 copy-start.57
  650.7 7.0 copy-start.68
  652.0 8.0 copy-start.85
  652.0 9.0 copy-start.27
  660.0 44.3 %copy-start.46 = (bf16[4,64,2048]{2,1,0:T(8,128)(2,1)S(1)}, bf16[4,64,2048]{2,1,0:T(8,128)(2,1)}, u32[]{:S(2)}) copy-start(bf16[4,64,2048]{2,1,0:T(8,128)(2,1)} %get-tuple-element.65) | copy-start | bytes 3145732
  660.0 48.8 %copy-start.77 = (f32[128]{0:T(128)}, f32[128]{0:T(128)S(1)}, u32[]{:S(2)}) copy-start(f32[128]{0:T(128)S(1)} %multiply_multiply_fusion.2) | copy-start | bytes 1540
  751.3 64.0 %copy-start.64 = (f32[512]{0:T(512)S(1)}, f32[512]{0:T(512)}, u32[]{:S(2)}) copy-start(f32[512]{0:T(512)} %copy-done.63) | copy-start | bytes 6148
  751.3 64.0 %copy-start.79 = (f32[128]{0:T(128)S(1)}, f32[128]{0:T(128)}, u32[]{:S(2)}) copy-start(f32[128]{0:T(128)} %fusion.35) | copy-start | bytes 1540
  751.3 65.3 %copy-start.83 = (f32[128]{0:T(128)S(1)}, f32[128]{0:T(128)}, u32[]{:S(2)}) copy-start(f32[128]{0:T(128)} %copy-done.82) | copy-start | bytes 1540
  832.6 69.3 %copy-start.53 = (bf16[8,64,256]{2,1,0:T(8,128)(2,1)S(1)}, bf16[8,64,256]{2,1,0:T(8,128)(2,1)}, u32[]{:S(2)}) copy-start(bf16[8,64,256]{2,1,0:T(8,128)(2,1)} %get-tuple-element.88) | copy-start | bytes 786436
  832.6 69.6 %copy-start.61 = (bf16[8,64,128]{2,1,0:T(8,128)(2,1)S(1)}, bf16[8,64,128]{2,1,0:T(8,128)(2,1)}, u32[]{:S(2)}) copy-start(bf16[8,64,128]{2,1,0:T(8,128)(2,1)} %get-tuple-element.89) | copy-start | bytes 393220
  832.6 73.6 %copy-start.81 = (f32[128]{0:T(128)S(1)}, f32[128]{0:T(128)}, u32[]{:S(2)}) copy-start(f32[128]{0:T(128)} %copy-done.80) | copy-start | bytes 1540
  832.6 73.6 %copy-start.86 = (f32[128]{0:T(128)S(1)}, f32[128]{0:T(128)}, u32[]{:S(2)}) copy-start(f32[128]{0:T(128)} %get-tuple-element.167) | copy-start | bytes 1540
  832.6 75.2 %copy-start.40 = (bf16[4,8,64,176]{3,2,1,0:T(8,128)(2,1)S(1)}, bf16[4,8,64,176]{3,2,1,0:T(8,128)(2,1)}, u32[]{:S(2)}) copy-start(bf16[4,8,64,176]{3,2,1,0:T(8,128)(2,1)} %get-tuple-element.93) | copy-start | bytes 2162692
  909.5 9.8 %copy-start.15 = (f32[128,2048]{1,0:T(8,128)S(1)}, f32[128,2048]{1,0:T(8,128)}, u32[]{:S(2)}) copy-start(f32[128,2048]{1,0:T(8,128)} %copy-done.14) | copy-start | bytes 3145732
  909.5 9.8 %copy-start.20 = (bf16[128,2048]{1,0:T(8,128)(2,1)S(1)}, bf16[128,2048]{1,0:T(8,128)(2,1)}, u32[]{:S(2)}) copy-start(bf16[128,2048]{1,0:T(8,128)(2,1)} %refs_5_.1) | copy-start | bytes 1572868
  909.5 9.8 %copy-start.28 = (bf16[128,2048]{1,0:T(8,128)(2,1)S(1)}, bf16[128,2048]{1,0:T(8,128)(2,1)}, u32[]{:S(2)}) copy-start(bf16[128,2048]{1,0:T(8,128)(2,1)} %param.35) | copy-start | bytes 1572868
  909.5 9.8 %copy-start.69 = (f32[128]{0:T(128)S(1)}, f32[128]{0:T(128)}, u32[]{:S(2)}) copy-start(f32[128]{0:T(128)} %copy-done.67) | copy-start | bytes 1540
  909.5 9.8 %copy-start.76 = (f32[128]{0:T(128)S(1)}, f32[128]{0:T(128)}, u32[]{:S(2)}) copy-start(f32[128]{0:T(128)} %fusion.36) | copy-start | bytes 1540
  909.5 9.8 %copy-start.78 = (f32[128]{0:T(128)S(1)}, f32[128]{0:T(128)}, u32[]{:S(2)}) copy-start(f32[128]{0:T(128)} %copy-done.77) | copy-start | bytes 1540
  924.1 12.0 %slice-start = ((s8[5767168]{0:T(1024)(128)(4,1)}), s8[4194304]{0:T(1024)(128)(4,1)S(1)}, s32[]{:S(2)}) async-start(s8[5767168]{0:T(1024)(128)(4,1)} %bitcast.144), calls=%async_computation.2 | async-start | bytes 8388608
  (49 other events, 180.3 us)
Sparse Core Ops, SparseCore 0:
  83.1 132.0 all-gather.1
